TPU v7x, 32 devices: a whole 2x2x4 slice. The times are simulated.
32 devices in a mesh: dp: 8 (over z, core), seq: 4 (over y, x).
Axes of the slice: x: 2, y: 2, z: 4, core: 2. Of those that a mesh axis runs over, the one named last changes fastest.
Arguments:
- frames: bfloat16 [8192, 1024], P(('dp', 'seq')), may hold values from -6 to 6
- out_grad: bfloat16 [8192, 1024], P(('dp', 'seq')), may hold values from -6 to 6
- time_emb: float32 [24, 1024], P('dp'), may hold values from -6 to 6
- clip_len: int32 [8, 3], P('dp'), may hold values from 1 to 512, 1024 in all within a row
- pad_len: int32 [8, 3], P('dp'), may hold values from 0 to 127
- w_qkv: float32 [3, 1024, 1024], P(None, 'seq'), may hold values from -0.21875 to 0.21875
- mom_qkv: float32 [3, 1024, 1024], P(None, 'seq'), may hold values from -28 to 28
- var_qkv: float32 [3, 1024, 1024], P(None, 'seq'), may hold values from 0.8192 to 24.576
- w_out: float32 [1024, 1024], P('seq'), may hold values from -0.875 to 0.875
- mom_out: float32 [1024, 1024], P('seq'), may hold values from -28 to 28
- var_out: float32 [1024, 1024], P('seq'), may hold values from 0.8192 to 24.576
- w_up: float32 [1024, 2048], P('seq'), may hold values from -0.21875 to 0.21875
- mom_up: float32 [1024, 2048], P('seq'), may hold values from -28 to 28
- var_up: float32 [1024, 2048], P('seq'), may hold values from 0.8192 to 24.576
- w_down: float32 [2048, 1024], P('seq'), may hold values from -0.15467961 to 0.15467961
- mom_down: float32 [2048, 1024], P('seq'), may hold values from -28 to 28
- var_down: float32 [2048, 1024], P('seq'), may hold values from 0.8192 to 24.576
- w_mod: float32 [1024, 6144], P('seq'), may hold values from -0.21875 to 0.21875
- mom_mod: float32 [1024, 6144], P('seq'), may hold values from -28 to 28
- var_mod: float32 [1024, 6144], P('seq'), may hold values from 0.8192 to 24.576
- b_mod: float32 [6144], P('seq'), may hold values from -3.5 to 3.5
- mom_bias: float32 [6144], P('seq'), may hold values from -28 to 28
- var_bias: float32 [6144], P('seq'), may hold values from 0.8192 to 24.576
Outputs:
- output: bfloat16 [8192, 1024], P(('dp', 'seq'))
- input_grad: float32 [8192, 1024], P(('dp', 'seq'))
- time_grad: float32 [24, 1024], P('dp')
- grad_qkv: float32 [3, 1024, 1024], P(None, 'seq')
- master_qkv: float32 [3, 1024, 1024], P(None, 'seq')
- moment_qkv: float32 [3, 1024, 1024], P(None, 'seq')
- second_qkv: float32 [3, 1024, 1024], P(None, 'seq')
- grad_out: float32 [1024, 1024], P('seq')
- master_out: float32 [1024, 1024], P('seq')
- moment_out: float32 [1024, 1024], P('seq')
- second_out: float32 [1024, 1024], P('seq')
- grad_up: float32 [1024, 2048], P('seq')
- master_up: float32 [1024, 2048], P('seq')
- moment_up: float32 [1024, 2048], P('seq')
- second_up: float32 [1024, 2048], P('seq')
- grad_down: float32 [2048, 1024], P('seq')
- master_down: float32 [2048, 1024], P('seq')
- moment_down: float32 [2048, 1024], P('seq')
- second_down: float32 [2048, 1024], P('seq')
- grad_mod: float32 [1024, 6144], P('seq')
- master_mod: float32 [1024, 6144], P('seq')
- moment_mod: float32 [1024, 6144], P('seq')
- second_mod: float32 [1024, 6144], P('seq')
- grad_bias: float32 [6144], P('seq')
- master_bias: float32 [6144], P('seq')
- moment_bias: float32 [6144], P('seq')
- second_bias: float32 [6144], P('seq')
Inputs may be any that keep to these rules, and one draw needn't show every extreme that they name: `clip_len`: row g lists the lengths of the 3 clips of data group g in frame order; each row sums to 1024, and the longest clip of every row has exactly 512 frames.
All inputs are finite; a program needn't handle non-finite values.
Results may differ from a plain program's by a relative error of at most 0.03.
The roundings to bfloat16 on the way count: a program that leaves them out, or rounds other values in their place, can miss the bound.
Values may be sent and summed in bfloat16 or wider, within the bound.
A program may use at most 256 MiB of HBM per device.

v0:
```python
import jax
import jax.numpy as jnp
from jax import lax
from jax.sharding import PartitionSpec as P

HEAD_DIM = 64


precise = lax.Precision.HIGHEST
norm_eps = 1e-06
masked_score = -1e30
beta_one = 0.9
beta_two = 0.999
adam_eps = 1e-08
weight_decay = 0.01
step_rate = 1.0
step_count = 10


def layer_norm(values):
    center = values - jnp.mean(values, axis=-1, keepdims=True)
    spread = jnp.mean(center * center, axis=-1, keepdims=True)
    return center * lax.rsqrt(spread + norm_eps)


def modulate(values, shift, scale):
    return layer_norm(values) * (1.0 + scale) + shift


def gelu_tanh(values):
    return jax.nn.gelu(values, approximate=True)


def rotate(values, places, turn_sign):
    frame_count = values.shape[0]
    half_dim = HEAD_DIM // 2
    exponent = jnp.arange(half_dim, dtype=jnp.float32) * (-2.0 / HEAD_DIM)
    frequency = jnp.power(jnp.float32(10000.0), exponent)
    angles = places.astype(jnp.float32)[:, None] * frequency[None, :]
    cos_table = jnp.cos(angles)[:, None, :]
    sin_table = turn_sign * jnp.sin(angles)[:, None, :]
    paired = values.reshape(frame_count, values.shape[1] // HEAD_DIM, half_dim, 2)
    even_part = paired[..., 0]
    odd_part = paired[..., 1]
    turned = jnp.stack(
        [
            even_part * cos_table - odd_part * sin_table,
            odd_part * cos_table + even_part * sin_table,
        ],
        axis=-1,
    )
    return turned.reshape(frame_count, values.shape[1])


def clip_tables(lengths, padding, frame_ids):
    starts = jnp.cumsum(lengths) - lengths
    finish = starts + lengths
    inside = (frame_ids[:, None] >= starts[None, :]) & (frame_ids[:, None] < finish[None, :])
    clip_ids = jnp.arange(lengths.shape[0], dtype=jnp.int32)
    owners = jnp.sum(jnp.where(inside, clip_ids[None, :], 0), axis=1)
    begins = jnp.sum(jnp.where(inside, starts[None, :], 0), axis=1)
    kept_len = jnp.maximum(lengths - padding, 1)
    limits = jnp.sum(jnp.where(inside, kept_len[None, :], 0), axis=1)
    places = frame_ids - begins
    return (inside.astype(jnp.float32), owners, places, places < limits)


def key_window(block_index, block_rows, span, frame_count):
    return jnp.clip(block_index * block_rows - (span - block_rows) // 2, 0, frame_count - span)


def block_inputs(queries, keys_all, values, owners, usable, block_index, block_rows, span):
    frame_count, columns = queries.shape
    heads_here = columns // HEAD_DIM
    row_start = block_index * block_rows
    window = key_window(block_index, block_rows, span, frame_count)
    query_rows = lax.dynamic_slice_in_dim(queries, row_start, block_rows, 0).reshape(
        block_rows, heads_here, HEAD_DIM
    )
    keys_win = keys_all.reshape(span, heads_here, HEAD_DIM)
    values_win = values.reshape(span, heads_here, HEAD_DIM)
    query_owner = lax.dynamic_slice_in_dim(owners, row_start, block_rows, 0)
    score_scale = HEAD_DIM ** (-0.5)
    scores = (
        jnp.einsum("qhd,khd->hqk", query_rows, keys_win, preferred_element_type=jnp.float32)
        * score_scale
    )
    allowed = (query_owner[:, None] == owners[None, :]) & usable[None, :]
    masked = jnp.where(allowed[None], scores, masked_score)
    return (row_start, window, query_rows, keys_win, values_win, masked)


def attend_forward(queries, keys_all, values, owners, usable, span):
    frame_count, columns = queries.shape
    block_rows = min(512, frame_count)

    def one_block(block_index):
        row_start, window, query_rows, keys_win, values_win, masked = block_inputs(
            queries, keys_all, values, owners, usable, block_index, block_rows, span
        )
        row_max = jnp.max(masked, axis=-1, keepdims=True)
        row_total = jnp.sum(jnp.exp(masked - row_max), axis=-1, keepdims=True)
        log_total = row_max + jnp.log(row_total)
        probs_low = jnp.exp(masked - log_total).astype(jnp.bfloat16)
        attended = jnp.einsum(
            "hqk,khd->qhd", probs_low, values_win, preferred_element_type=jnp.float32
        )
        return (attended.astype(jnp.bfloat16).reshape(block_rows, columns), log_total)

    outcome, log_totals = lax.map(one_block, jnp.arange(frame_count // block_rows, dtype=jnp.int32))
    return (outcome.reshape(frame_count, columns), log_totals)


def attend_backward(queries, keys_all, values, grad_attended, log_totals, owners, usable, span):
    frame_count, columns = queries.shape
    heads_here = columns // HEAD_DIM
    block_rows = min(512, frame_count)
    score_scale = HEAD_DIM ** (-0.5)

    def one_block(sums, block_data):
        key_sum, value_sum = sums
        block_index, log_total = block_data
        row_start, window, query_rows, keys_win, values_win, masked = block_inputs(
            queries, keys_all, values, owners, usable, block_index, block_rows, span
        )
        grad_rows = lax.dynamic_slice_in_dim(grad_attended, row_start, block_rows, 0).reshape(
            block_rows, heads_here, HEAD_DIM
        )
        probs_full = jnp.exp(masked - log_total)
        probs_low = probs_full.astype(jnp.bfloat16)
        grad_probs = jnp.einsum(
            "qhd,khd->hqk", grad_rows, values_win, preferred_element_type=jnp.float32
        )
        row_delta = jnp.sum(probs_full * grad_probs, axis=-1, keepdims=True)
        grad_scores = (probs_full * (grad_probs - row_delta)).astype(jnp.bfloat16)
        grad_query = (
            jnp.einsum("hqk,khd->qhd", grad_scores, keys_win, preferred_element_type=jnp.float32)
            * score_scale
        )
        grad_key = (
            jnp.einsum("hqk,qhd->khd", grad_scores, query_rows, preferred_element_type=jnp.float32)
            * score_scale
        )
        grad_value = jnp.einsum(
            "hqk,qhd->khd", probs_low, grad_rows, preferred_element_type=jnp.float32
        )
        old_keys = key_sum
        key_sum = old_keys + grad_key.reshape(span, columns)
        old_values = value_sum
        value_sum = old_values + grad_value.reshape(span, columns)
        return ((key_sum, value_sum), grad_query.astype(jnp.bfloat16).reshape(block_rows, columns))

    zeros = jnp.zeros((frame_count, columns), jnp.float32)
    indices = jnp.arange(frame_count // block_rows, dtype=jnp.int32)
    (key_sum, value_sum), grad_queries = lax.scan(one_block, (zeros, zeros), (indices, log_totals))
    return (
        grad_queries.reshape(frame_count, columns),
        key_sum.astype(jnp.bfloat16),
        value_sum.astype(jnp.bfloat16),
    )


def adam_direction(weight, moment, second, grad):
    moment_new = beta_one * moment + (1.0 - beta_one) * grad
    second_new = beta_two * second + (1.0 - beta_two) * grad * grad
    corrected = moment_new / (1.0 - beta_one**step_count)
    scaled = second_new / (1.0 - beta_two**step_count)
    direction = corrected / (jnp.sqrt(scaled) + adam_eps) + weight_decay * weight
    return (moment_new, second_new, direction)


def local(
    frames,
    out_grad,
    time_emb,
    clip_len,
    pad_len,
    w_qkv,
    mom_qkv,
    var_qkv,
    w_out,
    mom_out,
    var_out,
    w_up,
    mom_up,
    var_up,
    w_down,
    mom_down,
    var_down,
    w_mod,
    mom_mod,
    var_mod,
    b_mod,
    mom_bias,
    var_bias,
):
    seq_count = lax.axis_size("seq")
    seq_rank = lax.axis_index("seq")
    frame_rows = frames.shape[0]
    group_frames = frame_rows * seq_count
    qkv_full, out_full, up_full, down_full, mod_full, bias_full = (
        lax.all_gather(w_qkv.astype(jnp.bfloat16), "seq", axis=1, tiled=True),
        lax.all_gather(w_out.astype(jnp.bfloat16), "seq", axis=0, tiled=True),
        lax.all_gather(w_up.astype(jnp.bfloat16), "seq", axis=0, tiled=True),
        lax.all_gather(w_down.astype(jnp.bfloat16), "seq", axis=0, tiled=True),
        lax.all_gather(w_mod.astype(jnp.bfloat16), "seq", axis=0, tiled=True),
        lax.all_gather(b_mod.astype(jnp.bfloat16), "seq", axis=0, tiled=True),
    )
    inside_all, owners_all, places_all, usable_all = clip_tables(
        clip_len[0], pad_len[0], jnp.arange(group_frames, dtype=jnp.int32)
    )
    row_first = seq_rank * frame_rows
    inside_own = lax.dynamic_slice_in_dim(inside_all, row_first, frame_rows, 0)
    places_own = lax.dynamic_slice_in_dim(places_all, row_first, frame_rows, 0)
    silu_low = jax.nn.silu(time_emb).astype(jnp.bfloat16)
    modulation = jnp.dot(silu_low, mod_full, preferred_element_type=jnp.float32) + bias_full.astype(
        jnp.float32
    )
    mod_rows = jnp.dot(inside_own, modulation, precision=precise)
    shift_attn, scale_attn, gate_attn, shift_ff, scale_ff, gate_ff = jnp.split(mod_rows, 6, axis=1)
    inputs = frames.astype(jnp.float32)
    hidden, attn_norm_back = jax.vjp(modulate, inputs, shift_attn, scale_attn)
    hidden_low = hidden.astype(jnp.bfloat16)
    query_lin = jnp.dot(hidden_low, qkv_full[0], preferred_element_type=jnp.float32)
    key_lin = jnp.dot(hidden_low, qkv_full[1], preferred_element_type=jnp.float32)
    value_lin = jnp.dot(hidden_low, qkv_full[2], preferred_element_type=jnp.float32)
    query_send = rotate(query_lin, places_own, 1.0).astype(jnp.bfloat16)
    key_send = rotate(key_lin, places_own, 1.0).astype(jnp.bfloat16)
    value_send = value_lin.astype(jnp.bfloat16)
    query_heads, key_heads, value_heads = (
        lax.all_to_all(query_send, "seq", split_axis=1, concat_axis=0, tiled=True),
        lax.all_to_all(key_send, "seq", split_axis=1, concat_axis=0, tiled=True),
        lax.all_to_all(value_send, "seq", split_axis=1, concat_axis=0, tiled=True),
    )
    attended_heads, log_totals = attend_forward(
        query_heads, key_heads, value_heads, owners_all, usable_all, group_frames
    )
    attended = lax.all_to_all(attended_heads, "seq", split_axis=0, concat_axis=1, tiled=True)
    attn_proj = jnp.dot(attended, out_full, preferred_element_type=jnp.float32)
    mid = inputs + gate_attn * attn_proj
    hidden_ff, ff_norm_back = jax.vjp(modulate, mid, shift_ff, scale_ff)
    hidden_ff_low = hidden_ff.astype(jnp.bfloat16)
    pre_act = jnp.dot(hidden_ff_low, up_full, preferred_element_type=jnp.float32)
    active, gelu_back = jax.vjp(gelu_tanh, pre_act)
    active_low = active.astype(jnp.bfloat16)
    ff_proj = jnp.dot(active_low, down_full, preferred_element_type=jnp.float32)
    result = mid + gate_ff * ff_proj
    grad_result = out_grad.astype(jnp.float32)
    grad_gate_ff = grad_result * ff_proj
    grad_ff = (grad_result * gate_ff).astype(jnp.bfloat16)
    grad_down_local = jnp.einsum(
        "nf,nd->fd", active_low, grad_ff, preferred_element_type=jnp.float32
    )
    grad_active = jnp.einsum("nd,fd->nf", grad_ff, down_full, preferred_element_type=jnp.float32)
    (grad_pre,) = gelu_back(grad_active)
    grad_pre_low = grad_pre.astype(jnp.bfloat16)
    grad_up_local = jnp.einsum(
        "nd,nf->df", hidden_ff_low, grad_pre_low, preferred_element_type=jnp.float32
    )
    grad_hidden_ff = jnp.einsum(
        "nf,df->nd", grad_pre_low, up_full, preferred_element_type=jnp.float32
    )
    grad_mid_norm, grad_shift_ff, grad_scale_ff = ff_norm_back(grad_hidden_ff)
    grad_mid = grad_result + grad_mid_norm
    grad_gate_attn = grad_mid * attn_proj
    grad_proj = (grad_mid * gate_attn).astype(jnp.bfloat16)
    grad_out_local = jnp.einsum(
        "nd,ne->de", attended, grad_proj, preferred_element_type=jnp.float32
    )
    grad_attended = jnp.einsum(
        "ne,de->nd", grad_proj, out_full, preferred_element_type=jnp.float32
    ).astype(jnp.bfloat16)
    grad_heads = lax.all_to_all(grad_attended, "seq", split_axis=1, concat_axis=0, tiled=True)
    grad_query_heads, grad_key_heads, grad_value_heads = attend_backward(
        query_heads,
        key_heads,
        value_heads,
        grad_heads,
        log_totals,
        owners_all,
        usable_all,
        group_frames,
    )
    grad_query_rows, grad_key_rows, grad_value_rows = (
        lax.all_to_all(grad_query_heads, "seq", split_axis=0, concat_axis=1, tiled=True),
        lax.all_to_all(grad_key_heads, "seq", split_axis=0, concat_axis=1, tiled=True),
        lax.all_to_all(grad_value_heads, "seq", split_axis=0, concat_axis=1, tiled=True),
    )
    grad_query_lin = rotate(grad_query_rows.astype(jnp.float32), places_own, -1.0).astype(
        jnp.bfloat16
    )
    grad_key_lin = rotate(grad_key_rows.astype(jnp.float32), places_own, -1.0).astype(jnp.bfloat16)
    grad_qkv_local = jnp.stack(
        [
            jnp.einsum("nd,ne->de", hidden_low, grad_query_lin, preferred_element_type=jnp.float32),
            jnp.einsum("nd,ne->de", hidden_low, grad_key_lin, preferred_element_type=jnp.float32),
            jnp.einsum(
                "nd,ne->de", hidden_low, grad_value_rows, preferred_element_type=jnp.float32
            ),
        ]
    )
    grad_hidden = jnp.einsum(
        "ne,de->nd", grad_query_lin, qkv_full[0], preferred_element_type=jnp.float32
    )
    grad_hidden = grad_hidden + jnp.einsum(
        "ne,de->nd", grad_key_lin, qkv_full[1], preferred_element_type=jnp.float32
    )
    grad_hidden = grad_hidden + jnp.einsum(
        "ne,de->nd", grad_value_rows, qkv_full[2], preferred_element_type=jnp.float32
    )
    grad_input_norm, grad_shift_attn, grad_scale_attn = attn_norm_back(grad_hidden)
    input_grad = grad_mid + grad_input_norm
    grad_mod_rows = jnp.concatenate(
        [
            grad_shift_attn,
            grad_scale_attn,
            grad_gate_attn,
            grad_shift_ff,
            grad_scale_ff,
            grad_gate_ff,
        ],
        axis=1,
    )
    grad_mod_clip = jnp.einsum("nc,ne->ce", inside_own, grad_mod_rows, precision=precise)
    grad_bias_local = jnp.sum(grad_mod_clip, axis=0)
    grad_mod_local = jnp.einsum(
        "cd,ce->de", silu_low.astype(jnp.float32), grad_mod_clip, precision=precise
    )
    grad_silu = jnp.einsum(
        "ce,de->cd", grad_mod_clip, mod_full.astype(jnp.float32), precision=precise
    )
    time_part = jax.vjp(jax.nn.silu, time_emb)[1](grad_silu)[0]
    time_grad = lax.psum(time_part, "seq")
    shares = (
        lax.psum_scatter(
            grad_qkv_local.astype(jnp.bfloat16), "seq", scatter_dimension=1, tiled=True
        ).astype(jnp.float32),
        lax.psum_scatter(
            grad_out_local.astype(jnp.bfloat16), "seq", scatter_dimension=0, tiled=True
        ).astype(jnp.float32),
        lax.psum_scatter(
            grad_up_local.astype(jnp.bfloat16), "seq", scatter_dimension=0, tiled=True
        ).astype(jnp.float32),
        lax.psum_scatter(
            grad_down_local.astype(jnp.bfloat16), "seq", scatter_dimension=0, tiled=True
        ).astype(jnp.float32),
        lax.psum_scatter(
            grad_mod_local.astype(jnp.bfloat16), "seq", scatter_dimension=0, tiled=True
        ).astype(jnp.float32),
        lax.psum_scatter(
            grad_bias_local.astype(jnp.bfloat16), "seq", scatter_dimension=0, tiled=True
        ).astype(jnp.float32),
    )
    totals = (
        lax.psum(shares[0].astype(jnp.bfloat16), "dp").astype(jnp.float32),
        lax.psum(shares[1].astype(jnp.bfloat16), "dp").astype(jnp.float32),
        lax.psum(shares[2].astype(jnp.bfloat16), "dp").astype(jnp.float32),
        lax.psum(shares[3].astype(jnp.bfloat16), "dp").astype(jnp.float32),
        lax.psum(shares[4].astype(jnp.bfloat16), "dp").astype(jnp.float32),
        lax.psum(shares[5].astype(jnp.bfloat16), "dp").astype(jnp.float32),
    )
    masters = (w_qkv, w_out, w_up, w_down, w_mod, b_mod)
    moments = (mom_qkv, mom_out, mom_up, mom_down, mom_mod, mom_bias)
    seconds = (var_qkv, var_out, var_up, var_down, var_mod, var_bias)
    new_moments = []
    new_seconds = []
    directions = []
    weight_sums = []
    update_sums = []
    for param in range(6):
        moment_new, second_new, direction = adam_direction(
            masters[param], moments[param], seconds[param], totals[param]
        )
        sum_axes = (1, 2) if param == 0 else None
        new_moments.append(moment_new)
        new_seconds.append(second_new)
        directions.append(direction)
        weight_sums.append(jnp.sum(masters[param] * masters[param], axis=sum_axes, keepdims=True))
        update_sums.append(jnp.sum(direction * direction, axis=sum_axes, keepdims=True))
    norm_sums = lax.psum(
        (
            weight_sums[0],
            weight_sums[1],
            weight_sums[2],
            weight_sums[3],
            weight_sums[4],
            weight_sums[5],
            update_sums[0],
            update_sums[1],
            update_sums[2],
            update_sums[3],
            update_sums[4],
            update_sums[5],
        ),
        "seq",
    )
    new_masters = []
    for param in range(6):
        ratio = jnp.sqrt(norm_sums[param]) * lax.rsqrt(norm_sums[param + 6] + 1e-06)
        new_masters.append(masters[param] - step_rate * ratio * directions[param])
    return (
        result.astype(jnp.bfloat16),
        input_grad,
        time_grad,
        totals[0],
        new_masters[0],
        new_moments[0],
        new_seconds[0],
        totals[1],
        new_masters[1],
        new_moments[1],
        new_seconds[1],
        totals[2],
        new_masters[2],
        new_moments[2],
        new_seconds[2],
        totals[3],
        new_masters[3],
        new_moments[3],
        new_seconds[3],
        totals[4],
        new_masters[4],
        new_moments[4],
        new_seconds[4],
        totals[5],
        new_masters[5],
        new_moments[5],
        new_seconds[5],
    )


def solution(mesh):
    return jax.shard_map(
        local,
        mesh=mesh,
        in_specs=(
            P(("dp", "seq"), None),
            P(("dp", "seq"), None),
            P("dp", None),
            P("dp", None),
            P("dp", None),
            P(None, "seq", None),
            P(None, "seq", None),
            P(None, "seq", None),
            P("seq", None),
            P("seq", None),
            P("seq", None),
            P("seq", None),
            P("seq", None),
            P("seq", None),
            P("seq", None),
            P("seq", None),
            P("seq", None),
            P("seq", None),
            P("seq", None),
            P("seq", None),
            P("seq"),
            P("seq"),
            P("seq"),
        ),
        out_specs=(
            P(("dp", "seq"), None),
            P(("dp", "seq"), None),
            P("dp", None),
            P(None, "seq", None),
            P(None, "seq", None),
            P(None, "seq", None),
            P(None, "seq", None),
            P("seq", None),
            P("seq", None),
            P("seq", None),
            P("seq", None),
            P("seq", None),
            P("seq", None),
            P("seq", None),
            P("seq", None),
            P("seq", None),
            P("seq", None),
            P("seq", None),
            P("seq", None),
            P("seq", None),
            P("seq", None),
            P("seq", None),
            P("seq", None),
            P("seq"),
            P("seq"),
            P("seq"),
            P("seq"),
        ),
        check_vma=False,
    )
```

profile of v0, /device:TPU:0, one launch (start us, length us, event | category | flops | bytes accessed | tf_op | source)
XLA Modules:
  0.0 996.2 jit_solution(12467490266329652104)
XLA Ops:
  7.2 3.3 convert_element_type.201
  10.6 4.9 convert_element_type.197
  19.3 10.1 %all-gather = bf16[4,1,1536]{2,1,0:T(2,128)(2,1)S(1)} all-gather(bf16[1,1,1536]{2,1,0:T(2,128)(2,1)S(1)} %reshape.398), channel_id=1, replica_groups=mesh['dp'=8,'seq'=4] {'seq'}, dimensions={0}, use_global_device_ids=true | all-gather | bytes 15360 | tf_op jit(solution)/shard_map/all_gather | solution.py:207
  31.6 52.0 %all-gather.9.cloned.1.call-done = bf16[3,1024,1024]{2,1,0:T(8,128)(2,1)} async-done(((bf16[3,256,1024]{2,1,0:T(8,128)(2,1)}), bf16[3,1024,1024]{2,1,0:T(8,128)(2,1)}) %all-gather.9.cloned.1.call-update) | async-done | bytes 6291472 | tf_op jit(solution)/shard_map/all_gather | solution.py:202
  83.6 4.7 slice_bitcast_fusion.3
  88.3 2.9 copy.132
  93.4 3.2 copy.128
  98.8 109.7 %all-gather.7.cloned.1.call-done = bf16[1024,6144]{1,0:T(8,128)(2,1)} async-done(((bf16[256,6144]{1,0:T(8,128)(2,1)}), bf16[1024,6144]{1,0:T(8,128)(2,1)}) %all-gather.7.cloned.1.call-update) | async-done | bytes 12582928 | tf_op jit(solution)/shard_map/all_gather | solution.py:206
  208.4 6.3 convolution_add_fusion
  214.8 2.7 fusion.66
  217.5 2.7 copy-done.3
  225.3 3.9 all-to-all-start
  230.8 10.5 %all-to-all-done = bf16[256,4,256]{0,2,1:T(8,128)(2,1)S(1)} async-done(((bf16[256,4,256]{0,2,1:T(8,128)(2,1)}), bf16[256,4,256]{0,2,1:T(8,128)(2,1)S(1)}, u32[]{:S(2)}, u32[]{:S(2)}) %all-to-all-start) | async-done | bytes 524320 | tf_op jit(solution)/shard_map/all_to_all | solution.py:231
  241.3 4.1 all-to-all-start.1
  248.8 5.5 all-to-all-done.1
  254.3 3.5 all-to-all-start.2
  260.9 3.9 all-to-all-done.2
  267.0 16.6 %while.27 = (s32[]{:T(128)}, bf16[2,512,256]{2,1,0:T(8,128)(2,1)S(1)}, f32[2,4,512,1]{2,1,3,0:T(4,128)S(1)}, s32[2]{0:T(128)S(1)}, s32[1024]{0:T(1024)S(1)}, /*i...) while((s32[]{:T(128)}, ...), condition=%wide.region_9.10_spmd, body=%wide.region_6.9_spmd.sunk | while | flops 561117184 | bytes 30485704 | solution.py:110
  283.5 17.3 %all_to_all.134 = bf16[4,256,256]{2,1,0:T(8,128)(2,1)} all-to-all(bf16[4,256,256]{2,1,0:T(8,128)(2,1)S(1)} %bitcast.257), channel_id=1, replica_groups=mesh['dp'=8,'seq'=4] {'seq'}, dimensions={0} | all-to-all | bytes 1048576 | tf_op jit(solution)/shard_map/all_to_all | solution.py:238
  302.8 3.7 fusion.88
  306.9 2.7 fusion.55
  309.6 3.7 all-gather.13.cloned.1.call-done
  313.2 4.9 fusion.93
  318.2 49.9 %all-gather.15.cloned.1.call-done = bf16[2048,1024]{1,0:T(8,128)(2,1)} async-done(((bf16[512,1024]{1,0:T(8,128)(2,1)}), bf16[2048,1024]{1,0:T(8,128)(2,1)}) %all-gather.15.cloned.1.call-update) | async-done | bytes 4194320 | tf_op jit(solution)/shard_map/all_gather | solution.py:205
  368.1 5.6 fusion.21
  373.8 3.1 multiply_reduce_fusion.11
  377.3 4.3 fusion.87
  385.7 4.5 convolution_convert_fusion.2
  393.7 4.1 all-to-all-start.4
  398.1 5.8 convolution_convert_fusion.1
  403.9 7.3 all-to-all-done.4
  412.1 54.4 %while.28 = (s32[]{:T(128)}, f32[1024,256]{0,1:T(8,128)S(1)}, f32[1024,256]{0,1:T(8,128)}, bf16[2,512,256]{2,1,0:T(8,128)(2,1)}, s32[2]{0:T(128)S(1)}, /*index=5...) while((s32[]{:T(128)}, f32[1024,256]{0,1:T(8,128)S(1)}, ...), condition=%wide.region_16.17_spmd.clone, body=%wide.region_14.16_spmd.clone.sunk | while | flops 1376253952 | bytes 148181008 | solution.py:155
  414.0 4.5 fusion.169
  419.7 5.8 multiply_reduce_fusion.16
  430.1 3.4 fusion.170
  433.5 3.1 bitcast_add_fusion.3
  440.8 4.5 fusion.169
  446.5 5.8 multiply_reduce_fusion.16
  457.4 3.4 fusion.170
  460.8 3.4 bitcast_add_fusion.3
  466.5 3.6 all-to-all-start.5
  471.0 13.7 %all-to-all-done.5 = bf16[4,256,256]{2,1,0:T(8,128)(2,1)S(1)} async-done(((bf16[4,256,256]{2,1,0:T(8,128)(2,1)}), bf16[4,256,256]{2,1,0:T(8,128)(2,1)S(1)}, u32[]{:S(2)}, u32[]{:S(2)}) %all-to-all-start.5) | async-done | bytes 524320 | tf_op jit(solution)/shard_map/all_to_all | solution.py:285
  484.7 3.9 all-to-all-start.6
  491.7 4.4 all-to-all-done.6
  496.2 4.2 all-to-all-start.7
  506.5 8.0 all-to-all-done.7
  518.1 3.1 pad_maximum_fusion
  526.4 3.0 constant_dynamic-update-slice_fusion.3
  534.3 2.8 fusion.91
  537.1 12.5 %convolution_convert_fusion = bf16[1024,6144]{1,0:T(8,128)(2,1)} fusion(f32[3,6144]{1,0:T(4,128)S(1)} %get-tuple-element.388, f32[3,1024]{1,0:T(4,128)S(1)} %copy-done.67), kind=kOutput, calls=%fused_computation.32 | convolution fusion | flops 232799232 | bytes 12668928 | tf_op jit(solution)/shard_map/cd,ce->de/dot_general | solution.py:326
  550.2 73.6 %reduce-scatter.6.cloned.1.call-done = bf16[3,256,1024]{2,1,0:T(8,128)(2,1)} async-done(((bf16[3,1024,1024]{2,1,0:T(8,128)(2,1)}), bf16[3,256,1024]{2,1,0:T(8,128)(2,1)}) %reduce-scatter.6.cloned.1.call-update) | async-done | bytes 1572880 | tf_op jit(solution)/shard_map/reduce_scatter | solution.py:335
  623.8 123.6 %reduce-scatter.14.cloned.1.call-done = bf16[256,6144]{1,0:T(8,128)(2,1)} async-done(((bf16[1024,6144]{1,0:T(8,128)(2,1)}), bf16[256,6144]{1,0:T(8,128)(2,1)}) %reduce-scatter.14.cloned.1.call-update) | async-done | bytes 3145744 | tf_op jit(solution)/shard_map/reduce_scatter | solution.py:347
  749.3 15.1 %all-reduce = bf16[6144]{0:T(1024)(128)(2,1)S(1)} all-reduce(bf16[6144]{0:T(1024)(128)(2,1)S(1)} %get-tuple-element.387), channel_id=7, replica_groups=mesh['dp'=8,'seq'=4] {'seq'}, use_global_device_ids=true, to_apply=%region_51.52.clone | all-reduce | flops 6144 | bytes 24576
  764.4 14.7 %psum.149 = bf16[1536]{0:T(1024)(128)(2,1)S(1)} all-reduce(bf16[1536]{0:T(1024)(128)(2,1)S(1)} %dynamic-slice.1), channel_id=1, replica_groups=mesh['dp'=8,'seq'=4] {'dp'}, use_global_device_ids=true, to_apply=%region_52.53 | all-reduce | flops 1536 | bytes 6144 | tf_op jit(solution)/shard_map/psum | solution.py:360
  780.4 12.8 %fusion.61 = f32[3,1024]{1,0:T(4,128)S(1)} fusion(f32[3,1024]{1,0:T(4,128)S(1)} %copy-done.67, f32[3,6144]{1,0:T(4,128)S(1)} %get-tuple-element.388, bf16[1024,6144]{1,0:T(8,128)(2,1)} %all-gather.7.cloned.1.call-done), kind=kOutput, calls=%fused_computation.162 | convolution fusion | flops 226520064 | bytes 12681216 | tf_op jit(solution)/shard_map/ce,de->cd/dot_general | solution.py:329
  793.2 113.1 %all-reduce.5.cloned.1.call-done = (bf16[3,256,1024]{2,1,0:T(8,128)(2,1)}, bf16[256,1024]{1,0:T(8,128)(2,1)}, bf16[256,2048]{1,0:T(8,128)(2,1)}, bf16[512,1024]{1,0:T(8,128)(2,1)}, bf16[256,6144]{1,0:T(8,128)(2,1)}) async-done(((bf16[3,256,1024]{2,1,0:T(8,128)(2,1)}, bf16[256,1024]{1,0:T(8,128)(2,1)}, bf16[256,2048]{1,0:T(8,128)(2,1)}, bf16[512,1024]{1,0:T(8,128)(2,1)}, bf16[256,6144]{1,0:T(8,128)(2,1)}), ...) | async-done | bytes 7340048 | tf_op jit(solution)/shard_map/psum | solution.py:355
  906.3 16.5 %multiply_reduce_fusion.1 = (f32[]{:T(128)}, f32[]{:T(128)}, f32[256,6144]{1,0:T(8,128)}, f32[256,6144]{1,0:T(8,128)}, f32[256,6144]{1,0:T(8,128)}) fusion(f32[256,6144]{1,0:T(8,128)} %param.44, f32[256,6144]{1,0:T(8,128)} %param.45, f32[256,6144]{1,0:T(8,128)} %param.46, bf16[256,6144]{1,0:T(8,128)(2,1)} %get-tuple-element.320), kind=kLoop, calls=%fused_computation.38 | loop fusion | flops 28311552 | bytes 40894472 | tf_op jit(solution)/shard_map/reduce_sum | solution.py:379
  923.5 6.4 multiply_reduce_fusion.4
  929.9 4.4 multiply_reduce_fusion.7
  935.2 4.0 multiply_reduce_fusion.5
  939.3 2.6 multiply_reduce_fusion.9
  941.9 17.8 %all-reduce.1 = (f32[3,1024]{1,0:T(4,128)}, f32[3,1,1]{0,2,1:T(1,128)S(1)}, f32[3,1,1]{0,2,1:T(1,128)S(1)}, f32[1,1]{1,0:T(1,128)}, f32[1,1]{1,0:T(1,128)}, /*in...) all-reduce(f32[3,1024]{1,0:T(4,128)S(1)} %fusion.61, ...), channel_id=1, replica_groups=mesh['dp'=8,'seq'=4] {'seq'}, use_global_device_ids=true, to_apply=%region_19.20 | all-reduce | flops 3088 | bytes 24704 | tf_op jit(solution)/shard_map/psum | solution.py:333
  967.1 10.0 %multiply_subtract_fusion = f32[256,6144]{1,0:T(8,128)} fusion(f32[256,6144]{1,0:T(8,128)} %param.44, f32[]{:T(128)} %bitcast.56, f32[256,6144]{1,0:T(8,128)} %get-tuple-element.327, f32[256,6144]{1,0:T(8,128)} %get-tuple-element.326), kind=kLoop, calls=%fused_computation.37 | loop fusion | flops 12582912 | bytes 25165828 | tf_op jit(solution)/shard_map/sub | solution.py:400
  985.8 3.3 multiply_subtract_fusion.1
  (375 shorter events, 107.8 us)
Async XLA Ops:
  7.2 76.4 %all-gather.9.cloned.1.call-start = ((), (), s32[]{:S(2)}) async-start(), calls=%async_computation.14 | async-start | bytes 7864320 | tf_op jit(solution)/shard_map/all_gather | solution.py:202
  10.6 197.9 %all-gather.7.cloned.1.call-start = ((), (), s32[]{:S(2)}) async-start(), calls=%async_computation.13 | async-start | bytes 15728640 | tf_op jit(solution)/shard_map/all_gather | solution.py:206
  15.5 13.9 %copy-start.89 = (s32[1,3]{1,0:T(1,128)S(1)}, s32[1,3]{1,0:T(1,128)}, u32[]{:S(2)}) copy-start(s32[1,3]{1,0:T(1,128)} %param.31) | copy-start | bytes 40
  15.5 14.2 %copy-start.17 = (bf16[256,1024]{1,0:T(8,128)(2,1)S(1)}, bf16[256,1024]{1,0:T(8,128)(2,1)}, u32[]{:S(2)}) copy-start(bf16[256,1024]{1,0:T(8,128)(2,1)} %param.27) | copy-start | bytes 1572868
  15.6 287.3 %all-gather.11.cloned.1.call-start = ((), (), s32[]{:S(2)}) async-start(), calls=%async_computation.15 | async-start | bytes 2621440 | tf_op jit(solution)/shard_map/all_gather | solution.py:203
  17.9 295.3 %all-gather.13.cloned.1.call-start = ((), (), s32[]{:S(2)}) async-start(), calls=%async_computation.16 | async-start | bytes 5242880 | tf_op jit(solution)/shard_map/all_gather | solution.py:204
  29.9 187.6 %copy-start.73 = (f32[256]{0:T(256)}, f32[256]{0:T(256)S(1)}, u32[]{:S(2)}) copy-start(f32[256]{0:T(256)S(1)} %broadcast_multiply_fusion.2) | copy-start | bytes 3076
  30.7 186.7 %copy-start.82 = (f32[256]{0:T(256)}, f32[256]{0:T(256)S(1)}, u32[]{:S(2)}) copy-start(f32[256]{0:T(256)S(1)} %fusion.68) | copy-start | bytes 3076
  30.8 184.0 %copy-start.81 = (pred[1024,3]{0,1:T(4,128)(4,1)}, pred[1024,3]{0,1:T(4,128)(4,1)S(1)}, u32[]{:S(2)}) copy-start(pred[1024,3]{0,1:T(4,128)(4,1)S(1)} %fusion.62) | copy-start | bytes 9220
  31.6 191.7 %copy-start.64 = (f32[256,32]{0,1:T(8,128)}, f32[256,32]{0,1:T(8,128)S(1)}, u32[]{:S(2)}) copy-start(f32[256,32]{0,1:T(8,128)S(1)} %get-tuple-element.379) | copy-start | bytes 98308
  96.6 111.9 %copy-start.66 = (f32[3,1024]{1,0:T(4,128)S(1)}, f32[3,1024]{1,0:T(4,128)}, u32[]{:S(2)}) copy-start(f32[3,1024]{1,0:T(4,128)} %param.29) | copy-start | bytes 36868
  221.8 23.7 %copy-start.30 = (bf16[256,1024]{1,0:T(8,128)(2,1)}, bf16[256,1024]{1,0:T(8,128)(2,1)S(1)}, u32[]{:S(2)}) copy-start(bf16[256,1024]{1,0:T(8,128)(2,1)S(1)} %fusion.48) | copy-start | bytes 1572868
  225.3 16.0 %all-to-all-start = ((bf16[256,4,256]{0,2,1:T(8,128)(2,1)}), bf16[256,4,256]{0,2,1:T(8,128)(2,1)S(1)}, u32[]{:S(2)}, u32[]{:S(2)}) async-start(bf16[256,4,256]{0,2,1:T(8,128)(2,1)} %convert_element_type.203), calls=%async_computation | async-start | bytes 1048576 | tf_op jit(solution)/shard_map/all_to_all | solution.py:231
  241.3 13.0 %all-to-all-start.1 = ((bf16[256,4,256]{0,2,1:T(8,128)(2,1)}), bf16[256,4,256]{0,2,1:T(8,128)(2,1)}, u32[]{:S(2)}, u32[]{:S(2)}) async-start(bf16[256,4,256]{0,2,1:T(8,128)(2,1)} %convert_element_type.204), calls=%async_computation.1 | async-start | bytes 1048576 | tf_op jit(solution)/shard_map/all_to_all | solution.py:232
  245.5 12.3 %copy-start.11 = (f32[512,1024]{1,0:T(8,128)S(1)}, f32[512,1024]{1,0:T(8,128)}, u32[]{:S(2)}) copy-start(f32[512,1024]{1,0:T(8,128)} %param.41) | copy-start | bytes 6291460
  254.3 10.6 %all-to-all-start.2 = ((bf16[256,4,256]{2,0,1:T(8,128)(2,1)}), bf16[256,4,256]{2,0,1:T(8,128)(2,1)S(1)}, u32[]{:S(2)}, u32[]{:S(2)}) async-start(bf16[256,4,256]{2,0,1:T(8,128)(2,1)} %bitcast.181), calls=%async_computation.2 | async-start | bytes 1048576 | tf_op jit(solution)/shard_map/all_to_all | solution.py:233
  257.8 110.3 %all-gather.15.cloned.1.call-start = ((), (), s32[]{:S(2)}) async-start(), calls=%async_computation.17 | async-start | bytes 5242880 | tf_op jit(solution)/shard_map/all_gather | solution.py:205
  259.0 290.8 %reduce-scatter.8.cloned.1.call-start = ((), (), s32[]{:S(2)}) async-start(), calls=%async_computation.19 | async-start | bytes 2621440 | tf_op jit(solution)/shard_map/reduce_scatter | solution.py:338
  267.0 35.9 %copy-start.18 = (bf16[256,1024]{1,0:T(8,128)(2,1)S(1)}, bf16[256,1024]{1,0:T(8,128)(2,1)}, u32[]{:S(2)}) copy-start(bf16[256,1024]{1,0:T(8,128)(2,1)} %param.27) | copy-start | bytes 1572868
  306.6 70.4 %copy-start.20 = (f32[256,1024]{1,0:T(8,128)}, f32[256,1024]{1,0:T(8,128)S(1)}, u32[]{:S(2)}) copy-start(f32[256,1024]{1,0:T(8,128)S(1)} %get-tuple-element.346) | copy-start | bytes 3145732
  306.6 70.4 %copy-start.75 = (f32[256]{0:T(256)}, f32[256]{0:T(256)S(1)}, u32[]{:S(2)}) copy-start(f32[256]{0:T(256)S(1)} %broadcast_multiply_fusion.1) | copy-start | bytes 3076
  306.8 70.1 %copy-start.77 = (f32[256]{0:T(256)}, f32[256]{0:T(256)S(1)}, u32[]{:S(2)}) copy-start(f32[256]{0:T(256)S(1)} %fusion.69) | copy-start | bytes 3076
  309.6 58.5 %copy-start.32 = (bf16[256,1024]{1,0:T(8,128)(2,1)S(1)}, bf16[256,1024]{1,0:T(8,128)(2,1)}, u32[]{:S(2)}) copy-start(bf16[256,1024]{1,0:T(8,128)(2,1)} %param.28) | copy-start | bytes 1572868
  368.1 5.6 copy-start.90
  383.6 6.7 copy-start.55
  385.6 164.1 %reduce-scatter.10.cloned.1.call-start = ((), (), s32[]{:S(2)}) async-start(), calls=%async_computation.20 | async-start | bytes 5242880 | tf_op jit(solution)/shard_map/reduce_scatter | solution.py:341
  390.3 7.8 copy-start.33
  393.7 17.6 %all-to-all-start.4 = ((bf16[256,4,256]{2,0,1:T(8,128)(2,1)}), bf16[256,4,256]{2,0,1:T(8,128)(2,1)}, u32[]{:S(2)}, u32[]{:S(2)}) async-start(bf16[256,4,256]{2,0,1:T(8,128)(2,1)} %bitcast.255), calls=%async_computation.4 | async-start | bytes 1048576 | tf_op jit(solution)/shard_map/all_to_all | solution.py:273
  397.8 152.3 %reduce-scatter.12.cloned.1.call-start = ((), (), s32[]{:S(2)}) async-start(), calls=%async_computation.21 | async-start | bytes 5242880 | tf_op jit(solution)/shard_map/reduce_scatter | solution.py:344
  412.1 6.4 copy-start.9
  412.1 7.5 copy-start.7
  419.6 5.9 copy-start.5
  419.6 5.8 slice-start
  419.7 6.1 slice-start.1
  438.9 6.4 copy-start.9
  438.9 7.6 copy-start.7
  446.5 5.9 copy-start.5
  446.5 5.8 slice-start
  446.5 6.5 slice-start.1
  466.5 22.1 %copy-start.2 = (f32[1024,256]{0,1:T(8,128)S(1)}, f32[1024,256]{0,1:T(8,128)}, u32[]{:S(2)}) copy-start(f32[1024,256]{0,1:T(8,128)} %get-tuple-element.143) | copy-start | bytes 3145732
  466.5 18.2 %all-to-all-start.5 = ((bf16[4,256,256]{2,1,0:T(8,128)(2,1)}), bf16[4,256,256]{2,1,0:T(8,128)(2,1)S(1)}, u32[]{:S(2)}, u32[]{:S(2)}) async-start(bf16[4,256,256]{2,1,0:T(8,128)(2,1)} %bitcast.256), calls=%async_computation.5 | async-start | bytes 1048576 | tf_op jit(solution)/shard_map/all_to_all | solution.py:285
  484.7 11.4 %all-to-all-start.6 = ((bf16[4,256,256]{1,2,0:T(8,128)(2,1)}), bf16[4,256,256]{1,2,0:T(8,128)(2,1)S(1)}, u32[]{:S(2)}, u32[]{:S(2)}) async-start(bf16[4,256,256]{1,2,0:T(8,128)(2,1)} %bitcast.179), calls=%async_computation.6 | async-start | bytes 1048576 | tf_op jit(solution)/shard_map/all_to_all | solution.py:286
  496.2 18.3 %all-to-all-start.7 = ((bf16[4,256,256]{2,1,0:T(8,128)(2,1)}), bf16[4,256,256]{2,1,0:T(8,128)(2,1)}, u32[]{:S(2)}, u32[]{:S(2)}) async-start(bf16[4,256,256]{2,1,0:T(8,128)(2,1)} %bitcast.36), calls=%async_computation.7 | async-start | bytes 1048576 | tf_op jit(solution)/shard_map/all_to_all | solution.py:287
  500.4 123.4 %reduce-scatter.6.cloned.1.call-start = ((), (), s32[]{:S(2)}) async-start(), calls=%async_computation.18 | async-start | bytes 7864320 | tf_op jit(solution)/shard_map/reduce_scatter | solution.py:335
  504.9 10.8 %copy-start.31 = (bf16[256,1024]{1,0:T(8,128)(2,1)S(1)}, bf16[256,1024]{1,0:T(8,128)(2,1)}, u32[]{:S(2)}) copy-start(bf16[256,1024]{1,0:T(8,128)(2,1)} %copy-done.30) | copy-start | bytes 1572868
  521.2 226.2 %reduce-scatter.14.cloned.1.call-start = ((), (), s32[]{:S(2)}) async-start(), calls=%async_computation.22 | async-start | bytes 15728640 | tf_op jit(solution)/shard_map/reduce_scatter | solution.py:347
  549.7 356.7 %all-reduce.5.cloned.1.call-start = ((), (), s32[]{:S(2)}) async-start(), calls=%async_computation.23 | async-start | bytes 14680064 | tf_op jit(solution)/shard_map/psum | solution.py:355
  747.4 31.7 %copy-start.70 = (f32[1536]{0:T(1024)S(1)}, f32[1536]{0:T(1024)}, u32[]{:S(2)}) copy-start(f32[1536]{0:T(1024)} %param.47) | copy-start | bytes 18436
  747.4 31.7 %copy-start.86 = (f32[1536]{0:T(1024)S(1)}, f32[1536]{0:T(1024)}, u32[]{:S(2)}) copy-start(f32[1536]{0:T(1024)} %param.48) | copy-start | bytes 18436
  747.4 31.7 %copy-start.87 = (f32[1536]{0:T(1024)S(1)}, f32[1536]{0:T(1024)}, u32[]{:S(2)}) copy-start(f32[1536]{0:T(1024)} %param.49) | copy-start | bytes 18436
  780.4 186.1 %copy-start.71 = (f32[1536]{0:T(1024)}, f32[1536]{0:T(1024)S(1)}, u32[]{:S(2)}) copy-start(f32[1536]{0:T(1024)S(1)} %get-tuple-element.323) | copy-start | bytes 18436
  780.4 186.1 %copy-start.72 = (f32[1536]{0:T(1024)}, f32[1536]{0:T(1024)S(1)}, u32[]{:S(2)}) copy-start(f32[1536]{0:T(1024)S(1)} %get-tuple-element.324) | copy-start | bytes 18436
  906.3 16.5 %copy-start.4 = (f32[3,256,1024]{2,1,0:T(8,128)S(1)}, f32[3,256,1024]{2,1,0:T(8,128)}, u32[]{:S(2)}) copy-start(f32[3,256,1024]{2,1,0:T(8,128)} %param.32) | copy-start | bytes 9437188
  906.3 16.5 %copy-start.44 = (f32[3,256,1024]{2,1,0:T(8,128)S(1)}, f32[3,256,1024]{2,1,0:T(8,128)}, u32[]{:S(2)}) copy-start(f32[3,256,1024]{2,1,0:T(8,128)} %param.33) | copy-start | bytes 9437188
  906.3 16.5 %copy-start.45 = (f32[3,256,1024]{2,1,0:T(8,128)S(1)}, f32[3,256,1024]{2,1,0:T(8,128)}, u32[]{:S(2)}) copy-start(f32[3,256,1024]{2,1,0:T(8,128)} %param.34) | copy-start | bytes 9437188
  906.3 17.1 %copy-start.56 = (bf16[3,256,1024]{2,1,0:T(8,128)(2,1)S(1)}, bf16[3,256,1024]{2,1,0:T(8,128)(2,1)}, u32[]{:S(2)}) copy-start(bf16[3,256,1024]{2,1,0:T(8,128)(2,1)} %get-tuple-element.316) | copy-start | bytes 4718596
  923.5 6.4 copy-start.15
  923.5 6.4 copy-start.51
  923.5 6.4 copy-start.52
  923.5 6.4 copy-start.61
  929.9 5.3 copy-start.60
  967.1 10.0 %copy-start.13 = (f32[512,1024]{1,0:T(8,128)S(1)}, f32[512,1024]{1,0:T(8,128)}, u32[]{:S(2)}) copy-start(f32[512,1024]{1,0:T(8,128)} %param.41) | copy-start | bytes 6291460
  967.1 10.0 %copy-start.28 = (f32[512,1024]{1,0:T(8,128)S(1)}, f32[512,1024]{1,0:T(8,128)}, u32[]{:S(2)}) copy-start(f32[512,1024]{1,0:T(8,128)} %get-tuple-element.329) | copy-start | bytes 6291460
  967.1 10.0 %copy-start.29 = (f32[512,1024]{1,0:T(8,128)S(1)}, f32[512,1024]{1,0:T(8,128)}, u32[]{:S(2)}) copy-start(f32[512,1024]{1,0:T(8,128)} %get-tuple-element.330) | copy-start | bytes 6291460
  (60 other events, 163.7 us)
Sparse Core Ops, SparseCore 0:
  10.7 72.8 all-gather.8
  86.0 122.3 all-gather.6
  210.9 42.7 all-gather.10
  255.9 57.2 all-gather.12
  315.5 52.5 all-gather.14
  385.8 40.7 reduce-scatter.7
  430.1 58.1 reduce-scatter.9
  491.9 58.2 reduce-scatter.11
  553.7 70.0 reduce-scatter.5
  626.7 120.6 reduce-scatter.13
  750.1 156.1 all-reduce.4
where the time goes:
time: 1010 us; the launch traced here: 996 us
  waiting for transfers between devices  580 us (57%)
  matrix products  128 us (13%)
  other arithmetic  103 us (10%)
  blocking collectives  74.9 us (7%)
  local copies, waits for them, and re-layouts  56.7 us (6%)
  starting transfers between devices  28.2 us (3%)
  between operations  23.2 us (2%)
    reduce_scatter x1, waiting for transfers between devices, local(): lax.psum_scatter(grad_mod_local.astype(jnp.bfloat16), 'seq', scatter_dime...  124 us
    psum x1, waiting for transfers between devices, local(): lax.psum(shares[0].astype(jnp.bfloat16), 'dp').astype(jnp.float32)  113 us
    all_gather x1, waiting for transfers between devices, local(): lax.all_gather(w_mod.astype(jnp.bfloat16), 'seq', axis=0, tiled=True)  110 us
    reduce_scatter x1, waiting for transfers between devices, local(): lax.psum_scatter(grad_qkv_local.astype(jnp.bfloat16), 'seq', scatter_dime...  73.6 us
    all_gather x1, waiting for transfers between devices, local(): lax.all_gather(w_qkv.astype(jnp.bfloat16), 'seq', axis=1, tiled=True)  52 us
    all_gather x1, waiting for transfers between devices, local(): lax.all_gather(w_down.astype(jnp.bfloat16), 'seq', axis=0, tiled=True)  49.9 us
    reduce_sum x5, other arithmetic, local(): jnp.sum(direction * direction, axis=sum_axes, keepdims=True)  28.8 us
    sub x6, other arithmetic, local(): new_masters.append(masters[param] - step_rate * ratio * directions[param])  20.3 us
  transfers between devices with their start and end apart: 18, of which 15 were waited for; matrix products, arithmetic and copies ran while one was open for 20% of the time, Pallas kernels for 0%

commit v1 on v0

--- a/solution.py
+++ b/solution.py
@@ -198,14 +198,16 @@
     seq_rank = lax.axis_index("seq")
     frame_rows = frames.shape[0]
     group_frames = frame_rows * seq_count
-    qkv_full, out_full, up_full, down_full, mod_full, bias_full = (
+    qkv_full, out_full, up_full, down_full, bias_full = (
         lax.all_gather(w_qkv.astype(jnp.bfloat16), "seq", axis=1, tiled=True),
         lax.all_gather(w_out.astype(jnp.bfloat16), "seq", axis=0, tiled=True),
         lax.all_gather(w_up.astype(jnp.bfloat16), "seq", axis=0, tiled=True),
         lax.all_gather(w_down.astype(jnp.bfloat16), "seq", axis=0, tiled=True),
-        lax.all_gather(w_mod.astype(jnp.bfloat16), "seq", axis=0, tiled=True),
         lax.all_gather(b_mod.astype(jnp.bfloat16), "seq", axis=0, tiled=True),
     )
+    mod_low = w_mod.astype(jnp.bfloat16)
+    mod_rows_here = w_mod.shape[0]
+    mod_first = seq_rank * mod_rows_here
     inside_all, owners_all, places_all, usable_all = clip_tables(
         clip_len[0], pad_len[0], jnp.arange(group_frames, dtype=jnp.int32)
     )
@@ -213,9 +215,10 @@
     inside_own = lax.dynamic_slice_in_dim(inside_all, row_first, frame_rows, 0)
     places_own = lax.dynamic_slice_in_dim(places_all, row_first, frame_rows, 0)
     silu_low = jax.nn.silu(time_emb).astype(jnp.bfloat16)
-    modulation = jnp.dot(silu_low, mod_full, preferred_element_type=jnp.float32) + bias_full.astype(
-        jnp.float32
-    )
+    silu_part = lax.dynamic_slice_in_dim(silu_low, mod_first, mod_rows_here, 1)
+    modulation = lax.psum(
+        jnp.dot(silu_part, mod_low, preferred_element_type=jnp.float32), "seq"
+    ) + bias_full.astype(jnp.float32)
     mod_rows = jnp.dot(inside_own, modulation, precision=precise)
     shift_attn, scale_attn, gate_attn, shift_ff, scale_ff, gate_ff = jnp.split(mod_rows, 6, axis=1)
     inputs = frames.astype(jnp.float32)
@@ -321,16 +324,23 @@
         ],
         axis=1,
     )
-    grad_mod_clip = jnp.einsum("nc,ne->ce", inside_own, grad_mod_rows, precision=precise)
-    grad_bias_local = jnp.sum(grad_mod_clip, axis=0)
-    grad_mod_local = jnp.einsum(
-        "cd,ce->de", silu_low.astype(jnp.float32), grad_mod_clip, precision=precise
-    )
-    grad_silu = jnp.einsum(
-        "ce,de->cd", grad_mod_clip, mod_full.astype(jnp.float32), precision=precise
-    )
-    time_part = jax.vjp(jax.nn.silu, time_emb)[1](grad_silu)[0]
-    time_grad = lax.psum(time_part, "seq")
+    grad_mod_clip = lax.psum(
+        jnp.einsum("nc,ne->ce", inside_own, grad_mod_rows, precision=precise), "seq"
+    )
+    grad_mod_all = lax.all_gather(grad_mod_clip, "dp", axis=0, tiled=True)
+    silu_all = lax.all_gather(silu_part, "dp", axis=0, tiled=True)
+    bias_cols = b_mod.shape[0]
+    grad_bias_share = jnp.sum(
+        lax.dynamic_slice_in_dim(grad_mod_all, seq_rank * bias_cols, bias_cols, 1), axis=0
+    )
+    grad_mod_share = jnp.einsum(
+        "cd,ce->de", silu_all.astype(jnp.float32), grad_mod_all, precision=precise
+    )
+    grad_silu_part = jnp.einsum(
+        "ce,de->cd", grad_mod_clip, mod_low.astype(jnp.float32), precision=precise
+    )
+    grad_silu = lax.all_gather(grad_silu_part, "seq", axis=1, tiled=True)
+    time_grad = jax.vjp(jax.nn.silu, time_emb)[1](grad_silu)[0]
     shares = (
         lax.psum_scatter(
             grad_qkv_local.astype(jnp.bfloat16), "seq", scatter_dimension=1, tiled=True
@@ -344,20 +354,14 @@
         lax.psum_scatter(
             grad_down_local.astype(jnp.bfloat16), "seq", scatter_dimension=0, tiled=True
         ).astype(jnp.float32),
-        lax.psum_scatter(
-            grad_mod_local.astype(jnp.bfloat16), "seq", scatter_dimension=0, tiled=True
-        ).astype(jnp.float32),
-        lax.psum_scatter(
-            grad_bias_local.astype(jnp.bfloat16), "seq", scatter_dimension=0, tiled=True
-        ).astype(jnp.float32),
     )
     totals = (
         lax.psum(shares[0].astype(jnp.bfloat16), "dp").astype(jnp.float32),
         lax.psum(shares[1].astype(jnp.bfloat16), "dp").astype(jnp.float32),
         lax.psum(shares[2].astype(jnp.bfloat16), "dp").astype(jnp.float32),
         lax.psum(shares[3].astype(jnp.bfloat16), "dp").astype(jnp.float32),
-        lax.psum(shares[4].astype(jnp.bfloat16), "dp").astype(jnp.float32),
-        lax.psum(shares[5].astype(jnp.bfloat16), "dp").astype(jnp.float32),
+        grad_mod_share,
+        grad_bias_share,
     )
     masters = (w_qkv, w_out, w_up, w_down, w_mod, b_mod)
     moments = (mom_qkv, mom_out, mom_up, mom_down, mom_mod, mom_bias)

time: 1010 us -> 855 us (0.85)
  waiting for transfers between devices: 580 us -> 465 us
  other arithmetic: 103 us -> 78.6 us
  matrix products: 128 us -> 117 us
    reduce_scatter x1 -> x0, waiting for transfers between devices: 124 us -> none  [local(): lax.psum_scatter(grad_mod_local.astype(jnp.bfloat16), 'seq', scatter_dime...]
    all_gather x1 -> x0, waiting for transfers between devices: 110 us -> none  [local(): lax.all_gather(w_mod.astype(jnp.bfloat16), 'seq', axis=0, tiled=True)]
    reduce_scatter x1, waiting for transfers between devices: 0.02 us -> 56.2 us  [local(): lax.psum_scatter(grad_up_local.astype(jnp.bfloat16), 'seq', scatter_dimen...]
    reduce_scatter x1, waiting for transfers between devices: 0.38 us -> 56.2 us  [local(): lax.psum_scatter(grad_down_local.astype(jnp.bfloat16), 'seq', scatter_dim...]
    all_gather x0 -> x3, blocking collectives: none -> 37.5 us  [the longest x1 16.3 us: local(): grad_mod_all = lax.all_gather(grad_mod_clip, 'dp', axis=0, tiled=True)]
    psum x0 -> x2, waiting for transfers between devices: none -> 36.3 us  [the longest x1 27.8 us: local(): lax.psum(jnp.dot(silu_part, mod_low, preferred_element_type=jnp.float32),...]
    psum x1, waiting for transfers between devices: 113 us -> 77.3 us  [local(): lax.psum(shares[0].astype(jnp.bfloat16), 'dp').astype(jnp.float32)]
    psum x2 -> x1, blocking collectives: 32.5 us -> 11 us  [local(): lax.psum((weight_sums[0], weight_sums[1], weight_sums[2], weight_sums[3],...]
  transfers between devices with their start and end apart: 18 -> 18, of which waited for: 15 -> 16; matrix products, arithmetic and copies ran while one was open for 20% -> 15% of each run, Pallas kernels for 0% -> 0%
where the time goes in v1:
time: 855 us; the launch traced here: 845 us
  waiting for transfers between devices  465 us (54%)
  matrix products  117 us (14%)
  other arithmetic  78.6 us (9%)
  blocking collectives  74.1 us (9%)
  local copies, waits for them, and re-layouts  57.6 us (7%)
  starting transfers between devices  28.1 us (3%)
  between operations  22.7 us (3%)
    psum x1, waiting for transfers between devices, local(): lax.psum(shares[0].astype(jnp.bfloat16), 'dp').astype(jnp.float32)  77.3 us
    reduce_scatter x1, waiting for transfers between devices, local(): lax.psum_scatter(grad_qkv_local.astype(jnp.bfloat16), 'seq', scatter_dime...  73.4 us
    all_gather x1, waiting for transfers between devices, local(): lax.all_gather(w_qkv.astype(jnp.bfloat16), 'seq', axis=1, tiled=True)  65.8 us
    reduce_scatter x1, waiting for transfers between devices, local(): lax.psum_scatter(grad_up_local.astype(jnp.bfloat16), 'seq', scatter_dimen...  56.2 us
    reduce_scatter x1, waiting for transfers between devices, local(): lax.psum_scatter(grad_down_local.astype(jnp.bfloat16), 'seq', scatter_dim...  56.2 us
    all_gather x1, waiting for transfers between devices, local(): lax.all_gather(w_down.astype(jnp.bfloat16), 'seq', axis=0, tiled=True)  45.8 us
    psum x1, waiting for transfers between devices, local(): lax.psum(jnp.dot(silu_part, mod_low, preferred_element_type=jnp.float32),...  27.8 us
    sub x6, other arithmetic, local(): new_masters.append(masters[param] - step_rate * ratio * directions[param])  21.8 us
  transfers between devices with their start and end apart: 18, of which 16 were waited for; matrix products, arithmetic and copies ran while one was open for 15% of the time, Pallas kernels for 0%

profile of v1, /device:TPU:0, one launch (start us, length us, event | category | flops | bytes accessed | tf_op | source)
XLA Modules:
  0.0 845.2 jit_solution(11395283170139857258)
XLA Ops:
  9.3 4.1 fusion.38
  18.6 9.7 %all-gather = bf16[4,1,1536]{2,1,0:T(2,128)(2,1)S(1)} all-gather(bf16[1,1,1536]{2,1,0:T(2,128)(2,1)S(1)} %reshape.398), channel_id=1, replica_groups=mesh['dp'=8,'seq'=4] {'seq'}, dimensions={0}, use_global_device_ids=true | all-gather | bytes 15360 | tf_op jit(solution)/shard_map/all_gather | solution.py:206
  30.5 27.8 %all-reduce.6.cloned.1.call-done = f32[3,6144]{1,0:T(4,128)} async-done(((f32[3,6144]{1,0:T(4,128)}), f32[3,6144]{1,0:T(4,128)}) %all-reduce.6.cloned.1.call-update) | async-done | bytes 73744 | tf_op jit(solution)/shard_map/psum | solution.py:219
  58.4 3.6 fusion.64
  62.0 2.7 copy-done
  65.0 65.8 %all-gather.8.cloned.1.call-done = bf16[3,1024,1024]{2,1,0:T(8,128)(2,1)} async-done(((bf16[3,256,1024]{2,1,0:T(8,128)(2,1)}), bf16[3,1024,1024]{2,1,0:T(8,128)(2,1)}) %all-gather.8.cloned.1.call-update) | async-done | bytes 6291472 | tf_op jit(solution)/shard_map/all_gather | solution.py:202
  130.8 4.7 slice_bitcast_fusion.3
  135.5 2.9 copy.132
  140.6 2.9 copy.128
  145.7 2.5 fusion.28
  150.9 3.5 all-to-all-start
  156.0 12.9 %all-to-all-done = bf16[256,4,256]{0,2,1:T(8,128)(2,1)S(1)} async-done(((bf16[256,4,256]{0,2,1:T(8,128)(2,1)}), bf16[256,4,256]{0,2,1:T(8,128)(2,1)S(1)}, u32[]{:S(2)}, u32[]{:S(2)}) %all-to-all-start) | async-done | bytes 524320 | tf_op jit(solution)/shard_map/all_to_all | solution.py:234
  169.7 4.1 all-to-all-start.1
  173.8 2.4 fusion.48
  177.1 4.2 all-to-all-done.1
  181.3 4.2 all-to-all-start.2
  189.0 10.1 %all-to-all-done.2 = bf16[256,4,256]{2,0,1:T(8,128)(2,1)} async-done(((bf16[256,4,256]{2,0,1:T(8,128)(2,1)}), bf16[256,4,256]{2,0,1:T(8,128)(2,1)}, u32[]{:S(2)}, u32[]{:S(2)}) %all-to-all-start.2) | async-done | bytes 524320 | tf_op jit(solution)/shard_map/all_to_all | solution.py:236
  201.2 18.7 %while.27 = (s32[]{:T(128)}, bf16[2,512,256]{2,1,0:T(8,128)(2,1)S(1)}, f32[2,4,512,1]{2,1,3,0:T(4,128)S(1)}, s32[2]{0:T(128)S(1)}, s32[1024]{0:T(1024)S(1)}, /*i...) while((s32[]{:T(128)}, ...), condition=%wide.region_10.11_spmd, body=%wide.region_7.10_spmd.sunk | while | flops 561117184 | bytes 30485712 | solution.py:110
  207.1 3.3 fusion.163
  216.4 3.3 fusion.163
  219.9 15.9 %all_to_all.134 = bf16[4,256,256]{2,1,0:T(8,128)(2,1)S(1)} all-to-all(bf16[4,256,256]{2,1,0:T(8,128)(2,1)S(1)} %bitcast.255), channel_id=1, replica_groups=mesh['dp'=8,'seq'=4] {'seq'}, dimensions={0} | all-to-all | bytes 1048576 | tf_op jit(solution)/shard_map/all_to_all | solution.py:241
  236.1 3.7 fusion.95
  243.4 4.8 fusion.99
  248.2 45.8 %all-gather.14.cloned.1.call-done = bf16[2048,1024]{1,0:T(8,128)(2,1)} async-done(((bf16[512,1024]{1,0:T(8,128)(2,1)}), bf16[2048,1024]{1,0:T(8,128)(2,1)}) %all-gather.14.cloned.1.call-update) | async-done | bytes 4194320 | tf_op jit(solution)/shard_map/all_gather | solution.py:205
  294.0 5.6 fusion.21
  299.7 3.3 multiply_reduce_fusion.11
  303.2 4.4 fusion.94
  311.6 4.3 all-to-all-start.4
  315.9 8.2 all-to-all-done.4
  324.9 35.6 %while.28 = (s32[]{:T(128)}, f32[1024,256]{0,1:T(8,128)S(1)}, f32[1024,256]{0,1:T(8,128)S(1)}, bf16[2,512,256]{2,1,0:T(8,128)(2,1)}, s32[2]{0:T(128)S(1)}, /*ind...) while((s32[]{:T(128)}, f32[1024,256]{0,1:T(8,128)S(1)}, ...), condition=%wide.region_17.18_spmd.clone, body=%wide.region_15.17_spmd.clone.sunk | while | flops 1376253952 | bytes 78974200 | solution.py:155
  330.0 2.4 fusion.175
  332.5 4.2 multiply_reduce_fusion.16
  347.8 2.4 fusion.175
  350.3 4.2 multiply_reduce_fusion.16
  360.5 3.5 all-to-all-start.5
  365.9 5.4 all-to-all-done.5
  372.1 3.7 all-to-all-start.6
  382.3 3.5 all-to-all-start.7
  397.4 2.9 constant_dynamic-update-slice_fusion.3
  405.1 3.6 fusion.72
  411.3 5.6 convolution_convert_fusion
  418.0 4.5 convolution_convert_fusion.1
  425.9 3.1 pad_maximum_fusion
  429.7 12.8 %all-gather.1 = bf16[8,3,256]{2,1,0:T(4,128)(2,1)S(1)} all-gather(bf16[1,3,256]{2,1,0:T(4,128)(2,1)S(1)} %bitcast.263), channel_id=1, replica_groups=mesh['dp'=8,'seq'=4] {'dp'}, dimensions={0}, use_global_device_ids=true | all-gather | bytes 13824 | tf_op jit(solution)/shard_map/all_gather | solution.py:331
  442.5 8.5 %all-reduce.8.cloned.1.call-done = f32[3,6144]{1,0:T(4,128)} async-done(((f32[3,6144]{1,0:T(4,128)}), f32[3,6144]{1,0:T(4,128)}) %all-reduce.8.cloned.1.call-update) | async-done | bytes 73744 | tf_op jit(solution)/shard_map/psum | solution.py:327
  451.0 5.4 fusion.36
  456.4 8.4 all_gather.29
  464.8 16.3 %all-gather.2 = f32[8,3,6144]{2,1,0:T(4,128)S(1)} all-gather(f32[1,3,6144]{2,1,0:T(4,128)S(1)} %bitcast.261), channel_id=1, replica_groups=mesh['dp'=8,'seq'=4] {'dp'}, dimensions={0}, use_global_device_ids=true | all-gather | bytes 663552 | tf_op jit(solution)/shard_map/all_gather | solution.py:330
  481.1 8.7 %reduce-scatter.7.cloned.1.call-done = bf16[256,1024]{1,0:T(8,128)(2,1)} async-done(((bf16[1024,1024]{1,0:T(8,128)(2,1)}), bf16[256,1024]{1,0:T(8,128)(2,1)}) %reduce-scatter.7.cloned.1.call-update) | async-done | bytes 524304 | tf_op jit(solution)/shard_map/reduce_scatter | solution.py:348
  489.8 56.2 %reduce-scatter.11.cloned.1.call-done = bf16[512,1024]{1,0:T(8,128)(2,1)} async-done(((bf16[2048,1024]{1,0:T(8,128)(2,1)}), bf16[512,1024]{1,0:T(8,128)(2,1)}) %reduce-scatter.11.cloned.1.call-update) | async-done | bytes 1048592 | tf_op jit(solution)/shard_map/reduce_scatter | solution.py:354
  546.0 56.2 %reduce-scatter.9.cloned.1.call-done = bf16[256,2048]{1,0:T(8,128)(2,1)} async-done(((bf16[1024,2048]{1,0:T(8,128)(2,1)}), bf16[256,2048]{1,0:T(8,128)(2,1)}) %reduce-scatter.9.cloned.1.call-update) | async-done | bytes 1048592 | tf_op jit(solution)/shard_map/reduce_scatter | solution.py:351
  602.2 73.4 %reduce-scatter.5.cloned.1.call-done = bf16[3,256,1024]{2,1,0:T(8,128)(2,1)} async-done(((bf16[3,1024,1024]{2,1,0:T(8,128)(2,1)}), bf16[3,256,1024]{2,1,0:T(8,128)(2,1)}) %reduce-scatter.5.cloned.1.call-update) | async-done | bytes 1572880 | tf_op jit(solution)/shard_map/reduce_scatter | solution.py:345
  678.1 19.4 %multiply_reduce_fusion.1 = (f32[]{:T(128)}, f32[]{:T(128)}, f32[256,6144]{1,0:T(8,128)}, f32[256,6144]{1,0:T(8,128)}, f32[256,6144]{1,0:T(8,128)}) fusion(f32[256,6144]{1,0:T(8,128)} %param.44, f32[256,6144]{1,0:T(8,128)} %param.45, f32[256,6144]{1,0:T(8,128)} %param.46, bf16[24,256]{1,0:T(8,128)(2,1)S(1)} %reshape.401, f32[24,6144]{1,0:T(8,128)} %copy-done.53), kind=kOutput, calls=%fused_computation.36 | convolution fusion | flops 479723520 | bytes 38350856 | tf_op jit(solution)/shard_map/cd,ce->de/dot_general | solution.py:336
  697.5 77.3 %all-reduce.10.cloned.1.call-done = (bf16[3,256,1024]{2,1,0:T(8,128)(2,1)}, bf16[256,1024]{1,0:T(8,128)(2,1)}, bf16[256,2048]{1,0:T(8,128)(2,1)}, bf16[512,1024]{1,0:T(8,128)(2,1)}) async-done(((bf16[3,256,1024]{2,1,0:T(8,128)(2,1)}, bf16[256,1024]{1,0:T(8,128)(2,1)}, bf16[256,2048]{1,0:T(8,128)(2,1)}, bf16[512,1024]{1,0:T(8,128)(2,1)}), (bf16[3,256,1024]{2,1,0:T(8,128)(2,1)}, bf16[256,1024]{1,0:T(8,128)(2,1)}, ...) | async-done | bytes 4194320 | tf_op jit(solution)/shard_map/psum | solution.py:359
  774.9 3.8 multiply_reduce_fusion.9
  779.0 5.4 multiply_reduce_fusion.7
  784.5 4.3 multiply_reduce_fusion.5
  790.8 6.1 multiply_reduce_fusion.4
  797.0 11.0 %all-reduce = (f32[3,1,1]{0,2,1:T(1,128)S(1)}, f32[3,1,1]{0,2,1:T(1,128)S(1)}, f32[1,1]{1,0:T(1,128)}, f32[1,1]{1,0:T(1,128)}, f32[1,1]{1,0:T(1,128)}, /*index=5...) all-reduce(f32[3,1,1]{0,2,1:T(1,128)S(1)} %bitcast.267, ...), channel_id=1, replica_groups=mesh['dp'=8,'seq'=4] {'seq'}, use_global_device_ids=true, to_apply=%region_26.27 | all-reduce | flops 16 | bytes 128 | tf_op jit(solution)/shard_map/psum | solution.py:384
  816.0 3.4 multiply_subtract_fusion.4
  819.4 4.2 multiply_subtract_fusion.3
  823.6 2.4 multiply_subtract_fusion.2
  827.2 3.3 multiply_subtract_fusion.1
  830.5 8.0 multiply_subtract_fusion
  (329 shorter events, 105.5 us)
Async XLA Ops:
  7.2 51.1 %all-reduce.6.cloned.1.call-start = ((), (), s32[]{:S(2)}) async-start(), calls=%async_computation.12 | async-start | bytes 196608 | tf_op jit(solution)/shard_map/psum | solution.py:219
  9.3 4.2 copy-start.1
  13.4 117.4 %all-gather.8.cloned.1.call-start = ((), (), s32[]{:S(2)}) async-start(), calls=%async_computation.13 | async-start | bytes 7864320 | tf_op jit(solution)/shard_map/all_gather | solution.py:202
  14.9 13.5 %copy-start.76 = (s32[1,3]{1,0:T(1,128)S(1)}, s32[1,3]{1,0:T(1,128)}, u32[]{:S(2)}) copy-start(s32[1,3]{1,0:T(1,128)} %param.31) | copy-start | bytes 40
  14.9 13.7 %copy-start.10 = (bf16[256,1024]{1,0:T(8,128)(2,1)S(1)}, bf16[256,1024]{1,0:T(8,128)(2,1)}, u32[]{:S(2)}) copy-start(bf16[256,1024]{1,0:T(8,128)(2,1)} %param.27) | copy-start | bytes 1572868
  14.9 221.1 %all-gather.10.cloned.1.call-start = ((), (), s32[]{:S(2)}) async-start(), calls=%async_computation.14 | async-start | bytes 2621440 | tf_op jit(solution)/shard_map/all_gather | solution.py:203
  17.2 225.4 %all-gather.12.cloned.1.call-start = ((), (), s32[]{:S(2)}) async-start(), calls=%async_computation.15 | async-start | bytes 5242880 | tf_op jit(solution)/shard_map/all_gather | solution.py:204
  28.7 33.2 %copy-start.64 = (f32[256]{0:T(256)}, f32[256]{0:T(256)S(1)}, u32[]{:S(2)}) copy-start(f32[256]{0:T(256)S(1)} %broadcast_multiply_fusion.2) | copy-start | bytes 3076
  29.6 32.3 %copy-start.70 = (f32[256]{0:T(256)}, f32[256]{0:T(256)S(1)}, u32[]{:S(2)}) copy-start(f32[256]{0:T(256)S(1)} %fusion.77) | copy-start | bytes 3076
  29.7 32.3 %copy-start.72 = (pred[1024,3]{0,1:T(4,128)(4,1)}, pred[1024,3]{0,1:T(4,128)(4,1)S(1)}, u32[]{:S(2)}) copy-start(pred[1024,3]{0,1:T(4,128)(4,1)S(1)} %fusion.69) | copy-start | bytes 9220
  30.5 118.4 %copy-start.55 = (f32[256,32]{0,1:T(8,128)}, f32[256,32]{0,1:T(8,128)S(1)}, u32[]{:S(2)}) copy-start(f32[256,32]{0,1:T(8,128)S(1)} %get-tuple-element.375) | copy-start | bytes 98308
  65.0 108.8 %copy-start.21 = (bf16[256,1024]{1,0:T(8,128)(2,1)}, bf16[256,1024]{1,0:T(8,128)(2,1)S(1)}, u32[]{:S(2)}) copy-start(bf16[256,1024]{1,0:T(8,128)(2,1)S(1)} %fusion.52) | copy-start | bytes 1572868
  150.9 17.9 %all-to-all-start = ((bf16[256,4,256]{0,2,1:T(8,128)(2,1)}), bf16[256,4,256]{0,2,1:T(8,128)(2,1)S(1)}, u32[]{:S(2)}, u32[]{:S(2)}) async-start(bf16[256,4,256]{0,2,1:T(8,128)(2,1)} %convert_element_type.187), calls=%async_computation | async-start | bytes 1048576 | tf_op jit(solution)/shard_map/all_to_all | solution.py:234
  169.7 11.6 %all-to-all-start.1 = ((bf16[256,4,256]{0,2,1:T(8,128)(2,1)}), bf16[256,4,256]{0,2,1:T(8,128)(2,1)}, u32[]{:S(2)}, u32[]{:S(2)}) async-start(bf16[256,4,256]{0,2,1:T(8,128)(2,1)} %convert_element_type.188), calls=%async_computation.1 | async-start | bytes 1048576 | tf_op jit(solution)/shard_map/all_to_all | solution.py:235
  173.8 12.2 %copy-start.7 = (f32[512,1024]{1,0:T(8,128)S(1)}, f32[512,1024]{1,0:T(8,128)}, u32[]{:S(2)}) copy-start(f32[512,1024]{1,0:T(8,128)} %param.41) | copy-start | bytes 6291460
  176.3 10.9 %copy-start.40 = (bf16[256,4,256]{0,2,1:T(8,128)(2,1)S(1)}, bf16[256,4,256]{0,2,1:T(8,128)(2,1)}, u32[]{:S(2)}) copy-start(bf16[256,4,256]{0,2,1:T(8,128)(2,1)} %copy-done.39) | copy-start | bytes 1572868
  181.3 17.9 %all-to-all-start.2 = ((bf16[256,4,256]{2,0,1:T(8,128)(2,1)}), bf16[256,4,256]{2,0,1:T(8,128)(2,1)}, u32[]{:S(2)}, u32[]{:S(2)}) async-start(bf16[256,4,256]{2,0,1:T(8,128)(2,1)} %bitcast.253), calls=%async_computation.2 | async-start | bytes 1048576 | tf_op jit(solution)/shard_map/all_to_all | solution.py:236
  185.5 108.6 %all-gather.14.cloned.1.call-start = ((), (), s32[]{:S(2)}) async-start(), calls=%async_computation.16 | async-start | bytes 5242880 | tf_op jit(solution)/shard_map/all_gather | solution.py:205
  219.9 19.9 %copy-start.3 = (bf16[1024,256]{0,1:T(8,128)(2,1)}, bf16[1024,256]{0,1:T(8,128)(2,1)S(1)}, u32[]{:S(2)}) copy-start(bf16[1024,256]{0,1:T(8,128)(2,1)S(1)} %get-tuple-element.640) | copy-start | bytes 1572868
  236.0 3.8 copy-start.25
  242.6 51.4 %copy-start.23 = (bf16[256,1024]{1,0:T(8,128)(2,1)S(1)}, bf16[256,1024]{1,0:T(8,128)(2,1)}, u32[]{:S(2)}) copy-start(bf16[256,1024]{1,0:T(8,128)(2,1)} %param.28) | copy-start | bytes 1572868
  248.2 51.5 %copy-start.13 = (f32[256,1024]{1,0:T(8,128)S(1)}, f32[256,1024]{1,0:T(8,128)}, u32[]{:S(2)}) copy-start(f32[256,1024]{1,0:T(8,128)} %copy-done.12) | copy-start | bytes 3145732
  294.0 5.6 copy-start.77
  302.9 4.7 copy-start.27
  311.6 12.5 %all-to-all-start.4 = ((bf16[256,4,256]{2,0,1:T(8,128)(2,1)}), bf16[256,4,256]{2,0,1:T(8,128)(2,1)}, u32[]{:S(2)}, u32[]{:S(2)}) async-start(bf16[256,4,256]{2,0,1:T(8,128)(2,1)} %bitcast.180), calls=%async_computation.4 | async-start | bytes 1048576 | tf_op jit(solution)/shard_map/all_to_all | solution.py:276
  360.5 10.8 %all-to-all-start.5 = ((bf16[4,256,256]{2,1,0:T(8,128)(2,1)}), bf16[4,256,256]{2,1,0:T(8,128)(2,1)S(1)}, u32[]{:S(2)}, u32[]{:S(2)}) async-start(bf16[4,256,256]{2,1,0:T(8,128)(2,1)} %bitcast.254), calls=%async_computation.5 | async-start | bytes 1048576 | tf_op jit(solution)/shard_map/all_to_all | solution.py:288
  372.1 10.3 %all-to-all-start.6 = ((bf16[4,256,256]{1,2,0:T(8,128)(2,1)}), bf16[4,256,256]{1,2,0:T(8,128)(2,1)S(1)}, u32[]{:S(2)}, u32[]{:S(2)}) async-start(bf16[4,256,256]{1,2,0:T(8,128)(2,1)} %bitcast.179), calls=%async_computation.6 | async-start | bytes 1048576 | tf_op jit(solution)/shard_map/all_to_all | solution.py:289
  382.3 10.0 %all-to-all-start.7 = ((bf16[4,256,256]{2,1,0:T(8,128)(2,1)}), bf16[4,256,256]{2,1,0:T(8,128)(2,1)S(1)}, u32[]{:S(2)}, u32[]{:S(2)}) async-start(bf16[4,256,256]{2,1,0:T(8,128)(2,1)} %bitcast.36), calls=%async_computation.7 | async-start | bytes 1048576 | tf_op jit(solution)/shard_map/all_to_all | solution.py:290
  385.8 65.1 %all-reduce.8.cloned.1.call-start = ((), (), s32[]{:S(2)}) async-start(), calls=%async_computation.17 | async-start | bytes 196608 | tf_op jit(solution)/shard_map/psum | solution.py:327
  405.1 4.1 copy-start.26
  405.1 4.1 copy-start.46
  408.7 81.1 %reduce-scatter.7.cloned.1.call-start = ((), (), s32[]{:S(2)}) async-start(), calls=%async_computation.19 | async-start | bytes 2621440 | tf_op jit(solution)/shard_map/reduce_scatter | solution.py:348
  411.2 134.7 %reduce-scatter.11.cloned.1.call-start = ((), (), s32[]{:S(2)}) async-start(), calls=%async_computation.21 | async-start | bytes 5242880 | tf_op jit(solution)/shard_map/reduce_scatter | solution.py:354
  417.0 185.2 %reduce-scatter.9.cloned.1.call-start = ((), (), s32[]{:S(2)}) async-start(), calls=%async_computation.20 | async-start | bytes 5242880 | tf_op jit(solution)/shard_map/reduce_scatter | solution.py:351
  422.5 253.1 %reduce-scatter.5.cloned.1.call-start = ((), (), s32[]{:S(2)}) async-start(), calls=%async_computation.18 | async-start | bytes 7864320 | tf_op jit(solution)/shard_map/reduce_scatter | solution.py:345
  429.0 345.8 %all-reduce.10.cloned.1.call-start = ((), (), s32[]{:S(2)}) async-start(), calls=%async_computation.22 | async-start | bytes 8388608 | tf_op jit(solution)/shard_map/psum | solution.py:359
  451.0 13.9 %copy-start.54 = (f32[3,6144]{1,0:T(4,128)S(1)}, f32[3,6144]{1,0:T(4,128)}, u32[]{:S(2)}) copy-start(f32[3,6144]{1,0:T(4,128)} %all-reduce.8.cloned.1.call-done) | copy-start | bytes 221188
  456.4 219.3 %copy-start.58 = (f32[3,1024]{1,0:T(4,128)S(1)}, f32[3,1024]{1,0:T(4,128)}, u32[]{:S(2)}) copy-start(f32[3,1024]{1,0:T(4,128)} %param.29) | copy-start | bytes 36868
  464.8 212.6 %copy-start.60 = (f32[1536]{0:T(1024)S(1)}, f32[1536]{0:T(1024)}, u32[]{:S(2)}) copy-start(f32[1536]{0:T(1024)} %param.47) | copy-start | bytes 18436
  464.8 212.6 %copy-start.73 = (f32[1536]{0:T(1024)S(1)}, f32[1536]{0:T(1024)}, u32[]{:S(2)}) copy-start(f32[1536]{0:T(1024)} %param.48) | copy-start | bytes 18436
  464.8 212.6 %copy-start.74 = (f32[1536]{0:T(1024)S(1)}, f32[1536]{0:T(1024)}, u32[]{:S(2)}) copy-start(f32[1536]{0:T(1024)} %param.49) | copy-start | bytes 18436
  677.4 20.1 %copy-start.61 = (f32[1536]{0:T(1024)}, f32[1536]{0:T(1024)S(1)}, u32[]{:S(2)}) copy-start(f32[1536]{0:T(1024)S(1)} %dynamic-slice_reduce_fusion) | copy-start | bytes 18436
  678.1 137.2 %copy-start.62 = (f32[1536]{0:T(1024)}, f32[1536]{0:T(1024)S(1)}, u32[]{:S(2)}) copy-start(f32[1536]{0:T(1024)S(1)} %get-tuple-element.321) | copy-start | bytes 18436
  678.1 137.2 %copy-start.63 = (f32[1536]{0:T(1024)}, f32[1536]{0:T(1024)S(1)}, u32[]{:S(2)}) copy-start(f32[1536]{0:T(1024)S(1)} %get-tuple-element.322) | copy-start | bytes 18436
  678.1 96.7 %copy-start.17 = (f32[256,1024]{1,0:T(8,128)S(1)}, f32[256,1024]{1,0:T(8,128)}, u32[]{:S(2)}) copy-start(f32[256,1024]{1,0:T(8,128)} %param.35) | copy-start | bytes 3145732
  678.1 96.7 %copy-start.49 = (f32[256,1024]{1,0:T(8,128)S(1)}, f32[256,1024]{1,0:T(8,128)}, u32[]{:S(2)}) copy-start(f32[256,1024]{1,0:T(8,128)} %param.36) | copy-start | bytes 3145732
  678.1 96.7 %copy-start.50 = (f32[256,1024]{1,0:T(8,128)S(1)}, f32[256,1024]{1,0:T(8,128)}, u32[]{:S(2)}) copy-start(f32[256,1024]{1,0:T(8,128)} %param.37) | copy-start | bytes 3145732
  774.8 3.9 copy-start.5
  774.8 3.9 copy-start.41
  774.8 4.1 copy-start.42
  779.0 5.5 copy-start.8
  779.0 5.5 copy-start.43
  779.0 5.5 copy-start.44
  779.0 5.5 copy-start.52
  784.5 4.4 copy-start.2
  784.5 5.1 copy-start.34
  784.5 6.0 copy-start.35
  784.5 6.3 copy-start.47
  807.9 11.4 %copy-start.6 = (f32[256,2048]{1,0:T(8,128)S(1)}, f32[256,2048]{1,0:T(8,128)}, u32[]{:S(2)}) copy-start(f32[256,2048]{1,0:T(8,128)} %param.38) | copy-start | bytes 6291460
  807.9 11.4 %copy-start.18 = (f32[256,2048]{1,0:T(8,128)S(1)}, f32[256,2048]{1,0:T(8,128)}, u32[]{:S(2)}) copy-start(f32[256,2048]{1,0:T(8,128)} %get-tuple-element.328) | copy-start | bytes 6291460
  819.3 4.2 copy-start.9
  819.4 4.2 copy-start.19
  819.4 4.2 copy-start.20
  826.0 4.5 slice-start
  (36 other events, 73.9 us)
Sparse Core Ops, SparseCore 0:
  13.5 44.7 all-reduce.5
  60.8 70.0 all-gather.7
  133.3 40.7 all-gather.9
  176.4 62.7 all-gather.11
  241.4 52.5 all-gather.13
  408.8 42.0 all-reduce.7
  454.5 35.2 reduce-scatter.6
  493.4 52.5 reduce-scatter.10
  549.5 52.5 reduce-scatter.8
  605.6 70.0 reduce-scatter.4
  678.2 96.5 all-reduce.9

commit v2 on v1

--- a/solution.py
+++ b/solution.py
@@ -1,7 +1,7 @@
 import jax
 import jax.numpy as jnp
 from jax import lax
-from jax.sharding import PartitionSpec as P
+from jax.sharding import Mesh, PartitionSpec as P
 
 HEAD_DIM = 64
 
@@ -158,6 +158,40 @@
         key_sum.astype(jnp.bfloat16),
         value_sum.astype(jnp.bfloat16),
     )
+
+
+def butterfly_sum(values, axes, size):
+    step = 1
+    while step < size:
+        values = values + lax.ppermute(values, axes, [(i, i ^ step) for i in range(size)])
+        step *= 2
+    return values
+
+
+def doubling_gather(values, axes, size, index):
+    blocks = values[None]
+    step = 1
+    while step < size:
+        other = lax.ppermute(blocks, axes, [(i, i ^ step) for i in range(size)])
+        low_side = (index // step) % 2 == 0
+        blocks = jnp.concatenate(
+            [jnp.where(low_side, blocks, other), jnp.where(low_side, other, blocks)], axis=0
+        )
+        step *= 2
+    return blocks
+
+
+def gather_rows(shard, row_axis):
+    half = shard.shape[row_axis] // 2
+    core = lax.axis_index("core")
+    piece = lax.dynamic_slice_in_dim(shard, core * half, half, row_axis)
+    return lax.all_gather(piece, ("seq", "core"), axis=row_axis, tiled=True)
+
+
+def reduce_rows(partial, row_axis):
+    piece = lax.psum_scatter(partial, ("seq", "core"), scatter_dimension=row_axis, tiled=True)
+    piece = lax.psum(piece, "z")
+    return lax.all_gather(piece, "core", axis=row_axis, tiled=True)
 
 
 def adam_direction(weight, moment, second, grad):
@@ -198,13 +232,15 @@
     seq_rank = lax.axis_index("seq")
     frame_rows = frames.shape[0]
     group_frames = frame_rows * seq_count
-    qkv_full, out_full, up_full, down_full, bias_full = (
-        lax.all_gather(w_qkv.astype(jnp.bfloat16), "seq", axis=1, tiled=True),
-        lax.all_gather(w_out.astype(jnp.bfloat16), "seq", axis=0, tiled=True),
-        lax.all_gather(w_up.astype(jnp.bfloat16), "seq", axis=0, tiled=True),
-        lax.all_gather(w_down.astype(jnp.bfloat16), "seq", axis=0, tiled=True),
-        lax.all_gather(b_mod.astype(jnp.bfloat16), "seq", axis=0, tiled=True),
-    )
+    dp_count = lax.axis_size(("z", "core"))
+    dp_rank = lax.axis_index(("z", "core"))
+    qkv_full, out_full, up_full, down_full = (
+        gather_rows(w_qkv.astype(jnp.bfloat16), 1),
+        gather_rows(w_out.astype(jnp.bfloat16), 0),
+        gather_rows(w_up.astype(jnp.bfloat16), 0),
+        gather_rows(w_down.astype(jnp.bfloat16), 0),
+    )
+    bias_full = doubling_gather(b_mod.astype(jnp.bfloat16), "seq", seq_count, seq_rank).reshape(-1)
     mod_low = w_mod.astype(jnp.bfloat16)
     mod_rows_here = w_mod.shape[0]
     mod_first = seq_rank * mod_rows_here
@@ -216,8 +252,8 @@
     places_own = lax.dynamic_slice_in_dim(places_all, row_first, frame_rows, 0)
     silu_low = jax.nn.silu(time_emb).astype(jnp.bfloat16)
     silu_part = lax.dynamic_slice_in_dim(silu_low, mod_first, mod_rows_here, 1)
-    modulation = lax.psum(
-        jnp.dot(silu_part, mod_low, preferred_element_type=jnp.float32), "seq"
+    modulation = butterfly_sum(
+        jnp.dot(silu_part, mod_low, preferred_element_type=jnp.float32), "seq", seq_count
     ) + bias_full.astype(jnp.float32)
     mod_rows = jnp.dot(inside_own, modulation, precision=precise)
     shift_attn, scale_attn, gate_attn, shift_ff, scale_ff, gate_ff = jnp.split(mod_rows, 6, axis=1)
@@ -324,11 +360,15 @@
         ],
         axis=1,
     )
-    grad_mod_clip = lax.psum(
-        jnp.einsum("nc,ne->ce", inside_own, grad_mod_rows, precision=precise), "seq"
-    )
-    grad_mod_all = lax.all_gather(grad_mod_clip, "dp", axis=0, tiled=True)
-    silu_all = lax.all_gather(silu_part, "dp", axis=0, tiled=True)
+    grad_mod_clip = butterfly_sum(
+        jnp.einsum("nc,ne->ce", inside_own, grad_mod_rows, precision=precise), "seq", seq_count
+    )
+    grad_mod_all = doubling_gather(grad_mod_clip, ("z", "core"), dp_count, dp_rank).reshape(
+        -1, grad_mod_clip.shape[1]
+    )
+    silu_all = doubling_gather(silu_part, ("z", "core"), dp_count, dp_rank).reshape(
+        -1, silu_part.shape[1]
+    )
     bias_cols = b_mod.shape[0]
     grad_bias_share = jnp.sum(
         lax.dynamic_slice_in_dim(grad_mod_all, seq_rank * bias_cols, bias_cols, 1), axis=0
@@ -339,27 +379,15 @@
     grad_silu_part = jnp.einsum(
         "ce,de->cd", grad_mod_clip, mod_low.astype(jnp.float32), precision=precise
     )
-    grad_silu = lax.all_gather(grad_silu_part, "seq", axis=1, tiled=True)
+    grad_silu = jnp.concatenate(
+        list(doubling_gather(grad_silu_part, "seq", seq_count, seq_rank)), axis=1
+    )
     time_grad = jax.vjp(jax.nn.silu, time_emb)[1](grad_silu)[0]
-    shares = (
-        lax.psum_scatter(
-            grad_qkv_local.astype(jnp.bfloat16), "seq", scatter_dimension=1, tiled=True
-        ).astype(jnp.float32),
-        lax.psum_scatter(
-            grad_out_local.astype(jnp.bfloat16), "seq", scatter_dimension=0, tiled=True
-        ).astype(jnp.float32),
-        lax.psum_scatter(
-            grad_up_local.astype(jnp.bfloat16), "seq", scatter_dimension=0, tiled=True
-        ).astype(jnp.float32),
-        lax.psum_scatter(
-            grad_down_local.astype(jnp.bfloat16), "seq", scatter_dimension=0, tiled=True
-        ).astype(jnp.float32),
-    )
     totals = (
-        lax.psum(shares[0].astype(jnp.bfloat16), "dp").astype(jnp.float32),
-        lax.psum(shares[1].astype(jnp.bfloat16), "dp").astype(jnp.float32),
-        lax.psum(shares[2].astype(jnp.bfloat16), "dp").astype(jnp.float32),
-        lax.psum(shares[3].astype(jnp.bfloat16), "dp").astype(jnp.float32),
+        reduce_rows(grad_qkv_local.astype(jnp.bfloat16), 1).astype(jnp.float32),
+        reduce_rows(grad_out_local.astype(jnp.bfloat16), 0).astype(jnp.float32),
+        reduce_rows(grad_up_local.astype(jnp.bfloat16), 0).astype(jnp.float32),
+        reduce_rows(grad_down_local.astype(jnp.bfloat16), 0).astype(jnp.float32),
         grad_mod_share,
         grad_bias_share,
     )
@@ -381,23 +409,13 @@
         directions.append(direction)
         weight_sums.append(jnp.sum(masters[param] * masters[param], axis=sum_axes, keepdims=True))
         update_sums.append(jnp.sum(direction * direction, axis=sum_axes, keepdims=True))
-    norm_sums = lax.psum(
-        (
-            weight_sums[0],
-            weight_sums[1],
-            weight_sums[2],
-            weight_sums[3],
-            weight_sums[4],
-            weight_sums[5],
-            update_sums[0],
-            update_sums[1],
-            update_sums[2],
-            update_sums[3],
-            update_sums[4],
-            update_sums[5],
-        ),
-        "seq",
-    )
+    packed = jnp.concatenate([jnp.reshape(part, (-1,)) for part in weight_sums + update_sums])
+    packed = butterfly_sum(packed, "seq", seq_count)
+    norm_sums = []
+    offset = 0
+    for part in weight_sums + update_sums:
+        norm_sums.append(packed[offset : offset + part.size].reshape(part.shape))
+        offset += part.size
     new_masters = []
     for param in range(6):
         ratio = jnp.sqrt(norm_sums[param]) * lax.rsqrt(norm_sums[param + 6] + 1e-06)
@@ -434,15 +452,19 @@
 
 
 def solution(mesh):
+    devices = mesh.devices
+    chip_mesh = Mesh(
+        devices.reshape(devices.shape[0] // 2, 2, devices.shape[1]), ("z", "core", "seq")
+    )
     return jax.shard_map(
         local,
-        mesh=mesh,
+        mesh=chip_mesh,
         in_specs=(
-            P(("dp", "seq"), None),
-            P(("dp", "seq"), None),
-            P("dp", None),
-            P("dp", None),
-            P("dp", None),
+            P(("z", "core", "seq"), None),
+            P(("z", "core", "seq"), None),
+            P(("z", "core"), None),
+            P(("z", "core"), None),
+            P(("z", "core"), None),
             P(None, "seq", None),
             P(None, "seq", None),
             P(None, "seq", None),
@@ -463,9 +485,9 @@
             P("seq"),
         ),
         out_specs=(
-            P(("dp", "seq"), None),
-            P(("dp", "seq"), None),
-            P("dp", None),
+            P(("z", "core", "seq"), None),
+            P(("z", "core", "seq"), None),
+            P(("z", "core"), None),
             P(None, "seq", None),
             P(None, "seq", None),
             P(None, "seq", None),

time: 855 us -> 635 us (0.74)
  waiting for transfers between devices: 465 us -> 262 us
  blocking collectives: 74.1 us -> 19.3 us
  starting transfers between devices: 28.1 us -> 63.6 us
    reduce_scatter x4, waiting for transfers between devices: 195 us -> 73.3 us  [reduce_rows(): lax.psum_scatter(partial, ('seq', 'core'), scatter_dimension=row_axis, ti...]
    all_gather x4 -> x7, waiting for transfers between devices: 112 us -> 29.6 us  [the longest x4 29.6 us: gather_rows(): return lax.all_gather(piece, ('seq', 'core'), axis=row_axis, tiled=True)]
    all_gather x4 -> x1, blocking collectives: 47.2 us -> 2.3 us  [reduce_rows(): return lax.all_gather(piece, 'core', axis=row_axis, tiled=True)]
    ppermute x0 -> x16, starting transfers between devices: none -> 24.6 us  [the longest x10 16.4 us: doubling_gather(): other = lax.ppermute(blocks, axes, [(i, i ^ step) for i in range(size)])]
    ppermute x0 -> x16, waiting for transfers between devices: none -> 22.5 us  [the longest x6 17.1 us: butterfly_sum(): lax.ppermute(values, axes, [(i, i ^ step) for i in range(size)])]
    psum x3 -> x1, waiting for transfers between devices: 114 us -> 96.6 us  [reduce_rows(): piece = lax.psum(piece, 'z')]
    reduce_sum x4 -> x5, other arithmetic: 14.3 us -> 27.6 us  [local(): jnp.sum(direction * direction, axis=sum_axes, keepdims=True)]
    reduce_scatter x4, starting transfers between devices: 0.57 us -> 12.2 us  [reduce_rows(): lax.psum_scatter(partial, ('seq', 'core'), scatter_dimension=row_axis, ti...]
  transfers between devices with their start and end apart: 18 -> 35, of which waited for: 16 -> 21; matrix products, arithmetic and copies ran while one was open for 15% -> 31% of each run, Pallas kernels for 0% -> 0%
where the time goes in v2:
time: 635 us; the launch traced here: 628 us
  waiting for transfers between devices  262 us (41%)
  matrix products  113 us (18%)
  other arithmetic  79.6 us (13%)
  local copies, waits for them, and re-layouts  64 us (10%)
  starting transfers between devices  63.6 us (10%)
  between operations  22.7 us (4%)
  blocking collectives  19.3 us (3%)
    psum x1, waiting for transfers between devices, reduce_rows(): piece = lax.psum(piece, 'z')  96.6 us
    reduce_scatter x4, waiting for transfers between devices, reduce_rows(): lax.psum_scatter(partial, ('seq', 'core'), scatter_dimension=row_axis, ti...  73.3 us
    all_gather x4, waiting for transfers between devices, gather_rows(): return lax.all_gather(piece, ('seq', 'core'), axis=row_axis, tiled=True)  29.6 us
    reduce_sum x5, other arithmetic, local(): jnp.sum(direction * direction, axis=sum_axes, keepdims=True)  27.6 us
    sub x6, other arithmetic, local(): new_masters.append(masters[param] - step_rate * ratio * directions[param])  21.8 us
    ppermute x6, waiting for transfers between devices, butterfly_sum(): lax.ppermute(values, axes, [(i, i ^ step) for i in range(size)])  17.1 us
    all_to_all x1, blocking collectives, local(): lax.all_to_all(attended_heads, 'seq', split_axis=0, concat_axis=1, tiled=...  17 us
    dot_general x1, matrix products, local(): jnp.einsum('cd,ce->de', silu_all.astype(jnp.float32), grad_mod_all, preci...  17 us
  transfers between devices with their start and end apart: 35, of which 21 were waited for; matrix products, arithmetic and copies ran while one was open for 31% of the time, Pallas kernels for 0%

profile of v2, /device:TPU:0, one launch (start us, length us, event | category | flops | bytes accessed | tf_op | source)
XLA Modules:
  0.0 627.7 jit_solution(13455193235936842286)
XLA Ops:
  13.8 3.0 collective-permute-start.2
  16.9 3.4 fusion.38
  28.5 5.3 collective-permute-done.1
  33.9 2.7 fusion.68
  36.6 2.7 copy-done
  39.6 21.3 %all-gather.8.cloned.1.call-done = bf16[3,1024,1024]{2,1,0:T(8,128)(2,1)} async-done(((bf16[3,128,1024]{2,1,0:T(8,128)(2,1)}), bf16[3,1024,1024]{2,1,0:T(8,128)(2,1)}) %all-gather.8.cloned.1.call-update) | async-done | bytes 6291472 | tf_op jit(solution)/shard_map/all_gather | solution.py:188
  60.9 4.7 slice_bitcast_fusion.3
  65.6 2.9 copy.145
  70.6 2.9 copy.141
  75.7 2.5 fusion.28
  81.0 3.5 all-to-all-start
  86.0 9.2 %all-to-all-done = bf16[256,4,256]{0,2,1:T(8,128)(2,1)S(1)} async-done(((bf16[256,4,256]{0,2,1:T(8,128)(2,1)}), bf16[256,4,256]{0,2,1:T(8,128)(2,1)S(1)}, u32[]{:S(2)}, u32[]{:S(2)}) %all-to-all-start) | async-done | bytes 524320 | tf_op jit(solution)/shard_map/all_to_all | solution.py:270
  95.2 3.5 all-to-all-start.1
  101.9 5.2 all-to-all-done.1
  107.0 3.5 all-to-all-start.2
  112.7 11.7 %reduce-scatter.7.cloned.1.call-start = ((), (), s32[]{:S(2)}) async-start(), calls=%async_computation.18 | async-start | bytes 2359296 | tf_op jit(solution)/shard_map/reduce_scatter | solution.py:192
  126.3 18.7 %while.27 = (s32[]{:T(128)}, bf16[2,512,256]{2,1,0:T(8,128)(2,1)S(1)}, f32[2,4,512,1]{2,1,3,0:T(4,128)S(1)}, s32[2]{0:T(128)S(1)}, s32[1024]{0:T(1024)S(1)}, /*i...) while((s32[]{:T(128)}, ...), condition=%wide.region_9.10_spmd, body=%wide.region_6.9_spmd.sunk | while | flops 561117184 | bytes 30485712 | solution.py:110
  132.1 3.3 fusion.167
  141.5 3.3 fusion.167
  145.0 17.0 %all_to_all.134 = bf16[4,256,256]{2,1,0:T(8,128)(2,1)S(1)} all-to-all(bf16[4,256,256]{2,1,0:T(8,128)(2,1)S(1)} %bitcast.260), channel_id=1, replica_groups=mesh['z'=4,'core'=2,'seq'=4] {'seq'}, dimensions={0} | all-to-all | bytes 1048576 | tf_op jit(solution)/shard_map/all_to_all | solution.py:277
  162.3 3.6 fusion.101
  166.1 2.5 fusion.62
  168.7 5.0 fusion.106
  173.7 8.3 %all-gather.14.cloned.1.call-done = bf16[2048,1024]{1,0:T(8,128)(2,1)} async-done(((bf16[256,1024]{1,0:T(8,128)(2,1)}), bf16[2048,1024]{1,0:T(8,128)(2,1)}) %all-gather.14.cloned.1.call-update) | async-done | bytes 4194320 | tf_op jit(solution)/shard_map/all_gather | solution.py:188
  182.0 5.6 fusion.21
  187.6 3.1 multiply_reduce_fusion.11
  191.2 4.3 fusion.100
  200.1 5.7 convolution_convert_fusion
  210.1 4.2 all-to-all-start.4
  214.8 4.5 convolution_convert_fusion.1
  219.3 3.7 all-to-all-done.4
  223.9 35.6 %while.28 = (s32[]{:T(128)}, f32[1024,256]{0,1:T(8,128)S(1)}, f32[1024,256]{0,1:T(8,128)S(1)}, bf16[2,512,256]{2,1,0:T(8,128)(2,1)}, s32[2]{0:T(128)S(1)}, /*ind...) while((s32[]{:T(128)}, f32[1024,256]{0,1:T(8,128)S(1)}, ...), condition=%wide.region_16.17_spmd.clone, body=%wide.region_14.16_spmd.clone.sunk | while | flops 1376253952 | bytes 78974200 | solution.py:155
  229.0 2.4 fusion.179
  231.5 4.2 multiply_reduce_fusion.16
  246.8 2.4 fusion.179
  249.3 4.2 multiply_reduce_fusion.16
  259.5 3.5 all-to-all-start.5
  263.9 9.7 %all-to-all-done.5 = bf16[4,256,256]{2,1,0:T(8,128)(2,1)S(1)} async-done(((bf16[4,256,256]{2,1,0:T(8,128)(2,1)}), bf16[4,256,256]{2,1,0:T(8,128)(2,1)S(1)}, u32[]{:S(2)}, u32[]{:S(2)}) %all-to-all-start.5) | async-done | bytes 524320 | tf_op jit(solution)/shard_map/all_to_all | solution.py:324
  273.6 3.6 all-to-all-start.6
  280.4 7.3 %all-to-all-done.6 = bf16[4,256,256]{1,2,0:T(8,128)(2,1)S(1)} async-done(((bf16[4,256,256]{1,2,0:T(8,128)(2,1)}), bf16[4,256,256]{1,2,0:T(8,128)(2,1)S(1)}, u32[]{:S(2)}, u32[]{:S(2)}) %all-to-all-start.6) | async-done | bytes 524320 | tf_op jit(solution)/shard_map/all_to_all | solution.py:325
  287.7 4.1 all-to-all-start.7
  298.0 4.4 all-to-all-done.7
  305.9 3.1 pad_maximum_fusion
  317.0 2.6 fusion.45
  319.7 3.2 constant_dynamic-update-slice_fusion.3
  327.8 2.8 fusion.81
  334.6 2.6 collective-permute-done.4
  338.9 5.2 collective-permute-done.5
  344.2 5.4 fusion.51
  354.9 7.7 %reduce-scatter.9.cloned.1.call-done = bf16[128,2048]{1,0:T(8,128)(2,1)} async-done(((bf16[1024,2048]{1,0:T(8,128)(2,1)}), bf16[128,2048]{1,0:T(8,128)(2,1)}) %reduce-scatter.9.cloned.1.call-update) | async-done | bytes 524304 | tf_op jit(solution)/shard_map/reduce_scatter | solution.py:192
  362.6 65.6 %reduce-scatter.5.cloned.1.call-done = bf16[3,128,1024]{2,1,0:T(8,128)(2,1)} async-done(((bf16[3,1024,1024]{2,1,0:T(8,128)(2,1)}), bf16[3,128,1024]{2,1,0:T(8,128)(2,1)}) %reduce-scatter.5.cloned.1.call-update) | async-done | bytes 786448 | tf_op jit(solution)/shard_map/reduce_scatter | solution.py:192
  428.5 2.5 collective-permute-start.13
  431.0 96.6 %all-reduce.3.cloned.1.call-done = (bf16[3,128,1024]{2,1,0:T(8,128)(2,1)}, bf16[128,1024]{1,0:T(8,128)(2,1)}, bf16[128,2048]{1,0:T(8,128)(2,1)}, bf16[256,1024]{1,0:T(8,128)(2,1)}) async-done(((bf16[3,128,1024]{2,1,0:T(8,128)(2,1)}, bf16[128,1024]{1,0:T(8,128)(2,1)}, bf16[128,2048]{1,0:T(8,128)(2,1)}, bf16[256,1024]{1,0:T(8,128)(2,1)}), (bf16[3,128,1024]{2,1,0:T(8,128)(2,1)}, bf16[128,1024]{1,0:T(8,128)(2,1)}, ...) | async-done | bytes 2097168 | tf_op jit(solution)/shard_map/psum | solution.py:193
  528.9 17.0 %multiply_reduce_fusion.1 = (f32[]{:T(128)}, f32[]{:T(128)}, f32[256,6144]{1,0:T(8,128)}, f32[256,6144]{1,0:T(8,128)}, f32[256,6144]{1,0:T(8,128)}) fusion(f32[256,6144]{1,0:T(8,128)} %param.44, f32[256,6144]{1,0:T(8,128)} %param.45, f32[256,6144]{1,0:T(8,128)} %param.46, f32[8,3,6144]{2,1,0:T(4,128)S(1)} %pad_maximum_fusion.1, ...), kind=kOutput, calls=%fused_computation.37 | convolution fusion | flops 479748096 | bytes 38350856 | tf_op jit(solution)/shard_map/cd,ce->de/dot_general | solution.py:376
  549.3 4.5 multiply_reduce_fusion.9
  553.8 6.6 %multiply_reduce_fusion.5 = (f32[]{:T(128)}, f32[]{:T(128)}, f32[512,1024]{1,0:T(8,128)}, f32[512,1024]{1,0:T(8,128)}, f32[512,1024]{1,0:T(8,128)}) fusion(f32[512,1024]{1,0:T(8,128)S(1)} %copy-done.9, f32[512,1024]{1,0:T(8,128)} %param.42, f32[512,1024]{1,0:T(8,128)} %param.43, bf16[512,1024]{1,0:T(8,128)(2,1)} %all-gather.20.cloned.1.call-done), kind=kLoop, calls=%fused_computation.74 | loop fusion | flops 9437182 | bytes 13631496 | tf_op jit(solution)/shard_map/reduce_sum | solution.py:411
  560.4 7.4 %multiply_reduce_fusion.6 = (f32[]{:T(128)}, f32[]{:T(128)}, f32[256,2048]{1,0:T(8,128)}, f32[256,2048]{1,0:T(8,128)}, f32[256,2048]{1,0:T(8,128)}) fusion(f32[256,2048]{1,0:T(8,128)} %param.38, f32[256,2048]{1,0:T(8,128)} %param.39, f32[256,2048]{1,0:T(8,128)} %param.40, bf16[256,2048]{1,0:T(8,128)(2,1)} %all-gather.18.cloned.1.call-done), kind=kLoop, calls=%fused_computation.77 | loop fusion | flops 9437182 | bytes 13631496 | tf_op jit(solution)/shard_map/reduce_sum | solution.py:411
  567.8 8.5 %multiply_reduce_fusion.3 = (f32[3]{0:T(128)S(1)}, f32[3]{0:T(128)S(1)}, f32[3,256,1024]{2,1,0:T(8,128)}, f32[3,256,1024]{2,1,0:T(8,128)}, f32[3,256,1024]{2,1,0:T(8,128)}) fusion(f32[3,256,1024]{2,1,0:T(8,128)S(1)} %copy-done.6, f32[3,256,1024]{2,1,0:T(8,128)} %param.33, f32[3,256,1024]{2,1,0:T(8,128)} %param.34, ...), kind=kLoop, calls=%fused_computation.48 | loop fusion | flops 14155770 | bytes 20447256 | tf_op jit(solution)/shard_map/reduce_sum | solution.py:411
  576.3 6.5 %concatenate.47 = f32[16]{0:T(128)S(1)} concatenate(f32[3]{0:T(128)S(1)} %get-tuple-element.249, f32[1]{0:T(128)} %bitcast.46, f32[1]{0:T(128)} %bitcast.47, f32[1]{0:T(128)} %bitcast.48, f32[1]{0:T(128)} %bitcast.49, f32[1]{0:T(128)} %bitcast.50, f32[3]{0:T(128)S(1)} %get-tuple-element.248, f32[1]{0:T(128)} %bitcast.51, f32[1]{0:T(128)} %bitcast.52, f32[1]{0:T(128)} %bitcast.53, ...), dimensions={0} | concatenate | bytes 128 | tf_op jit(solution)/shard_map/concatenate | solution.py:412
  598.2 3.4 multiply_subtract_fusion.4
  601.6 4.2 multiply_subtract_fusion.2
  605.8 2.4 multiply_subtract_fusion.3
  609.4 3.3 multiply_subtract_fusion.1
  612.7 8.0 %multiply_subtract_fusion = f32[256,6144]{1,0:T(8,128)} fusion(f32[256,6144]{1,0:T(8,128)S(1)} %bitcast.245, f32[]{:T(128)} %bitcast.62, f32[256,6144]{1,0:T(8,128)} %get-tuple-element.312, f32[256,6144]{1,0:T(8,128)} %get-tuple-element.311), kind=kLoop, calls=%fused_computation.36 | loop fusion | flops 12582912 | bytes 25165828 | tf_op jit(solution)/shard_map/sub | solution.py:422
  (361 shorter events, 125.1 us)
Async XLA Ops:
  7.2 6.5 %copy-start.40 = (f32[1536]{0:T(1024)S(1)}, f32[1536]{0:T(1024)}, u32[]{:S(2)}) copy-start(f32[1536]{0:T(1024)} %param.47) | copy-start | bytes 18436
  7.2 9.6 %copy-start.38 = (f32[3,1024]{1,0:T(4,128)S(1)}, f32[3,1024]{1,0:T(4,128)}, u32[]{:S(2)}) copy-start(f32[3,1024]{1,0:T(4,128)} %param.29) | copy-start | bytes 36868
  7.2 53.7 %all-gather.8.cloned.1.call-start = ((), (), s32[]{:S(2)}) async-start(), calls=%async_computation.12 | async-start | bytes 7077888 | tf_op jit(solution)/shard_map/all_gather | solution.py:188
  9.7 152.5 %all-gather.10.cloned.1.call-start = ((), (), s32[]{:S(2)}) async-start(), calls=%async_computation.13 | async-start | bytes 2359296 | tf_op jit(solution)/shard_map/all_gather | solution.py:188
  11.6 157.1 %all-gather.12.cloned.1.call-start = ((), (), s32[]{:S(2)}) async-start(), calls=%async_computation.14 | async-start | bytes 4718592 | tf_op jit(solution)/shard_map/all_gather | solution.py:188
  13.8 8.3 %collective-permute-start.2 = (bf16[1,1536]{1,0:T(2,128)(2,1)S(1)}, bf16[1,1536]{1,0:T(2,128)(2,1)S(1)}, u32[]{:S(2)}, u32[]{:S(2)}) collective-permute-start(bf16[1,1536]{1,0:T(2,128)(2,1)S(1)} %broadcast_in_dim.128), channel_id=1, source_target_pairs={{0,1},{1,0},{2,3},{3,2},{4,5},{5,4},{6,7},{7,6},{8,9},{9,8},{10,11... | collective-permute-start | bytes 9224 | tf_op jit(solution)/shard_map/ppermute | solution.py:175
  20.3 6.6 %collective-permute-start = (f32[3,6144]{1,0:T(4,128)S(1)}, f32[3,6144]{1,0:T(4,128)S(1)}, u32[]{:S(2)}, u32[]{:S(2)}) collective-permute-start(f32[3,6144]{1,0:T(4,128)S(1)} %fusion.38), channel_id=1, source_target_pairs={{0,1},{1,0},{2,3},{3,2},{4,5},{5,4},{6,7},{7,6},{8,9},{9,8},{10,11... | collective-permute-start | bytes 221192 | tf_op jit(solution)/shard_map/ppermute | solution.py:166
  20.9 15.7 %copy-start.47 = (f32[256]{0:T(256)}, f32[256]{0:T(256)S(1)}, u32[]{:S(2)}) copy-start(f32[256]{0:T(256)S(1)} %broadcast_multiply_fusion.2) | copy-start | bytes 3076
  21.0 15.6 %copy-start.59 = (pred[1024,3]{0,1:T(4,128)(4,1)}, pred[1024,3]{0,1:T(4,128)(4,1)S(1)}, u32[]{:S(2)}) copy-start(pred[1024,3]{0,1:T(4,128)(4,1)S(1)} %fusion.75) | copy-start | bytes 9220
  21.8 57.2 %copy-start.34 = (f32[256,32]{0,1:T(8,128)}, f32[256,32]{0,1:T(8,128)S(1)}, u32[]{:S(2)}) copy-start(f32[256,32]{0,1:T(8,128)S(1)} %get-tuple-element.387) | copy-start | bytes 98308
  22.2 3.9 collective-permute-start.3
  24.2 12.3 %copy-start.55 = (f32[256]{0:T(256)}, f32[256]{0:T(256)S(1)}, u32[]{:S(2)}) copy-start(f32[256]{0:T(256)S(1)} %fusion.82) | copy-start | bytes 3076
  26.9 6.9 %collective-permute-start.1 = (f32[3,6144]{1,0:T(4,128)S(1)}, f32[3,6144]{1,0:T(4,128)S(1)}, u32[]{:S(2)}, u32[]{:S(2)}) collective-permute-start(f32[3,6144]{1,0:T(4,128)S(1)} %add.324), channel_id=1, source_target_pairs={{0,2},{1,3},{2,0},{3,1},{4,6},{5,7},{6,4},{7,5},{8,10},{9,11},{10,... | collective-permute-start | bytes 221192 | tf_op jit(solution)/shard_map/ppermute | solution.py:166
  39.6 59.1 %copy-start.15 = (bf16[256,1024]{1,0:T(8,128)(2,1)}, bf16[256,1024]{1,0:T(8,128)(2,1)S(1)}, u32[]{:S(2)}) copy-start(bf16[256,1024]{1,0:T(8,128)(2,1)S(1)} %fusion.55) | copy-start | bytes 1572868
  81.0 14.2 %all-to-all-start = ((bf16[256,4,256]{0,2,1:T(8,128)(2,1)}), bf16[256,4,256]{0,2,1:T(8,128)(2,1)S(1)}, u32[]{:S(2)}, u32[]{:S(2)}) async-start(bf16[256,4,256]{0,2,1:T(8,128)(2,1)} %convert_element_type.187), calls=%async_computation | async-start | bytes 1048576 | tf_op jit(solution)/shard_map/all_to_all | solution.py:270
  95.2 11.8 %all-to-all-start.1 = ((bf16[256,4,256]{0,2,1:T(8,128)(2,1)}), bf16[256,4,256]{0,2,1:T(8,128)(2,1)S(1)}, u32[]{:S(2)}, u32[]{:S(2)}) async-start(bf16[256,4,256]{0,2,1:T(8,128)(2,1)} %convert_element_type.188), calls=%async_computation.1 | async-start | bytes 1048576 | tf_op jit(solution)/shard_map/all_to_all | solution.py:271
  107.0 18.2 %all-to-all-start.2 = ((bf16[256,4,256]{2,0,1:T(8,128)(2,1)}), bf16[256,4,256]{2,0,1:T(8,128)(2,1)S(1)}, u32[]{:S(2)}, u32[]{:S(2)}) async-start(bf16[256,4,256]{2,0,1:T(8,128)(2,1)} %bitcast.186), calls=%async_computation.2 | async-start | bytes 1048576 | tf_op jit(solution)/shard_map/all_to_all | solution.py:272
  110.5 71.5 %all-gather.14.cloned.1.call-start = ((), (), s32[]{:S(2)}) async-start(), calls=%async_computation.15 | async-start | bytes 4718592 | tf_op jit(solution)/shard_map/all_gather | solution.py:188
  112.7 242.2 %reduce-scatter.7.cloned.1.call-start = ((), (), s32[]{:S(2)}) async-start(), calls=%async_computation.18 | async-start | bytes 2359296 | tf_op jit(solution)/shard_map/reduce_scatter | solution.py:192
  145.0 20.9 %copy-start.1 = (bf16[1024,256]{0,1:T(8,128)(2,1)}, bf16[1024,256]{0,1:T(8,128)(2,1)S(1)}, u32[]{:S(2)}) copy-start(bf16[1024,256]{0,1:T(8,128)(2,1)S(1)} %get-tuple-element.663) | copy-start | bytes 1572868
  165.8 25.0 %copy-start.4 = (f32[256,1024]{1,0:T(8,128)}, f32[256,1024]{1,0:T(8,128)S(1)}, u32[]{:S(2)}) copy-start(f32[256,1024]{1,0:T(8,128)S(1)} %get-tuple-element.330) | copy-start | bytes 3145732
  165.8 25.0 %copy-start.49 = (f32[256]{0:T(256)}, f32[256]{0:T(256)S(1)}, u32[]{:S(2)}) copy-start(f32[256]{0:T(256)S(1)} %broadcast_multiply_fusion.1) | copy-start | bytes 3076
  166.1 24.7 %copy-start.51 = (f32[256]{0:T(256)}, f32[256]{0:T(256)S(1)}, u32[]{:S(2)}) copy-start(f32[256]{0:T(256)S(1)} %fusion.83) | copy-start | bytes 3076
  168.6 5.0 copy-start.25
  168.6 13.3 %copy-start.18 = (bf16[256,1024]{1,0:T(8,128)(2,1)S(1)}, bf16[256,1024]{1,0:T(8,128)(2,1)}, u32[]{:S(2)}) copy-start(bf16[256,1024]{1,0:T(8,128)(2,1)} %param.28) | copy-start | bytes 1572868
  182.0 5.6 copy-start.64
  190.8 4.7 copy-start.20
  200.0 154.8 %reduce-scatter.11.cloned.1.call-start = ((), (), s32[]{:S(2)}) async-start(), calls=%async_computation.21 | async-start | bytes 4718592 | tf_op jit(solution)/shard_map/reduce_scatter | solution.py:192
  207.4 7.4 %copy-start.26 = (bf16[256,1024]{1,0:T(8,128)(2,1)S(1)}, bf16[256,1024]{1,0:T(8,128)(2,1)}, u32[]{:S(2)}) copy-start(bf16[256,1024]{1,0:T(8,128)(2,1)} %copy-done.25) | copy-start | bytes 1572868
  210.1 12.9 %all-to-all-start.4 = ((bf16[256,4,256]{2,0,1:T(8,128)(2,1)}), bf16[256,4,256]{2,0,1:T(8,128)(2,1)}, u32[]{:S(2)}, u32[]{:S(2)}) async-start(bf16[256,4,256]{2,0,1:T(8,128)(2,1)} %bitcast.185), calls=%async_computation.4 | async-start | bytes 1048576 | tf_op jit(solution)/shard_map/all_to_all | solution.py:312
  214.3 148.3 %reduce-scatter.9.cloned.1.call-start = ((), (), s32[]{:S(2)}) async-start(), calls=%async_computation.19 | async-start | bytes 4718592 | tf_op jit(solution)/shard_map/reduce_scatter | solution.py:192
  259.5 14.1 %all-to-all-start.5 = ((bf16[4,256,256]{2,1,0:T(8,128)(2,1)}), bf16[4,256,256]{2,1,0:T(8,128)(2,1)S(1)}, u32[]{:S(2)}, u32[]{:S(2)}) async-start(bf16[4,256,256]{2,1,0:T(8,128)(2,1)} %bitcast.259), calls=%async_computation.5 | async-start | bytes 1048576 | tf_op jit(solution)/shard_map/all_to_all | solution.py:324
  273.6 14.1 %all-to-all-start.6 = ((bf16[4,256,256]{1,2,0:T(8,128)(2,1)}), bf16[4,256,256]{1,2,0:T(8,128)(2,1)S(1)}, u32[]{:S(2)}, u32[]{:S(2)}) async-start(bf16[4,256,256]{1,2,0:T(8,128)(2,1)} %bitcast.184), calls=%async_computation.6 | async-start | bytes 1048576 | tf_op jit(solution)/shard_map/all_to_all | solution.py:325
  287.7 14.7 %all-to-all-start.7 = ((bf16[4,256,256]{2,1,0:T(8,128)(2,1)}), bf16[4,256,256]{2,1,0:T(8,128)(2,1)}, u32[]{:S(2)}, u32[]{:S(2)}) async-start(bf16[4,256,256]{2,1,0:T(8,128)(2,1)} %bitcast.35), calls=%async_computation.7 | async-start | bytes 1048576 | tf_op jit(solution)/shard_map/all_to_all | solution.py:326
  291.8 136.4 %reduce-scatter.5.cloned.1.call-start = ((), (), s32[]{:S(2)}) async-start(), calls=%async_computation.16 | async-start | bytes 7077888 | tf_op jit(solution)/shard_map/reduce_scatter | solution.py:192
  296.4 7.3 %copy-start.16 = (bf16[256,1024]{1,0:T(8,128)(2,1)S(1)}, bf16[256,1024]{1,0:T(8,128)(2,1)}, u32[]{:S(2)}) copy-start(bf16[256,1024]{1,0:T(8,128)(2,1)} %copy-done.15) | copy-start | bytes 1572868
  309.1 218.5 %all-reduce.3.cloned.1.call-start = ((), (), s32[]{:S(2)}) async-start(), calls=%async_computation.23 | async-start | bytes 4194304 | tf_op jit(solution)/shard_map/psum | solution.py:193
  309.8 1.2 collective-permute-start.8
  311.0 3.7 collective-permute-start.9
  330.6 6.6 %collective-permute-start.4 = (f32[3,6144]{1,0:T(4,128)S(1)}, f32[3,6144]{1,0:T(4,128)S(1)}, u32[]{:S(2)}, u32[]{:S(2)}) collective-permute-start(f32[3,6144]{1,0:T(4,128)S(1)} %fusion.81), channel_id=1, source_target_pairs={{0,1},{1,0},{2,3},{3,2},{4,5},{5,4},{6,7},{7,6},{8,9},{9,8},{10,11... | collective-permute-start | bytes 221192 | tf_op jit(solution)/shard_map/ppermute | solution.py:166
  332.2 6.6 %collective-permute-start.10 = (bf16[4,3,256]{2,0,1:T(4,128)(2,1)S(1)}, bf16[4,3,256]{2,0,1:T(4,128)(2,1)S(1)}, u32[]{:S(2)}, u32[]{:S(2)}) collective-permute-start(bf16[4,3,256]{2,0,1:T(4,128)(2,1)S(1)} %pad_maximum_fusion.9), channel_id=1, source_target_pairs={{0,16},{4,20},{8,24},{12,28},{16,0},{20,4},{24,8},{28,12},{1,17},{... | collective-permute-start | bytes 18440 | tf_op jit(solution)/shard_map/ppermute | solution.py:175
  337.2 6.8 %collective-permute-start.5 = (f32[3,6144]{1,0:T(4,128)S(1)}, f32[3,6144]{1,0:T(4,128)S(1)}, u32[]{:S(2)}, u32[]{:S(2)}) collective-permute-start(f32[3,6144]{1,0:T(4,128)S(1)} %add.350), channel_id=1, source_target_pairs={{0,2},{1,3},{2,0},{3,1},{4,6},{5,7},{6,4},{7,5},{8,10},{9,11},{10,... | collective-permute-start | bytes 221192 | tf_op jit(solution)/shard_map/ppermute | solution.py:166
  344.1 7.7 %collective-permute-start.11 = (f32[1,3,6144]{2,1,0:T(4,128)S(1)}, f32[1,3,6144]{2,1,0:T(4,128)S(1)}, u32[]{:S(2)}, u32[]{:S(2)}) collective-permute-start(f32[1,3,6144]{2,1,0:T(4,128)S(1)} %add_bitcast_fusion), channel_id=1, source_target_pairs={{0,4},{4,0},{8,12},{12,8},{16,20},{20,16},{24,28},{28,24},{1,5},{5... | collective-permute-start | bytes 221192 | tf_op jit(solution)/shard_map/ppermute | solution.py:175
  349.6 3.8 collective-permute-start.6
  351.9 76.3 %collective-permute-start.12 = (f32[2,3,6144]{2,1,0:T(4,128)S(1)}, f32[2,3,6144]{2,1,0:T(4,128)S(1)}, u32[]{:S(2)}, u32[]{:S(2)}) collective-permute-start(f32[2,3,6144]{2,1,0:T(4,128)S(1)} %pad_maximum_fusion.5), channel_id=1, source_target_pairs={{0,8},{4,12},{8,0},{12,4},{16,24},{20,28},{24,16},{28,20},{1,9},{5... | collective-permute-start | bytes 442376 | tf_op jit(solution)/shard_map/ppermute | solution.py:175
  353.4 77.5 %collective-permute-start.7 = (f32[2,3,256]{2,1,0:T(4,128)S(1)}, f32[2,3,256]{2,1,0:T(4,128)S(1)}, u32[]{:S(2)}, u32[]{:S(2)}) collective-permute-start(f32[2,3,256]{2,1,0:T(4,128)S(1)} %pad_maximum_fusion.7), channel_id=1, source_target_pairs={{0,2},{1,3},{2,0},{3,1},{4,6},{5,7},{6,4},{7,5},{8,10},{9,11},{10,... | collective-permute-start | bytes 18440 | tf_op jit(solution)/shard_map/ppermute | solution.py:175
  428.2 125.6 %all-gather.20.cloned.1.call-start = ((), (), s32[]{:S(2)}) async-start(), calls=%async_computation.22 | async-start | bytes 1572864 | tf_op jit(solution)/shard_map/all_gather | solution.py:194
  428.5 99.2 %collective-permute-start.13 = (f32[4,3,6144]{2,1,0:T(4,128)S(1)}, f32[4,3,6144]{2,1,0:T(4,128)S(1)}, u32[]{:S(2)}, u32[]{:S(2)}) collective-permute-start(f32[4,3,6144]{2,1,0:T(4,128)S(1)} %pad_maximum_fusion.4), channel_id=1, source_target_pairs={{0,16},{4,20},{8,24},{12,28},{16,0},{20,4},{24,8},{28,12},{1,17},{... | collective-permute-start | bytes 884744 | tf_op jit(solution)/shard_map/ppermute | solution.py:175
  527.6 32.8 %all-gather.18.cloned.1.call-start = ((), (), s32[]{:S(2)}) async-start(), calls=%async_computation.20 | async-start | bytes 1572864 | tf_op jit(solution)/shard_map/all_gather | solution.py:194
  528.4 39.4 %all-gather.16.cloned.1.call-start = ((), (), s32[]{:S(2)}) async-start(), calls=%async_computation.17 | async-start | bytes 2359296 | tf_op jit(solution)/shard_map/all_gather | solution.py:194
  528.8 17.4 %copy-start.41 = (f32[1536]{0:T(1024)S(1)}, f32[1536]{0:T(1024)}, u32[]{:S(2)}) copy-start(f32[1536]{0:T(1024)} %param.47) | copy-start | bytes 18436
  528.8 17.4 %copy-start.60 = (f32[1536]{0:T(1024)S(1)}, f32[1536]{0:T(1024)}, u32[]{:S(2)}) copy-start(f32[1536]{0:T(1024)} %param.48) | copy-start | bytes 18436
  528.8 17.4 %copy-start.61 = (f32[1536]{0:T(1024)S(1)}, f32[1536]{0:T(1024)}, u32[]{:S(2)}) copy-start(f32[1536]{0:T(1024)} %param.49) | copy-start | bytes 18436
  528.9 18.1 %copy-start.36 = (bf16[128,1024]{1,0:T(8,128)(2,1)S(1)}, bf16[128,1024]{1,0:T(8,128)(2,1)}, u32[]{:S(2)}) copy-start(bf16[128,1024]{1,0:T(8,128)(2,1)} %get-tuple-element.304) | copy-start | bytes 786436
  546.2 7.5 %copy-start.44 = (f32[1536]{0:T(1024)}, f32[1536]{0:T(1024)S(1)}, u32[]{:S(2)}) copy-start(f32[1536]{0:T(1024)S(1)} %dynamic-slice_reduce_fusion) | copy-start | bytes 18436
  546.9 50.6 %copy-start.45 = (f32[1536]{0:T(1024)}, f32[1536]{0:T(1024)S(1)}, u32[]{:S(2)}) copy-start(f32[1536]{0:T(1024)S(1)} %get-tuple-element.309) | copy-start | bytes 18436
  546.9 50.6 %copy-start.46 = (f32[1536]{0:T(1024)}, f32[1536]{0:T(1024)S(1)}, u32[]{:S(2)}) copy-start(f32[1536]{0:T(1024)S(1)} %get-tuple-element.310) | copy-start | bytes 18436
  549.3 4.5 copy-start.9
  560.4 7.4 %copy-start.6 = (f32[3,256,1024]{2,1,0:T(8,128)S(1)}, f32[3,256,1024]{2,1,0:T(8,128)}, u32[]{:S(2)}) copy-start(f32[3,256,1024]{2,1,0:T(8,128)} %param.32) | copy-start | bytes 9437188
  567.8 20.3 %copy-start.39 = (f32[3,1024]{1,0:T(4,128)S(1)}, f32[3,1024]{1,0:T(4,128)}, u32[]{:S(2)}) copy-start(f32[3,1024]{1,0:T(4,128)} %param.29) | copy-start | bytes 36868
  582.7 18.8 %copy-start.10 = (f32[512,1024]{1,0:T(8,128)S(1)}, f32[512,1024]{1,0:T(8,128)}, u32[]{:S(2)}) copy-start(f32[512,1024]{1,0:T(8,128)} %param.41) | copy-start | bytes 6291460
  582.8 18.8 %copy-start.12 = (f32[512,1024]{1,0:T(8,128)S(1)}, f32[512,1024]{1,0:T(8,128)}, u32[]{:S(2)}) copy-start(f32[512,1024]{1,0:T(8,128)} %get-tuple-element.313) | copy-start | bytes 6291460
  582.8 3.6 collective-permute-start.14
  586.4 3.6 collective-permute-start.15
  (40 other events, 115.3 us)
Sparse Core Ops, SparseCore 0:
  10.5 50.3 all-gather.7
  63.4 32.6 all-gather.9
  98.5 39.5 all-gather.11
  140.4 41.5 all-gather.13
  200.1 41.1 reduce-scatter.6
  245.1 60.0 reduce-scatter.10
  309.2 53.3 reduce-scatter.8
  366.5 61.6 reduce-scatter.4
  430.8 96.7 all-reduce.2
  529.0 8.0 all-gather.19
  538.6 10.2 all-gather.17
  550.3 10.9 all-gather.15

commit v3 on v2

--- a/solution.py
+++ b/solution.py
@@ -188,10 +188,39 @@
     return lax.all_gather(piece, ("seq", "core"), axis=row_axis, tiled=True)
 
 
+def halving_sum(values, axis_name, size):
+    index = lax.axis_index(axis_name)
+    total = values.astype(jnp.float32)
+    step = 1
+    while step < size:
+        half = total.shape[-1] // 2
+        low_side = (index // step) % 2 == 0
+        keep = jnp.where(low_side, total[..., :half], total[..., half:])
+        send = jnp.where(low_side, total[..., half:], total[..., :half]).astype(jnp.bfloat16)
+        total = keep + lax.ppermute(send, axis_name, [(i, i ^ step) for i in range(size)]).astype(
+            jnp.float32
+        )
+        step *= 2
+    blocks = total.astype(jnp.bfloat16)
+    step = size // 2
+    while step >= 1:
+        other = lax.ppermute(blocks, axis_name, [(i, i ^ step) for i in range(size)])
+        low_side = (index // step) % 2 == 0
+        blocks = jnp.concatenate(
+            [jnp.where(low_side, blocks, other), jnp.where(low_side, other, blocks)], axis=-1
+        )
+        step //= 2
+    return blocks
+
+
 def reduce_rows(partial, row_axis):
     piece = lax.psum_scatter(partial, ("seq", "core"), scatter_dimension=row_axis, tiled=True)
-    piece = lax.psum(piece, "z")
-    return lax.all_gather(piece, "core", axis=row_axis, tiled=True)
+    piece = halving_sum(piece, "z", lax.axis_size("z"))
+    other = lax.ppermute(piece, "core", [(0, 1), (1, 0)])
+    first = lax.axis_index("core") == 0
+    return jnp.concatenate(
+        [jnp.where(first, piece, other), jnp.where(first, other, piece)], axis=row_axis
+    )
 
 
 def adam_direction(weight, moment, second, grad):
@@ -409,16 +438,12 @@
         directions.append(direction)
         weight_sums.append(jnp.sum(masters[param] * masters[param], axis=sum_axes, keepdims=True))
         update_sums.append(jnp.sum(direction * direction, axis=sum_axes, keepdims=True))
-    packed = jnp.concatenate([jnp.reshape(part, (-1,)) for part in weight_sums + update_sums])
-    packed = butterfly_sum(packed, "seq", seq_count)
-    norm_sums = []
-    offset = 0
-    for part in weight_sums + update_sums:
-        norm_sums.append(packed[offset : offset + part.size].reshape(part.shape))
-        offset += part.size
     new_masters = []
     for param in range(6):
-        ratio = jnp.sqrt(norm_sums[param]) * lax.rsqrt(norm_sums[param + 6] + 1e-06)
+        pair = butterfly_sum(
+            jnp.concatenate([weight_sums[param], update_sums[param]], axis=-1), "seq", seq_count
+        )
+        ratio = jnp.sqrt(pair[..., :1]) * lax.rsqrt(pair[..., 1:] + 1e-06)
         new_masters.append(masters[param] - step_rate * ratio * directions[param])
     return (
         result.astype(jnp.bfloat16),

time: 635 us -> 583 us (0.918)
  waiting for transfers between devices: 262 us -> 178 us
  starting transfers between devices: 63.6 us -> 88.4 us
  other arithmetic: 79.6 us -> 98.2 us
  blocking collectives: 19.3 us -> 11 us
    psum x1 -> x0, waiting for transfers between devices: 96.6 us -> none  [reduce_rows(): piece = lax.psum(piece, 'z')]
    reduce_scatter x4, waiting for transfers between devices: 73.3 us -> 0.06 us  [reduce_rows(): lax.psum_scatter(partial, ('seq', 'core'), scatter_dimension=row_axis, ti...]
    ppermute x0 -> x20, waiting for transfers between devices: none -> 58.5 us  [the longest x8 34.5 us: halving_sum(): lax.ppermute(blocks, axis_name, [(i, i ^ step) for i in range(size)])]
    ppermute x10, waiting for transfers between devices: 5.43 us -> 26.5 us  [doubling_gather(): other = lax.ppermute(blocks, axes, [(i, i ^ step) for i in range(size)])]
    ppermute x0 -> x20, starting transfers between devices: none -> 16.5 us  [the longest x8 9.46 us: halving_sum(): lax.ppermute(send, axis_name, [(i, i ^ step) for i in range(size)])]
    add x4 -> x14, other arithmetic: 0.06 us -> 13.9 us  [butterfly_sum(): values + lax.ppermute(values, axes, [(i, i ^ step) for i in range(size)])]
    ppermute x6 -> x16, starting transfers between devices: 8.19 us -> 18.2 us  [butterfly_sum(): lax.ppermute(values, axes, [(i, i ^ step) for i in range(size)])]
    reduce_sum x5, other arithmetic: 27.6 us -> 18.4 us  [local(): jnp.sum(masters[param] * masters[param], axis=sum_axes, keepdims=True)]
  transfers between devices with their start and end apart: 35 -> 61, of which waited for: 21 -> 36; matrix products, arithmetic and copies ran while one was open for 31% -> 41% of each run, Pallas kernels for 0% -> 0%
where the time goes in v3:
time: 583 us; the launch traced here: 573 us
  waiting for transfers between devices  178 us (31%)
  matrix products  112 us (19%)
  other arithmetic  98.2 us (17%)
  starting transfers between devices  88.4 us (15%)
  local copies, waits for them, and re-layouts  58.8 us (10%)
  between operations  23.4 us (4%)
  blocking collectives  11 us (2%)
    all_gather x4, waiting for transfers between devices, gather_rows(): return lax.all_gather(piece, ('seq', 'core'), axis=row_axis, tiled=True)  37 us
    ppermute x8, waiting for transfers between devices, halving_sum(): lax.ppermute(blocks, axis_name, [(i, i ^ step) for i in range(size)])  34.5 us
    ppermute x10, waiting for transfers between devices, doubling_gather(): other = lax.ppermute(blocks, axes, [(i, i ^ step) for i in range(size)])  26.5 us
    ppermute x8, waiting for transfers between devices, halving_sum(): lax.ppermute(send, axis_name, [(i, i ^ step) for i in range(size)])  24.1 us
    ppermute x16, waiting for transfers between devices, butterfly_sum(): lax.ppermute(values, axes, [(i, i ^ step) for i in range(size)])  22.4 us
    sub x6, other arithmetic, local(): new_masters.append(masters[param] - step_rate * ratio * directions[param])  22.2 us
    dot_general x1, matrix products, local(): jnp.einsum('cd,ce->de', silu_all.astype(jnp.float32), grad_mod_all, preci...  18.6 us
    reduce_sum x5, other arithmetic, local(): jnp.sum(masters[param] * masters[param], axis=sum_axes, keepdims=True)  18.4 us
  transfers between devices with their start and end apart: 61, of which 36 were waited for; matrix products, arithmetic and copies ran while one was open for 41% of the time, Pallas kernels for 0%

profile of v3, /device:TPU:0, one launch (start us, length us, event | category | flops | bytes accessed | tf_op | source)
XLA Modules:
  0.0 572.8 jit_solution(2263374687820032034)
XLA Ops:
  13.8 3.0 collective-permute-start.2
  16.9 3.4 fusion.38
  28.5 5.3 collective-permute-done.1
  33.8 2.7 fusion.68
  36.5 2.7 copy-done
  39.6 21.3 %all-gather.5.cloned.1.call-done = bf16[3,1024,1024]{2,1,0:T(8,128)(2,1)} async-done(((bf16[3,128,1024]{2,1,0:T(8,128)(2,1)}), bf16[3,1024,1024]{2,1,0:T(8,128)(2,1)}) %all-gather.5.cloned.1.call-update) | async-done | bytes 6291472 | tf_op jit(solution)/shard_map/all_gather | solution.py:188
  60.9 4.7 slice_bitcast_fusion.3
  65.6 2.9 copy.145
  70.6 2.9 copy.141
  81.0 3.5 all-to-all-start
  86.0 9.2 %all-to-all-done = bf16[256,4,256]{0,2,1:T(8,128)(2,1)S(1)} async-done(((bf16[256,4,256]{0,2,1:T(8,128)(2,1)}), bf16[256,4,256]{0,2,1:T(8,128)(2,1)S(1)}, u32[]{:S(2)}, u32[]{:S(2)}) %all-to-all-start) | async-done | bytes 524320 | tf_op jit(solution)/shard_map/all_to_all | solution.py:299
  95.2 3.5 all-to-all-start.1
  101.9 5.2 all-to-all-done.1
  107.0 3.5 all-to-all-start.2
  113.9 5.8 %all-to-all-done.2 = bf16[256,4,256]{2,0,1:T(8,128)(2,1)S(1)} async-done(((bf16[256,4,256]{2,0,1:T(8,128)(2,1)}), bf16[256,4,256]{2,0,1:T(8,128)(2,1)S(1)}, u32[]{:S(2)}, u32[]{:S(2)}) %all-to-all-start.2) | async-done | bytes 524320 | tf_op jit(solution)/shard_map/all_to_all | solution.py:301
  120.8 18.7 %while.27 = (s32[]{:T(128)}, bf16[2,512,256]{2,1,0:T(8,128)(2,1)S(1)}, f32[2,4,512,1]{2,1,3,0:T(4,128)S(1)}, s32[2]{0:T(128)S(1)}, s32[1024]{0:T(1024)S(1)}, /*i...) while((s32[]{:T(128)}, ...), condition=%wide.region_9.10_spmd, body=%wide.region_6.9_spmd.sunk | while | flops 561117184 | bytes 30485712 | solution.py:110
  126.6 3.3 fusion.183
  135.9 3.3 fusion.183
  139.4 11.0 %all_to_all.134 = bf16[4,256,256]{2,1,0:T(8,128)(2,1)S(1)} all-to-all(bf16[4,256,256]{2,1,0:T(8,128)(2,1)S(1)} %bitcast.265), channel_id=1, replica_groups=mesh['z'=4,'core'=2,'seq'=4] {'seq'}, dimensions={0} | all-to-all | bytes 1048576 | tf_op jit(solution)/shard_map/all_to_all | solution.py:306
  150.7 3.6 fusion.102
  156.5 5.0 fusion.111
  161.5 15.7 %all-gather.11.cloned.1.call-done = bf16[2048,1024]{1,0:T(8,128)(2,1)} async-done(((bf16[256,1024]{1,0:T(8,128)(2,1)}), bf16[2048,1024]{1,0:T(8,128)(2,1)}) %all-gather.11.cloned.1.call-update) | async-done | bytes 4194320 | tf_op jit(solution)/shard_map/all_gather | solution.py:188
  177.1 5.6 fusion.21
  182.8 3.1 multiply_reduce_fusion.11
  186.3 4.3 fusion.101
  199.2 4.2 all-to-all-start.4
  203.4 10.6 %reduce-scatter.9.cloned.1.call-start = ((), (), s32[]{:S(2)}) async-start(), calls=%async_computation.18 | async-start | bytes 4718592 | tf_op jit(solution)/shard_map/reduce_scatter | solution.py:217
  215.5 4.5 convolution_convert_fusion.1
  221.0 35.7 %while.28 = (s32[]{:T(128)}, f32[1024,256]{0,1:T(8,128)S(1)}, f32[1024,256]{0,1:T(8,128)S(1)}, bf16[2,512,256]{2,1,0:T(8,128)(2,1)}, s32[2]{0:T(128)S(1)}, /*ind...) while((s32[]{:T(128)}, f32[1024,256]{0,1:T(8,128)S(1)}, ...), condition=%wide.region_16.17_spmd.clone, body=%wide.region_14.16_spmd.clone.sunk | while | flops 1376253952 | bytes 78974200 | solution.py:155
  228.5 4.2 multiply_reduce_fusion.16
  246.3 4.3 multiply_reduce_fusion.16
  256.6 4.0 all-to-all-start.5
  266.2 8.7 %all-to-all-done.5 = bf16[4,256,256]{2,1,0:T(8,128)(2,1)S(1)} async-done(((bf16[4,256,256]{2,1,0:T(8,128)(2,1)}), bf16[4,256,256]{2,1,0:T(8,128)(2,1)S(1)}, u32[]{:S(2)}, u32[]{:S(2)}) %all-to-all-start.5) | async-done | bytes 524320 | tf_op jit(solution)/shard_map/all_to_all | solution.py:353
  274.9 3.5 all-to-all-start.6
  278.5 5.6 convolution_convert_fusion
  286.2 4.2 all-to-all-start.7
  297.7 4.2 all-to-all-done.7
  308.0 2.9 constant_dynamic-update-slice_fusion.3
  315.9 3.0 fusion.81
  332.4 3.1 pad_maximum_fusion
  336.5 3.2 collective-permute-done.7
  340.7 4.7 collective-permute-done.40
  345.7 3.2 collective-permute-start.41
  349.5 13.7 %collective-permute-done.41 = f32[4,3,6144]{2,1,0:T(4,128)S(1)} collective-permute-done((f32[4,3,6144]{2,1,0:T(4,128)S(1)}, f32[4,3,6144]{2,1,0:T(4,128)S(1)}, u32[]{:S(2)}, u32[]{:S(2)}) %collective-permute-start.41) | collective-permute-done | bytes 294944 | tf_op jit(solution)/shard_map/ppermute | solution.py:175
  367.7 18.6 %multiply_reduce_fusion.2 = (f32[]{:T(128)}, f32[]{:T(128)}, f32[256,6144]{1,0:T(8,128)}, f32[256,6144]{1,0:T(8,128)}, f32[256,6144]{1,0:T(8,128)}) fusion(f32[256,6144]{1,0:T(8,128)} %param.44, f32[256,6144]{1,0:T(8,128)} %param.45, f32[256,6144]{1,0:T(8,128)} %param.46, f32[8,3,6144]{2,1,0:T(4,128)S(1)} %pad_maximum_fusion.2, ...), kind=kOutput, calls=%fused_computation.40 | convolution fusion | flops 479748096 | bytes 38350856 | tf_op jit(solution)/shard_map/cd,ce->de/dot_general | solution.py:405
  402.0 3.2 collective-permute-done.16
  405.3 11.7 %multiply_subtract_fusion = f32[256,6144]{1,0:T(8,128)} fusion(f32[256,6144]{1,0:T(8,128)} %param.44, f32[]{:T(128)} %bitcast.63, f32[256,6144]{1,0:T(8,128)} %get-tuple-element.308, f32[256,6144]{1,0:T(8,128)} %get-tuple-element.307), kind=kLoop, calls=%fused_computation.36 | loop fusion | flops 12582912 | bytes 25165828 | tf_op jit(solution)/shard_map/sub | solution.py:447
  417.0 3.2 collective-permute-start.18
  426.0 2.8 multiply_reduce_fusion.10
  447.3 3.5 collective-permute-done.22
  450.9 2.8 collective-permute-start.23
  458.4 3.1 collective-permute-start.24
  461.5 5.9 %collective-permute-done.30 = bf16[256,256]{1,0:T(8,128)(2,1)S(1)} collective-permute-done((bf16[256,256]{1,0:T(8,128)(2,1)S(1)}, bf16[256,256]{1,0:T(8,128)(2,1)S(1)}, u32[]{:S(2)}, u32[]{:S(2)}) %collective-permute-start.30) | collective-permute-done | bytes 131104 | tf_op jit(solution)/shard_map/ppermute | solution.py:200
  470.3 5.7 %collective-permute-done.31 = bf16[256,256]{1,0:T(8,128)(2,1)S(1)} collective-permute-done((bf16[256,256]{1,0:T(8,128)(2,1)S(1)}, bf16[256,256]{1,0:T(8,128)(2,1)S(1)}, u32[]{:S(2)}, u32[]{:S(2)}) %collective-permute-start.31) | collective-permute-done | bytes 131104 | tf_op jit(solution)/shard_map/ppermute | solution.py:207
  476.1 5.5 collective-permute-done.25
  483.4 3.4 collective-permute-done.32
  487.3 4.1 multiply_reduce_fusion.8
  495.9 5.3 multiply_reduce_fusion.6
  511.1 7.8 %collective-permute-done.9 = bf16[3,128,256]{2,1,0:T(8,128)(2,1)S(1)} collective-permute-done((bf16[3,128,256]{2,1,0:T(8,128)(2,1)S(1)}, bf16[3,128,256]{2,1,0:T(8,128)(2,1)S(1)}, u32[]{:S(2)}, u32[]{:S(2)}) %collective-permute-start.9) | collective-permute-done | bytes 196640 | tf_op jit(solution)/shard_map/ppermute | solution.py:200
  522.4 7.6 %collective-permute-done.10 = bf16[3,128,256]{2,1,0:T(8,128)(2,1)S(1)} collective-permute-done((bf16[3,128,256]{2,1,0:T(8,128)(2,1)S(1)}, bf16[3,128,256]{2,1,0:T(8,128)(2,1)S(1)}, u32[]{:S(2)}, u32[]{:S(2)}) %collective-permute-start.10) | collective-permute-done | bytes 196640 | tf_op jit(solution)/shard_map/ppermute | solution.py:207
  532.6 8.1 %collective-permute-done.11 = bf16[3,128,512]{2,1,0:T(8,128)(2,1)S(1)} collective-permute-done((bf16[3,128,512]{2,1,0:T(8,128)(2,1)S(1)}, bf16[3,128,512]{2,1,0:T(8,128)(2,1)S(1)}, u32[]{:S(2)}, u32[]{:S(2)}) %collective-permute-start.11) | collective-permute-done | bytes 393248 | tf_op jit(solution)/shard_map/ppermute | solution.py:207
  544.4 2.7 multiply_subtract_fusion.3
  549.2 5.6 multiply_reduce_fusion.4
  562.2 3.3 multiply_subtract_fusion.1
  (467 shorter events, 206.7 us)
Async XLA Ops:
  7.2 53.7 %all-gather.5.cloned.1.call-start = ((), (), s32[]{:S(2)}) async-start(), calls=%async_computation.12 | async-start | bytes 7077888 | tf_op jit(solution)/shard_map/all_gather | solution.py:188
  9.7 140.9 %all-gather.7.cloned.1.call-start = ((), (), s32[]{:S(2)}) async-start(), calls=%async_computation.13 | async-start | bytes 2359296 | tf_op jit(solution)/shard_map/all_gather | solution.py:188
  11.6 144.9 %all-gather.9.cloned.1.call-start = ((), (), s32[]{:S(2)}) async-start(), calls=%async_computation.14 | async-start | bytes 4718592 | tf_op jit(solution)/shard_map/all_gather | solution.py:188
  13.8 8.3 %collective-permute-start.2 = (bf16[1,1536]{1,0:T(2,128)(2,1)S(1)}, bf16[1,1536]{1,0:T(2,128)(2,1)S(1)}, u32[]{:S(2)}, u32[]{:S(2)}) collective-permute-start(bf16[1,1536]{1,0:T(2,128)(2,1)S(1)} %broadcast_in_dim.158), channel_id=1, source_target_pairs={{0,1},{1,0},{2,3},{3,2},{4,5},{5,4},{6,7},{7,6},{8,9},{9,8},{10,11... | collective-permute-start | bytes 9224 | tf_op jit(solution)/shard_map/ppermute | solution.py:175
  20.3 6.6 %collective-permute-start = (f32[3,6144]{1,0:T(4,128)S(1)}, f32[3,6144]{1,0:T(4,128)S(1)}, u32[]{:S(2)}, u32[]{:S(2)}) collective-permute-start(f32[3,6144]{1,0:T(4,128)S(1)} %fusion.38), channel_id=1, source_target_pairs={{0,1},{1,0},{2,3},{3,2},{4,5},{5,4},{6,7},{7,6},{8,9},{9,8},{10,11... | collective-permute-start | bytes 221192 | tf_op jit(solution)/shard_map/ppermute | solution.py:166
  22.1 3.9 collective-permute-start.3
  26.9 6.9 %collective-permute-start.1 = (f32[3,6144]{1,0:T(4,128)S(1)}, f32[3,6144]{1,0:T(4,128)S(1)}, u32[]{:S(2)}, u32[]{:S(2)}) collective-permute-start(f32[3,6144]{1,0:T(4,128)S(1)} %add.387), channel_id=1, source_target_pairs={{0,2},{1,3},{2,0},{3,1},{4,6},{5,7},{6,4},{7,5},{8,10},{9,11},{10,... | collective-permute-start | bytes 221192 | tf_op jit(solution)/shard_map/ppermute | solution.py:166
  39.6 59.2 %copy-start.16 = (bf16[256,1024]{1,0:T(8,128)(2,1)}, bf16[256,1024]{1,0:T(8,128)(2,1)S(1)}, u32[]{:S(2)}) copy-start(bf16[256,1024]{1,0:T(8,128)(2,1)S(1)} %fusion.55) | copy-start | bytes 1572868
  81.0 14.2 %all-to-all-start = ((bf16[256,4,256]{0,2,1:T(8,128)(2,1)}), bf16[256,4,256]{0,2,1:T(8,128)(2,1)S(1)}, u32[]{:S(2)}, u32[]{:S(2)}) async-start(bf16[256,4,256]{0,2,1:T(8,128)(2,1)} %convert_element_type.259), calls=%async_computation | async-start | bytes 1048576 | tf_op jit(solution)/shard_map/all_to_all | solution.py:299
  95.2 11.8 %all-to-all-start.1 = ((bf16[256,4,256]{0,2,1:T(8,128)(2,1)}), bf16[256,4,256]{0,2,1:T(8,128)(2,1)S(1)}, u32[]{:S(2)}, u32[]{:S(2)}) async-start(bf16[256,4,256]{0,2,1:T(8,128)(2,1)} %convert_element_type.260), calls=%async_computation.1 | async-start | bytes 1048576 | tf_op jit(solution)/shard_map/all_to_all | solution.py:300
  107.0 12.7 %all-to-all-start.2 = ((bf16[256,4,256]{2,0,1:T(8,128)(2,1)}), bf16[256,4,256]{2,0,1:T(8,128)(2,1)S(1)}, u32[]{:S(2)}, u32[]{:S(2)}) async-start(bf16[256,4,256]{2,0,1:T(8,128)(2,1)} %bitcast.190), calls=%async_computation.2 | async-start | bytes 1048576 | tf_op jit(solution)/shard_map/all_to_all | solution.py:301
  110.5 66.6 %all-gather.11.cloned.1.call-start = ((), (), s32[]{:S(2)}) async-start(), calls=%async_computation.15 | async-start | bytes 4718592 | tf_op jit(solution)/shard_map/all_gather | solution.py:188
  112.7 280.1 %reduce-scatter.7.cloned.1.call-start = ((), (), s32[]{:S(2)}) async-start(), calls=%async_computation.17 | async-start | bytes 2359296 | tf_op jit(solution)/shard_map/reduce_scatter | solution.py:217
  194.6 1.2 collective-permute-start.36
  199.2 20.9 %all-to-all-start.4 = ((bf16[256,4,256]{2,0,1:T(8,128)(2,1)}), bf16[256,4,256]{2,0,1:T(8,128)(2,1)}, u32[]{:S(2)}, u32[]{:S(2)}) async-start(bf16[256,4,256]{2,0,1:T(8,128)(2,1)} %bitcast.263), calls=%async_computation.4 | async-start | bytes 1048576 | tf_op jit(solution)/shard_map/all_to_all | solution.py:341
  203.4 236.7 %reduce-scatter.9.cloned.1.call-start = ((), (), s32[]{:S(2)}) async-start(), calls=%async_computation.18 | async-start | bytes 4718592 | tf_op jit(solution)/shard_map/reduce_scatter | solution.py:217
  214.0 46.7 %collective-permute-start.37 = (bf16[2,3,256]{2,0,1:T(2,128)(2,1)S(1)}, bf16[2,3,256]{2,0,1:T(2,128)(2,1)S(1)}, u32[]{:S(2)}, u32[]{:S(2)}) collective-permute-start(bf16[2,3,256]{2,0,1:T(2,128)(2,1)S(1)} %pad_maximum_fusion.18), channel_id=1, source_target_pairs={{0,8},{4,12},{8,0},{12,4},{16,24},{20,28},{24,16},{28,20},{1,9},{5... | collective-permute-start | bytes 9224 | tf_op jit(solution)/shard_map/ppermute | solution.py:175
  256.6 18.3 %all-to-all-start.5 = ((bf16[4,256,256]{2,1,0:T(8,128)(2,1)}), bf16[4,256,256]{2,1,0:T(8,128)(2,1)S(1)}, u32[]{:S(2)}, u32[]{:S(2)}) async-start(bf16[4,256,256]{2,1,0:T(8,128)(2,1)} %bitcast.264), calls=%async_computation.5 | async-start | bytes 1048576 | tf_op jit(solution)/shard_map/all_to_all | solution.py:353
  260.7 4.6 collective-permute-start.38
  274.9 11.2 %all-to-all-start.6 = ((bf16[4,256,256]{1,2,0:T(8,128)(2,1)}), bf16[4,256,256]{1,2,0:T(8,128)(2,1)S(1)}, u32[]{:S(2)}, u32[]{:S(2)}) async-start(bf16[4,256,256]{1,2,0:T(8,128)(2,1)} %bitcast.188), calls=%async_computation.6 | async-start | bytes 1048576 | tf_op jit(solution)/shard_map/all_to_all | solution.py:354
  278.4 167.6 %reduce-scatter.11.cloned.1.call-start = ((), (), s32[]{:S(2)}) async-start(), calls=%async_computation.19 | async-start | bytes 4718592 | tf_op jit(solution)/shard_map/reduce_scatter | solution.py:217
  286.2 15.8 %all-to-all-start.7 = ((bf16[4,256,256]{2,1,0:T(8,128)(2,1)}), bf16[4,256,256]{2,1,0:T(8,128)(2,1)}, u32[]{:S(2)}, u32[]{:S(2)}) async-start(bf16[4,256,256]{2,1,0:T(8,128)(2,1)} %bitcast.35), calls=%async_computation.7 | async-start | bytes 1048576 | tf_op jit(solution)/shard_map/all_to_all | solution.py:355
  290.4 203.7 %reduce-scatter.5.cloned.1.call-start = ((), (), s32[]{:S(2)}) async-start(), calls=%async_computation.16 | async-start | bytes 7077888 | tf_op jit(solution)/shard_map/reduce_scatter | solution.py:217
  318.8 4.7 collective-permute-start.4
  323.7 4.7 collective-permute-start.5
  330.9 4.7 collective-permute-start.6
  335.6 4.0 collective-permute-start.7
  336.4 3.3 collective-permute-start.39
  339.8 5.7 %collective-permute-start.40 = (f32[2,3,6144]{2,1,0:T(4,128)S(1)}, f32[2,3,6144]{2,1,0:T(4,128)S(1)}, u32[]{:S(2)}, u32[]{:S(2)}) collective-permute-start(f32[2,3,6144]{2,1,0:T(4,128)S(1)} %pad_maximum_fusion.12), channel_id=1, source_target_pairs={{0,8},{4,12},{8,0},{12,4},{16,24},{20,28},{24,16},{28,20},{1,9},{5... | collective-permute-start | bytes 442376 | tf_op jit(solution)/shard_map/ppermute | solution.py:175
  345.7 17.5 %collective-permute-start.41 = (f32[4,3,6144]{2,1,0:T(4,128)S(1)}, f32[4,3,6144]{2,1,0:T(4,128)S(1)}, u32[]{:S(2)}, u32[]{:S(2)}) collective-permute-start(f32[4,3,6144]{2,1,0:T(4,128)S(1)} %pad_maximum_fusion.8), channel_id=1, source_target_pairs={{0,16},{4,20},{8,24},{12,28},{16,0},{20,4},{24,8},{28,12},{1,17},{... | collective-permute-start | bytes 884744 | tf_op jit(solution)/shard_map/ppermute | solution.py:175
  364.6 60.7 %copy-start.51 = (f32[1536]{0:T(1024)}, f32[1536]{0:T(1024)S(1)}, u32[]{:S(2)}) copy-start(f32[1536]{0:T(1024)S(1)} %get-tuple-element.305) | copy-start | bytes 18436
  364.6 60.7 %copy-start.52 = (f32[1536]{0:T(1024)}, f32[1536]{0:T(1024)S(1)}, u32[]{:S(2)}) copy-start(f32[1536]{0:T(1024)S(1)} %get-tuple-element.306) | copy-start | bytes 18436
  366.0 21.8 %collective-permute-start.44 = (f32[2]{0:T(128)S(1)}, f32[2]{0:T(128)S(1)}, u32[]{:S(2)}, u32[]{:S(2)}) collective-permute-start(f32[2]{0:T(128)S(1)} %pad_maximum_fusion.24), channel_id=1, source_target_pairs={{0,1},{1,0},{2,3},{3,2},{4,5},{5,4},{6,7},{7,6},{8,9},{9,8},{10,11... | collective-permute-start | bytes 32 | tf_op jit(solution)/shard_map/ppermute | solution.py:166
  387.7 3.7 collective-permute-start.42
  389.1 31.1 %collective-permute-start.45 = (f32[2]{0:T(128)S(1)}, f32[2]{0:T(128)S(1)}, u32[]{:S(2)}, u32[]{:S(2)}) collective-permute-start(f32[2]{0:T(128)S(1)} %fusion.150), channel_id=1, source_target_pairs={{0,2},{1,3},{2,0},{3,1},{4,6},{5,7},{6,4},{7,5},{8,10},{9,11},{10,... | collective-permute-start | bytes 32 | tf_op jit(solution)/shard_map/ppermute | solution.py:166
  392.8 3.7 collective-permute-start.43
  393.9 5.0 collective-permute-start.15
  399.0 6.2 %collective-permute-start.16 = (bf16[128,256]{1,0:T(8,128)(2,1)S(1)}, bf16[128,256]{1,0:T(8,128)(2,1)S(1)}, u32[]{:S(2)}, u32[]{:S(2)}) collective-permute-start(bf16[128,256]{1,0:T(8,128)(2,1)S(1)} %select_convert_fusion.7), channel_id=1, source_target_pairs={{0,16},{8,24},{16,0},{24,8},{1,17},{9,25},{17,1},{25,9},{2,18},{10... | collective-permute-start | bytes 196616 | tf_op jit(solution)/shard_map/ppermute | solution.py:200
  405.2 11.8 %collective-permute-start.17 = (bf16[128,256]{1,0:T(8,128)(2,1)S(1)}, bf16[128,256]{1,0:T(8,128)(2,1)S(1)}, u32[]{:S(2)}, u32[]{:S(2)}) collective-permute-start(bf16[128,256]{1,0:T(8,128)(2,1)S(1)} %add_convert_fusion.6), channel_id=1, source_target_pairs={{0,16},{8,24},{16,0},{24,8},{1,17},{9,25},{17,1},{25,9},{2,18},{10... | collective-permute-start | bytes 196616 | tf_op jit(solution)/shard_map/ppermute | solution.py:207
  417.0 6.1 %collective-permute-start.18 = (bf16[128,512]{1,0:T(8,128)(2,1)S(1)}, bf16[128,512]{1,0:T(8,128)(2,1)S(1)}, u32[]{:S(2)}, u32[]{:S(2)}) collective-permute-start(bf16[128,512]{1,0:T(8,128)(2,1)S(1)} %pad_maximum_fusion.13), channel_id=1, source_target_pairs={{0,8},{8,0},{16,24},{24,16},{1,9},{9,1},{17,25},{25,17},{2,10},{10... | collective-permute-start | bytes 393224 | tf_op jit(solution)/shard_map/ppermute | solution.py:207
  423.2 2.7 collective-permute-start.19
  430.2 3.6 collective-permute-start.20
  435.2 3.6 collective-permute-start.21
  442.0 8.8 %collective-permute-start.22 = (bf16[128,1024]{1,0:T(8,128)(2,1)}, bf16[128,1024]{1,0:T(8,128)(2,1)S(1)}, u32[]{:S(2)}, u32[]{:S(2)}) collective-permute-start(bf16[128,1024]{1,0:T(8,128)(2,1)} %select_convert_fusion.2), channel_id=1, source_target_pairs={{0,8},{8,0},{16,24},{24,16},{1,9},{9,1},{17,25},{25,17},{2,10},{10... | collective-permute-start | bytes 786440 | tf_op jit(solution)/shard_map/ppermute | solution.py:200
  447.2 9.1 %collective-permute-start.29 = (bf16[256,512]{1,0:T(8,128)(2,1)S(1)}, bf16[256,512]{1,0:T(8,128)(2,1)S(1)}, u32[]{:S(2)}, u32[]{:S(2)}) collective-permute-start(bf16[256,512]{1,0:T(8,128)(2,1)S(1)} %select_convert_fusion.1), channel_id=1, source_target_pairs={{0,8},{8,0},{16,24},{24,16},{1,9},{9,1},{17,25},{25,17},{2,10},{10... | collective-permute-start | bytes 786440 | tf_op jit(solution)/shard_map/ppermute | solution.py:200
  450.9 7.4 %collective-permute-start.23 = (bf16[128,512]{1,0:T(8,128)(2,1)S(1)}, bf16[128,512]{1,0:T(8,128)(2,1)S(1)}, u32[]{:S(2)}, u32[]{:S(2)}) collective-permute-start(bf16[128,512]{1,0:T(8,128)(2,1)S(1)} %select_convert_fusion.5), channel_id=1, source_target_pairs={{0,16},{8,24},{16,0},{24,8},{1,17},{9,25},{17,1},{25,9},{2,18},{10... | collective-permute-start | bytes 393224 | tf_op jit(solution)/shard_map/ppermute | solution.py:200
  456.5 10.9 %collective-permute-start.30 = (bf16[256,256]{1,0:T(8,128)(2,1)S(1)}, bf16[256,256]{1,0:T(8,128)(2,1)S(1)}, u32[]{:S(2)}, u32[]{:S(2)}) collective-permute-start(bf16[256,256]{1,0:T(8,128)(2,1)S(1)} %select_convert_fusion.4), channel_id=1, source_target_pairs={{0,16},{8,24},{16,0},{24,8},{1,17},{9,25},{17,1},{25,9},{2,18},{10... | collective-permute-start | bytes 393224 | tf_op jit(solution)/shard_map/ppermute | solution.py:200
  458.4 11.8 %collective-permute-start.24 = (bf16[128,512]{1,0:T(8,128)(2,1)S(1)}, bf16[128,512]{1,0:T(8,128)(2,1)S(1)}, u32[]{:S(2)}, u32[]{:S(2)}) collective-permute-start(bf16[128,512]{1,0:T(8,128)(2,1)S(1)} %add_convert_fusion.5), channel_id=1, source_target_pairs={{0,16},{8,24},{16,0},{24,8},{1,17},{9,25},{17,1},{25,9},{2,18},{10... | collective-permute-start | bytes 393224 | tf_op jit(solution)/shard_map/ppermute | solution.py:207
  467.5 8.5 %collective-permute-start.31 = (bf16[256,256]{1,0:T(8,128)(2,1)S(1)}, bf16[256,256]{1,0:T(8,128)(2,1)S(1)}, u32[]{:S(2)}, u32[]{:S(2)}) collective-permute-start(bf16[256,256]{1,0:T(8,128)(2,1)S(1)} %add_convert_fusion.4), channel_id=1, source_target_pairs={{0,16},{8,24},{16,0},{24,8},{1,17},{9,25},{17,1},{25,9},{2,18},{10... | collective-permute-start | bytes 393224 | tf_op jit(solution)/shard_map/ppermute | solution.py:207
  470.2 11.4 %collective-permute-start.25 = (bf16[128,1024]{1,0:T(8,128)(2,1)S(1)}, bf16[128,1024]{1,0:T(8,128)(2,1)S(1)}, u32[]{:S(2)}, u32[]{:S(2)}) collective-permute-start(bf16[128,1024]{1,0:T(8,128)(2,1)S(1)} %pad_maximum_fusion.10), channel_id=1, source_target_pairs={{0,8},{8,0},{16,24},{24,16},{1,9},{9,1},{17,25},{25,17},{2,10},{10... | collective-permute-start | bytes 786440 | tf_op jit(solution)/shard_map/ppermute | solution.py:207
  476.0 10.8 %collective-permute-start.32 = (bf16[256,512]{1,0:T(8,128)(2,1)S(1)}, bf16[256,512]{1,0:T(8,128)(2,1)S(1)}, u32[]{:S(2)}, u32[]{:S(2)}) collective-permute-start(bf16[256,512]{1,0:T(8,128)(2,1)S(1)} %pad_maximum_fusion.11), channel_id=1, source_target_pairs={{0,8},{8,0},{16,24},{24,16},{1,9},{9,1},{17,25},{25,17},{2,10},{10... | collective-permute-start | bytes 786440 | tf_op jit(solution)/shard_map/ppermute | solution.py:207
  481.8 5.3 collective-permute-start.26
  487.0 6.8 %collective-permute-start.33 = (bf16[256,1024]{1,0:T(8,128)(2,1)S(1)}, bf16[256,1024]{1,0:T(8,128)(2,1)S(1)}, u32[]{:S(2)}, u32[]{:S(2)}) collective-permute-start(bf16[256,1024]{1,0:T(8,128)(2,1)S(1)} %pad_maximum_fusion.6), channel_id=1, source_target_pairs={{0,4},{4,0},{1,5},{5,1},{2,6},{6,2},{3,7},{7,3},{8,12},{12,8},{9,1... | collective-permute-start | bytes 1572872 | tf_op jit(solution)/shard_map/ppermute | solution.py:219
  492.9 10.8 %collective-permute-start.27 = (f32[1,2]{1,0:T(1,128)S(1)}, f32[1,2]{1,0:T(1,128)S(1)}, u32[]{:S(2)}, u32[]{:S(2)}) collective-permute-start(f32[1,2]{1,0:T(1,128)S(1)} %pad_maximum_fusion.21), channel_id=1, source_target_pairs={{0,1},{1,0},{2,3},{3,2},{4,5},{5,4},{6,7},{7,6},{8,9},{9,8},{10,11... | collective-permute-start | bytes 32 | tf_op jit(solution)/shard_map/ppermute | solution.py:166
  495.6 11.4 %collective-permute-start.8 = (bf16[3,128,512]{2,1,0:T(8,128)(2,1)S(1)}, bf16[3,128,512]{2,1,0:T(8,128)(2,1)S(1)}, u32[]{:S(2)}, u32[]{:S(2)}) collective-permute-start(bf16[3,128,512]{2,1,0:T(8,128)(2,1)S(1)} %select_convert_fusion), channel_id=1, source_target_pairs={{0,8},{8,0},{16,24},{24,16},{1,9},{9,1},{17,25},{25,17},{2,10},{10... | collective-permute-start | bytes 1179656 | tf_op jit(solution)/shard_map/ppermute | solution.py:200
  502.6 6.4 %collective-permute-start.34 = (f32[1,2]{1,0:T(1,128)S(1)}, f32[1,2]{1,0:T(1,128)S(1)}, u32[]{:S(2)}, u32[]{:S(2)}) collective-permute-start(f32[1,2]{1,0:T(1,128)S(1)} %pad_maximum_fusion.22), channel_id=1, source_target_pairs={{0,1},{1,0},{2,3},{3,2},{4,5},{5,4},{6,7},{7,6},{8,9},{9,8},{10,11... | collective-permute-start | bytes 32 | tf_op jit(solution)/shard_map/ppermute | solution.py:166
  505.1 35.9 %collective-permute-start.28 = (f32[1,2]{1,0:T(1,128)S(1)}, f32[1,2]{1,0:T(1,128)S(1)}, u32[]{:S(2)}, u32[]{:S(2)}) collective-permute-start(f32[1,2]{1,0:T(1,128)S(1)} %fusion.153), channel_id=1, source_target_pairs={{0,2},{1,3},{2,0},{3,1},{4,6},{5,7},{6,4},{7,5},{8,10},{9,11},{10,... | collective-permute-start | bytes 32 | tf_op jit(solution)/shard_map/ppermute | solution.py:166
  507.3 11.6 %collective-permute-start.9 = (bf16[3,128,256]{2,1,0:T(8,128)(2,1)S(1)}, bf16[3,128,256]{2,1,0:T(8,128)(2,1)S(1)}, u32[]{:S(2)}, u32[]{:S(2)}) collective-permute-start(bf16[3,128,256]{2,1,0:T(8,128)(2,1)S(1)} %select_convert_fusion.3), channel_id=1, source_target_pairs={{0,16},{8,24},{16,0},{24,8},{1,17},{9,25},{17,1},{25,9},{2,18},{10... | collective-permute-start | bytes 589832 | tf_op jit(solution)/shard_map/ppermute | solution.py:200
  510.3 8.8 %collective-permute-start.35 = (f32[1,2]{1,0:T(1,128)S(1)}, f32[1,2]{1,0:T(1,128)S(1)}, u32[]{:S(2)}, u32[]{:S(2)}) collective-permute-start(f32[1,2]{1,0:T(1,128)S(1)} %fusion.152), channel_id=1, source_target_pairs={{0,2},{1,3},{2,0},{3,1},{4,6},{5,7},{6,4},{7,5},{8,10},{9,11},{10,... | collective-permute-start | bytes 32 | tf_op jit(solution)/shard_map/ppermute | solution.py:166
  519.0 11.0 %collective-permute-start.10 = (bf16[3,128,256]{2,1,0:T(8,128)(2,1)S(1)}, bf16[3,128,256]{2,1,0:T(8,128)(2,1)S(1)}, u32[]{:S(2)}, u32[]{:S(2)}) collective-permute-start(bf16[3,128,256]{2,1,0:T(8,128)(2,1)S(1)} %add_convert_fusion.3), channel_id=1, source_target_pairs={{0,16},{8,24},{16,0},{24,8},{1,17},{9,25},{17,1},{25,9},{2,18},{10... | collective-permute-start | bytes 589832 | tf_op jit(solution)/shard_map/ppermute | solution.py:207
  530.1 10.6 %collective-permute-start.11 = (bf16[3,128,512]{2,1,0:T(8,128)(2,1)S(1)}, bf16[3,128,512]{2,1,0:T(8,128)(2,1)S(1)}, u32[]{:S(2)}, u32[]{:S(2)}) collective-permute-start(bf16[3,128,512]{2,1,0:T(8,128)(2,1)S(1)} %pad_maximum_fusion.7), channel_id=1, source_target_pairs={{0,8},{8,0},{16,24},{24,16},{1,9},{9,1},{17,25},{25,17},{2,10},{10... | collective-permute-start | bytes 1179656 | tf_op jit(solution)/shard_map/ppermute | solution.py:207
  540.9 6.2 %collective-permute-start.12 = (bf16[3,128,1024]{2,1,0:T(8,128)(2,1)S(1)}, bf16[3,128,1024]{2,1,0:T(8,128)(2,1)S(1)}, u32[]{:S(2)}, u32[]{:S(2)}) collective-permute-start(bf16[3,128,1024]{2,1,0:T(8,128)(2,1)S(1)} %pad_maximum_fusion.1), channel_id=1, source_target_pairs={{0,4},{4,0},{1,5},{5,1},{2,6},{6,2},{3,7},{7,3},{8,12},{12,8},{9,1... | collective-permute-start | bytes 2359304 | tf_op jit(solution)/shard_map/ppermute | solution.py:219
  554.9 3.6 collective-permute-start.13
  558.5 3.6 collective-permute-start.14
  (66 other events, 713.1 us)
Sparse Core Ops, SparseCore 0:
  10.5 50.3 all-gather.4
  63.4 32.6 all-gather.6
  98.6 39.5 all-gather.8
  140.5 36.5 all-gather.10
  194.7 41.0 reduce-scatter.6
  239.1 63.9 reduce-scatter.8
  306.4 50.6 reduce-scatter.10
  360.5 61.6 reduce-scatter.4

commit v4 on v3

--- a/solution.py
+++ b/solution.py
@@ -192,14 +192,15 @@
     index = lax.axis_index(axis_name)
     total = values.astype(jnp.float32)
     step = 1
+    last = total.ndim - 1
     while step < size:
         half = total.shape[-1] // 2
-        low_side = (index // step) % 2 == 0
-        keep = jnp.where(low_side, total[..., :half], total[..., half:])
-        send = jnp.where(low_side, total[..., half:], total[..., :half]).astype(jnp.bfloat16)
-        total = keep + lax.ppermute(send, axis_name, [(i, i ^ step) for i in range(size)]).astype(
-            jnp.float32
-        )
+        high_bit = (index // step) % 2
+        keep = lax.dynamic_slice_in_dim(total, high_bit * half, half, last)
+        send = lax.dynamic_slice_in_dim(total, (1 - high_bit) * half, half, last)
+        total = keep + lax.ppermute(
+            send.astype(jnp.bfloat16), axis_name, [(i, i ^ step) for i in range(size)]
+        ).astype(jnp.float32)
         step *= 2
     blocks = total.astype(jnp.bfloat16)
     step = size // 2
@@ -413,7 +414,9 @@
     )
     time_grad = jax.vjp(jax.nn.silu, time_emb)[1](grad_silu)[0]
     totals = (
-        reduce_rows(grad_qkv_local.astype(jnp.bfloat16), 1).astype(jnp.float32),
+        jnp.stack(
+            [reduce_rows(grad_qkv_local[part].astype(jnp.bfloat16), 0) for part in range(3)]
+        ).astype(jnp.float32),
         reduce_rows(grad_out_local.astype(jnp.bfloat16), 0).astype(jnp.float32),
         reduce_rows(grad_up_local.astype(jnp.bfloat16), 0).astype(jnp.float32),
         reduce_rows(grad_down_local.astype(jnp.bfloat16), 0).astype(jnp.float32),

time: 583 us -> 599 us (1.027)
  blocking collectives: 11 us -> 23.6 us
    all_to_all x0 -> x1, blocking collectives: none -> 12.6 us  [local(): lax.all_to_all(grad_value_heads, 'seq', split_axis=0, concat_axis=1, tile...]
    ppermute x8 -> x12, waiting for transfers between devices: 34.5 us -> 23.2 us  [halving_sum(): lax.ppermute(blocks, axis_name, [(i, i ^ step) for i in range(size)])]
    ppermute x8 -> x12, waiting for transfers between devices: 24.1 us -> 33.9 us  [halving_sum(): lax.ppermute(send.astype(jnp.bfloat16), axis_name, [(i, i ^ step) for i i...]
    ppermute x8 -> x12, starting transfers between devices: 9.46 us -> 16.7 us  [halving_sum(): lax.ppermute(send.astype(jnp.bfloat16), axis_name, [(i, i ^ step) for i i...]
  transfers between devices with their start and end apart: 61 -> 72, of which waited for: 36 -> 46; matrix products, arithmetic and copies ran while one was open for 41% -> 41% of each run, Pallas kernels for 0% -> 0%
where the time goes in v4:
time: 599 us; the launch traced here: 591 us
  waiting for transfers between devices  175 us (29%)
  matrix products  117 us (20%)
  other arithmetic  96.1 us (16%)
  starting transfers between devices  88.5 us (15%)
  local copies, waits for them, and re-layouts  64.7 us (11%)
  blocking collectives  23.6 us (4%)
  between operations  23.3 us (4%)
    all_gather x4, waiting for transfers between devices, gather_rows(): return lax.all_gather(piece, ('seq', 'core'), axis=row_axis, tiled=True)  36.8 us
    ppermute x12, waiting for transfers between devices, halving_sum(): lax.ppermute(send.astype(jnp.bfloat16), axis_name, [(i, i ^ step) for i i...  33.9 us
    ppermute x10, waiting for transfers between devices, doubling_gather(): other = lax.ppermute(blocks, axes, [(i, i ^ step) for i in range(size)])  27 us
    ppermute x16, waiting for transfers between devices, butterfly_sum(): lax.ppermute(values, axes, [(i, i ^ step) for i in range(size)])  23.9 us
    ppermute x12, waiting for transfers between devices, halving_sum(): lax.ppermute(blocks, axis_name, [(i, i ^ step) for i in range(size)])  23.2 us
    sub x6, other arithmetic, local(): new_masters.append(masters[param] - step_rate * ratio * directions[param])  21.9 us
    ppermute x16, starting transfers between devices, butterfly_sum(): lax.ppermute(values, axes, [(i, i ^ step) for i in range(size)])  18.8 us
    reduce_sum x5, other arithmetic, local(): jnp.sum(masters[param] * masters[param], axis=sum_axes, keepdims=True)  17.4 us
  transfers between devices with their start and end apart: 72, of which 46 were waited for; matrix products, arithmetic and copies ran while one was open for 41% of the time, Pallas kernels for 0%

profile of v4, /device:TPU:0, one launch (start us, length us, event | category | flops | bytes accessed | tf_op | source)
XLA Modules:
  0.0 591.1 jit_solution(13898546770577660374)
XLA Ops:
  13.8 3.0 collective-permute-start.2
  16.9 3.4 fusion.38
  28.5 5.3 collective-permute-done.1
  33.9 2.7 fusion.68
  36.6 2.7 copy-done
  39.6 21.3 %all-gather.5.cloned.1.call-done = bf16[3,1024,1024]{2,1,0:T(8,128)(2,1)} async-done(((bf16[3,128,1024]{2,1,0:T(8,128)(2,1)}), bf16[3,1024,1024]{2,1,0:T(8,128)(2,1)}) %all-gather.5.cloned.1.call-update) | async-done | bytes 6291472 | tf_op jit(solution)/shard_map/all_gather | solution.py:188
  60.9 4.7 slice_bitcast_fusion.3
  65.6 2.9 copy.145
  70.6 2.9 copy.141
  81.0 3.5 all-to-all-start
  86.0 9.2 %all-to-all-done = bf16[256,4,256]{0,2,1:T(8,128)(2,1)S(1)} async-done(((bf16[256,4,256]{0,2,1:T(8,128)(2,1)}), bf16[256,4,256]{0,2,1:T(8,128)(2,1)S(1)}, u32[]{:S(2)}, u32[]{:S(2)}) %all-to-all-start) | async-done | bytes 524320 | tf_op jit(solution)/shard_map/all_to_all | solution.py:300
  95.2 3.5 all-to-all-start.1
  101.9 5.2 all-to-all-done.1
  107.0 3.5 all-to-all-start.2
  113.8 5.9 all-to-all-done.2
  120.7 18.7 %while.27 = (s32[]{:T(128)}, bf16[2,512,256]{2,1,0:T(8,128)(2,1)S(1)}, f32[2,4,512,1]{2,1,3,0:T(4,128)S(1)}, s32[2]{0:T(128)S(1)}, s32[1024]{0:T(1024)S(1)}, /*i...) while((s32[]{:T(128)}, ...), condition=%wide.region_9.10_spmd, body=%wide.region_6.9_spmd.sunk | while | flops 561117184 | bytes 30485712 | solution.py:110
  126.5 3.3 fusion.184
  135.9 3.3 fusion.184
  139.4 11.0 %all_to_all.134 = bf16[4,256,256]{2,1,0:T(8,128)(2,1)S(1)} all-to-all(bf16[4,256,256]{2,1,0:T(8,128)(2,1)S(1)} %bitcast.262), channel_id=1, replica_groups=mesh['z'=4,'core'=2,'seq'=4] {'seq'}, dimensions={0} | all-to-all | bytes 1048576 | tf_op jit(solution)/shard_map/all_to_all | solution.py:307
  150.6 3.7 fusion.103
  156.6 5.0 fusion.112
  161.6 15.5 %all-gather.11.cloned.1.call-done = bf16[2048,1024]{1,0:T(8,128)(2,1)} async-done(((bf16[256,1024]{1,0:T(8,128)(2,1)}), bf16[2048,1024]{1,0:T(8,128)(2,1)}) %all-gather.11.cloned.1.call-update) | async-done | bytes 4194320 | tf_op jit(solution)/shard_map/all_gather | solution.py:188
  177.1 5.6 fusion.21
  182.8 3.1 multiply_reduce_fusion.11
  186.3 4.3 fusion.102
  194.5 4.2 all-to-all-start.4
  198.8 3.1 convolution_convert_fusion.2
  201.9 8.6 %reduce-scatter.11.cloned.1.call-start = ((), (), s32[]{:S(2)}) async-start(), calls=%async_computation.20 | async-start | bytes 2359296 | tf_op jit(solution)/shard_map/reduce_scatter | solution.py:218
  211.4 35.6 %while.28 = (s32[]{:T(128)}, f32[1024,256]{0,1:T(8,128)S(1)}, f32[1024,256]{0,1:T(8,128)S(1)}, bf16[2,512,256]{2,1,0:T(8,128)(2,1)}, s32[2]{0:T(128)S(1)}, /*ind...) while((s32[]{:T(128)}, f32[1024,256]{0,1:T(8,128)S(1)}, ...), condition=%wide.region_16.17_spmd.clone, body=%wide.region_14.16_spmd.clone.sunk | while | flops 1376253952 | bytes 78974200 | solution.py:155
  219.0 4.2 multiply_reduce_fusion.16
  236.8 4.2 multiply_reduce_fusion.16
  247.2 12.6 %all_to_all.135 = bf16[4,256,256]{2,1,0:T(8,128)(2,1)S(1)} all-to-all(bf16[4,256,256]{2,1,0:T(8,128)(2,1)S(1)} %bitcast.257), channel_id=1, replica_groups=mesh['z'=4,'core'=2,'seq'=4] {'seq'}, dimensions={0} | all-to-all | bytes 1048576 | tf_op jit(solution)/shard_map/all_to_all | solution.py:356
  262.1 3.5 all-to-all-start.5
  266.5 5.9 all-to-all-done.5
  272.4 3.5 all-to-all-start.6
  279.4 3.0 all-to-all-done.6
  283.5 2.8 reshape.410
  296.1 4.6 convolution_convert_fusion.1
  311.1 3.0 constant_dynamic-update-slice_fusion.3
  319.1 2.8 fusion.82
  328.2 5.0 collective-permute-done.5
  333.2 5.4 fusion.51
  340.0 5.1 convolution_convert_fusion
  345.9 3.0 collective-permute-done.7
  350.6 4.2 collective-permute-done.50
  358.0 14.6 %collective-permute-done.51 = f32[4,3,6144]{2,1,0:T(4,128)S(1)} collective-permute-done((f32[4,3,6144]{2,1,0:T(4,128)S(1)}, f32[4,3,6144]{2,1,0:T(4,128)S(1)}, u32[]{:S(2)}, u32[]{:S(2)}) %collective-permute-start.51) | collective-permute-done | bytes 294944 | tf_op jit(solution)/shard_map/ppermute | solution.py:175
  375.4 3.0 collective-permute-start.54
  378.4 17.2 %multiply_reduce_fusion.2 = (f32[]{:T(128)}, f32[]{:T(128)}, f32[256,6144]{1,0:T(8,128)}, f32[256,6144]{1,0:T(8,128)}, f32[256,6144]{1,0:T(8,128)}) fusion(f32[256,6144]{1,0:T(8,128)} %param.44, f32[256,6144]{1,0:T(8,128)} %param.45, f32[256,6144]{1,0:T(8,128)} %param.46, f32[8,3,6144]{2,1,0:T(4,128)S(1)} %pad_maximum_fusion, ...), kind=kOutput, calls=%fused_computation.39 | convolution fusion | flops 479748096 | bytes 38350856 | tf_op jit(solution)/shard_map/cd,ce->de/dot_general | solution.py:406
  411.6 3.8 collective-permute-done.26
  415.5 11.7 %multiply_subtract_fusion = f32[256,6144]{1,0:T(8,128)} fusion(f32[256,6144]{1,0:T(8,128)} %param.44, f32[]{:T(128)} %bitcast.63, f32[256,6144]{1,0:T(8,128)} %get-tuple-element.308, f32[256,6144]{1,0:T(8,128)} %get-tuple-element.307), kind=kLoop, calls=%fused_computation.35 | loop fusion | flops 12582912 | bytes 25165828 | tf_op jit(solution)/shard_map/sub | solution.py:450
  460.2 2.8 collective-permute-start.19
  469.7 3.5 collective-permute-done.9
  473.3 2.7 collective-permute-done.14
  481.5 3.2 collective-permute-done.21
  491.1 6.9 %multiply_reduce_fusion.4 = (f32[3]{0:T(128)S(1)}, f32[3]{0:T(128)S(1)}, f32[3,256,1024]{2,1,0:T(8,128)}, f32[3,256,1024]{2,1,0:T(8,128)}, f32[3,256,1024]{2,1,0:T(8,128)}) fusion(f32[3,256,1024]{2,1,0:T(8,128)S(1)} %copy-done.6, f32[3,256,1024]{2,1,0:T(8,128)S(1)} %copy-done.32, f32[3,256,1024]{2,1,0:T(8,128)S(1)} %copy-done.33, ...), kind=kLoop, calls=%fused_computation.50 | loop fusion | flops 15728634 | bytes 20447256 | tf_op jit(solution)/shard_map/reduce_sum | solution.py:442
  511.6 7.0 %collective-permute-done.32 = bf16[128,1024]{1,0:T(8,128)(2,1)S(1)} collective-permute-done((bf16[128,1024]{1,0:T(8,128)(2,1)}, bf16[128,1024]{1,0:T(8,128)(2,1)S(1)}, u32[]{:S(2)}, u32[]{:S(2)}) %collective-permute-start.32) | collective-permute-done | bytes 262176 | tf_op jit(solution)/shard_map/ppermute | solution.py:201
  522.9 7.7 %collective-permute-done.33 = bf16[128,512]{1,0:T(8,128)(2,1)S(1)} collective-permute-done((bf16[128,512]{1,0:T(8,128)(2,1)S(1)}, bf16[128,512]{1,0:T(8,128)(2,1)S(1)}, u32[]{:S(2)}, u32[]{:S(2)}) %collective-permute-start.33) | collective-permute-done | bytes 131104 | tf_op jit(solution)/shard_map/ppermute | solution.py:201
  530.7 5.4 collective-permute-done.40
  538.8 3.7 collective-permute-done.41
  542.6 5.5 collective-permute-done.35
  548.3 3.3 multiply_subtract_fusion.1
  553.9 3.7 multiply_reduce_fusion.8
  557.6 2.9 pad_maximum_fusion.24
  561.5 3.7 multiply_reduce_fusion.6
  (519 shorter events, 229.8 us)
Async XLA Ops:
  7.2 53.7 %all-gather.5.cloned.1.call-start = ((), (), s32[]{:S(2)}) async-start(), calls=%async_computation.14 | async-start | bytes 7077888 | tf_op jit(solution)/shard_map/all_gather | solution.py:188
  9.7 140.9 %all-gather.7.cloned.1.call-start = ((), (), s32[]{:S(2)}) async-start(), calls=%async_computation.15 | async-start | bytes 2359296 | tf_op jit(solution)/shard_map/all_gather | solution.py:188
  11.6 145.0 %all-gather.9.cloned.1.call-start = ((), (), s32[]{:S(2)}) async-start(), calls=%async_computation.16 | async-start | bytes 4718592 | tf_op jit(solution)/shard_map/all_gather | solution.py:188
  13.8 8.3 %collective-permute-start.2 = (bf16[1,1536]{1,0:T(2,128)(2,1)S(1)}, bf16[1,1536]{1,0:T(2,128)(2,1)S(1)}, u32[]{:S(2)}, u32[]{:S(2)}) collective-permute-start(bf16[1,1536]{1,0:T(2,128)(2,1)S(1)} %broadcast_in_dim.158), channel_id=1, source_target_pairs={{0,1},{1,0},{2,3},{3,2},{4,5},{5,4},{6,7},{7,6},{8,9},{9,8},{10,11... | collective-permute-start | bytes 9224 | tf_op jit(solution)/shard_map/ppermute | solution.py:175
  20.3 6.6 %collective-permute-start = (f32[3,6144]{1,0:T(4,128)S(1)}, f32[3,6144]{1,0:T(4,128)S(1)}, u32[]{:S(2)}, u32[]{:S(2)}) collective-permute-start(f32[3,6144]{1,0:T(4,128)S(1)} %fusion.38), channel_id=1, source_target_pairs={{0,1},{1,0},{2,3},{3,2},{4,5},{5,4},{6,7},{7,6},{8,9},{9,8},{10,11... | collective-permute-start | bytes 221192 | tf_op jit(solution)/shard_map/ppermute | solution.py:166
  22.2 3.9 collective-permute-start.3
  26.9 6.9 %collective-permute-start.1 = (f32[3,6144]{1,0:T(4,128)S(1)}, f32[3,6144]{1,0:T(4,128)S(1)}, u32[]{:S(2)}, u32[]{:S(2)}) collective-permute-start(f32[3,6144]{1,0:T(4,128)S(1)} %add.451), channel_id=1, source_target_pairs={{0,2},{1,3},{2,0},{3,1},{4,6},{5,7},{6,4},{7,5},{8,10},{9,11},{10,... | collective-permute-start | bytes 221192 | tf_op jit(solution)/shard_map/ppermute | solution.py:166
  81.0 14.2 %all-to-all-start = ((bf16[256,4,256]{0,2,1:T(8,128)(2,1)}), bf16[256,4,256]{0,2,1:T(8,128)(2,1)S(1)}, u32[]{:S(2)}, u32[]{:S(2)}) async-start(bf16[256,4,256]{0,2,1:T(8,128)(2,1)} %convert_element_type.303), calls=%async_computation | async-start | bytes 1048576 | tf_op jit(solution)/shard_map/all_to_all | solution.py:300
  95.2 11.8 %all-to-all-start.1 = ((bf16[256,4,256]{0,2,1:T(8,128)(2,1)}), bf16[256,4,256]{0,2,1:T(8,128)(2,1)S(1)}, u32[]{:S(2)}, u32[]{:S(2)}) async-start(bf16[256,4,256]{0,2,1:T(8,128)(2,1)} %convert_element_type.304), calls=%async_computation.1 | async-start | bytes 1048576 | tf_op jit(solution)/shard_map/all_to_all | solution.py:301
  107.0 12.6 %all-to-all-start.2 = ((bf16[256,4,256]{2,0,1:T(8,128)(2,1)}), bf16[256,4,256]{2,0,1:T(8,128)(2,1)S(1)}, u32[]{:S(2)}, u32[]{:S(2)}) async-start(bf16[256,4,256]{2,0,1:T(8,128)(2,1)} %bitcast.190), calls=%async_computation.2 | async-start | bytes 1048576 | tf_op jit(solution)/shard_map/all_to_all | solution.py:302
  110.5 66.6 %all-gather.11.cloned.1.call-start = ((), (), s32[]{:S(2)}) async-start(), calls=%async_computation.17 | async-start | bytes 4718592 | tf_op jit(solution)/shard_map/all_gather | solution.py:188
  194.5 16.0 %all-to-all-start.4 = ((bf16[256,4,256]{2,0,1:T(8,128)(2,1)}), bf16[256,4,256]{2,0,1:T(8,128)(2,1)}, u32[]{:S(2)}, u32[]{:S(2)}) async-start(bf16[256,4,256]{2,0,1:T(8,128)(2,1)} %bitcast.189), calls=%async_computation.4 | async-start | bytes 1048576 | tf_op jit(solution)/shard_map/all_to_all | solution.py:342
  198.7 203.3 %reduce-scatter.13.cloned.1.call-start = ((), (), s32[]{:S(2)}) async-start(), calls=%async_computation.21 | async-start | bytes 2359296 | tf_op jit(solution)/shard_map/reduce_scatter | solution.py:218
  201.9 250.8 %reduce-scatter.11.cloned.1.call-start = ((), (), s32[]{:S(2)}) async-start(), calls=%async_computation.20 | async-start | bytes 2359296 | tf_op jit(solution)/shard_map/reduce_scatter | solution.py:218
  262.1 10.3 %all-to-all-start.5 = ((bf16[4,256,256]{2,1,0:T(8,128)(2,1)}), bf16[4,256,256]{2,1,0:T(8,128)(2,1)S(1)}, u32[]{:S(2)}, u32[]{:S(2)}) async-start(bf16[4,256,256]{2,1,0:T(8,128)(2,1)} %bitcast.32), calls=%async_computation.5 | async-start | bytes 1048576 | tf_op jit(solution)/shard_map/all_to_all | solution.py:354
  272.4 10.0 %all-to-all-start.6 = ((bf16[4,256,256]{1,2,0:T(8,128)(2,1)}), bf16[4,256,256]{1,2,0:T(8,128)(2,1)S(1)}, u32[]{:S(2)}, u32[]{:S(2)}) async-start(bf16[4,256,256]{1,2,0:T(8,128)(2,1)} %bitcast.188), calls=%async_computation.6 | async-start | bytes 1048576 | tf_op jit(solution)/shard_map/all_to_all | solution.py:355
  275.9 180.0 %reduce-scatter.7.cloned.1.call-start = ((), (), s32[]{:S(2)}) async-start(), calls=%async_computation.18 | async-start | bytes 2359296 | tf_op jit(solution)/shard_map/reduce_scatter | solution.py:218
  293.0 164.0 %reduce-scatter.9.cloned.1.call-start = ((), (), s32[]{:S(2)}) async-start(), calls=%async_computation.19 | async-start | bytes 2359296 | tf_op jit(solution)/shard_map/reduce_scatter | solution.py:218
  296.0 209.4 %reduce-scatter.15.cloned.1.call-start = ((), (), s32[]{:S(2)}) async-start(), calls=%async_computation.22 | async-start | bytes 4718592 | tf_op jit(solution)/shard_map/reduce_scatter | solution.py:218
  300.7 207.8 %reduce-scatter.17.cloned.1.call-start = ((), (), s32[]{:S(2)}) async-start(), calls=%async_computation.23 | async-start | bytes 4718592 | tf_op jit(solution)/shard_map/reduce_scatter | solution.py:218
  302.6 3.7 collective-permute-start.47
  322.0 4.7 collective-permute-start.4
  323.4 4.8 collective-permute-start.48
  326.7 6.5 %collective-permute-start.5 = (f32[3,6144]{1,0:T(4,128)S(1)}, f32[3,6144]{1,0:T(4,128)S(1)}, u32[]{:S(2)}, u32[]{:S(2)}) collective-permute-start(f32[3,6144]{1,0:T(4,128)S(1)} %add.477), channel_id=1, source_target_pairs={{0,2},{1,3},{2,0},{3,1},{4,6},{5,7},{6,4},{7,5},{8,10},{9,11},{10,... | collective-permute-start | bytes 221192 | tf_op jit(solution)/shard_map/ppermute | solution.py:166
  338.6 6.6 %collective-permute-start.6 = (f32[1,3,256]{2,1,0:T(4,128)S(1)}, f32[1,3,256]{2,1,0:T(4,128)S(1)}, u32[]{:S(2)}, u32[]{:S(2)}) collective-permute-start(f32[1,3,256]{2,1,0:T(4,128)S(1)} %fusion.51), channel_id=1, source_target_pairs={{0,1},{1,0},{2,3},{3,2},{4,5},{5,4},{6,7},{7,6},{8,9},{9,8},{10,11... | collective-permute-start | bytes 9224 | tf_op jit(solution)/shard_map/ppermute | solution.py:175
  345.2 3.7 collective-permute-start.7
  349.0 5.7 collective-permute-start.50
  354.9 17.7 %collective-permute-start.51 = (f32[4,3,6144]{2,1,0:T(4,128)S(1)}, f32[4,3,6144]{2,1,0:T(4,128)S(1)}, u32[]{:S(2)}, u32[]{:S(2)}) collective-permute-start(f32[4,3,6144]{2,1,0:T(4,128)S(1)} %pad_maximum_fusion.5), channel_id=1, source_target_pairs={{0,16},{4,20},{8,24},{12,28},{16,0},{20,4},{24,8},{28,12},{1,17},{... | collective-permute-start | bytes 884744 | tf_op jit(solution)/shard_map/ppermute | solution.py:175
  375.4 21.6 %collective-permute-start.54 = (f32[2]{0:T(128)S(1)}, f32[2]{0:T(128)S(1)}, u32[]{:S(2)}, u32[]{:S(2)}) collective-permute-start(f32[2]{0:T(128)S(1)} %pad_maximum_fusion.27), channel_id=1, source_target_pairs={{0,1},{1,0},{2,3},{3,2},{4,5},{5,4},{6,7},{7,6},{8,9},{9,8},{10,11... | collective-permute-start | bytes 32 | tf_op jit(solution)/shard_map/ppermute | solution.py:166
  397.0 3.6 collective-permute-start.52
  398.4 31.1 %collective-permute-start.55 = (f32[2]{0:T(128)S(1)}, f32[2]{0:T(128)S(1)}, u32[]{:S(2)}, u32[]{:S(2)}) collective-permute-start(f32[2]{0:T(128)S(1)} %fusion.151), channel_id=1, source_target_pairs={{0,2},{1,3},{2,0},{3,1},{4,6},{5,7},{6,4},{7,5},{8,10},{9,11},{10,... | collective-permute-start | bytes 32 | tf_op jit(solution)/shard_map/ppermute | solution.py:166
  403.1 5.0 collective-permute-start.25
  408.2 7.3 %collective-permute-start.26 = (bf16[128,256]{1,0:T(8,128)(2,1)S(1)}, bf16[128,256]{1,0:T(8,128)(2,1)S(1)}, u32[]{:S(2)}, u32[]{:S(2)}) collective-permute-start(bf16[128,256]{1,0:T(8,128)(2,1)S(1)} %dynamic-slice_convert_fusion.12), channel_id=1, source_target_pairs={{0,16},{8,24},{16,0},{24,8},{1,17},{9,25},{17,1},{25,9},{2,18},{10... | collective-permute-start | bytes 196616 | tf_op jit(solution)/shard_map/ppermute | solution.py:201
  415.5 11.8 %collective-permute-start.27 = (bf16[128,256]{1,0:T(8,128)(2,1)S(1)}, bf16[128,256]{1,0:T(8,128)(2,1)S(1)}, u32[]{:S(2)}, u32[]{:S(2)}) collective-permute-start(bf16[128,256]{1,0:T(8,128)(2,1)S(1)} %add_convert_fusion.5), channel_id=1, source_target_pairs={{0,16},{8,24},{16,0},{24,8},{1,17},{9,25},{17,1},{25,9},{2,18},{10... | collective-permute-start | bytes 196616 | tf_op jit(solution)/shard_map/ppermute | solution.py:208
  427.2 5.2 collective-permute-start.28
  439.3 3.6 collective-permute-start.30
  453.7 6.4 %collective-permute-start.18 = (bf16[128,512]{1,0:T(8,128)(2,1)S(1)}, bf16[128,512]{1,0:T(8,128)(2,1)S(1)}, u32[]{:S(2)}, u32[]{:S(2)}) collective-permute-start(bf16[128,512]{1,0:T(8,128)(2,1)S(1)} %dynamic-slice_convert_fusion.9), channel_id=1, source_target_pairs={{0,8},{8,0},{16,24},{24,16},{1,9},{9,1},{17,25},{25,17},{2,10},{10... | collective-permute-start | bytes 393224 | tf_op jit(solution)/shard_map/ppermute | solution.py:201
  456.9 6.8 %collective-permute-start.8 = (bf16[128,512]{1,0:T(8,128)(2,1)S(1)}, bf16[128,512]{1,0:T(8,128)(2,1)S(1)}, u32[]{:S(2)}, u32[]{:S(2)}) collective-permute-start(bf16[128,512]{1,0:T(8,128)(2,1)S(1)} %dynamic-slice_convert_fusion.11), channel_id=1, source_target_pairs={{0,8},{8,0},{16,24},{24,16},{1,9},{9,1},{17,25},{25,17},{2,10},{10... | collective-permute-start | bytes 393224 | tf_op jit(solution)/shard_map/ppermute | solution.py:201
  458.0 8.5 %collective-permute-start.13 = (bf16[128,512]{1,0:T(8,128)(2,1)S(1)}, bf16[128,512]{1,0:T(8,128)(2,1)S(1)}, u32[]{:S(2)}, u32[]{:S(2)}) collective-permute-start(bf16[128,512]{1,0:T(8,128)(2,1)S(1)} %dynamic-slice_convert_fusion.10), channel_id=1, source_target_pairs={{0,8},{8,0},{16,24},{24,16},{1,9},{9,1},{17,25},{25,17},{2,10},{10... | collective-permute-start | bytes 393224 | tf_op jit(solution)/shard_map/ppermute | solution.py:201
  460.2 8.4 %collective-permute-start.19 = (bf16[128,256]{1,0:T(8,128)(2,1)S(1)}, bf16[128,256]{1,0:T(8,128)(2,1)S(1)}, u32[]{:S(2)}, u32[]{:S(2)}) collective-permute-start(bf16[128,256]{1,0:T(8,128)(2,1)S(1)} %dynamic-slice_convert_fusion.13), channel_id=1, source_target_pairs={{0,16},{8,24},{16,0},{24,8},{1,17},{9,25},{17,1},{25,9},{2,18},{10... | collective-permute-start | bytes 196616 | tf_op jit(solution)/shard_map/ppermute | solution.py:201
  463.8 9.4 %collective-permute-start.9 = (bf16[128,256]{1,0:T(8,128)(2,1)S(1)}, bf16[128,256]{1,0:T(8,128)(2,1)S(1)}, u32[]{:S(2)}, u32[]{:S(2)}) collective-permute-start(bf16[128,256]{1,0:T(8,128)(2,1)S(1)} %dynamic-slice_convert_fusion.15), channel_id=1, source_target_pairs={{0,16},{8,24},{16,0},{24,8},{1,17},{9,25},{17,1},{25,9},{2,18},{10... | collective-permute-start | bytes 196616 | tf_op jit(solution)/shard_map/ppermute | solution.py:201
  466.6 9.4 %collective-permute-start.14 = (bf16[128,256]{1,0:T(8,128)(2,1)S(1)}, bf16[128,256]{1,0:T(8,128)(2,1)S(1)}, u32[]{:S(2)}, u32[]{:S(2)}) collective-permute-start(bf16[128,256]{1,0:T(8,128)(2,1)S(1)} %dynamic-slice_convert_fusion.14), channel_id=1, source_target_pairs={{0,16},{8,24},{16,0},{24,8},{1,17},{9,25},{17,1},{25,9},{2,18},{10... | collective-permute-start | bytes 196616 | tf_op jit(solution)/shard_map/ppermute | solution.py:201
  468.6 9.6 %collective-permute-start.20 = (bf16[128,256]{1,0:T(8,128)(2,1)S(1)}, bf16[128,256]{1,0:T(8,128)(2,1)S(1)}, u32[]{:S(2)}, u32[]{:S(2)}) collective-permute-start(bf16[128,256]{1,0:T(8,128)(2,1)S(1)} %add_convert_fusion.6), channel_id=1, source_target_pairs={{0,16},{8,24},{16,0},{24,8},{1,17},{9,25},{17,1},{25,9},{2,18},{10... | collective-permute-start | bytes 196616 | tf_op jit(solution)/shard_map/ppermute | solution.py:208
  473.2 5.9 %collective-permute-start.10 = (bf16[128,256]{1,0:T(8,128)(2,1)S(1)}, bf16[128,256]{1,0:T(8,128)(2,1)S(1)}, u32[]{:S(2)}, u32[]{:S(2)}) collective-permute-start(bf16[128,256]{1,0:T(8,128)(2,1)S(1)} %add_convert_fusion.8), channel_id=1, source_target_pairs={{0,16},{8,24},{16,0},{24,8},{1,17},{9,25},{17,1},{25,9},{2,18},{10... | collective-permute-start | bytes 196616 | tf_op jit(solution)/shard_map/ppermute | solution.py:208
  476.0 5.3 collective-permute-start.15
  478.2 6.4 %collective-permute-start.21 = (bf16[128,512]{1,0:T(8,128)(2,1)S(1)}, bf16[128,512]{1,0:T(8,128)(2,1)S(1)}, u32[]{:S(2)}, u32[]{:S(2)}) collective-permute-start(bf16[128,512]{1,0:T(8,128)(2,1)S(1)} %pad_maximum_fusion.15), channel_id=1, source_target_pairs={{0,8},{8,0},{16,24},{24,16},{1,9},{9,1},{17,25},{25,17},{2,10},{10... | collective-permute-start | bytes 393224 | tf_op jit(solution)/shard_map/ppermute | solution.py:208
  479.2 7.6 %collective-permute-start.11 = (bf16[128,512]{1,0:T(8,128)(2,1)S(1)}, bf16[128,512]{1,0:T(8,128)(2,1)S(1)}, u32[]{:S(2)}, u32[]{:S(2)}) collective-permute-start(bf16[128,512]{1,0:T(8,128)(2,1)S(1)} %pad_maximum_fusion.13), channel_id=1, source_target_pairs={{0,8},{8,0},{16,24},{24,16},{1,9},{9,1},{17,25},{25,17},{2,10},{10... | collective-permute-start | bytes 393224 | tf_op jit(solution)/shard_map/ppermute | solution.py:208
  481.4 6.8 %collective-permute-start.16 = (bf16[128,512]{1,0:T(8,128)(2,1)S(1)}, bf16[128,512]{1,0:T(8,128)(2,1)S(1)}, u32[]{:S(2)}, u32[]{:S(2)}) collective-permute-start(bf16[128,512]{1,0:T(8,128)(2,1)S(1)} %pad_maximum_fusion.14), channel_id=1, source_target_pairs={{0,8},{8,0},{16,24},{24,16},{1,9},{9,1},{17,25},{25,17},{2,10},{10... | collective-permute-start | bytes 393224 | tf_op jit(solution)/shard_map/ppermute | solution.py:208
  484.7 3.6 collective-permute-start.22
  498.0 3.7 collective-permute-start.23
  501.7 3.6 collective-permute-start.24
  508.2 10.3 %collective-permute-start.32 = (bf16[128,1024]{1,0:T(8,128)(2,1)}, bf16[128,1024]{1,0:T(8,128)(2,1)S(1)}, u32[]{:S(2)}, u32[]{:S(2)}) collective-permute-start(bf16[128,1024]{1,0:T(8,128)(2,1)} %dynamic-slice_convert_fusion.5), channel_id=1, source_target_pairs={{0,8},{8,0},{16,24},{24,16},{1,9},{9,1},{17,25},{25,17},{2,10},{10... | collective-permute-start | bytes 786440 | tf_op jit(solution)/shard_map/ppermute | solution.py:201
  509.7 11.7 %collective-permute-start.39 = (bf16[256,512]{1,0:T(8,128)(2,1)S(1)}, bf16[256,512]{1,0:T(8,128)(2,1)S(1)}, u32[]{:S(2)}, u32[]{:S(2)}) collective-permute-start(bf16[256,512]{1,0:T(8,128)(2,1)S(1)} %dynamic-slice_convert_fusion.4), channel_id=1, source_target_pairs={{0,8},{8,0},{16,24},{24,16},{1,9},{9,1},{17,25},{25,17},{2,10},{10... | collective-permute-start | bytes 786440 | tf_op jit(solution)/shard_map/ppermute | solution.py:201
  519.7 10.9 %collective-permute-start.33 = (bf16[128,512]{1,0:T(8,128)(2,1)S(1)}, bf16[128,512]{1,0:T(8,128)(2,1)S(1)}, u32[]{:S(2)}, u32[]{:S(2)}) collective-permute-start(bf16[128,512]{1,0:T(8,128)(2,1)S(1)} %dynamic-slice_convert_fusion.7), channel_id=1, source_target_pairs={{0,16},{8,24},{16,0},{24,8},{1,17},{9,25},{17,1},{25,9},{2,18},{10... | collective-permute-start | bytes 393224 | tf_op jit(solution)/shard_map/ppermute | solution.py:201
  521.5 14.6 %collective-permute-start.40 = (bf16[256,256]{1,0:T(8,128)(2,1)S(1)}, bf16[256,256]{1,0:T(8,128)(2,1)S(1)}, u32[]{:S(2)}, u32[]{:S(2)}) collective-permute-start(bf16[256,256]{1,0:T(8,128)(2,1)S(1)} %dynamic-slice_convert_fusion.6), channel_id=1, source_target_pairs={{0,16},{8,24},{16,0},{24,8},{1,17},{9,25},{17,1},{25,9},{2,18},{10... | collective-permute-start | bytes 393224 | tf_op jit(solution)/shard_map/ppermute | solution.py:201
  530.6 8.0 %collective-permute-start.34 = (bf16[128,512]{1,0:T(8,128)(2,1)S(1)}, bf16[128,512]{1,0:T(8,128)(2,1)S(1)}, u32[]{:S(2)}, u32[]{:S(2)}) collective-permute-start(bf16[128,512]{1,0:T(8,128)(2,1)S(1)} %add_convert_fusion.4), channel_id=1, source_target_pairs={{0,16},{8,24},{16,0},{24,8},{1,17},{9,25},{17,1},{25,9},{2,18},{10... | collective-permute-start | bytes 393224 | tf_op jit(solution)/shard_map/ppermute | solution.py:208
  536.1 6.4 %collective-permute-start.41 = (bf16[256,256]{1,0:T(8,128)(2,1)S(1)}, bf16[256,256]{1,0:T(8,128)(2,1)S(1)}, u32[]{:S(2)}, u32[]{:S(2)}) collective-permute-start(bf16[256,256]{1,0:T(8,128)(2,1)S(1)} %add_convert_fusion.3), channel_id=1, source_target_pairs={{0,16},{8,24},{16,0},{24,8},{1,17},{9,25},{17,1},{25,9},{2,18},{10... | collective-permute-start | bytes 393224 | tf_op jit(solution)/shard_map/ppermute | solution.py:208
  538.7 9.4 %collective-permute-start.35 = (bf16[128,1024]{1,0:T(8,128)(2,1)S(1)}, bf16[128,1024]{1,0:T(8,128)(2,1)S(1)}, u32[]{:S(2)}, u32[]{:S(2)}) collective-permute-start(bf16[128,1024]{1,0:T(8,128)(2,1)S(1)} %pad_maximum_fusion.10), channel_id=1, source_target_pairs={{0,8},{8,0},{16,24},{24,16},{1,9},{9,1},{17,25},{25,17},{2,10},{10... | collective-permute-start | bytes 786440 | tf_op jit(solution)/shard_map/ppermute | solution.py:208
  542.5 9.1 %collective-permute-start.42 = (bf16[256,512]{1,0:T(8,128)(2,1)S(1)}, bf16[256,512]{1,0:T(8,128)(2,1)S(1)}, u32[]{:S(2)}, u32[]{:S(2)}) collective-permute-start(bf16[256,512]{1,0:T(8,128)(2,1)S(1)} %pad_maximum_fusion.11), channel_id=1, source_target_pairs={{0,8},{8,0},{16,24},{24,16},{1,9},{9,1},{17,25},{25,17},{2,10},{10... | collective-permute-start | bytes 786440 | tf_op jit(solution)/shard_map/ppermute | solution.py:208
  548.2 4.1 collective-permute-start.36
  551.8 9.4 %collective-permute-start.43 = (bf16[256,1024]{1,0:T(8,128)(2,1)S(1)}, bf16[256,1024]{1,0:T(8,128)(2,1)S(1)}, u32[]{:S(2)}, u32[]{:S(2)}) collective-permute-start(bf16[256,1024]{1,0:T(8,128)(2,1)S(1)} %pad_maximum_fusion.4), channel_id=1, source_target_pairs={{0,4},{4,0},{1,5},{5,1},{2,6},{6,2},{3,7},{7,3},{8,12},{12,8},{9,1... | collective-permute-start | bytes 1572872 | tf_op jit(solution)/shard_map/ppermute | solution.py:220
  560.4 7.3 %collective-permute-start.37 = (f32[1,2]{1,0:T(1,128)S(1)}, f32[1,2]{1,0:T(1,128)S(1)}, u32[]{:S(2)}, u32[]{:S(2)}) collective-permute-start(f32[1,2]{1,0:T(1,128)S(1)} %pad_maximum_fusion.24), channel_id=1, source_target_pairs={{0,1},{1,0},{2,3},{3,2},{4,5},{5,4},{6,7},{7,6},{8,9},{9,8},{10,11... | collective-permute-start | bytes 32 | tf_op jit(solution)/shard_map/ppermute | solution.py:166
  566.4 3.6 collective-permute-start.44
  571.2 4.8 collective-permute-start.45
  (80 other events, 855.3 us)
Sparse Core Ops, SparseCore 0:
  10.5 50.3 all-gather.4
  63.4 32.6 all-gather.6
  98.5 39.5 all-gather.8
  140.5 36.5 all-gather.10
  203.1 42.4 reduce-scatter.12
  262.2 40.5 reduce-scatter.10
  306.7 42.1 reduce-scatter.6
  352.7 41.1 reduce-scatter.8
  397.2 51.1 reduce-scatter.14
  451.7 51.1 reduce-scatter.16

commit v5 on v3

--- a/solution.py
+++ b/solution.py
@@ -221,6 +221,65 @@
     return jnp.concatenate(
         [jnp.where(first, piece, other), jnp.where(first, other, piece)], axis=row_axis
     )
+
+
+def gather_batch(shards):
+    core = lax.axis_index("core")
+    flat = []
+    for shard in shards:
+        half = shard.shape[0] // 2
+        flat.append(lax.dynamic_slice_in_dim(shard, core * half, half, 0).reshape(-1))
+    blocks = lax.all_gather(jnp.concatenate(flat), ("seq", "core"), axis=0, tiled=False)
+    fulls = []
+    offset = 0
+    for shard, piece in zip(shards, flat):
+        fulls.append(
+            blocks[:, offset : offset + piece.size].reshape(-1, shard.shape[1])
+        )
+        offset += piece.size
+    return fulls
+
+
+def reduce_batch(partials):
+    groups = lax.axis_size("seq") * 2
+    flat = jnp.concatenate([part.reshape(groups, -1) for part in partials], axis=1)
+    flat = flat.reshape(groups * 8, -1)
+    piece = lax.psum_scatter(flat, ("seq", "core"), scatter_dimension=0, tiled=True).reshape(1, -1)
+    piece = halving_sum(piece, "z", lax.axis_size("z"))
+    other = lax.ppermute(piece, "core", [(0, 1), (1, 0)])
+    first = lax.axis_index("core") == 0
+    low = jnp.where(first, piece, other)
+    high = jnp.where(first, other, piece)
+    shares = []
+    offset = 0
+    for part in partials:
+        size = part.size // groups
+        rows = (-1, part.shape[1])
+        shares.append(
+            jnp.concatenate(
+                [
+                    low[:, offset : offset + size].reshape(rows),
+                    high[:, offset : offset + size].reshape(rows),
+                ],
+                axis=0,
+            )
+        )
+        offset += size
+    return shares
+
+
+def lamb_update(weight, moment, second, grad, sum_axes, seq_count):
+    moment_new, second_new, direction = adam_direction(weight, moment, second, grad)
+    sums = jnp.concatenate(
+        [
+            jnp.sum(weight * weight, axis=sum_axes, keepdims=True),
+            jnp.sum(direction * direction, axis=sum_axes, keepdims=True),
+        ],
+        axis=-1,
+    )
+    sums = butterfly_sum(sums, "seq", seq_count)
+    ratio = jnp.sqrt(sums[..., :1]) * lax.rsqrt(sums[..., 1:] + 1e-06)
+    return (weight - step_rate * ratio * direction, moment_new, second_new)
 
 
 def adam_direction(weight, moment, second, grad):
@@ -263,11 +322,9 @@
     group_frames = frame_rows * seq_count
     dp_count = lax.axis_size(("z", "core"))
     dp_rank = lax.axis_index(("z", "core"))
-    qkv_full, out_full, up_full, down_full = (
-        gather_rows(w_qkv.astype(jnp.bfloat16), 1),
-        gather_rows(w_out.astype(jnp.bfloat16), 0),
-        gather_rows(w_up.astype(jnp.bfloat16), 0),
-        gather_rows(w_down.astype(jnp.bfloat16), 0),
+    qkv_full = gather_rows(w_qkv.astype(jnp.bfloat16), 1)
+    out_full, up_full, down_full = gather_batch(
+        [w_out.astype(jnp.bfloat16), w_up.astype(jnp.bfloat16), w_down.astype(jnp.bfloat16)]
     )
     bias_full = doubling_gather(b_mod.astype(jnp.bfloat16), "seq", seq_count, seq_rank).reshape(-1)
     mod_low = w_mod.astype(jnp.bfloat16)
@@ -412,39 +469,39 @@
         list(doubling_gather(grad_silu_part, "seq", seq_count, seq_rank)), axis=1
     )
     time_grad = jax.vjp(jax.nn.silu, time_emb)[1](grad_silu)[0]
-    totals = (
-        reduce_rows(grad_qkv_local.astype(jnp.bfloat16), 1).astype(jnp.float32),
-        reduce_rows(grad_out_local.astype(jnp.bfloat16), 0).astype(jnp.float32),
-        reduce_rows(grad_up_local.astype(jnp.bfloat16), 0).astype(jnp.float32),
-        reduce_rows(grad_down_local.astype(jnp.bfloat16), 0).astype(jnp.float32),
-        grad_mod_share,
-        grad_bias_share,
-    )
-    masters = (w_qkv, w_out, w_up, w_down, w_mod, b_mod)
-    moments = (mom_qkv, mom_out, mom_up, mom_down, mom_mod, mom_bias)
-    seconds = (var_qkv, var_out, var_up, var_down, var_mod, var_bias)
-    new_moments = []
-    new_seconds = []
-    directions = []
-    weight_sums = []
-    update_sums = []
-    for param in range(6):
-        moment_new, second_new, direction = adam_direction(
-            masters[param], moments[param], seconds[param], totals[param]
-        )
-        sum_axes = (1, 2) if param == 0 else None
-        new_moments.append(moment_new)
-        new_seconds.append(second_new)
-        directions.append(direction)
-        weight_sums.append(jnp.sum(masters[param] * masters[param], axis=sum_axes, keepdims=True))
-        update_sums.append(jnp.sum(direction * direction, axis=sum_axes, keepdims=True))
-    new_masters = []
-    for param in range(6):
-        pair = butterfly_sum(
-            jnp.concatenate([weight_sums[param], update_sums[param]], axis=-1), "seq", seq_count
-        )
-        ratio = jnp.sqrt(pair[..., :1]) * lax.rsqrt(pair[..., 1:] + 1e-06)
-        new_masters.append(masters[param] - step_rate * ratio * directions[param])
+    grad_out, grad_up, grad_down = [
+        share.astype(jnp.float32)
+        for share in reduce_batch(
+            [
+                grad_out_local.astype(jnp.bfloat16),
+                grad_up_local.astype(jnp.bfloat16),
+                grad_down_local.astype(jnp.bfloat16),
+            ]
+        )
+    ]
+    qkv_piece = lax.psum_scatter(
+        grad_qkv_local.astype(jnp.bfloat16), ("seq", "core"), scatter_dimension=1, tiled=True
+    )
+    updated = [
+        lamb_update(w_out, mom_out, var_out, grad_out, None, seq_count),
+        lamb_update(w_up, mom_up, var_up, grad_up, None, seq_count),
+        lamb_update(w_down, mom_down, var_down, grad_down, None, seq_count),
+        lamb_update(w_mod, mom_mod, var_mod, grad_mod_share, None, seq_count),
+        lamb_update(b_mod, mom_bias, var_bias, grad_bias_share, None, seq_count),
+    ]
+    qkv_piece, updated = lax.optimization_barrier((qkv_piece, updated))
+    qkv_piece = halving_sum(qkv_piece, "z", lax.axis_size("z"))
+    qkv_other = lax.ppermute(qkv_piece, "core", [(0, 1), (1, 0)])
+    qkv_first = lax.axis_index("core") == 0
+    grad_qkv = jnp.concatenate(
+        [jnp.where(qkv_first, qkv_piece, qkv_other), jnp.where(qkv_first, qkv_other, qkv_piece)],
+        axis=1,
+    ).astype(jnp.float32)
+    updated = [lamb_update(w_qkv, mom_qkv, var_qkv, grad_qkv, (1, 2), seq_count)] + updated
+    totals = (grad_qkv, grad_out, grad_up, grad_down, grad_mod_share, grad_bias_share)
+    new_masters = [entry[0] for entry in updated]
+    new_moments = [entry[1] for entry in updated]
+    new_seconds = [entry[2] for entry in updated]
     return (
         result.astype(jnp.bfloat16),
         input_grad,

time: 583 us -> 778 us (1.33)
  local copies, waits for them, and re-layouts: 58.8 us -> 165 us
  other arithmetic: 98.2 us -> 173 us
  waiting for transfers between devices: 178 us -> 239 us
  starting transfers between devices: 88.4 us -> 66.5 us
  matrix products: 112 us -> 99 us
  blocking collectives: 11 us -> 0 us
    reshape x0 -> x13, local copies, waits for them, and re-layouts: none -> 49.4 us  [the longest x3 14.7 us: reduce_batch(): part.reshape(groups, -1)]
    slice x5 -> x12, local copies, waits for them, and re-layouts: 2.92 us -> 38.5 us  [the longest x2 14.7 us: reduce_batch(): low[:, offset:offset + size].reshape(rows)]
    ppermute x8 -> x4, waiting for transfers between devices: 24.1 us -> 54.7 us  [halving_sum(): lax.ppermute(send, axis_name, [(i, i ^ step) for i in range(size)])]
    ppermute x8 -> x4, waiting for transfers between devices: 34.5 us -> 62.6 us  [halving_sum(): lax.ppermute(blocks, axis_name, [(i, i ^ step) for i in range(size)])]
    concatenate x6 -> x8, other arithmetic: 7.05 us -> 34.1 us  [the longest x1 26 us: reduce_batch(): jnp.concatenate([part.reshape(groups, -1) for part in partials], axis=1)]
    concatenate x8 -> x4, other arithmetic: 0.29 us -> 24.7 us  [halving_sum(): jnp.concatenate([jnp.where(low_side, blocks, other), jnp.where(low_side,...]
    all_gather x4 -> x1, waiting for transfers between devices: 37 us -> 20.2 us  [gather_rows(): return lax.all_gather(piece, ('seq', 'core'), axis=row_axis, tiled=True)]
    select_n x4 -> x2, other arithmetic: 0.91 us -> 16.2 us  [the longest x1 15.8 us: reduce_batch(): low = jnp.where(first, piece, other)]
  transfers between devices with their start and end apart: 61 -> 48, of which waited for: 36 -> 30; matrix products, arithmetic and copies ran while one was open for 41% -> 46% of each run, Pallas kernels for 0% -> 0%
where the time goes in v5:
time: 778 us; the launch traced here: 768 us
  waiting for transfers between devices  239 us (31%)
  other arithmetic  173 us (22%)
  local copies, waits for them, and re-layouts  165 us (21%)
  matrix products  99 us (13%)
  starting transfers between devices  66.5 us (9%)
  between operations  22.8 us (3%)
    ppermute x4, waiting for transfers between devices, halving_sum(): lax.ppermute(blocks, axis_name, [(i, i ^ step) for i in range(size)])  62.6 us
    ppermute x4, waiting for transfers between devices, halving_sum(): lax.ppermute(send, axis_name, [(i, i ^ step) for i in range(size)])  54.7 us
    ppermute x10, waiting for transfers between devices, doubling_gather(): other = lax.ppermute(blocks, axes, [(i, i ^ step) for i in range(size)])  27.3 us
    concatenate x1, other arithmetic, reduce_batch(): jnp.concatenate([part.reshape(groups, -1) for part in partials], axis=1)  26 us
    concatenate x4, other arithmetic, halving_sum(): jnp.concatenate([jnp.where(low_side, blocks, other), jnp.where(low_side,...  24.7 us
    all_gather x1, waiting for transfers between devices, gather_rows(): return lax.all_gather(piece, ('seq', 'core'), axis=row_axis, tiled=True)  20.2 us
    reduce_sum x5, other arithmetic, lamb_update(): jnp.sum(weight * weight, axis=sum_axes, keepdims=True)  19.4 us
    ppermute x16, waiting for transfers between devices, butterfly_sum(): lax.ppermute(values, axes, [(i, i ^ step) for i in range(size)])  17.3 us
  transfers between devices with their start and end apart: 48, of which 30 were waited for; matrix products, arithmetic and copies ran while one was open for 46% of the time, Pallas kernels for 0%

profile of v5, /device:TPU:0, one launch (start us, length us, event | category | flops | bytes accessed | tf_op | source)
XLA Modules:
  0.0 768.5 jit_solution(9655790085427886093)
XLA Ops:
  18.1 3.8 fusion.38
  30.6 4.0 collective-permute-done.1
  40.4 20.2 %all-gather.4.cloned.1.call-done = bf16[3,1024,1024]{2,1,0:T(8,128)(2,1)} async-done(((bf16[3,128,1024]{2,1,0:T(8,128)(2,1)}), bf16[3,1024,1024]{2,1,0:T(8,128)(2,1)}) %all-gather.4.cloned.1.call-update) | async-done | bytes 6291472 | tf_op jit(solution)/shard_map/all_gather | solution.py:188
  60.6 4.7 slice_bitcast_fusion.3
  80.9 3.5 all-to-all-start
  85.9 8.1 %all-to-all-done = bf16[256,4,256]{0,2,1:T(8,128)(2,1)S(1)} async-done(((bf16[256,4,256]{0,2,1:T(8,128)(2,1)}), bf16[256,4,256]{0,2,1:T(8,128)(2,1)S(1)}, u32[]{:S(2)}, u32[]{:S(2)}) %all-to-all-start) | async-done | bytes 524320 | tf_op jit(solution)/shard_map/all_to_all | solution.py:356
  94.0 3.5 all-to-all-start.1
  101.3 10.8 %all-to-all-done.1 = bf16[256,4,256]{0,2,1:T(8,128)(2,1)S(1)} async-done(((bf16[256,4,256]{0,2,1:T(8,128)(2,1)}), bf16[256,4,256]{0,2,1:T(8,128)(2,1)S(1)}, u32[]{:S(2)}, u32[]{:S(2)}) %all-to-all-start.1) | async-done | bytes 524320 | tf_op jit(solution)/shard_map/all_to_all | solution.py:357
  112.0 3.7 all-to-all-start.2
  120.3 9.8 %all-to-all-done.2 = bf16[256,4,256]{2,0,1:T(8,128)(2,1)S(1)} async-done(((bf16[256,4,256]{2,0,1:T(8,128)(2,1)}), bf16[256,4,256]{2,0,1:T(8,128)(2,1)S(1)}, u32[]{:S(2)}, u32[]{:S(2)}) %all-to-all-start.2) | async-done | bytes 524320 | tf_op jit(solution)/shard_map/all_to_all | solution.py:358
  131.9 20.0 %while.27 = (s32[]{:T(128)}, bf16[2,512,256]{2,1,0:T(8,128)(2,1)}, f32[2,4,512,1]{2,1,3,0:T(4,128)S(1)}, s32[2]{0:T(128)S(1)}, s32[1024]{0:T(1024)S(1)}, /*index...) while((s32[]{:T(128)}, bf16[2,512,256]{2,1,0:T(8,128)(2,1)}, ...), condition=%wide.region_9.10_spmd, body=%wide.region_6.9_spmd.sunk | while | flops 561117184 | bytes 30485712 | solution.py:110
  137.7 3.3 fusion.192
  147.7 3.3 fusion.192
  151.9 3.5 all-to-all-start.3
  155.4 6.8 all-to-all-done.3
  163.2 12.2 %reshape.491 = bf16[8,655360]{1,0:T(8,128)(2,1)} reshape(bf16[5242880]{0:T(1024)(128)(2,1)} %all-gather.6.cloned.1.call-done) | data formatting | bytes 20971520 | tf_op jit(solution)/shard_map/all_gather | solution.py:232
  175.5 6.4 fusion.111
  184.1 6.1 reshape.474
  190.2 6.2 reshape.475
  196.4 3.7 fusion.110
  204.6 3.9 convolution_convert_fusion
  220.5 3.3 convolution_convert_fusion.1
  224.6 4.1 all-to-all-start.4
  228.8 6.1 reshape.478
  237.5 6.1 reshape.477
  243.5 26.0 %pad_maximum_fusion = bf16[8,655360]{1,0:T(8,128)(2,1)} fusion(bf16[8,262144]{1,0:T(8,128)(2,1)} %reshape.478, bf16[8,262144]{1,0:T(8,128)(2,1)} %reshape.477, bf16[8,131072]{1,0:T(8,128)(2,1)S(1)} %reshape.476), kind=kLoop, calls=%fused_computation.32 | loop fusion | flops 31457280 | bytes 20971520 | tf_op jit(solution)/shard_map/concatenate | solution.py:245
  269.5 12.7 %reshape.479 = bf16[64,81920]{1,0:T(8,128)(2,1)} reshape(bf16[8,655360]{1,0:T(8,128)(2,1)} %pad_maximum_fusion) | data formatting | bytes 20971520 | tf_op jit(solution)/shard_map/reshape | solution.py:246
  283.9 36.2 %while.28 = (s32[]{:T(128)}, f32[1024,256]{0,1:T(8,128)S(1)}, f32[1024,256]{0,1:T(8,128)S(1)}, bf16[2,512,256]{2,1,0:T(8,128)(2,1)}, s32[2]{0:T(128)S(1)}, /*ind...) while((s32[]{:T(128)}, f32[1024,256]{0,1:T(8,128)S(1)}, ...), condition=%wide.region_16.17_spmd.clone, body=%wide.region_14.16_spmd.clone.sunk | while | flops 1376253952 | bytes 78974200 | solution.py:155
  291.9 4.3 multiply_reduce_fusion.16
  309.8 4.2 multiply_reduce_fusion.16
  320.1 4.2 all-to-all-start.5
  328.1 9.9 %all-to-all-done.5 = bf16[4,256,256]{2,1,0:T(8,128)(2,1)S(1)} async-done(((bf16[4,256,256]{2,1,0:T(8,128)(2,1)}), bf16[4,256,256]{2,1,0:T(8,128)(2,1)S(1)}, u32[]{:S(2)}, u32[]{:S(2)}) %all-to-all-start.5) | async-done | bytes 524320 | tf_op jit(solution)/shard_map/all_to_all | solution.py:410
  338.0 3.5 all-to-all-start.6
  346.0 6.2 all-to-all-done.6
  352.2 4.1 all-to-all-start.7
  362.7 5.4 all-to-all-done.7
  398.2 4.8 collective-permute-done.23
  405.6 3.2 pad_maximum_fusion.1
  408.8 14.1 %collective-permute-done.24 = f32[4,3,6144]{2,1,0:T(4,128)S(1)} collective-permute-done((f32[4,3,6144]{2,1,0:T(4,128)S(1)}, f32[4,3,6144]{2,1,0:T(4,128)S(1)}, u32[]{:S(2)}, u32[]{:S(2)}) %collective-permute-start.24) | collective-permute-done | bytes 294944 | tf_op jit(solution)/shard_map/ppermute | solution.py:175
  433.5 15.1 %multiply_reduce_fusion.2 = (f32[]{:T(128)}, f32[]{:T(128)}, f32[256,6144]{1,0:T(8,128)S(1)}, f32[256,6144]{1,0:T(8,128)}, f32[256,6144]{1,0:T(8,128)}) fusion(f32[256,6144]{1,0:T(8,128)S(1)} %bitcast.262, f32[256,6144]{1,0:T(8,128)} %param.45, f32[256,6144]{1,0:T(8,128)} %param.46, f32[8,3,6144]{2,1,0:T(4,128)S(1)} %pad_maximum_fusion.5, ...), kind=kOutput, calls=%fused_computation.41 | convolution fusion | flops 479748096 | bytes 38350856 | tf_op jit(solution)/shard_map/cd,ce->de/dot_general | solution.py:462
  448.6 14.0 %collective-permute-done.8 = bf16[1,327680]{1,0:T(2,128)(2,1)} collective-permute-done((bf16[1,327680]{1,0:T(2,128)(2,1)S(1)}, bf16[1,327680]{1,0:T(2,128)(2,1)}, u32[]{:S(2)}, u32[]{:S(2)}) %collective-permute-start.8) | collective-permute-done | bytes 655392 | tf_op jit(solution)/shard_map/ppermute | solution.py:200
  462.6 3.6 fusion.48
  474.8 23.3 %collective-permute-done.9 = bf16[1,163840]{1,0:T(2,128)(2,1)S(1)} collective-permute-done((bf16[1,163840]{1,0:T(2,128)(2,1)S(1)}, bf16[1,163840]{1,0:T(2,128)(2,1)S(1)}, u32[]{:S(2)}, u32[]{:S(2)}) %collective-permute-start.9) | collective-permute-done | bytes 327712 | tf_op jit(solution)/shard_map/ppermute | solution.py:200
  502.8 27.3 %collective-permute-done.10 = bf16[1,163840]{1,0:T(2,128)(2,1)S(1)} collective-permute-done((bf16[1,163840]{1,0:T(2,128)(2,1)S(1)}, bf16[1,163840]{1,0:T(2,128)(2,1)S(1)}, u32[]{:S(2)}, u32[]{:S(2)}) %collective-permute-start.10) | collective-permute-done | bytes 327712 | tf_op jit(solution)/shard_map/ppermute | solution.py:207
  531.9 9.2 %pad_maximum_fusion.4 = bf16[1,327680]{1,0:T(2,128)(2,1)S(1)} fusion(bf16[1,163840]{1,0:T(2,128)(2,1)S(1)} %get-tuple-element.384, bf16[1,163840]{1,0:T(2,128)(2,1)S(1)} %get-tuple-element.383), kind=kLoop, calls=%fused_computation.126 | loop fusion | flops 1310720 | bytes 1310720 | tf_op jit(solution)/shard_map/concatenate | solution.py:209
  547.1 23.0 %collective-permute-done.11 = bf16[1,327680]{1,0:T(2,128)(2,1)S(1)} collective-permute-done((bf16[1,327680]{1,0:T(2,128)(2,1)S(1)}, bf16[1,327680]{1,0:T(2,128)(2,1)S(1)}, u32[]{:S(2)}, u32[]{:S(2)}) %collective-permute-start.11) | collective-permute-done | bytes 655392 | tf_op jit(solution)/shard_map/ppermute | solution.py:207
  570.1 9.5 %broadcast_select_fusion.3 = (bf16[1,327680]{1,0:T(2,128)(2,1)S(1)}, bf16[1,327680]{1,0:T(2,128)(2,1)S(1)}) fusion(bf16[1,327680]{1,0:T(2,128)(2,1)S(1)} %collective-permute-done.11, pred[]{:T(512)S(6)} %eq.92, bf16[1,163840]{1,0:T(2,128)(2,1)S(1)} %get-tuple-element.384, bf16[1,163840]{1,0:T(2,128)(2,1)S(1)} %get-tuple-element.383), kind=kLoop, calls=%fused_computation.60 | loop fusion | flops 1966080 | bytes 2621441 | tf_op jit(solution)/shard_map/jit(_where)/select_n | solution.py:210
  579.6 15.4 %pad_maximum_fusion.2 = bf16[1,655360]{1,0:T(2,128)(2,1)S(1)} fusion(bf16[1,327680]{1,0:T(2,128)(2,1)S(1)} %get-tuple-element.377, bf16[1,327680]{1,0:T(2,128)(2,1)S(1)} %get-tuple-element.376), kind=kLoop, calls=%fused_computation.57 | loop fusion | flops 2621440 | bytes 2621440 | tf_op jit(solution)/shard_map/concatenate | solution.py:209
  595.1 5.1 multiply_subtract_fusion
  600.2 15.8 %broadcast_select_fusion.1 = (bf16[1,655360]{1,0:T(2,128)(2,1)S(1)}, bf16[1,655360]{1,0:T(2,128)(2,1)S(1)}) fusion(bf16[1,655360]{1,0:T(2,128)(2,1)S(1)} %collective-permute-done.12, pred[]{:T(512)S(6)} %eq.91, bf16[1,327680]{1,0:T(2,128)(2,1)S(1)} %get-tuple-element.377, bf16[1,327680]{1,0:T(2,128)(2,1)S(1)} %get-tuple-element.376), kind=kLoop, calls=%fused_computation.43 | loop fusion | flops 3932160 | bytes 5242881 | tf_op jit(solution)/shard_map/jit(_where)/select_n | solution.py:251
  617.5 12.1 %slice_reduce_fusion.1 = (bf16[262144]{0:T(1024)(128)(2,1)S(1)}, bf16[262144]{0:T(1024)(128)(2,1)}) fusion(bf16[1,655360]{1,0:T(2,128)(2,1)S(1)} %get-tuple-element.374), kind=kLoop, calls=%fused_computation.145 | loop fusion | bytes 2097152 | tf_op jit(solution)/shard_map/slice | solution.py:261
  633.4 12.3 %slice_reduce_fusion = (bf16[262144]{0:T(1024)(128)(2,1)S(1)}, bf16[262144]{0:T(1024)(128)(2,1)}) fusion(bf16[1,655360]{1,0:T(2,128)(2,1)S(1)} %get-tuple-element.375), kind=kLoop, calls=%fused_computation.144 | loop fusion | bytes 2097152 | tf_op jit(solution)/shard_map/slice | solution.py:262
  654.3 3.8 multiply_reduce_fusion.10
  660.3 5.6 multiply_reduce_fusion.8
  669.0 3.7 multiply_reduce_fusion.6
  700.5 9.4 %collective-permute-done.29 = bf16[3,128,512]{2,1,0:T(8,128)(2,1)S(1)} collective-permute-done((bf16[3,128,512]{2,1,0:T(8,128)(2,1)S(1)}, bf16[3,128,512]{2,1,0:T(8,128)(2,1)S(1)}, u32[]{:S(2)}, u32[]{:S(2)}) %collective-permute-start.29) | collective-permute-done | bytes 393248 | tf_op jit(solution)/shard_map/ppermute | solution.py:200
  712.0 8.0 %collective-permute-done.30 = bf16[3,128,256]{2,1,0:T(8,128)(2,1)S(1)} collective-permute-done((bf16[3,128,256]{2,1,0:T(8,128)(2,1)S(1)}, bf16[3,128,256]{2,1,0:T(8,128)(2,1)S(1)}, u32[]{:S(2)}, u32[]{:S(2)}) %collective-permute-start.30) | collective-permute-done | bytes 196640 | tf_op jit(solution)/shard_map/ppermute | solution.py:200
  720.2 10.9 %collective-permute-done.31 = bf16[3,128,256]{2,1,0:T(8,128)(2,1)S(1)} collective-permute-done((bf16[3,128,256]{2,1,0:T(8,128)(2,1)S(1)}, bf16[3,128,256]{2,1,0:T(8,128)(2,1)S(1)}, u32[]{:S(2)}, u32[]{:S(2)}) %collective-permute-start.31) | collective-permute-done | bytes 196640 | tf_op jit(solution)/shard_map/ppermute | solution.py:207
  731.4 5.5 fusion.53
  737.2 3.3 collective-permute-done.6
  745.4 5.7 multiply_reduce_fusion.4
  751.5 3.3 collective-permute-done.34
  755.2 3.2 collective-permute-done.35
  758.4 3.3 multiply_subtract_fusion.1
  (477 shorter events, 241.6 us)
Async XLA Ops:
  7.2 53.3 %all-gather.4.cloned.1.call-start = ((), (), s32[]{:S(2)}) async-start(), calls=%async_computation.10 | async-start | bytes 7077888 | tf_op jit(solution)/shard_map/all_gather | solution.py:188
  9.7 153.5 %all-gather.6.cloned.1.call-start = ((), (), s32[]{:S(2)}) async-start(), calls=%async_computation.13 | async-start | bytes 11796480 | tf_op jit(solution)/shard_map/all_gather | solution.py:232
  15.0 8.7 %collective-permute-start.2 = (bf16[1,1536]{1,0:T(2,128)(2,1)S(1)}, bf16[1,1536]{1,0:T(2,128)(2,1)S(1)}, u32[]{:S(2)}, u32[]{:S(2)}) collective-permute-start(bf16[1,1536]{1,0:T(2,128)(2,1)S(1)} %broadcast_in_dim.158), channel_id=1, source_target_pairs={{0,1},{1,0},{2,3},{3,2},{4,5},{5,4},{6,7},{7,6},{8,9},{9,8},{10,11... | collective-permute-start | bytes 9224 | tf_op jit(solution)/shard_map/ppermute | solution.py:175
  21.9 7.2 collective-permute-start
  23.4 55.4 %copy-start.50 = (f32[256,32]{0,1:T(8,128)}, f32[256,32]{0,1:T(8,128)S(1)}, u32[]{:S(2)}) copy-start(f32[256,32]{0,1:T(8,128)S(1)} %get-tuple-element.433) | copy-start | bytes 98308
  23.8 3.9 collective-permute-start.3
  29.1 5.5 collective-permute-start.1
  40.4 57.1 %copy-start.19 = (bf16[256,1024]{1,0:T(8,128)(2,1)}, bf16[256,1024]{1,0:T(8,128)(2,1)S(1)}, u32[]{:S(2)}) copy-start(bf16[256,1024]{1,0:T(8,128)(2,1)S(1)} %fusion.57) | copy-start | bytes 1572868
  80.9 13.1 %all-to-all-start = ((bf16[256,4,256]{0,2,1:T(8,128)(2,1)}), bf16[256,4,256]{0,2,1:T(8,128)(2,1)S(1)}, u32[]{:S(2)}, u32[]{:S(2)}) async-start(bf16[256,4,256]{0,2,1:T(8,128)(2,1)} %convert_element_type.234), calls=%async_computation | async-start | bytes 1048576 | tf_op jit(solution)/shard_map/all_to_all | solution.py:356
  94.0 18.0 %all-to-all-start.1 = ((bf16[256,4,256]{0,2,1:T(8,128)(2,1)}), bf16[256,4,256]{0,2,1:T(8,128)(2,1)S(1)}, u32[]{:S(2)}, u32[]{:S(2)}) async-start(bf16[256,4,256]{0,2,1:T(8,128)(2,1)} %convert_element_type.235), calls=%async_computation.1 | async-start | bytes 1048576 | tf_op jit(solution)/shard_map/all_to_all | solution.py:357
  112.0 18.0 %all-to-all-start.2 = ((bf16[256,4,256]{2,0,1:T(8,128)(2,1)}), bf16[256,4,256]{2,0,1:T(8,128)(2,1)S(1)}, u32[]{:S(2)}, u32[]{:S(2)}) async-start(bf16[256,4,256]{2,0,1:T(8,128)(2,1)} %bitcast.203), calls=%async_computation.2 | async-start | bytes 1048576 | tf_op jit(solution)/shard_map/all_to_all | solution.py:358
  151.9 23.6 %copy-start.3 = (bf16[1024,256]{0,1:T(8,128)(2,1)}, bf16[1024,256]{0,1:T(8,128)(2,1)S(1)}, u32[]{:S(2)}) copy-start(bf16[1024,256]{0,1:T(8,128)(2,1)S(1)} %get-tuple-element.694) | copy-start | bytes 1572868
  151.9 10.3 %all-to-all-start.3 = ((bf16[4,256,256]{2,1,0:T(8,128)(2,1)}), bf16[4,256,256]{2,1,0:T(8,128)(2,1)S(1)}, u32[]{:S(2)}, u32[]{:S(2)}) async-start(bf16[4,256,256]{2,1,0:T(8,128)(2,1)} %bitcast.26), calls=%async_computation.3 | async-start | bytes 1048576 | tf_op jit(solution)/shard_map/all_to_all | solution.py:363
  224.6 57.6 %all-to-all-start.4 = ((bf16[256,4,256]{2,0,1:T(8,128)(2,1)}), bf16[256,4,256]{2,0,1:T(8,128)(2,1)}, u32[]{:S(2)}, u32[]{:S(2)}) async-start(bf16[256,4,256]{2,0,1:T(8,128)(2,1)} %bitcast.202), calls=%async_computation.4 | async-start | bytes 1048576 | tf_op jit(solution)/shard_map/all_to_all | solution.py:398
  228.8 198.4 %reduce-scatter.5.cloned.1.call-start = ((), (), s32[]{:S(2)}) async-start(), calls=%async_computation.12 | async-start | bytes 11796480 | tf_op jit(solution)/shard_map/reduce_scatter | solution.py:247
  283.9 40.4 %copy-start.58 = (bf16[3,256]{1,0:T(4,128)(2,1)S(1)}, bf16[3,256]{1,0:T(4,128)(2,1)}, u32[]{:S(2)}) copy-start(bf16[3,256]{1,0:T(4,128)(2,1)} %copy-done.57) | copy-start | bytes 4612
  320.1 17.8 %all-to-all-start.5 = ((bf16[4,256,256]{2,1,0:T(8,128)(2,1)}), bf16[4,256,256]{2,1,0:T(8,128)(2,1)S(1)}, u32[]{:S(2)}, u32[]{:S(2)}) async-start(bf16[4,256,256]{2,1,0:T(8,128)(2,1)} %bitcast.285), calls=%async_computation.5 | async-start | bytes 1048576 | tf_op jit(solution)/shard_map/all_to_all | solution.py:410
  324.3 1.2 collective-permute-start.19
  325.6 15.8 %collective-permute-start.20 = (bf16[2,3,256]{2,0,1:T(2,128)(2,1)S(1)}, bf16[2,3,256]{2,0,1:T(2,128)(2,1)S(1)}, u32[]{:S(2)}, u32[]{:S(2)}) collective-permute-start(bf16[2,3,256]{2,0,1:T(2,128)(2,1)S(1)} %pad_maximum_fusion.16), channel_id=1, source_target_pairs={{0,8},{4,12},{8,0},{12,4},{16,24},{20,28},{24,16},{28,20},{1,9},{5... | collective-permute-start | bytes 9224 | tf_op jit(solution)/shard_map/ppermute | solution.py:175
  338.0 14.3 %all-to-all-start.6 = ((bf16[4,256,256]{1,2,0:T(8,128)(2,1)}), bf16[4,256,256]{1,2,0:T(8,128)(2,1)S(1)}, u32[]{:S(2)}, u32[]{:S(2)}) async-start(bf16[4,256,256]{1,2,0:T(8,128)(2,1)} %bitcast.201), calls=%async_computation.6 | async-start | bytes 1048576 | tf_op jit(solution)/shard_map/all_to_all | solution.py:411
  341.5 45.0 %collective-permute-start.21 = (bf16[4,3,256]{2,0,1:T(4,128)(2,1)S(1)}, bf16[4,3,256]{2,0,1:T(4,128)(2,1)S(1)}, u32[]{:S(2)}, u32[]{:S(2)}) collective-permute-start(bf16[4,3,256]{2,0,1:T(4,128)(2,1)S(1)} %pad_maximum_fusion.15), channel_id=1, source_target_pairs={{0,16},{4,20},{8,24},{12,28},{16,0},{20,4},{24,8},{28,12},{1,17},{... | collective-permute-start | bytes 18440 | tf_op jit(solution)/shard_map/ppermute | solution.py:175
  352.2 15.9 %all-to-all-start.7 = ((bf16[4,256,256]{2,1,0:T(8,128)(2,1)}), bf16[4,256,256]{2,1,0:T(8,128)(2,1)}, u32[]{:S(2)}, u32[]{:S(2)}) async-start(bf16[4,256,256]{2,1,0:T(8,128)(2,1)} %bitcast.35), calls=%async_computation.7 | async-start | bytes 1048576 | tf_op jit(solution)/shard_map/all_to_all | solution.py:412
  356.4 342.4 %reduce-scatter.3.cloned.1.call-start = ((), (), s32[]{:S(2)}) async-start(), calls=%async_computation.11 | async-start | bytes 7077888 | tf_op jit(solution)/shard_map/reduce_scatter | solution.py:482
  385.0 4.7 collective-permute-start.4
  389.7 4.7 collective-permute-start.5
  394.4 1.4 collective-permute-start.22
  395.8 7.1 collective-permute-start.23
  403.1 19.8 %collective-permute-start.24 = (f32[4,3,6144]{2,1,0:T(4,128)S(1)}, f32[4,3,6144]{2,1,0:T(4,128)S(1)}, u32[]{:S(2)}, u32[]{:S(2)}) collective-permute-start(f32[4,3,6144]{2,1,0:T(4,128)S(1)} %pad_maximum_fusion.9), channel_id=1, source_target_pairs={{0,16},{4,20},{8,24},{12,28},{16,0},{20,4},{24,8},{28,12},{1,17},{... | collective-permute-start | bytes 884744 | tf_op jit(solution)/shard_map/ppermute | solution.py:175
  424.3 122.2 %copy-start.60 = (f32[1536]{0:T(1024)}, f32[1536]{0:T(1024)S(1)}, u32[]{:S(2)}) copy-start(f32[1536]{0:T(1024)S(1)} %get-tuple-element.153) | copy-start | bytes 18436
  424.3 122.2 %copy-start.61 = (f32[1536]{0:T(1024)}, f32[1536]{0:T(1024)S(1)}, u32[]{:S(2)}) copy-start(f32[1536]{0:T(1024)S(1)} %get-tuple-element.154) | copy-start | bytes 18436
  425.7 46.3 %collective-permute-start.27 = (f32[2]{0:T(128)S(1)}, f32[2]{0:T(128)S(1)}, u32[]{:S(2)}, u32[]{:S(2)}) collective-permute-start(f32[2]{0:T(128)S(1)} %pad_maximum_fusion.22), channel_id=1, source_target_pairs={{0,1},{1,0},{2,3},{3,2},{4,5},{5,4},{6,7},{7,6},{8,9},{9,8},{10,11... | collective-permute-start | bytes 32 | tf_op jit(solution)/shard_map/ppermute | solution.py:166
  432.9 29.7 %collective-permute-start.8 = (bf16[1,327680]{1,0:T(2,128)(2,1)S(1)}, bf16[1,327680]{1,0:T(2,128)(2,1)}, u32[]{:S(2)}, u32[]{:S(2)}) collective-permute-start(bf16[1,327680]{1,0:T(2,128)(2,1)S(1)} %fusion.49), channel_id=1, source_target_pairs={{0,8},{8,0},{16,24},{24,16},{1,9},{9,1},{17,25},{25,17},{2,10},{10... | collective-permute-start | bytes 1966088 | tf_op jit(solution)/shard_map/ppermute | solution.py:200
  448.6 146.4 %copy-start.21 = (f32[256,6144]{1,0:T(8,128)}, f32[256,6144]{1,0:T(8,128)S(1)}, u32[]{:S(2)}) copy-start(f32[256,6144]{1,0:T(8,128)S(1)} %get-tuple-element.149) | copy-start | bytes 18874372
  466.9 31.2 %collective-permute-start.9 = (bf16[1,163840]{1,0:T(2,128)(2,1)S(1)}, bf16[1,163840]{1,0:T(2,128)(2,1)S(1)}, u32[]{:S(2)}, u32[]{:S(2)}) collective-permute-start(bf16[1,163840]{1,0:T(2,128)(2,1)S(1)} %fusion.69), channel_id=1, source_target_pairs={{0,16},{8,24},{16,0},{24,8},{1,17},{9,25},{17,1},{25,9},{2,18},{10... | collective-permute-start | bytes 983048 | tf_op jit(solution)/shard_map/ppermute | solution.py:200
  471.4 28.0 %collective-permute-start.25 = (f32[1,2]{1,0:T(1,128)S(1)}, f32[1,2]{1,0:T(1,128)S(1)}, u32[]{:S(2)}, u32[]{:S(2)}) collective-permute-start(f32[1,2]{1,0:T(1,128)S(1)} %pad_maximum_fusion.21), channel_id=1, source_target_pairs={{0,1},{1,0},{2,3},{3,2},{4,5},{5,4},{6,7},{7,6},{8,9},{9,8},{10,11... | collective-permute-start | bytes 32 | tf_op jit(solution)/shard_map/ppermute | solution.py:166
  473.4 28.0 %collective-permute-start.28 = (f32[2]{0:T(128)S(1)}, f32[2]{0:T(128)S(1)}, u32[]{:S(2)}, u32[]{:S(2)}) collective-permute-start(f32[2]{0:T(128)S(1)} %fusion.160), channel_id=1, source_target_pairs={{0,2},{1,3},{2,0},{3,1},{4,6},{5,7},{6,4},{7,5},{8,10},{9,11},{10,... | collective-permute-start | bytes 32 | tf_op jit(solution)/shard_map/ppermute | solution.py:166
  499.3 30.8 %collective-permute-start.10 = (bf16[1,163840]{1,0:T(2,128)(2,1)S(1)}, bf16[1,163840]{1,0:T(2,128)(2,1)S(1)}, u32[]{:S(2)}, u32[]{:S(2)}) collective-permute-start(bf16[1,163840]{1,0:T(2,128)(2,1)S(1)} %fusion.68), channel_id=1, source_target_pairs={{0,16},{8,24},{16,0},{24,8},{1,17},{9,25},{17,1},{25,9},{2,18},{10... | collective-permute-start | bytes 983048 | tf_op jit(solution)/shard_map/ppermute | solution.py:207
  500.8 42.3 %collective-permute-start.26 = (f32[1,2]{1,0:T(1,128)S(1)}, f32[1,2]{1,0:T(1,128)S(1)}, u32[]{:S(2)}, u32[]{:S(2)}) collective-permute-start(f32[1,2]{1,0:T(1,128)S(1)} %fusion.161), channel_id=1, source_target_pairs={{0,2},{1,3},{2,0},{3,1},{4,6},{5,7},{6,4},{7,5},{8,10},{9,11},{10,... | collective-permute-start | bytes 32 | tf_op jit(solution)/shard_map/ppermute | solution.py:166
  531.9 63.2 %slice-start.5 = ((s8[6291456]{0:T(1024)(128)(4,1)}), s8[4194304]{0:T(1024)(128)(4,1)S(1)}, s32[]{:S(2)}) async-start(s8[6291456]{0:T(1024)(128)(4,1)} %bitcast.272), calls=%async_computation.19 | async-start | bytes 8388608
  541.1 29.0 %collective-permute-start.11 = (bf16[1,327680]{1,0:T(2,128)(2,1)S(1)}, bf16[1,327680]{1,0:T(2,128)(2,1)S(1)}, u32[]{:S(2)}, u32[]{:S(2)}) collective-permute-start(bf16[1,327680]{1,0:T(2,128)(2,1)S(1)} %pad_maximum_fusion.4), channel_id=1, source_target_pairs={{0,8},{8,0},{16,24},{24,16},{1,9},{9,1},{17,25},{25,17},{2,10},{10... | collective-permute-start | bytes 1966088 | tf_op jit(solution)/shard_map/ppermute | solution.py:207
  547.1 48.0 %slice-start.6 = ((s8[6291456]{0:T(1024)(128)(4,1)}), s8[2097152]{0:T(1024)(128)(4,1)S(1)}, s32[]{:S(2)}) async-start(s8[6291456]{0:T(1024)(128)(4,1)} %bitcast.272), calls=%async_computation.20 | async-start | bytes 4194304
  595.0 5.3 collective-permute-start.12
  658.1 34.2 %copy-start.28 = (f32[256,1024]{1,0:T(8,128)}, f32[256,1024]{1,0:T(8,128)S(1)}, u32[]{:S(2)}) copy-start(f32[256,1024]{1,0:T(8,128)S(1)} %get-tuple-element.137) | copy-start | bytes 3145732
  658.1 34.3 %copy-start.29 = (f32[256,1024]{1,0:T(8,128)}, f32[256,1024]{1,0:T(8,128)S(1)}, u32[]{:S(2)}) copy-start(f32[256,1024]{1,0:T(8,128)S(1)} %get-tuple-element.138) | copy-start | bytes 3145732
  659.6 14.9 %collective-permute-start.13 = (f32[1,2]{1,0:T(1,128)S(1)}, f32[1,2]{1,0:T(1,128)S(1)}, u32[]{:S(2)}, u32[]{:S(2)}) collective-permute-start(f32[1,2]{1,0:T(1,128)S(1)} %pad_maximum_fusion.18), channel_id=1, source_target_pairs={{0,1},{1,0},{2,3},{3,2},{4,5},{5,4},{6,7},{7,6},{8,9},{9,8},{10,11... | collective-permute-start | bytes 32 | tf_op jit(solution)/shard_map/ppermute | solution.py:166
  665.9 30.5 %copy-start.15 = (f32[256,2048]{1,0:T(8,128)}, f32[256,2048]{1,0:T(8,128)S(1)}, u32[]{:S(2)}) copy-start(f32[256,2048]{1,0:T(8,128)S(1)} %get-tuple-element.141) | copy-start | bytes 6291460
  665.9 30.5 %copy-start.16 = (f32[256,2048]{1,0:T(8,128)}, f32[256,2048]{1,0:T(8,128)S(1)}, u32[]{:S(2)}) copy-start(f32[256,2048]{1,0:T(8,128)S(1)} %get-tuple-element.142) | copy-start | bytes 6291460
  667.3 10.3 %collective-permute-start.15 = (f32[1,2]{1,0:T(1,128)S(1)}, f32[1,2]{1,0:T(1,128)S(1)}, u32[]{:S(2)}, u32[]{:S(2)}) collective-permute-start(f32[1,2]{1,0:T(1,128)S(1)} %pad_maximum_fusion.19), channel_id=1, source_target_pairs={{0,1},{1,0},{2,3},{3,2},{4,5},{5,4},{6,7},{7,6},{8,9},{9,8},{10,11... | collective-permute-start | bytes 32 | tf_op jit(solution)/shard_map/ppermute | solution.py:166
  672.7 23.6 %copy-start.17 = (f32[512,1024]{1,0:T(8,128)}, f32[512,1024]{1,0:T(8,128)S(1)}, u32[]{:S(2)}) copy-start(f32[512,1024]{1,0:T(8,128)S(1)} %get-tuple-element.145) | copy-start | bytes 6291460
  672.7 23.6 %copy-start.18 = (f32[512,1024]{1,0:T(8,128)}, f32[512,1024]{1,0:T(8,128)S(1)}, u32[]{:S(2)}) copy-start(f32[512,1024]{1,0:T(8,128)S(1)} %get-tuple-element.146) | copy-start | bytes 6291460
  674.1 5.1 collective-permute-start.17
  675.8 6.5 collective-permute-start.14
  678.9 6.7 collective-permute-start.16
  680.6 8.4 %collective-permute-start.18 = (f32[1,2]{1,0:T(1,128)S(1)}, f32[1,2]{1,0:T(1,128)S(1)}, u32[]{:S(2)}, u32[]{:S(2)}) collective-permute-start(f32[1,2]{1,0:T(1,128)S(1)} %fusion.162), channel_id=1, source_target_pairs={{0,2},{1,3},{2,0},{3,1},{4,6},{5,7},{6,4},{7,5},{8,10},{9,11},{10,... | collective-permute-start | bytes 32 | tf_op jit(solution)/shard_map/ppermute | solution.py:166
  700.1 31.2 %copy-start.49 = (f32[3,6144]{1,0:T(4,128)S(1)}, f32[3,6144]{1,0:T(4,128)}, u32[]{:S(2)}) copy-start(f32[3,6144]{1,0:T(4,128)} %copy-done.48) | copy-start | bytes 221188
  700.2 9.8 %collective-permute-start.29 = (bf16[3,128,512]{2,1,0:T(8,128)(2,1)S(1)}, bf16[3,128,512]{2,1,0:T(8,128)(2,1)S(1)}, u32[]{:S(2)}, u32[]{:S(2)}) collective-permute-start(bf16[3,128,512]{2,1,0:T(8,128)(2,1)S(1)} %select_convert_fusion), channel_id=1, source_target_pairs={{0,8},{8,0},{16,24},{24,16},{1,9},{9,1},{17,25},{25,17},{2,10},{10... | collective-permute-start | bytes 1179656 | tf_op jit(solution)/shard_map/ppermute | solution.py:200
  710.2 9.8 %collective-permute-start.30 = (bf16[3,128,256]{2,1,0:T(8,128)(2,1)S(1)}, bf16[3,128,256]{2,1,0:T(8,128)(2,1)S(1)}, u32[]{:S(2)}, u32[]{:S(2)}) collective-permute-start(bf16[3,128,256]{2,1,0:T(8,128)(2,1)S(1)} %select_convert_fusion.1), channel_id=1, source_target_pairs={{0,16},{8,24},{16,0},{24,8},{1,17},{9,25},{17,1},{25,9},{2,18},{10... | collective-permute-start | bytes 589832 | tf_op jit(solution)/shard_map/ppermute | solution.py:200
  720.1 11.0 %collective-permute-start.31 = (bf16[3,128,256]{2,1,0:T(8,128)(2,1)S(1)}, bf16[3,128,256]{2,1,0:T(8,128)(2,1)S(1)}, u32[]{:S(2)}, u32[]{:S(2)}) collective-permute-start(bf16[3,128,256]{2,1,0:T(8,128)(2,1)S(1)} %add_convert_fusion.3), channel_id=1, source_target_pairs={{0,16},{8,24},{16,0},{24,8},{1,17},{9,25},{17,1},{25,9},{2,18},{10... | collective-permute-start | bytes 589832 | tf_op jit(solution)/shard_map/ppermute | solution.py:207
  731.1 11.3 %collective-permute-start.32 = (bf16[3,128,512]{2,1,0:T(8,128)(2,1)S(1)}, bf16[3,128,512]{2,1,0:T(8,128)(2,1)S(1)}, u32[]{:S(2)}, u32[]{:S(2)}) collective-permute-start(bf16[3,128,512]{2,1,0:T(8,128)(2,1)S(1)} %pad_maximum_fusion.10), channel_id=1, source_target_pairs={{0,8},{8,0},{16,24},{24,16},{1,9},{9,1},{17,25},{25,17},{2,10},{10... | collective-permute-start | bytes 1179656 | tf_op jit(solution)/shard_map/ppermute | solution.py:207
  736.9 3.6 collective-permute-start.6
  740.5 3.7 collective-permute-start.7
  742.7 2.4 collective-permute-start.33
  751.1 3.6 collective-permute-start.34
  754.8 3.6 collective-permute-start.35
  (70 other events, 401.6 us)
Sparse Core Ops, SparseCore 0:
  10.5 50.0 all-gather.3
  63.0 77.6 all-gather.5
  282.3 96.2 reduce-scatter.4
  408.9 59.7 reduce-scatter.2

commit v6 on v5

--- a/solution.py
+++ b/solution.py
@@ -225,26 +225,28 @@
 
 def gather_batch(shards):
     core = lax.axis_index("core")
-    flat = []
+    base = min(shard.shape[1] for shard in shards)
+    pieces = []
     for shard in shards:
         half = shard.shape[0] // 2
-        flat.append(lax.dynamic_slice_in_dim(shard, core * half, half, 0).reshape(-1))
-    blocks = lax.all_gather(jnp.concatenate(flat), ("seq", "core"), axis=0, tiled=False)
+        piece = lax.dynamic_slice_in_dim(shard, core * half, half, 0)
+        pieces.append(piece.reshape(-1, base))
+    blocks = lax.all_gather(jnp.concatenate(pieces, axis=0), ("seq", "core"), axis=0, tiled=False)
     fulls = []
     offset = 0
-    for shard, piece in zip(shards, flat):
-        fulls.append(
-            blocks[:, offset : offset + piece.size].reshape(-1, shard.shape[1])
-        )
-        offset += piece.size
+    for shard, piece in zip(shards, pieces):
+        rows = piece.shape[0]
+        fulls.append(blocks[:, offset : offset + rows].reshape(-1, shard.shape[1]))
+        offset += rows
     return fulls
 
 
 def reduce_batch(partials):
     groups = lax.axis_size("seq") * 2
-    flat = jnp.concatenate([part.reshape(groups, -1) for part in partials], axis=1)
-    flat = flat.reshape(groups * 8, -1)
-    piece = lax.psum_scatter(flat, ("seq", "core"), scatter_dimension=0, tiled=True).reshape(1, -1)
+    base = min(part.shape[1] for part in partials)
+    views = [part.reshape(groups, -1, base) for part in partials]
+    flat = jnp.concatenate(views, axis=1)
+    piece = lax.psum_scatter(flat, ("seq", "core"), scatter_dimension=0, tiled=True)[0]
     piece = halving_sum(piece, "z", lax.axis_size("z"))
     other = lax.ppermute(piece, "core", [(0, 1), (1, 0)])
     first = lax.axis_index("core") == 0
@@ -252,19 +254,19 @@
     high = jnp.where(first, other, piece)
     shares = []
     offset = 0
-    for part in partials:
-        size = part.size // groups
-        rows = (-1, part.shape[1])
+    for part, view in zip(partials, views):
+        rows = view.shape[1]
+        shape = (-1, part.shape[1])
         shares.append(
             jnp.concatenate(
                 [
-                    low[:, offset : offset + size].reshape(rows),
-                    high[:, offset : offset + size].reshape(rows),
+                    low[offset : offset + rows].reshape(shape),
+                    high[offset : offset + rows].reshape(shape),
                 ],
                 axis=0,
             )
         )
-        offset += size
+        offset += rows
     return shares
 
 

time: 778 us -> 577 us (0.74)
  local copies, waits for them, and re-layouts: 165 us -> 89.2 us
  other arithmetic: 173 us -> 99.2 us
  waiting for transfers between devices: 239 us -> 183 us
    reshape x13 -> x5, local copies, waits for them, and re-layouts: 49.4 us -> 16.9 us  [the longest x1 7.57 us: gather_batch(): fulls.append(blocks[:, offset:offset + rows].reshape(-1, shard.shape[1]))]
    ppermute x4, waiting for transfers between devices: 54.7 us -> 26.3 us  [halving_sum(): lax.ppermute(send, axis_name, [(i, i ^ step) for i in range(size)])]
    ppermute x4, waiting for transfers between devices: 62.6 us -> 34.4 us  [halving_sum(): lax.ppermute(blocks, axis_name, [(i, i ^ step) for i in range(size)])]
    slice x7 -> x6, local copies, waits for them, and re-layouts: 35.6 us -> 10.9 us  [the longest x2 9.1 us: gather_batch(): fulls.append(blocks[:, offset:offset + rows].reshape(-1, shard.shape[1]))]
    concatenate x4, other arithmetic: 24.7 us -> 0.34 us  [halving_sum(): jnp.concatenate([jnp.where(low_side, blocks, other), jnp.where(low_side,...]
    concatenate x2, other arithmetic: 27.1 us -> 9.33 us  [the longest x1 8.18 us: reduce_batch(): flat = jnp.concatenate(views, axis=1)]
    select_n x1, other arithmetic: 15.8 us -> 0.55 us  [reduce_batch(): low = jnp.where(first, piece, other)]
    all_gather x1 -> x0, local copies, waits for them, and re-layouts: 12.2 us -> none  [gather_batch(): lax.all_gather(jnp.concatenate(flat), ('seq', 'core'), axis=0, tiled=False)]
  transfers between devices with their start and end apart: 48 -> 48, of which waited for: 30 -> 27; matrix products, arithmetic and copies ran while one was open for 46% -> 40% of each run, Pallas kernels for 0% -> 0%
where the time goes in v6:
time: 577 us; the launch traced here: 566 us
  waiting for transfers between devices  183 us (32%)
  matrix products  99.7 us (17%)
  other arithmetic  99.2 us (17%)
  local copies, waits for them, and re-layouts  89.2 us (15%)
  starting transfers between devices  69.8 us (12%)
  between operations  22.8 us (4%)
    ppermute x4, waiting for transfers between devices, halving_sum(): lax.ppermute(blocks, axis_name, [(i, i ^ step) for i in range(size)])  34.4 us
    ppermute x10, waiting for transfers between devices, doubling_gather(): other = lax.ppermute(blocks, axes, [(i, i ^ step) for i in range(size)])  27.5 us
    ppermute x4, waiting for transfers between devices, halving_sum(): lax.ppermute(send, axis_name, [(i, i ^ step) for i in range(size)])  26.3 us
    all_gather x1, waiting for transfers between devices, gather_rows(): return lax.all_gather(piece, ('seq', 'core'), axis=row_axis, tiled=True)  20.3 us
    reduce_sum x5, other arithmetic, lamb_update(): jnp.sum(weight * weight, axis=sum_axes, keepdims=True)  19.5 us
    ppermute x16, starting transfers between devices, butterfly_sum(): lax.ppermute(values, axes, [(i, i ^ step) for i in range(size)])  17.6 us
    dot_general x1, matrix products, local(): jnp.einsum('cd,ce->de', silu_all.astype(jnp.float32), grad_mod_all, preci...  16 us
    sub x6, other arithmetic, lamb_update(): return (weight - step_rate * ratio * direction, moment_new, second_new)  15.5 us
  transfers between devices with their start and end apart: 48, of which 27 were waited for; matrix products, arithmetic and copies ran while one was open for 40% of the time, Pallas kernels for 0%

profile of v6, /device:TPU:0, one launch (start us, length us, event | category | flops | bytes accessed | tf_op | source)
XLA Modules:
  0.0 566.1 jit_solution(8648467969295384801)
XLA Ops:
  14.9 3.0 collective-permute-start.2
  18.0 3.7 fusion.38
  30.4 4.2 collective-permute-done.1
  34.6 2.7 fusion.68
  37.3 2.7 copy-done
  40.4 20.3 %all-gather.4.cloned.1.call-done = bf16[3,1024,1024]{2,1,0:T(8,128)(2,1)} async-done(((bf16[3,128,1024]{2,1,0:T(8,128)(2,1)}), bf16[3,1024,1024]{2,1,0:T(8,128)(2,1)}) %all-gather.4.cloned.1.call-update) | async-done | bytes 6291472 | tf_op jit(solution)/shard_map/all_gather | solution.py:188
  60.6 4.7 slice_bitcast_fusion.3
  65.3 2.9 copy.145
  70.4 3.0 copy.141
  75.7 2.5 fusion.28
  81.0 3.5 all-to-all-start
  86.0 8.1 %all-to-all-done = bf16[256,4,256]{0,2,1:T(8,128)(2,1)S(1)} async-done(((bf16[256,4,256]{0,2,1:T(8,128)(2,1)}), bf16[256,4,256]{0,2,1:T(8,128)(2,1)S(1)}, u32[]{:S(2)}, u32[]{:S(2)}) %all-to-all-start) | async-done | bytes 524320 | tf_op jit(solution)/shard_map/all_to_all | solution.py:358
  94.1 3.5 all-to-all-start.1
  97.6 2.9 fusion.48
  101.3 10.8 %all-to-all-done.1 = bf16[256,4,256]{0,2,1:T(8,128)(2,1)S(1)} async-done(((bf16[256,4,256]{0,2,1:T(8,128)(2,1)}), bf16[256,4,256]{0,2,1:T(8,128)(2,1)S(1)}, u32[]{:S(2)}, u32[]{:S(2)}) %all-to-all-start.1) | async-done | bytes 524320 | tf_op jit(solution)/shard_map/all_to_all | solution.py:359
  112.1 3.8 all-to-all-start.2
  118.6 11.6 %all-to-all-done.2 = bf16[256,4,256]{2,0,1:T(8,128)(2,1)S(1)} async-done(((bf16[256,4,256]{2,0,1:T(8,128)(2,1)}), bf16[256,4,256]{2,0,1:T(8,128)(2,1)S(1)}, u32[]{:S(2)}, u32[]{:S(2)}) %all-to-all-start.2) | async-done | bytes 524320 | tf_op jit(solution)/shard_map/all_to_all | solution.py:360
  132.1 20.0 %while.27 = (s32[]{:T(128)}, bf16[2,512,256]{2,1,0:T(8,128)(2,1)}, f32[2,4,512,1]{2,1,3,0:T(4,128)S(1)}, s32[2]{0:T(128)S(1)}, s32[1024]{0:T(1024)S(1)}, /*index...) while((s32[]{:T(128)}, bf16[2,512,256]{2,1,0:T(8,128)(2,1)}, ...), condition=%wide.region_9.10_spmd, body=%wide.region_6.9_spmd.sunk | while | flops 561117184 | bytes 30485712 | solution.py:110
  137.9 3.3 fusion.186
  147.9 3.3 fusion.186
  152.1 4.1 all-to-all-start.3
  156.2 6.9 %all-to-all-done.3 = bf16[4,256,256]{2,1,0:T(8,128)(2,1)} async-done(((bf16[4,256,256]{2,1,0:T(8,128)(2,1)}), bf16[4,256,256]{2,1,0:T(8,128)(2,1)}, u32[]{:S(2)}, u32[]{:S(2)}) %all-to-all-start.3) | async-done | bytes 524320 | tf_op jit(solution)/shard_map/all_to_all | solution.py:365
  165.2 3.1 slice.178
  168.3 6.0 %fusion.103 = (bf16[8,256,1024]{2,1,0:T(8,128)(2,1)}, bf16[8,256,1024]{2,1,0:T(8,128)(2,1)}) fusion(bf16[8,640,1024]{2,1,0:T(8,128)(2,1)} %bitcast.265), kind=kLoop, calls=%fused_computation.298 | loop fusion | bytes 16777216 | tf_op jit(solution)/shard_map/slice | solution.py:239
  174.3 7.6 %reshape.438 = bf16[1024,2048]{1,0:T(8,128)(2,1)} reshape(bf16[8,256,1024]{2,1,0:T(8,128)(2,1)} %get-tuple-element.365) | data formatting | bytes 8388608 | tf_op jit(solution)/shard_map/reshape | solution.py:239
  181.9 3.9 fusion.102
  190.3 3.9 convolution_convert_fusion
  198.2 2.8 fusion.101
  205.8 3.3 convolution_convert_fusion.1
  209.9 4.1 all-to-all-start.4
  214.1 7.3 %reshape.441 = bf16[8,256,1024]{2,1,0:T(8,128)(2,1)} reshape(bf16[1024,2048]{1,0:T(8,128)(2,1)} %convolution_convert_fusion.1) | data formatting | bytes 8388608 | tf_op jit(solution)/shard_map/reshape | solution.py:247
  221.4 8.2 %pad_maximum_fusion = bf16[8,640,1024]{2,1,0:T(8,128)(2,1)} fusion(bf16[8,256,1024]{2,1,0:T(8,128)(2,1)} %bitcast.274, bf16[8,256,1024]{2,1,0:T(8,128)(2,1)} %reshape.441, bf16[8,128,1024]{2,1,0:T(8,128)(2,1)} %bitcast.266), kind=kLoop, calls=%fused_computation.32 | loop fusion | flops 31457280 | bytes 20971520 | tf_op jit(solution)/shard_map/concatenate | solution.py:248
  230.4 35.6 %while.28 = (s32[]{:T(128)}, f32[1024,256]{0,1:T(8,128)S(1)}, f32[1024,256]{0,1:T(8,128)S(1)}, bf16[2,512,256]{2,1,0:T(8,128)(2,1)}, s32[2]{0:T(128)S(1)}, /*ind...) while((s32[]{:T(128)}, f32[1024,256]{0,1:T(8,128)S(1)}, ...), condition=%wide.region_16.17_spmd.clone, body=%wide.region_14.16_spmd.clone.sunk | while | flops 1376253952 | bytes 78974200 | solution.py:155
  238.0 4.2 multiply_reduce_fusion.16
  255.8 4.2 multiply_reduce_fusion.16
  266.1 4.1 all-to-all-start.5
  273.9 10.0 %all-to-all-done.5 = bf16[4,256,256]{2,1,0:T(8,128)(2,1)S(1)} async-done(((bf16[4,256,256]{2,1,0:T(8,128)(2,1)}), bf16[4,256,256]{2,1,0:T(8,128)(2,1)S(1)}, u32[]{:S(2)}, u32[]{:S(2)}) %all-to-all-start.5) | async-done | bytes 524320 | tf_op jit(solution)/shard_map/all_to_all | solution.py:412
  283.9 3.5 all-to-all-start.6
  287.4 2.5 collective-permute-start.21
  291.9 7.6 %all-to-all-done.6 = bf16[4,256,256]{1,2,0:T(8,128)(2,1)S(1)} async-done(((bf16[4,256,256]{1,2,0:T(8,128)(2,1)}), bf16[4,256,256]{1,2,0:T(8,128)(2,1)S(1)}, u32[]{:S(2)}, u32[]{:S(2)}) %all-to-all-start.6) | async-done | bytes 524320 | tf_op jit(solution)/shard_map/all_to_all | solution.py:413
  299.6 4.1 all-to-all-start.7
  310.0 3.7 all-to-all-done.7
  319.9 2.9 constant_dynamic-update-slice_fusion.3
  327.7 2.9 fusion.81
  331.9 3.3 collective-permute-done.4
  343.6 5.1 collective-permute-done.23
  351.2 3.2 pad_maximum_fusion.1
  354.5 14.3 %collective-permute-done.24 = f32[4,3,6144]{2,1,0:T(4,128)S(1)} collective-permute-done((f32[4,3,6144]{2,1,0:T(4,128)S(1)}, f32[4,3,6144]{2,1,0:T(4,128)S(1)}, u32[]{:S(2)}, u32[]{:S(2)}) %collective-permute-start.24) | collective-permute-done | bytes 294944 | tf_op jit(solution)/shard_map/ppermute | solution.py:175
  375.3 16.0 %multiply_reduce_fusion.2 = (f32[]{:T(128)}, f32[]{:T(128)}, f32[256,6144]{1,0:T(8,128)S(1)}, f32[256,6144]{1,0:T(8,128)S(1)}, f32[256,6144]{1,0:T(8,128)}) fusion(f32[256,6144]{1,0:T(8,128)} %param.44, f32[256,6144]{1,0:T(8,128)} %param.45, f32[256,6144]{1,0:T(8,128)} %param.46, f32[8,3,6144]{2,1,0:T(4,128)S(1)} %pad_maximum_fusion.4, ...), kind=kOutput, calls=%fused_computation.41 | convolution fusion | flops 479748096 | bytes 38350856 | tf_op jit(solution)/shard_map/cd,ce->de/dot_general | solution.py:464
  391.7 3.4 collective-permute-start.9
  400.6 8.6 %collective-permute-done.9 = bf16[640,256]{1,0:T(8,128)(2,1)S(1)} collective-permute-done((bf16[640,256]{1,0:T(8,128)(2,1)S(1)}, bf16[640,256]{1,0:T(8,128)(2,1)S(1)}, u32[]{:S(2)}, u32[]{:S(2)}) %collective-permute-start.9) | collective-permute-done | bytes 327712 | tf_op jit(solution)/shard_map/ppermute | solution.py:200
  412.5 13.1 %collective-permute-done.10 = bf16[640,256]{1,0:T(8,128)(2,1)S(1)} collective-permute-done((bf16[640,256]{1,0:T(8,128)(2,1)S(1)}, bf16[640,256]{1,0:T(8,128)(2,1)S(1)}, u32[]{:S(2)}, u32[]{:S(2)}) %collective-permute-start.10) | collective-permute-done | bytes 327712 | tf_op jit(solution)/shard_map/ppermute | solution.py:207
  431.8 10.7 %collective-permute-done.11 = bf16[640,512]{1,0:T(8,128)(2,1)S(1)} collective-permute-done((bf16[640,512]{1,0:T(8,128)(2,1)S(1)}, bf16[640,512]{1,0:T(8,128)(2,1)S(1)}, u32[]{:S(2)}, u32[]{:S(2)}) %collective-permute-start.11) | collective-permute-done | bytes 655392 | tf_op jit(solution)/shard_map/ppermute | solution.py:207
  443.1 5.2 multiply_subtract_fusion
  452.7 4.1 multiply_reduce_fusion.10
  458.3 5.4 multiply_reduce_fusion.8
  467.0 3.7 multiply_reduce_fusion.6
  498.6 9.4 %collective-permute-done.29 = bf16[3,128,512]{2,1,0:T(8,128)(2,1)S(1)} collective-permute-done((bf16[3,128,512]{2,1,0:T(8,128)(2,1)S(1)}, bf16[3,128,512]{2,1,0:T(8,128)(2,1)S(1)}, u32[]{:S(2)}, u32[]{:S(2)}) %collective-permute-start.29) | collective-permute-done | bytes 393248 | tf_op jit(solution)/shard_map/ppermute | solution.py:200
  509.7 8.3 %collective-permute-done.30 = bf16[3,128,256]{2,1,0:T(8,128)(2,1)S(1)} collective-permute-done((bf16[3,128,256]{2,1,0:T(8,128)(2,1)S(1)}, bf16[3,128,256]{2,1,0:T(8,128)(2,1)S(1)}, u32[]{:S(2)}, u32[]{:S(2)}) %collective-permute-start.30) | collective-permute-done | bytes 196640 | tf_op jit(solution)/shard_map/ppermute | solution.py:200
  518.1 10.6 %collective-permute-done.31 = bf16[3,128,256]{2,1,0:T(8,128)(2,1)S(1)} collective-permute-done((bf16[3,128,256]{2,1,0:T(8,128)(2,1)S(1)}, bf16[3,128,256]{2,1,0:T(8,128)(2,1)S(1)}, u32[]{:S(2)}, u32[]{:S(2)}) %collective-permute-start.31) | collective-permute-done | bytes 196640 | tf_op jit(solution)/shard_map/ppermute | solution.py:207
  528.9 5.7 %fusion.51 = f32[1,3,256]{2,1,0:T(4,128)S(1)} fusion(f32[256,6144]{1,0:T(8,128)} %param.44, f32[3,6144]{1,0:T(4,128)S(1)} %add.389, f32[3,6144]{1,0:T(4,128)S(1)} %copy-done.46), kind=kOutput, calls=%fused_computation.126 | convolution fusion | flops 58214400 | bytes 6441984 | tf_op jit(solution)/shard_map/ce,de->cd/dot_general | solution.py:467
  535.1 3.1 collective-permute-done.6
  543.0 5.7 %multiply_reduce_fusion.4 = (f32[3]{0:T(128)S(1)}, f32[3]{0:T(128)S(1)}, f32[3,256,1024]{2,1,0:T(8,128)S(1)}, f32[3,256,1024]{2,1,0:T(8,128)S(1)}, f32[3,256,1024]{2,1,0:T(8,128)}) fusion(f32[3,256,1024]{2,1,0:T(8,128)S(1)} %copy-done.6, f32[3,256,1024]{2,1,0:T(8,128)S(1)} %copy-done.33, f32[3,256,1024]{2,1,0:T(8,128)S(1)} %copy-done.34, ...), kind=kLoop, calls=%fused_computation.50 | loop fusion | flops 16515066 | bytes 20447256 | tf_op jit(solution)/shard_map/reduce_sum | solution.py:277
  556.0 3.3 multiply_subtract_fusion.1
  (448 shorter events, 187.0 us)
Async XLA Ops:
  7.2 53.4 %all-gather.4.cloned.1.call-start = ((), (), s32[]{:S(2)}) async-start(), calls=%async_computation.10 | async-start | bytes 7077888 | tf_op jit(solution)/shard_map/all_gather | solution.py:188
  9.7 155.5 %all-gather.6.cloned.1.call-start = ((), (), s32[]{:S(2)}) async-start(), calls=%async_computation.13 | async-start | bytes 11796480 | tf_op jit(solution)/shard_map/all_gather | solution.py:234
  14.9 8.7 %collective-permute-start.2 = (bf16[1,1536]{1,0:T(2,128)(2,1)S(1)}, bf16[1,1536]{1,0:T(2,128)(2,1)S(1)}, u32[]{:S(2)}, u32[]{:S(2)}) collective-permute-start(bf16[1,1536]{1,0:T(2,128)(2,1)S(1)} %broadcast_in_dim.158), channel_id=1, source_target_pairs={{0,1},{1,0},{2,3},{3,2},{4,5},{5,4},{6,7},{7,6},{8,9},{9,8},{10,11... | collective-permute-start | bytes 9224 | tf_op jit(solution)/shard_map/ppermute | solution.py:175
  21.7 7.1 %collective-permute-start = (f32[3,6144]{1,0:T(4,128)S(1)}, f32[3,6144]{1,0:T(4,128)S(1)}, u32[]{:S(2)}, u32[]{:S(2)}) collective-permute-start(f32[3,6144]{1,0:T(4,128)S(1)} %fusion.38), channel_id=1, source_target_pairs={{0,1},{1,0},{2,3},{3,2},{4,5},{5,4},{6,7},{7,6},{8,9},{9,8},{10,11... | collective-permute-start | bytes 221192 | tf_op jit(solution)/shard_map/ppermute | solution.py:166
  23.2 55.7 %copy-start.47 = (f32[256,32]{0,1:T(8,128)}, f32[256,32]{0,1:T(8,128)S(1)}, u32[]{:S(2)}) copy-start(f32[256,32]{0,1:T(8,128)S(1)} %get-tuple-element.433) | copy-start | bytes 98308
  23.6 3.9 collective-permute-start.3
  28.9 5.7 %collective-permute-start.1 = (f32[3,6144]{1,0:T(4,128)S(1)}, f32[3,6144]{1,0:T(4,128)S(1)}, u32[]{:S(2)}, u32[]{:S(2)}) collective-permute-start(f32[3,6144]{1,0:T(4,128)S(1)} %add.363), channel_id=1, source_target_pairs={{0,2},{1,3},{2,0},{3,1},{4,6},{5,7},{6,4},{7,5},{8,10},{9,11},{10,... | collective-permute-start | bytes 221192 | tf_op jit(solution)/shard_map/ppermute | solution.py:166
  40.4 57.2 %copy-start.16 = (bf16[256,1024]{1,0:T(8,128)(2,1)}, bf16[256,1024]{1,0:T(8,128)(2,1)S(1)}, u32[]{:S(2)}) copy-start(bf16[256,1024]{1,0:T(8,128)(2,1)S(1)} %fusion.55) | copy-start | bytes 1572868
  81.0 13.1 %all-to-all-start = ((bf16[256,4,256]{0,2,1:T(8,128)(2,1)}), bf16[256,4,256]{0,2,1:T(8,128)(2,1)S(1)}, u32[]{:S(2)}, u32[]{:S(2)}) async-start(bf16[256,4,256]{0,2,1:T(8,128)(2,1)} %convert_element_type.226), calls=%async_computation | async-start | bytes 1048576 | tf_op jit(solution)/shard_map/all_to_all | solution.py:358
  94.1 18.0 %all-to-all-start.1 = ((bf16[256,4,256]{0,2,1:T(8,128)(2,1)}), bf16[256,4,256]{0,2,1:T(8,128)(2,1)S(1)}, u32[]{:S(2)}, u32[]{:S(2)}) async-start(bf16[256,4,256]{0,2,1:T(8,128)(2,1)} %convert_element_type.227), calls=%async_computation.1 | async-start | bytes 1048576 | tf_op jit(solution)/shard_map/all_to_all | solution.py:359
  112.1 18.1 %all-to-all-start.2 = ((bf16[256,4,256]{2,0,1:T(8,128)(2,1)}), bf16[256,4,256]{2,0,1:T(8,128)(2,1)S(1)}, u32[]{:S(2)}, u32[]{:S(2)}) async-start(bf16[256,4,256]{2,0,1:T(8,128)(2,1)} %bitcast.198), calls=%async_computation.2 | async-start | bytes 1048576 | tf_op jit(solution)/shard_map/all_to_all | solution.py:360
  152.1 11.1 %all-to-all-start.3 = ((bf16[4,256,256]{2,1,0:T(8,128)(2,1)}), bf16[4,256,256]{2,1,0:T(8,128)(2,1)}, u32[]{:S(2)}, u32[]{:S(2)}) async-start(bf16[4,256,256]{2,1,0:T(8,128)(2,1)} %bitcast.26), calls=%async_computation.3 | async-start | bytes 1048576 | tf_op jit(solution)/shard_map/all_to_all | solution.py:365
  209.9 19.7 %all-to-all-start.4 = ((bf16[256,4,256]{2,0,1:T(8,128)(2,1)}), bf16[256,4,256]{2,0,1:T(8,128)(2,1)}, u32[]{:S(2)}, u32[]{:S(2)}) async-start(bf16[256,4,256]{2,0,1:T(8,128)(2,1)} %bitcast.197), calls=%async_computation.4 | async-start | bytes 1048576 | tf_op jit(solution)/shard_map/all_to_all | solution.py:400
  214.1 158.9 %reduce-scatter.5.cloned.1.call-start = ((), (), s32[]{:S(2)}) async-start(), calls=%async_computation.12 | async-start | bytes 11796480 | tf_op jit(solution)/shard_map/reduce_scatter | solution.py:249
  230.4 39.7 %copy-start.55 = (bf16[3,256]{1,0:T(4,128)(2,1)S(1)}, bf16[3,256]{1,0:T(4,128)(2,1)}, u32[]{:S(2)}) copy-start(bf16[3,256]{1,0:T(4,128)(2,1)} %copy-done.54) | copy-start | bytes 4612
  266.1 17.8 %all-to-all-start.5 = ((bf16[4,256,256]{2,1,0:T(8,128)(2,1)}), bf16[4,256,256]{2,1,0:T(8,128)(2,1)S(1)}, u32[]{:S(2)}, u32[]{:S(2)}) async-start(bf16[4,256,256]{2,1,0:T(8,128)(2,1)} %bitcast.281), calls=%async_computation.5 | async-start | bytes 1048576 | tf_op jit(solution)/shard_map/all_to_all | solution.py:412
  270.1 1.2 collective-permute-start.19
  271.4 15.9 %collective-permute-start.20 = (bf16[2,3,256]{2,0,1:T(2,128)(2,1)S(1)}, bf16[2,3,256]{2,0,1:T(2,128)(2,1)S(1)}, u32[]{:S(2)}, u32[]{:S(2)}) collective-permute-start(bf16[2,3,256]{2,0,1:T(2,128)(2,1)S(1)} %pad_maximum_fusion.16), channel_id=1, source_target_pairs={{0,8},{4,12},{8,0},{12,4},{16,24},{20,28},{24,16},{28,20},{1,9},{5... | collective-permute-start | bytes 9224 | tf_op jit(solution)/shard_map/ppermute | solution.py:175
  283.9 15.7 %all-to-all-start.6 = ((bf16[4,256,256]{1,2,0:T(8,128)(2,1)}), bf16[4,256,256]{1,2,0:T(8,128)(2,1)S(1)}, u32[]{:S(2)}, u32[]{:S(2)}) async-start(bf16[4,256,256]{1,2,0:T(8,128)(2,1)} %bitcast.196), calls=%async_computation.6 | async-start | bytes 1048576 | tf_op jit(solution)/shard_map/all_to_all | solution.py:413
  287.4 44.5 %collective-permute-start.21 = (bf16[4,3,256]{2,0,1:T(4,128)(2,1)S(1)}, bf16[4,3,256]{2,0,1:T(4,128)(2,1)S(1)}, u32[]{:S(2)}, u32[]{:S(2)}) collective-permute-start(bf16[4,3,256]{2,0,1:T(4,128)(2,1)S(1)} %pad_maximum_fusion.15), channel_id=1, source_target_pairs={{0,16},{4,20},{8,24},{12,28},{16,0},{20,4},{24,8},{28,12},{1,17},{... | collective-permute-start | bytes 18440 | tf_op jit(solution)/shard_map/ppermute | solution.py:175
  299.6 14.2 %all-to-all-start.7 = ((bf16[4,256,256]{2,1,0:T(8,128)(2,1)}), bf16[4,256,256]{2,1,0:T(8,128)(2,1)}, u32[]{:S(2)}, u32[]{:S(2)}) async-start(bf16[4,256,256]{2,1,0:T(8,128)(2,1)} %bitcast.38), calls=%async_computation.7 | async-start | bytes 1048576 | tf_op jit(solution)/shard_map/all_to_all | solution.py:414
  303.7 193.1 %reduce-scatter.3.cloned.1.call-start = ((), (), s32[]{:S(2)}) async-start(), calls=%async_computation.11 | async-start | bytes 7077888 | tf_op jit(solution)/shard_map/reduce_scatter | solution.py:484
  330.5 4.7 collective-permute-start.4
  335.2 4.7 collective-permute-start.5
  339.9 1.4 collective-permute-start.22
  341.4 7.3 %collective-permute-start.23 = (f32[2,3,6144]{2,1,0:T(4,128)S(1)}, f32[2,3,6144]{2,1,0:T(4,128)S(1)}, u32[]{:S(2)}, u32[]{:S(2)}) collective-permute-start(f32[2,3,6144]{2,1,0:T(4,128)S(1)} %pad_maximum_fusion.11), channel_id=1, source_target_pairs={{0,8},{4,12},{8,0},{12,4},{16,24},{20,28},{24,16},{28,20},{1,9},{5... | collective-permute-start | bytes 442376 | tf_op jit(solution)/shard_map/ppermute | solution.py:175
  348.9 20.0 %collective-permute-start.24 = (f32[4,3,6144]{2,1,0:T(4,128)S(1)}, f32[4,3,6144]{2,1,0:T(4,128)S(1)}, u32[]{:S(2)}, u32[]{:S(2)}) collective-permute-start(f32[4,3,6144]{2,1,0:T(4,128)S(1)} %pad_maximum_fusion.9), channel_id=1, source_target_pairs={{0,16},{4,20},{8,24},{12,28},{16,0},{20,4},{24,8},{28,12},{1,17},{... | collective-permute-start | bytes 884744 | tf_op jit(solution)/shard_map/ppermute | solution.py:175
  370.2 60.9 %copy-start.57 = (f32[1536]{0:T(1024)}, f32[1536]{0:T(1024)S(1)}, u32[]{:S(2)}) copy-start(f32[1536]{0:T(1024)S(1)} %get-tuple-element.153) | copy-start | bytes 18436
  370.2 60.9 %copy-start.58 = (f32[1536]{0:T(1024)}, f32[1536]{0:T(1024)S(1)}, u32[]{:S(2)}) copy-start(f32[1536]{0:T(1024)S(1)} %get-tuple-element.154) | copy-start | bytes 18436
  371.6 26.0 %collective-permute-start.27 = (f32[2]{0:T(128)S(1)}, f32[2]{0:T(128)S(1)}, u32[]{:S(2)}, u32[]{:S(2)}) collective-permute-start(f32[2]{0:T(128)S(1)} %pad_maximum_fusion.22), channel_id=1, source_target_pairs={{0,1},{1,0},{2,3},{3,2},{4,5},{5,4},{6,7},{7,6},{8,9},{9,8},{10,11... | collective-permute-start | bytes 32 | tf_op jit(solution)/shard_map/ppermute | solution.py:166
  374.7 16.5 %collective-permute-start.8 = (bf16[640,512]{1,0:T(8,128)(2,1)S(1)}, bf16[640,512]{1,0:T(8,128)(2,1)S(1)}, u32[]{:S(2)}, u32[]{:S(2)}) collective-permute-start(bf16[640,512]{1,0:T(8,128)(2,1)S(1)} %select_convert_fusion), channel_id=1, source_target_pairs={{0,8},{8,0},{16,24},{24,16},{1,9},{9,1},{17,25},{25,17},{2,10},{10... | collective-permute-start | bytes 1966088 | tf_op jit(solution)/shard_map/ppermute | solution.py:200
  391.3 51.8 %copy-start.18 = (f32[256,6144]{1,0:T(8,128)}, f32[256,6144]{1,0:T(8,128)S(1)}, u32[]{:S(2)}) copy-start(f32[256,6144]{1,0:T(8,128)S(1)} %get-tuple-element.149) | copy-start | bytes 18874372
  391.3 51.8 %copy-start.19 = (f32[256,6144]{1,0:T(8,128)}, f32[256,6144]{1,0:T(8,128)S(1)}, u32[]{:S(2)}) copy-start(f32[256,6144]{1,0:T(8,128)S(1)} %get-tuple-element.150) | copy-start | bytes 18874372
  391.3 51.8 %slice-start = ((s8[6291456]{0:T(1024)(128)(4,1)}), s8[4194304]{0:T(1024)(128)(4,1)S(1)}, s32[]{:S(2)}) async-start(s8[6291456]{0:T(1024)(128)(4,1)} %bitcast.256), calls=%async_computation.14 | async-start | bytes 8388608
  391.7 17.5 %collective-permute-start.9 = (bf16[640,256]{1,0:T(8,128)(2,1)S(1)}, bf16[640,256]{1,0:T(8,128)(2,1)S(1)}, u32[]{:S(2)}, u32[]{:S(2)}) collective-permute-start(bf16[640,256]{1,0:T(8,128)(2,1)S(1)} %select_convert_fusion.2), channel_id=1, source_target_pairs={{0,16},{8,24},{16,0},{24,8},{1,17},{9,25},{17,1},{25,9},{2,18},{10... | collective-permute-start | bytes 983048 | tf_op jit(solution)/shard_map/ppermute | solution.py:200
  397.1 12.3 %collective-permute-start.25 = (f32[1,2]{1,0:T(1,128)S(1)}, f32[1,2]{1,0:T(1,128)S(1)}, u32[]{:S(2)}, u32[]{:S(2)}) collective-permute-start(f32[1,2]{1,0:T(1,128)S(1)} %pad_maximum_fusion.21), channel_id=1, source_target_pairs={{0,1},{1,0},{2,3},{3,2},{4,5},{5,4},{6,7},{7,6},{8,9},{9,8},{10,11... | collective-permute-start | bytes 32 | tf_op jit(solution)/shard_map/ppermute | solution.py:166
  398.9 12.2 %collective-permute-start.28 = (f32[2]{0:T(128)S(1)}, f32[2]{0:T(128)S(1)}, u32[]{:S(2)}, u32[]{:S(2)}) collective-permute-start(f32[2]{0:T(128)S(1)} %fusion.154), channel_id=1, source_target_pairs={{0,2},{1,3},{2,0},{3,1},{4,6},{5,7},{6,4},{7,5},{8,10},{9,11},{10,... | collective-permute-start | bytes 32 | tf_op jit(solution)/shard_map/ppermute | solution.py:166
  409.3 16.4 %collective-permute-start.10 = (bf16[640,256]{1,0:T(8,128)(2,1)S(1)}, bf16[640,256]{1,0:T(8,128)(2,1)S(1)}, u32[]{:S(2)}, u32[]{:S(2)}) collective-permute-start(bf16[640,256]{1,0:T(8,128)(2,1)S(1)} %add_convert_fusion.1), channel_id=1, source_target_pairs={{0,16},{8,24},{16,0},{24,8},{1,17},{9,25},{17,1},{25,9},{2,18},{10... | collective-permute-start | bytes 983048 | tf_op jit(solution)/shard_map/ppermute | solution.py:207
  410.7 17.1 %collective-permute-start.26 = (f32[1,2]{1,0:T(1,128)S(1)}, f32[1,2]{1,0:T(1,128)S(1)}, u32[]{:S(2)}, u32[]{:S(2)}) collective-permute-start(f32[1,2]{1,0:T(1,128)S(1)} %fusion.155), channel_id=1, source_target_pairs={{0,2},{1,3},{2,0},{3,1},{4,6},{5,7},{6,4},{7,5},{8,10},{9,11},{10,... | collective-permute-start | bytes 32 | tf_op jit(solution)/shard_map/ppermute | solution.py:166
  412.5 30.5 %slice-start.1 = ((s8[6291456]{0:T(1024)(128)(4,1)}), s8[2097152]{0:T(1024)(128)(4,1)S(1)}, s32[]{:S(2)}) async-start(s8[6291456]{0:T(1024)(128)(4,1)} %bitcast.256), calls=%async_computation.15 | async-start | bytes 4194304
  425.8 16.7 %collective-permute-start.11 = (bf16[640,512]{1,0:T(8,128)(2,1)S(1)}, bf16[640,512]{1,0:T(8,128)(2,1)S(1)}, u32[]{:S(2)}, u32[]{:S(2)}) collective-permute-start(bf16[640,512]{1,0:T(8,128)(2,1)S(1)} %pad_maximum_fusion.6), channel_id=1, source_target_pairs={{0,8},{8,0},{16,24},{24,16},{1,9},{9,1},{17,25},{25,17},{2,10},{10... | collective-permute-start | bytes 1966088 | tf_op jit(solution)/shard_map/ppermute | solution.py:207
  443.0 5.4 collective-permute-start.12
  456.8 33.6 %copy-start.25 = (f32[256,1024]{1,0:T(8,128)}, f32[256,1024]{1,0:T(8,128)S(1)}, u32[]{:S(2)}) copy-start(f32[256,1024]{1,0:T(8,128)S(1)} %get-tuple-element.137) | copy-start | bytes 3145732
  456.8 33.7 %copy-start.26 = (f32[256,1024]{1,0:T(8,128)}, f32[256,1024]{1,0:T(8,128)S(1)}, u32[]{:S(2)}) copy-start(f32[256,1024]{1,0:T(8,128)S(1)} %get-tuple-element.138) | copy-start | bytes 3145732
  458.2 14.1 %collective-permute-start.13 = (f32[1,2]{1,0:T(1,128)S(1)}, f32[1,2]{1,0:T(1,128)S(1)}, u32[]{:S(2)}, u32[]{:S(2)}) collective-permute-start(f32[1,2]{1,0:T(1,128)S(1)} %pad_maximum_fusion.18), channel_id=1, source_target_pairs={{0,1},{1,0},{2,3},{3,2},{4,5},{5,4},{6,7},{7,6},{8,9},{9,8},{10,11... | collective-permute-start | bytes 32 | tf_op jit(solution)/shard_map/ppermute | solution.py:166
  463.8 30.6 %copy-start.12 = (f32[256,2048]{1,0:T(8,128)}, f32[256,2048]{1,0:T(8,128)S(1)}, u32[]{:S(2)}) copy-start(f32[256,2048]{1,0:T(8,128)S(1)} %get-tuple-element.141) | copy-start | bytes 6291460
  463.8 30.6 %copy-start.13 = (f32[256,2048]{1,0:T(8,128)}, f32[256,2048]{1,0:T(8,128)S(1)}, u32[]{:S(2)}) copy-start(f32[256,2048]{1,0:T(8,128)S(1)} %get-tuple-element.142) | copy-start | bytes 6291460
  465.2 10.4 %collective-permute-start.15 = (f32[1,2]{1,0:T(1,128)S(1)}, f32[1,2]{1,0:T(1,128)S(1)}, u32[]{:S(2)}, u32[]{:S(2)}) collective-permute-start(f32[1,2]{1,0:T(1,128)S(1)} %pad_maximum_fusion.19), channel_id=1, source_target_pairs={{0,1},{1,0},{2,3},{3,2},{4,5},{5,4},{6,7},{7,6},{8,9},{9,8},{10,11... | collective-permute-start | bytes 32 | tf_op jit(solution)/shard_map/ppermute | solution.py:166
  470.7 23.7 %copy-start.14 = (f32[512,1024]{1,0:T(8,128)}, f32[512,1024]{1,0:T(8,128)S(1)}, u32[]{:S(2)}) copy-start(f32[512,1024]{1,0:T(8,128)S(1)} %get-tuple-element.145) | copy-start | bytes 6291460
  470.7 23.7 %copy-start.15 = (f32[512,1024]{1,0:T(8,128)}, f32[512,1024]{1,0:T(8,128)S(1)}, u32[]{:S(2)}) copy-start(f32[512,1024]{1,0:T(8,128)S(1)} %get-tuple-element.146) | copy-start | bytes 6291460
  472.1 5.0 collective-permute-start.17
  473.7 6.7 %collective-permute-start.14 = (f32[1,2]{1,0:T(1,128)S(1)}, f32[1,2]{1,0:T(1,128)S(1)}, u32[]{:S(2)}, u32[]{:S(2)}) collective-permute-start(f32[1,2]{1,0:T(1,128)S(1)} %fusion.158), channel_id=1, source_target_pairs={{0,2},{1,3},{2,0},{3,1},{4,6},{5,7},{6,4},{7,5},{8,10},{9,11},{10,... | collective-permute-start | bytes 32 | tf_op jit(solution)/shard_map/ppermute | solution.py:166
  477.0 6.7 %collective-permute-start.16 = (f32[1,2]{1,0:T(1,128)S(1)}, f32[1,2]{1,0:T(1,128)S(1)}, u32[]{:S(2)}, u32[]{:S(2)}) collective-permute-start(f32[1,2]{1,0:T(1,128)S(1)} %fusion.157), channel_id=1, source_target_pairs={{0,2},{1,3},{2,0},{3,1},{4,6},{5,7},{6,4},{7,5},{8,10},{9,11},{10,... | collective-permute-start | bytes 32 | tf_op jit(solution)/shard_map/ppermute | solution.py:166
  478.5 8.6 %collective-permute-start.18 = (f32[1,2]{1,0:T(1,128)S(1)}, f32[1,2]{1,0:T(1,128)S(1)}, u32[]{:S(2)}, u32[]{:S(2)}) collective-permute-start(f32[1,2]{1,0:T(1,128)S(1)} %fusion.156), channel_id=1, source_target_pairs={{0,2},{1,3},{2,0},{3,1},{4,6},{5,7},{6,4},{7,5},{8,10},{9,11},{10,... | collective-permute-start | bytes 32 | tf_op jit(solution)/shard_map/ppermute | solution.py:166
  498.2 30.7 %copy-start.46 = (f32[3,6144]{1,0:T(4,128)S(1)}, f32[3,6144]{1,0:T(4,128)}, u32[]{:S(2)}) copy-start(f32[3,6144]{1,0:T(4,128)} %copy-done.45) | copy-start | bytes 221188
  498.2 9.8 %collective-permute-start.29 = (bf16[3,128,512]{2,1,0:T(8,128)(2,1)S(1)}, bf16[3,128,512]{2,1,0:T(8,128)(2,1)S(1)}, u32[]{:S(2)}, u32[]{:S(2)}) collective-permute-start(bf16[3,128,512]{2,1,0:T(8,128)(2,1)S(1)} %select_convert_fusion.1), channel_id=1, source_target_pairs={{0,8},{8,0},{16,24},{24,16},{1,9},{9,1},{17,25},{25,17},{2,10},{10... | collective-permute-start | bytes 1179656 | tf_op jit(solution)/shard_map/ppermute | solution.py:200
  508.2 9.7 %collective-permute-start.30 = (bf16[3,128,256]{2,1,0:T(8,128)(2,1)S(1)}, bf16[3,128,256]{2,1,0:T(8,128)(2,1)S(1)}, u32[]{:S(2)}, u32[]{:S(2)}) collective-permute-start(bf16[3,128,256]{2,1,0:T(8,128)(2,1)S(1)} %select_convert_fusion.3), channel_id=1, source_target_pairs={{0,16},{8,24},{16,0},{24,8},{1,17},{9,25},{17,1},{25,9},{2,18},{10... | collective-permute-start | bytes 589832 | tf_op jit(solution)/shard_map/ppermute | solution.py:200
  518.0 10.7 %collective-permute-start.31 = (bf16[3,128,256]{2,1,0:T(8,128)(2,1)S(1)}, bf16[3,128,256]{2,1,0:T(8,128)(2,1)S(1)}, u32[]{:S(2)}, u32[]{:S(2)}) collective-permute-start(bf16[3,128,256]{2,1,0:T(8,128)(2,1)S(1)} %add_convert_fusion.4), channel_id=1, source_target_pairs={{0,16},{8,24},{16,0},{24,8},{1,17},{9,25},{17,1},{25,9},{2,18},{10... | collective-permute-start | bytes 589832 | tf_op jit(solution)/shard_map/ppermute | solution.py:207
  528.8 11.2 %collective-permute-start.32 = (bf16[3,128,512]{2,1,0:T(8,128)(2,1)S(1)}, bf16[3,128,512]{2,1,0:T(8,128)(2,1)S(1)}, u32[]{:S(2)}, u32[]{:S(2)}) collective-permute-start(bf16[3,128,512]{2,1,0:T(8,128)(2,1)S(1)} %pad_maximum_fusion.10), channel_id=1, source_target_pairs={{0,8},{8,0},{16,24},{24,16},{1,9},{9,1},{17,25},{25,17},{2,10},{10... | collective-permute-start | bytes 1179656 | tf_op jit(solution)/shard_map/ppermute | solution.py:207
  534.6 3.6 collective-permute-start.6
  538.2 3.7 collective-permute-start.7
  540.2 2.4 collective-permute-start.33
  548.7 3.6 collective-permute-start.34
  552.3 3.6 collective-permute-start.35
  (62 other events, 362.9 us)
Sparse Core Ops, SparseCore 0:
  10.5 50.1 all-gather.3
  63.1 77.6 all-gather.5
  229.7 96.2 reduce-scatter.4
  354.6 59.9 reduce-scatter.2

commit v7 on v6

--- a/solution.py
+++ b/solution.py
@@ -354,10 +354,8 @@
     query_send = rotate(query_lin, places_own, 1.0).astype(jnp.bfloat16)
     key_send = rotate(key_lin, places_own, 1.0).astype(jnp.bfloat16)
     value_send = value_lin.astype(jnp.bfloat16)
-    query_heads, key_heads, value_heads = (
-        lax.all_to_all(query_send, "seq", split_axis=1, concat_axis=0, tiled=True),
-        lax.all_to_all(key_send, "seq", split_axis=1, concat_axis=0, tiled=True),
-        lax.all_to_all(value_send, "seq", split_axis=1, concat_axis=0, tiled=True),
+    query_heads, key_heads, value_heads = lax.all_to_all(
+        jnp.stack([query_send, key_send, value_send]), "seq", split_axis=2, concat_axis=1, tiled=True
     )
     attended_heads, log_totals = attend_forward(
         query_heads, key_heads, value_heads, owners_all, usable_all, group_frames
@@ -408,10 +406,12 @@
         usable_all,
         group_frames,
     )
-    grad_query_rows, grad_key_rows, grad_value_rows = (
-        lax.all_to_all(grad_query_heads, "seq", split_axis=0, concat_axis=1, tiled=True),
-        lax.all_to_all(grad_key_heads, "seq", split_axis=0, concat_axis=1, tiled=True),
-        lax.all_to_all(grad_value_heads, "seq", split_axis=0, concat_axis=1, tiled=True),
+    grad_query_rows, grad_key_rows, grad_value_rows = lax.all_to_all(
+        jnp.stack([grad_query_heads, grad_key_heads, grad_value_heads]),
+        "seq",
+        split_axis=1,
+        concat_axis=2,
+        tiled=True,
     )
     grad_query_lin = rotate(grad_query_rows.astype(jnp.float32), places_own, -1.0).astype(
         jnp.bfloat16
@@ -471,19 +471,21 @@
         list(doubling_gather(grad_silu_part, "seq", seq_count, seq_rank)), axis=1
     )
     time_grad = jax.vjp(jax.nn.silu, time_emb)[1](grad_silu)[0]
-    grad_out, grad_up, grad_down = [
-        share.astype(jnp.float32)
-        for share in reduce_batch(
-            [
-                grad_out_local.astype(jnp.bfloat16),
-                grad_up_local.astype(jnp.bfloat16),
-                grad_down_local.astype(jnp.bfloat16),
-            ]
-        )
-    ]
+    batch_shares = reduce_batch(
+        [
+            grad_out_local.astype(jnp.bfloat16),
+            grad_up_local.astype(jnp.bfloat16),
+            grad_down_local.astype(jnp.bfloat16),
+        ]
+    )
+    batch_shares, grad_mod_share, grad_bias_share = lax.optimization_barrier(
+        (batch_shares, grad_mod_share, grad_bias_share)
+    )
+    grad_out, grad_up, grad_down = [share.astype(jnp.float32) for share in batch_shares]
     qkv_piece = lax.psum_scatter(
         grad_qkv_local.astype(jnp.bfloat16), ("seq", "core"), scatter_dimension=1, tiled=True
     )
+    qkv_piece, batch_shares = lax.optimization_barrier((qkv_piece, batch_shares))
     updated = [
         lamb_update(w_out, mom_out, var_out, grad_out, None, seq_count),
         lamb_update(w_up, mom_up, var_up, grad_up, None, seq_count),
@@ -491,7 +493,6 @@
         lamb_update(w_mod, mom_mod, var_mod, grad_mod_share, None, seq_count),
         lamb_update(b_mod, mom_bias, var_bias, grad_bias_share, None, seq_count),
     ]
-    qkv_piece, updated = lax.optimization_barrier((qkv_piece, updated))
     qkv_piece = halving_sum(qkv_piece, "z", lax.axis_size("z"))
     qkv_other = lax.ppermute(qkv_piece, "core", [(0, 1), (1, 0)])
     qkv_first = lax.axis_index("core") == 0

time: 577 us -> 604 us (1.047)
  other arithmetic: 99.2 us -> 119 us
  matrix products: 99.7 us -> 84.9 us
  local copies, waits for them, and re-layouts: 89.2 us -> 103 us
  waiting for transfers between devices: 183 us -> 195 us
    all_to_all x6 -> x2, waiting for transfers between devices: 51.9 us -> 73.7 us  [the longest x1 46.9 us: local(): lax.all_to_all(jnp.stack([query_send, key_send, value_send]), 'seq', spli...]
    ppermute x10, waiting for transfers between devices: 27.5 us -> 10.8 us  [doubling_gather(): other = lax.ppermute(blocks, axes, [(i, i ^ step) for i in range(size)])]
    all_to_all x6 -> x2, starting transfers between devices: 22.4 us -> 8.28 us  [the longest x1 4.2 us: local(): lax.all_to_all(jnp.stack([grad_query_heads, grad_key_heads, grad_value_he...]
    another operation x2 -> x11, local copies, waits for them, and re-layouts: 1.66 us -> 15.6 us  [the longest x6 8.57 us: local(): query_heads, key_heads, value_heads = lax.all_to_all(jnp.stack([query_sen...]
    dot_general x1, matrix products: 16 us -> 4.97 us  [local(): jnp.einsum('cd,ce->de', silu_all.astype(jnp.float32), grad_mod_all, preci...]
    reduce_sum x5 -> x6, other arithmetic: 19.5 us -> 29 us  [lamb_update(): jnp.sum(weight * weight, axis=sum_axes, keepdims=True)]
    ppermute x4, waiting for transfers between devices: 34.4 us -> 40.6 us  [halving_sum(): lax.ppermute(blocks, axis_name, [(i, i ^ step) for i in range(size)])]
  transfers between devices with their start and end apart: 48 -> 44, of which waited for: 27 -> 23; matrix products, arithmetic and copies ran while one was open for 40% -> 41% of each run, Pallas kernels for 0% -> 0%
where the time goes in v7:
time: 604 us; the launch traced here: 593 us
  waiting for transfers between devices  195 us (32%)
  other arithmetic  119 us (20%)
  local copies, waits for them, and re-layouts  103 us (17%)
  matrix products  84.9 us (14%)
  starting transfers between devices  65.5 us (11%)
  between operations  22.8 us (4%)
    all_to_all x1, waiting for transfers between devices, local(): lax.all_to_all(jnp.stack([query_send, key_send, value_send]), 'seq', spli...  46.9 us
    ppermute x4, waiting for transfers between devices, halving_sum(): lax.ppermute(blocks, axis_name, [(i, i ^ step) for i in range(size)])  40.6 us
    reduce_sum x6, other arithmetic, lamb_update(): jnp.sum(weight * weight, axis=sum_axes, keepdims=True)  29 us
    ppermute x4, waiting for transfers between devices, halving_sum(): lax.ppermute(send, axis_name, [(i, i ^ step) for i in range(size)])  27.6 us
    all_to_all x1, waiting for transfers between devices, local(): lax.all_to_all(jnp.stack([grad_query_heads, grad_key_heads, grad_value_he...  26.8 us
    ppermute x16, starting transfers between devices, butterfly_sum(): lax.ppermute(values, axes, [(i, i ^ step) for i in range(size)])  22 us
    all_gather x1, waiting for transfers between devices, gather_rows(): return lax.all_gather(piece, ('seq', 'core'), axis=row_axis, tiled=True)  20.3 us
    sub x6, other arithmetic, lamb_update(): return (weight - step_rate * ratio * direction, moment_new, second_new)  17.5 us
  transfers between devices with their start and end apart: 44, of which 23 were waited for; matrix products, arithmetic and copies ran while one was open for 41% of the time, Pallas kernels for 0%

profile of v7, /device:TPU:0, one launch (start us, length us, event | category | flops | bytes accessed | tf_op | source)
XLA Modules:
  0.0 592.9 jit_solution(12717196484987492351)
XLA Ops:
  14.9 3.0 collective-permute-start.2
  18.0 3.7 fusion.38
  30.4 4.2 collective-permute-done.1
  34.6 2.7 fusion.69
  37.3 2.7 copy-done
  40.4 20.3 %all-gather.4.cloned.1.call-done = bf16[3,1024,1024]{2,1,0:T(8,128)(2,1)} async-done(((bf16[3,128,1024]{2,1,0:T(8,128)(2,1)}), bf16[3,1024,1024]{2,1,0:T(8,128)(2,1)}) %all-gather.4.cloned.1.call-update) | async-done | bytes 6291472 | tf_op jit(solution)/shard_map/all_gather | solution.py:188
  60.6 4.7 slice_bitcast_fusion.4
  65.3 2.9 copy.147
  70.4 3.0 copy.150
  75.7 2.5 fusion.28
  84.7 2.5 copy.155
  87.2 4.1 all-to-all-start
  91.3 46.9 %all-to-all-done = bf16[3,256,1024]{1,0,2:T(4,128)(2,1)S(1)} async-done(((bf16[3,256,1024]{1,0,2:T(4,128)(2,1)}), bf16[3,256,1024]{1,0,2:T(4,128)(2,1)S(1)}, u32[]{:S(2)}, u32[]{:S(2)}) %all-to-all-start) | async-done | bytes 1572896 | tf_op jit(solution)/shard_map/all_to_all | solution.py:357
  138.2 3.2 fusion.105
  147.7 20.0 %while.27 = (s32[]{:T(128)}, bf16[2,512,256]{2,1,0:T(8,128)(2,1)}, f32[2,4,512,1]{2,1,3,0:T(4,128)S(1)}, s32[2]{0:T(128)S(1)}, s32[1024]{0:T(1024)S(1)}, /*index...) while((s32[]{:T(128)}, bf16[2,512,256]{2,1,0:T(8,128)(2,1)}, ...), condition=%wide.region_9.10_spmd, body=%wide.region_6.9_spmd.sunk | while | flops 561117184 | bytes 30485712 | solution.py:110
  153.5 3.3 fusion.189
  163.5 3.3 fusion.189
  167.7 4.1 all-to-all-start.1
  171.9 6.7 %all-to-all-done.1 = bf16[4,256,256]{2,1,0:T(8,128)(2,1)} async-done(((bf16[4,256,256]{2,1,0:T(8,128)(2,1)}), bf16[4,256,256]{2,1,0:T(8,128)(2,1)}, u32[]{:S(2)}, u32[]{:S(2)}) %all-to-all-start.1) | async-done | bytes 524320 | tf_op jit(solution)/shard_map/all_to_all | solution.py:363
  180.6 3.1 slice.184
  183.7 6.0 %fusion.104 = (bf16[8,256,1024]{2,1,0:T(8,128)(2,1)}, bf16[8,256,1024]{2,1,0:T(8,128)(2,1)}) fusion(bf16[8,640,1024]{2,1,0:T(8,128)(2,1)} %bitcast.279), kind=kLoop, calls=%fused_computation.301 | loop fusion | bytes 16777216 | tf_op jit(solution)/shard_map/slice | solution.py:239
  189.7 7.2 %reshape.434 = bf16[1024,2048]{1,0:T(8,128)(2,1)} reshape(bf16[8,256,1024]{2,1,0:T(8,128)(2,1)} %get-tuple-element.318) | data formatting | bytes 8388608 | tf_op jit(solution)/shard_map/reshape | solution.py:239
  197.0 3.9 fusion.103
  210.6 2.8 fusion.102
  218.2 3.9 convolution_convert_fusion
  222.0 3.3 convolution_convert_fusion.1
  226.2 4.1 all-to-all-start.2
  230.4 7.5 %reshape.437 = bf16[8,256,1024]{2,1,0:T(8,128)(2,1)} reshape(bf16[1024,2048]{1,0:T(8,128)(2,1)} %convolution_convert_fusion.1) | data formatting | bytes 8388608 | tf_op jit(solution)/shard_map/reshape | solution.py:247
  237.8 8.2 %pad_maximum_fusion = bf16[8,640,1024]{2,1,0:T(8,128)(2,1)} fusion(bf16[8,256,1024]{2,1,0:T(8,128)(2,1)} %bitcast.289, bf16[8,256,1024]{2,1,0:T(8,128)(2,1)} %reshape.437, bf16[8,128,1024]{2,1,0:T(8,128)(2,1)} %bitcast.280), kind=kLoop, calls=%fused_computation.32 | loop fusion | flops 31457280 | bytes 20971520 | tf_op jit(solution)/shard_map/concatenate | solution.py:248
  246.9 35.6 %while.28 = (s32[]{:T(128)}, f32[1024,256]{0,1:T(8,128)S(1)}, f32[1024,256]{0,1:T(8,128)S(1)}, bf16[2,512,256]{2,1,0:T(8,128)(2,1)}, s32[2]{0:T(128)S(1)}, /*ind...) while((s32[]{:T(128)}, f32[1024,256]{0,1:T(8,128)S(1)}, ...), condition=%wide.region_16.17_spmd.clone, body=%wide.region_14.16_spmd.clone.sunk | while | flops 1376253952 | bytes 78974200 | solution.py:155
  252.0 2.4 fusion.201
  254.5 4.2 multiply_reduce_fusion.16
  269.8 2.4 fusion.201
  272.3 4.2 multiply_reduce_fusion.16
  283.7 2.7 copy.166
  286.4 4.2 all-to-all-start.3
  295.8 2.4 collective-permute-start.15
  300.4 26.8 %all-to-all-done.3 = bf16[3,1024,256]{2,0,1:T(4,128)(2,1)S(1)} async-done(((bf16[3,1024,256]{2,0,1:T(4,128)(2,1)}), bf16[3,1024,256]{2,0,1:T(4,128)(2,1)S(1)}, u32[]{:S(2)}, u32[]{:S(2)}) %all-to-all-start.3) | async-done | bytes 1572896 | tf_op jit(solution)/shard_map/all_to_all | solution.py:409
  329.8 2.5 copy.168
  340.8 2.5 fusion.45
  343.4 2.9 constant_dynamic-update-slice_fusion.3
  351.1 3.2 fusion.82
  363.7 2.5 fusion.52
  367.8 3.1 pad_maximum_fusion.1
  371.5 3.1 collective-permute-done.7
  378.7 12.5 %collective-permute-done.8 = bf16[640,512]{1,0:T(8,128)(2,1)S(1)} collective-permute-done((bf16[640,512]{1,0:T(8,128)(2,1)S(1)}, bf16[640,512]{1,0:T(8,128)(2,1)S(1)}, u32[]{:S(2)}, u32[]{:S(2)}) %collective-permute-start.8) | collective-permute-done | bytes 655392 | tf_op jit(solution)/shard_map/ppermute | solution.py:200
  391.6 2.9 collective-permute-start.9
  395.8 10.0 %collective-permute-done.9 = bf16[640,256]{1,0:T(8,128)(2,1)S(1)} collective-permute-done((bf16[640,256]{1,0:T(8,128)(2,1)S(1)}, bf16[640,256]{1,0:T(8,128)(2,1)S(1)}, u32[]{:S(2)}, u32[]{:S(2)}) %collective-permute-start.9) | collective-permute-done | bytes 327712 | tf_op jit(solution)/shard_map/ppermute | solution.py:200
  406.0 15.9 %collective-permute-done.10 = bf16[640,256]{1,0:T(8,128)(2,1)S(1)} collective-permute-done((bf16[640,256]{1,0:T(8,128)(2,1)S(1)}, bf16[640,256]{1,0:T(8,128)(2,1)S(1)}, u32[]{:S(2)}, u32[]{:S(2)}) %collective-permute-start.10) | collective-permute-done | bytes 327712 | tf_op jit(solution)/shard_map/ppermute | solution.py:207
  423.3 3.1 collective-permute-start.18
  426.4 16.1 %collective-permute-done.11 = bf16[640,512]{1,0:T(8,128)(2,1)S(1)} collective-permute-done((bf16[640,512]{1,0:T(8,128)(2,1)S(1)}, bf16[640,512]{1,0:T(8,128)(2,1)S(1)}, u32[]{:S(2)}, u32[]{:S(2)}) %collective-permute-start.11) | collective-permute-done | bytes 655392 | tf_op jit(solution)/shard_map/ppermute | solution.py:207
  445.5 5.0 convolution_bitcast_fusion
  461.2 6.2 %collective-permute-start.34 = (f32[2]{0:T(128)S(1)}, f32[2]{0:T(128)S(1)}, u32[]{:S(2)}, u32[]{:S(2)}) collective-permute-start(f32[2]{0:T(128)S(1)} %pad_maximum_fusion.27), channel_id=1, source_target_pairs={{0,1},{1,0},{2,3},{3,2},{4,5},{5,4},{6,7},{7,6},{8,9},{9,8},{10,11... | collective-permute-start | bytes 32 | tf_op jit(solution)/shard_map/ppermute | solution.py:166
  471.1 2.7 multiply_reduce_fusion.10
  475.4 4.4 multiply_reduce_fusion.8
  479.8 2.4 pad_maximum_fusion.24
  483.3 4.1 multiply_reduce_fusion.6
  489.8 10.9 %multiply_reduce_fusion.2 = (f32[]{:T(128)}, f32[]{:T(128)}, f32[256,6144]{1,0:T(8,128)S(1)}, f32[256,6144]{1,0:T(8,128)}) fusion(f32[256,6144]{1,0:T(8,128)S(1)} %bitcast.265, f32[256,6144]{1,0:T(8,128)S(1)} %bitcast.275, f32[256,6144]{1,0:T(8,128)} %param.45, f32[256,6144]{1,0:T(8,128)} %param.46), kind=kLoop, calls=%fused_computation.41 | loop fusion | flops 26738688 | bytes 37748744 | tf_op jit(solution)/shard_map/reduce_sum | solution.py:277
  523.0 7.2 %multiply_subtract_fusion = f32[256,6144]{1,0:T(8,128)} fusion(f32[256,6144]{1,0:T(8,128)S(1)} %bitcast.265, f32[]{:T(128)} %bitcast.68, f32[256,6144]{1,0:T(8,128)} %get-tuple-element.293, f32[256,6144]{1,0:T(8,128)S(1)} %get-tuple-element.292), kind=kLoop, calls=%fused_computation.37 | loop fusion | flops 12582912 | bytes 25165828 | tf_op jit(solution)/shard_map/sub | solution.py:284
  542.9 5.1 collective-permute-done.20
  549.5 6.4 %collective-permute-done.21 = bf16[3,128,256]{2,1,0:T(8,128)(2,1)S(1)} collective-permute-done((bf16[3,128,256]{2,1,0:T(8,128)(2,1)S(1)}, bf16[3,128,256]{2,1,0:T(8,128)(2,1)S(1)}, u32[]{:S(2)}, u32[]{:S(2)}) %collective-permute-start.21) | collective-permute-done | bytes 196640 | tf_op jit(solution)/shard_map/ppermute | solution.py:207
  556.0 2.5 collective-permute-start.22
  569.9 5.6 multiply_reduce_fusion.4
  582.9 3.3 multiply_subtract_fusion.1
  (481 shorter events, 198.1 us)
Async XLA Ops:
  7.2 53.4 %all-gather.4.cloned.1.call-start = ((), (), s32[]{:S(2)}) async-start(), calls=%async_computation.6 | async-start | bytes 7077888 | tf_op jit(solution)/shard_map/all_gather | solution.py:188
  9.7 170.9 %all-gather.6.cloned.1.call-start = ((), (), s32[]{:S(2)}) async-start(), calls=%async_computation.9 | async-start | bytes 11796480 | tf_op jit(solution)/shard_map/all_gather | solution.py:234
  14.9 8.7 %collective-permute-start.2 = (bf16[1,1536]{1,0:T(2,128)(2,1)S(1)}, bf16[1,1536]{1,0:T(2,128)(2,1)S(1)}, u32[]{:S(2)}, u32[]{:S(2)}) collective-permute-start(bf16[1,1536]{1,0:T(2,128)(2,1)S(1)} %broadcast_in_dim.158), channel_id=1, source_target_pairs={{0,1},{1,0},{2,3},{3,2},{4,5},{5,4},{6,7},{7,6},{8,9},{9,8},{10,11... | collective-permute-start | bytes 9224 | tf_op jit(solution)/shard_map/ppermute | solution.py:175
  21.7 7.1 %collective-permute-start = (f32[3,6144]{1,0:T(4,128)S(1)}, f32[3,6144]{1,0:T(4,128)S(1)}, u32[]{:S(2)}, u32[]{:S(2)}) collective-permute-start(f32[3,6144]{1,0:T(4,128)S(1)} %fusion.38), channel_id=1, source_target_pairs={{0,1},{1,0},{2,3},{3,2},{4,5},{5,4},{6,7},{7,6},{8,9},{9,8},{10,11... | collective-permute-start | bytes 221192 | tf_op jit(solution)/shard_map/ppermute | solution.py:166
  22.3 15.0 %copy-start.65 = (f32[256]{0:T(256)}, f32[256]{0:T(256)S(1)}, u32[]{:S(2)}) copy-start(f32[256]{0:T(256)S(1)} %broadcast_multiply_fusion.2) | copy-start | bytes 3076
  22.4 14.9 %copy-start.77 = (pred[1024,3]{0,1:T(4,128)(4,1)}, pred[1024,3]{0,1:T(4,128)(4,1)S(1)}, u32[]{:S(2)}) copy-start(pred[1024,3]{0,1:T(4,128)(4,1)S(1)} %fusion.76) | copy-start | bytes 9220
  23.2 55.7 %copy-start.53 = (f32[256,32]{0,1:T(8,128)}, f32[256,32]{0,1:T(8,128)S(1)}, u32[]{:S(2)}) copy-start(f32[256,32]{0,1:T(8,128)S(1)} %get-tuple-element.392) | copy-start | bytes 98308
  23.6 3.9 collective-permute-start.3
  25.3 12.0 %copy-start.73 = (f32[256]{0:T(256)}, f32[256]{0:T(256)S(1)}, u32[]{:S(2)}) copy-start(f32[256]{0:T(256)S(1)} %fusion.83) | copy-start | bytes 3076
  28.9 5.7 collective-permute-start.1
  40.4 41.7 %copy-start.21 = (bf16[256,1024]{1,0:T(8,128)(2,1)}, bf16[256,1024]{1,0:T(8,128)(2,1)S(1)}, u32[]{:S(2)}) copy-start(bf16[256,1024]{1,0:T(8,128)(2,1)S(1)} %fusion.56) | copy-start | bytes 1572868
  87.2 51.0 %all-to-all-start = ((bf16[3,256,1024]{1,0,2:T(4,128)(2,1)}), bf16[3,256,1024]{1,0,2:T(4,128)(2,1)S(1)}, u32[]{:S(2)}, u32[]{:S(2)}) async-start(bf16[3,256,1024]{1,0,2:T(4,128)(2,1)} %copy.155), calls=%async_computation | async-start | bytes 4194304 | tf_op jit(solution)/shard_map/all_to_all | solution.py:357
  167.7 10.8 %all-to-all-start.1 = ((bf16[4,256,256]{2,1,0:T(8,128)(2,1)}), bf16[4,256,256]{2,1,0:T(8,128)(2,1)}, u32[]{:S(2)}, u32[]{:S(2)}) async-start(bf16[4,256,256]{2,1,0:T(8,128)(2,1)} %bitcast.24), calls=%async_computation.1 | async-start | bytes 1048576 | tf_op jit(solution)/shard_map/all_to_all | solution.py:363
  226.2 19.9 %all-to-all-start.2 = ((bf16[256,4,256]{2,0,1:T(8,128)(2,1)}), bf16[256,4,256]{2,0,1:T(8,128)(2,1)}, u32[]{:S(2)}, u32[]{:S(2)}) async-start(bf16[256,4,256]{2,0,1:T(8,128)(2,1)} %bitcast.206), calls=%async_computation.2 | async-start | bytes 1048576 | tf_op jit(solution)/shard_map/all_to_all | solution.py:398
  230.3 145.0 %reduce-scatter.5.cloned.1.call-start = ((), (), s32[]{:S(2)}) async-start(), calls=%async_computation.8 | async-start | bytes 11796480 | tf_op jit(solution)/shard_map/reduce_scatter | solution.py:249
  286.4 40.8 %all-to-all-start.3 = ((bf16[3,1024,256]{2,0,1:T(4,128)(2,1)}), bf16[3,1024,256]{2,0,1:T(4,128)(2,1)S(1)}, u32[]{:S(2)}, u32[]{:S(2)}) async-start(bf16[3,1024,256]{2,0,1:T(4,128)(2,1)} %copy.166), calls=%async_computation.3 | async-start | bytes 4194304 | tf_op jit(solution)/shard_map/all_to_all | solution.py:409
  290.6 167.9 %reduce-scatter.3.cloned.1.call-start = ((), (), s32[]{:S(2)}) async-start(), calls=%async_computation.7 | async-start | bytes 7077888 | tf_op jit(solution)/shard_map/reduce_scatter | solution.py:485
  290.8 1.2 collective-permute-start.13
  292.1 3.7 collective-permute-start.14
  295.8 4.6 collective-permute-start.15
  351.1 12.6 %slice-start = ((s8[6291456]{0:T(1024)(128)(4,1)}), s8[4194304]{0:T(1024)(128)(4,1)S(1)}, s32[]{:S(2)}) async-start(s8[6291456]{0:T(1024)(128)(4,1)} %bitcast.262), calls=%async_computation.10 | async-start | bytes 8388608
  354.3 4.7 collective-permute-start.4
  359.0 4.7 collective-permute-start.5
  366.3 4.6 collective-permute-start.6
  370.9 3.7 collective-permute-start.7
  371.5 7.2 %collective-permute-start.16 = (f32[1,3,6144]{2,1,0:T(4,128)S(1)}, f32[1,3,6144]{2,1,0:T(4,128)S(1)}, u32[]{:S(2)}, u32[]{:S(2)}) collective-permute-start(f32[1,3,6144]{2,1,0:T(4,128)S(1)} %add_bitcast_fusion), channel_id=1, source_target_pairs={{0,4},{4,0},{8,12},{12,8},{16,20},{20,16},{24,28},{28,24},{1,5},{5... | collective-permute-start | bytes 221192 | tf_op jit(solution)/shard_map/ppermute | solution.py:175
  377.3 13.9 %collective-permute-start.8 = (bf16[640,512]{1,0:T(8,128)(2,1)S(1)}, bf16[640,512]{1,0:T(8,128)(2,1)S(1)}, u32[]{:S(2)}, u32[]{:S(2)}) collective-permute-start(bf16[640,512]{1,0:T(8,128)(2,1)S(1)} %select_convert_fusion), channel_id=1, source_target_pairs={{0,8},{8,0},{16,24},{24,16},{1,9},{9,1},{17,25},{25,17},{2,10},{10... | collective-permute-start | bytes 1966088 | tf_op jit(solution)/shard_map/ppermute | solution.py:200
  391.6 14.1 %collective-permute-start.9 = (bf16[640,256]{1,0:T(8,128)(2,1)S(1)}, bf16[640,256]{1,0:T(8,128)(2,1)S(1)}, u32[]{:S(2)}, u32[]{:S(2)}) collective-permute-start(bf16[640,256]{1,0:T(8,128)(2,1)S(1)} %select_convert_fusion.2), channel_id=1, source_target_pairs={{0,16},{8,24},{16,0},{24,8},{1,17},{9,25},{17,1},{25,9},{2,18},{10... | collective-permute-start | bytes 983048 | tf_op jit(solution)/shard_map/ppermute | solution.py:200
  394.5 11.4 %collective-permute-start.17 = (f32[2,3,6144]{2,1,0:T(4,128)S(1)}, f32[2,3,6144]{2,1,0:T(4,128)S(1)}, u32[]{:S(2)}, u32[]{:S(2)}) collective-permute-start(f32[2,3,6144]{2,1,0:T(4,128)S(1)} %pad_maximum_fusion.16), channel_id=1, source_target_pairs={{0,8},{4,12},{8,0},{12,4},{16,24},{20,28},{24,16},{28,20},{1,9},{5... | collective-permute-start | bytes 442376 | tf_op jit(solution)/shard_map/ppermute | solution.py:175
  405.9 16.1 %collective-permute-start.10 = (bf16[640,256]{1,0:T(8,128)(2,1)S(1)}, bf16[640,256]{1,0:T(8,128)(2,1)S(1)}, u32[]{:S(2)}, u32[]{:S(2)}) collective-permute-start(bf16[640,256]{1,0:T(8,128)(2,1)S(1)} %add_convert_fusion.1), channel_id=1, source_target_pairs={{0,16},{8,24},{16,0},{24,8},{1,17},{9,25},{17,1},{25,9},{2,18},{10... | collective-permute-start | bytes 983048 | tf_op jit(solution)/shard_map/ppermute | solution.py:207
  422.1 20.5 %collective-permute-start.11 = (bf16[640,512]{1,0:T(8,128)(2,1)S(1)}, bf16[640,512]{1,0:T(8,128)(2,1)S(1)}, u32[]{:S(2)}, u32[]{:S(2)}) collective-permute-start(bf16[640,512]{1,0:T(8,128)(2,1)S(1)} %pad_maximum_fusion.10), channel_id=1, source_target_pairs={{0,8},{8,0},{16,24},{24,16},{1,9},{9,1},{17,25},{25,17},{2,10},{10... | collective-permute-start | bytes 1966088 | tf_op jit(solution)/shard_map/ppermute | solution.py:207
  423.3 19.7 %collective-permute-start.18 = (f32[4,3,6144]{2,1,0:T(4,128)S(1)}, f32[4,3,6144]{2,1,0:T(4,128)S(1)}, u32[]{:S(2)}, u32[]{:S(2)}) collective-permute-start(f32[4,3,6144]{2,1,0:T(4,128)S(1)} %pad_maximum_fusion.14), channel_id=1, source_target_pairs={{0,16},{4,20},{8,24},{12,28},{16,0},{20,4},{24,8},{28,12},{1,17},{... | collective-permute-start | bytes 884744 | tf_op jit(solution)/shard_map/ppermute | solution.py:175
  443.0 7.5 %collective-permute-start.12 = (bf16[640,1024]{1,0:T(8,128)(2,1)S(1)}, bf16[640,1024]{1,0:T(8,128)(2,1)}, u32[]{:S(2)}, u32[]{:S(2)}) collective-permute-start(bf16[640,1024]{1,0:T(8,128)(2,1)S(1)} %pad_maximum_fusion.5), channel_id=1, source_target_pairs={{0,4},{4,0},{1,5},{5,1},{2,6},{6,2},{3,7},{7,3},{8,12},{12,8},{9,1... | collective-permute-start | bytes 3932168 | tf_op jit(solution)/shard_map/ppermute | solution.py:251
  445.5 13.0 %copy-start.62 = (f32[1536]{0:T(1024)}, f32[1536]{0:T(1024)S(1)}, u32[]{:S(2)}) copy-start(f32[1536]{0:T(1024)S(1)} %dynamic-slice_reduce_fusion) | copy-start | bytes 18436
  457.5 13.6 %copy-start.23 = (f32[256,1024]{1,0:T(8,128)S(1)}, f32[256,1024]{1,0:T(8,128)}, u32[]{:S(2)}) copy-start(f32[256,1024]{1,0:T(8,128)} %param.35) | copy-start | bytes 3145732
  458.5 12.6 %copy-start.51 = (f32[256,1024]{1,0:T(8,128)S(1)}, f32[256,1024]{1,0:T(8,128)}, u32[]{:S(2)}) copy-start(f32[256,1024]{1,0:T(8,128)} %param.36) | copy-start | bytes 3145732
  458.6 12.5 %copy-start.52 = (f32[256,1024]{1,0:T(8,128)S(1)}, f32[256,1024]{1,0:T(8,128)}, u32[]{:S(2)}) copy-start(f32[256,1024]{1,0:T(8,128)} %param.37) | copy-start | bytes 3145732
  459.9 104.7 %copy-start.63 = (f32[1536]{0:T(1024)}, f32[1536]{0:T(1024)S(1)}, u32[]{:S(2)}) copy-start(f32[1536]{0:T(1024)S(1)} %get-tuple-element.290) | copy-start | bytes 18436
  461.2 40.9 %collective-permute-start.34 = (f32[2]{0:T(128)S(1)}, f32[2]{0:T(128)S(1)}, u32[]{:S(2)}, u32[]{:S(2)}) collective-permute-start(f32[2]{0:T(128)S(1)} %pad_maximum_fusion.27), channel_id=1, source_target_pairs={{0,1},{1,0},{2,3},{3,2},{4,5},{5,4},{6,7},{7,6},{8,9},{9,8},{10,11... | collective-permute-start | bytes 32 | tf_op jit(solution)/shard_map/ppermute | solution.py:166
  470.0 65.3 %collective-permute-start.19 = (bf16[3,128,512]{2,1,0:T(8,128)(2,1)}, bf16[3,128,512]{2,1,0:T(8,128)(2,1)}, u32[]{:S(2)}, u32[]{:S(2)}) collective-permute-start(bf16[3,128,512]{2,1,0:T(8,128)(2,1)} %select_convert_fusion.1), channel_id=1, source_target_pairs={{0,8},{8,0},{16,24},{24,16},{1,9},{9,1},{17,25},{25,17},{2,10},{10... | collective-permute-start | bytes 1179656 | tf_op jit(solution)/shard_map/ppermute | solution.py:200
  471.1 18.7 %slice-start.6 = ((s8[6291456]{0:T(1024)(128)(4,1)}), s8[4194304]{0:T(1024)(128)(4,1)S(1)}, s32[]{:S(2)}) async-start(s8[6291456]{0:T(1024)(128)(4,1)} %bitcast.274), calls=%async_computation.16 | async-start | bytes 8388608
  475.3 14.4 %slice-start.7 = ((s8[6291456]{0:T(1024)(128)(4,1)}), s8[2097152]{0:T(1024)(128)(4,1)S(1)}, s32[]{:S(2)}) async-start(s8[6291456]{0:T(1024)(128)(4,1)} %bitcast.274), calls=%async_computation.17 | async-start | bytes 4194304
  475.3 29.1 %collective-permute-start.26 = (f32[1,2]{1,0:T(1,128)S(1)}, f32[1,2]{1,0:T(1,128)S(1)}, u32[]{:S(2)}, u32[]{:S(2)}) collective-permute-start(f32[1,2]{1,0:T(1,128)S(1)} %pad_maximum_fusion.23), channel_id=1, source_target_pairs={{0,1},{1,0},{2,3},{3,2},{4,5},{5,4},{6,7},{7,6},{8,9},{9,8},{10,11... | collective-permute-start | bytes 32 | tf_op jit(solution)/shard_map/ppermute | solution.py:166
  482.3 25.0 %collective-permute-start.28 = (f32[1,2]{1,0:T(1,128)S(1)}, f32[1,2]{1,0:T(1,128)S(1)}, u32[]{:S(2)}, u32[]{:S(2)}) collective-permute-start(f32[1,2]{1,0:T(1,128)S(1)} %pad_maximum_fusion.24), channel_id=1, source_target_pairs={{0,1},{1,0},{2,3},{3,2},{4,5},{5,4},{6,7},{7,6},{8,9},{9,8},{10,11... | collective-permute-start | bytes 32 | tf_op jit(solution)/shard_map/ppermute | solution.py:166
  488.7 20.5 %collective-permute-start.30 = (f32[1,2]{1,0:T(1,128)S(1)}, f32[1,2]{1,0:T(1,128)S(1)}, u32[]{:S(2)}, u32[]{:S(2)}) collective-permute-start(f32[1,2]{1,0:T(1,128)S(1)} %pad_maximum_fusion.25), channel_id=1, source_target_pairs={{0,1},{1,0},{2,3},{3,2},{4,5},{5,4},{6,7},{7,6},{8,9},{9,8},{10,11... | collective-permute-start | bytes 32 | tf_op jit(solution)/shard_map/ppermute | solution.py:166
  500.7 29.5 %copy-start.1 = (f32[256,6144]{1,0:T(8,128)}, f32[256,6144]{1,0:T(8,128)S(1)}, u32[]{:S(2)}) copy-start(f32[256,6144]{1,0:T(8,128)S(1)} %get-tuple-element.292) | copy-start | bytes 18874372
  502.1 13.6 %copy-start.80 = (f32[2]{0:T(128)}, f32[2]{0:T(128)S(1)}, u32[]{:S(2)}) copy-start(f32[2]{0:T(128)S(1)} %collective-permute-done.34) | copy-start | bytes 28
  502.1 10.0 %collective-permute-start.32 = (f32[1,2]{1,0:T(1,128)S(1)}, f32[1,2]{1,0:T(1,128)S(1)}, u32[]{:S(2)}, u32[]{:S(2)}) collective-permute-start(f32[1,2]{1,0:T(1,128)S(1)} %pad_maximum_fusion.26), channel_id=1, source_target_pairs={{0,1},{1,0},{2,3},{3,2},{4,5},{5,4},{6,7},{7,6},{8,9},{9,8},{10,11... | collective-permute-start | bytes 32 | tf_op jit(solution)/shard_map/ppermute | solution.py:166
  504.4 25.7 %collective-permute-start.35 = (f32[2]{0:T(128)S(1)}, f32[2]{0:T(128)S(1)}, u32[]{:S(2)}, u32[]{:S(2)}) collective-permute-start(f32[2]{0:T(128)S(1)} %fusion.156), channel_id=1, source_target_pairs={{0,2},{1,3},{2,0},{3,1},{4,6},{5,7},{6,4},{7,5},{8,10},{9,11},{10,... | collective-permute-start | bytes 32 | tf_op jit(solution)/shard_map/ppermute | solution.py:166
  507.3 24.2 %collective-permute-start.27 = (f32[1,2]{1,0:T(1,128)S(1)}, f32[1,2]{1,0:T(1,128)S(1)}, u32[]{:S(2)}, u32[]{:S(2)}) collective-permute-start(f32[1,2]{1,0:T(1,128)S(1)} %fusion.160), channel_id=1, source_target_pairs={{0,2},{1,3},{2,0},{3,1},{4,6},{5,7},{6,4},{7,5},{8,10},{9,11},{10,... | collective-permute-start | bytes 32 | tf_op jit(solution)/shard_map/ppermute | solution.py:166
  509.2 38.9 %collective-permute-start.29 = (f32[1,2]{1,0:T(1,128)S(1)}, f32[1,2]{1,0:T(1,128)S(1)}, u32[]{:S(2)}, u32[]{:S(2)}) collective-permute-start(f32[1,2]{1,0:T(1,128)S(1)} %fusion.159), channel_id=1, source_target_pairs={{0,2},{1,3},{2,0},{3,1},{4,6},{5,7},{6,4},{7,5},{8,10},{9,11},{10,... | collective-permute-start | bytes 32 | tf_op jit(solution)/shard_map/ppermute | solution.py:166
  512.1 3.6 collective-permute-start.31
  515.7 3.9 collective-permute-start.33
  535.3 25.2 %copy-start.24 = (f32[256,1024]{1,0:T(8,128)S(1)}, f32[256,1024]{1,0:T(8,128)}, u32[]{:S(2)}) copy-start(f32[256,1024]{1,0:T(8,128)} %param.35) | copy-start | bytes 3145732
  535.3 25.2 %copy-start.29 = (f32[256,1024]{1,0:T(8,128)S(1)}, f32[256,1024]{1,0:T(8,128)}, u32[]{:S(2)}) copy-start(f32[256,1024]{1,0:T(8,128)} %get-tuple-element.300) | copy-start | bytes 3145732
  535.3 25.2 %copy-start.30 = (f32[256,1024]{1,0:T(8,128)S(1)}, f32[256,1024]{1,0:T(8,128)}, u32[]{:S(2)}) copy-start(f32[256,1024]{1,0:T(8,128)} %get-tuple-element.301) | copy-start | bytes 3145732
  536.7 11.3 %collective-permute-start.20 = (bf16[3,128,256]{2,1,0:T(8,128)(2,1)S(1)}, bf16[3,128,256]{2,1,0:T(8,128)(2,1)S(1)}, u32[]{:S(2)}, u32[]{:S(2)}) collective-permute-start(bf16[3,128,256]{2,1,0:T(8,128)(2,1)S(1)} %select_convert_fusion.3), channel_id=1, source_target_pairs={{0,16},{8,24},{16,0},{24,8},{1,17},{9,25},{17,1},{25,9},{2,18},{10... | collective-permute-start | bytes 589832 | tf_op jit(solution)/shard_map/ppermute | solution.py:200
  548.1 7.8 %collective-permute-start.21 = (bf16[3,128,256]{2,1,0:T(8,128)(2,1)S(1)}, bf16[3,128,256]{2,1,0:T(8,128)(2,1)S(1)}, u32[]{:S(2)}, u32[]{:S(2)}) collective-permute-start(bf16[3,128,256]{2,1,0:T(8,128)(2,1)S(1)} %add_convert_fusion.4), channel_id=1, source_target_pairs={{0,16},{8,24},{16,0},{24,8},{1,17},{9,25},{17,1},{25,9},{2,18},{10... | collective-permute-start | bytes 589832 | tf_op jit(solution)/shard_map/ppermute | solution.py:207
  556.0 8.3 %collective-permute-start.22 = (bf16[3,128,512]{2,1,0:T(8,128)(2,1)S(1)}, bf16[3,128,512]{2,1,0:T(8,128)(2,1)S(1)}, u32[]{:S(2)}, u32[]{:S(2)}) collective-permute-start(bf16[3,128,512]{2,1,0:T(8,128)(2,1)S(1)} %pad_maximum_fusion.15), channel_id=1, source_target_pairs={{0,8},{8,0},{16,24},{24,16},{1,9},{9,1},{17,25},{25,17},{2,10},{10... | collective-permute-start | bytes 1179656 | tf_op jit(solution)/shard_map/ppermute | solution.py:207
  564.5 3.2 collective-permute-start.23
  575.6 10.6 %copy-start.8 = (f32[3,256,1024]{2,1,0:T(8,128)}, f32[3,256,1024]{2,1,0:T(8,128)S(1)}, u32[]{:S(2)}) copy-start(f32[3,256,1024]{2,1,0:T(8,128)S(1)} %get-tuple-element.303) | copy-start | bytes 9437188
  575.6 10.7 %copy-start.9 = (f32[3,256,1024]{2,1,0:T(8,128)}, f32[3,256,1024]{2,1,0:T(8,128)S(1)}, u32[]{:S(2)}) copy-start(f32[3,256,1024]{2,1,0:T(8,128)S(1)} %get-tuple-element.304) | copy-start | bytes 9437188
  575.6 3.6 collective-permute-start.24
  579.2 3.6 collective-permute-start.25
  (72 other events, 312.2 us)
Sparse Core Ops, SparseCore 0:
  10.5 50.1 all-gather.3
  63.1 83.8 all-gather.5
  246.2 105.7 reduce-scatter.4
  371.0 61.6 reduce-scatter.2

commit v8 on v6

--- a/solution.py
+++ b/solution.py
@@ -471,19 +471,18 @@
         list(doubling_gather(grad_silu_part, "seq", seq_count, seq_rank)), axis=1
     )
     time_grad = jax.vjp(jax.nn.silu, time_emb)[1](grad_silu)[0]
-    grad_out, grad_up, grad_down = [
-        share.astype(jnp.float32)
-        for share in reduce_batch(
-            [
-                grad_out_local.astype(jnp.bfloat16),
-                grad_up_local.astype(jnp.bfloat16),
-                grad_down_local.astype(jnp.bfloat16),
-            ]
-        )
-    ]
-    qkv_piece = lax.psum_scatter(
-        grad_qkv_local.astype(jnp.bfloat16), ("seq", "core"), scatter_dimension=1, tiled=True
-    )
+    batch_shares = reduce_batch(
+        [
+            grad_out_local.astype(jnp.bfloat16),
+            grad_up_local.astype(jnp.bfloat16),
+            grad_down_local.astype(jnp.bfloat16),
+        ]
+    )
+    qkv_partial, batch_shares, grad_mod_share, grad_bias_share = lax.optimization_barrier(
+        (grad_qkv_local.astype(jnp.bfloat16), batch_shares, grad_mod_share, grad_bias_share)
+    )
+    grad_out, grad_up, grad_down = [share.astype(jnp.float32) for share in batch_shares]
+    qkv_piece = lax.psum_scatter(qkv_partial, ("seq", "core"), scatter_dimension=1, tiled=True)
     updated = [
         lamb_update(w_out, mom_out, var_out, grad_out, None, seq_count),
         lamb_update(w_up, mom_up, var_up, grad_up, None, seq_count),
@@ -491,7 +490,6 @@
         lamb_update(w_mod, mom_mod, var_mod, grad_mod_share, None, seq_count),
         lamb_update(b_mod, mom_bias, var_bias, grad_bias_share, None, seq_count),
     ]
-    qkv_piece, updated = lax.optimization_barrier((qkv_piece, updated))
     qkv_piece = halving_sum(qkv_piece, "z", lax.axis_size("z"))
     qkv_other = lax.ppermute(qkv_piece, "core", [(0, 1), (1, 0)])
     qkv_first = lax.axis_index("core") == 0

time: 577 us -> 585 us (1.014)
  other arithmetic: 99.2 us -> 123 us
  matrix products: 99.7 us -> 88.1 us
    ppermute x10, waiting for transfers between devices: 27.5 us -> 7.7 us  [doubling_gather(): other = lax.ppermute(blocks, axes, [(i, i ^ step) for i in range(size)])]
    ppermute x4, waiting for transfers between devices: 34.4 us -> 53.8 us  [halving_sum(): lax.ppermute(blocks, axis_name, [(i, i ^ step) for i in range(size)])]
    reduce_sum x5 -> x6, other arithmetic: 19.5 us -> 32.9 us  [lamb_update(): jnp.sum(weight * weight, axis=sum_axes, keepdims=True)]
    dot_general x1, matrix products: 16 us -> 4.96 us  [local(): jnp.einsum('cd,ce->de', silu_all.astype(jnp.float32), grad_mod_all, preci...]
  transfers between devices with their start and end apart: 48 -> 48, of which waited for: 27 -> 26; matrix products, arithmetic and copies ran while one was open for 40% -> 41% of each run, Pallas kernels for 0% -> 0%
where the time goes in v8:
time: 585 us; the launch traced here: 575 us
  waiting for transfers between devices  181 us (31%)
  other arithmetic  123 us (21%)
  local copies, waits for them, and re-layouts  88.6 us (15%)
  matrix products  88.1 us (15%)
  starting transfers between devices  68.9 us (12%)
  between operations  22.7 us (4%)
    ppermute x4, waiting for transfers between devices, halving_sum(): lax.ppermute(blocks, axis_name, [(i, i ^ step) for i in range(size)])  53.8 us
    reduce_sum x6, other arithmetic, lamb_update(): jnp.sum(weight * weight, axis=sum_axes, keepdims=True)  32.9 us
    ppermute x4, waiting for transfers between devices, halving_sum(): lax.ppermute(send, axis_name, [(i, i ^ step) for i in range(size)])  29.5 us
    all_gather x1, waiting for transfers between devices, gather_rows(): return lax.all_gather(piece, ('seq', 'core'), axis=row_axis, tiled=True)  20.3 us
    sub x6, other arithmetic, lamb_update(): return (weight - step_rate * ratio * direction, moment_new, second_new)  19.5 us
    ppermute x16, starting transfers between devices, butterfly_sum(): lax.ppermute(values, axes, [(i, i ^ step) for i in range(size)])  16.5 us
    ppermute x10, starting transfers between devices, doubling_gather(): other = lax.ppermute(blocks, axes, [(i, i ^ step) for i in range(size)])  14.5 us
    add x14, other arithmetic, butterfly_sum(): values + lax.ppermute(values, axes, [(i, i ^ step) for i in range(size)])  13.9 us
  transfers between devices with their start and end apart: 48, of which 26 were waited for; matrix products, arithmetic and copies ran while one was open for 41% of the time, Pallas kernels for 0%

profile of v8, /device:TPU:0, one launch (start us, length us, event | category | flops | bytes accessed | tf_op | source)
XLA Modules:
  0.0 575.3 jit_solution(9246313062346657966)
XLA Ops:
  14.9 3.0 collective-permute-start.2
  18.0 3.7 fusion.38
  30.4 4.2 collective-permute-done.1
  34.6 2.7 fusion.68
  37.3 2.7 copy-done
  40.4 20.3 %all-gather.4.cloned.1.call-done = bf16[3,1024,1024]{2,1,0:T(8,128)(2,1)} async-done(((bf16[3,128,1024]{2,1,0:T(8,128)(2,1)}), bf16[3,1024,1024]{2,1,0:T(8,128)(2,1)}) %all-gather.4.cloned.1.call-update) | async-done | bytes 6291472 | tf_op jit(solution)/shard_map/all_gather | solution.py:188
  60.7 4.7 slice_bitcast_fusion.3
  65.3 2.9 copy.145
  70.4 3.0 copy.141
  81.0 3.5 all-to-all-start
  86.0 8.1 %all-to-all-done = bf16[256,4,256]{0,2,1:T(8,128)(2,1)S(1)} async-done(((bf16[256,4,256]{0,2,1:T(8,128)(2,1)}), bf16[256,4,256]{0,2,1:T(8,128)(2,1)S(1)}, u32[]{:S(2)}, u32[]{:S(2)}) %all-to-all-start) | async-done | bytes 524320 | tf_op jit(solution)/shard_map/all_to_all | solution.py:358
  94.1 3.5 all-to-all-start.1
  97.6 2.9 fusion.48
  101.4 10.8 %all-to-all-done.1 = bf16[256,4,256]{0,2,1:T(8,128)(2,1)S(1)} async-done(((bf16[256,4,256]{0,2,1:T(8,128)(2,1)}), bf16[256,4,256]{0,2,1:T(8,128)(2,1)S(1)}, u32[]{:S(2)}, u32[]{:S(2)}) %all-to-all-start.1) | async-done | bytes 524320 | tf_op jit(solution)/shard_map/all_to_all | solution.py:359
  112.1 3.9 all-to-all-start.2
  118.8 11.6 %all-to-all-done.2 = bf16[256,4,256]{2,0,1:T(8,128)(2,1)S(1)} async-done(((bf16[256,4,256]{2,0,1:T(8,128)(2,1)}), bf16[256,4,256]{2,0,1:T(8,128)(2,1)S(1)}, u32[]{:S(2)}, u32[]{:S(2)}) %all-to-all-start.2) | async-done | bytes 524320 | tf_op jit(solution)/shard_map/all_to_all | solution.py:360
  132.3 20.0 %while.27 = (s32[]{:T(128)}, bf16[2,512,256]{2,1,0:T(8,128)(2,1)}, f32[2,4,512,1]{2,1,3,0:T(4,128)S(1)}, s32[2]{0:T(128)S(1)}, s32[1024]{0:T(1024)S(1)}, /*index...) while((s32[]{:T(128)}, bf16[2,512,256]{2,1,0:T(8,128)(2,1)}, ...), condition=%wide.region_9.10_spmd, body=%wide.region_6.9_spmd.sunk | while | flops 561117184 | bytes 30485712 | solution.py:110
  138.1 3.3 fusion.186
  148.1 3.3 fusion.186
  152.3 4.1 all-to-all-start.3
  158.2 5.1 all-to-all-done.3
  165.4 3.1 slice.178
  168.5 6.0 %fusion.103 = (bf16[8,256,1024]{2,1,0:T(8,128)(2,1)}, bf16[8,256,1024]{2,1,0:T(8,128)(2,1)}) fusion(bf16[8,640,1024]{2,1,0:T(8,128)(2,1)} %bitcast.267), kind=kLoop, calls=%fused_computation.298 | loop fusion | bytes 16777216 | tf_op jit(solution)/shard_map/slice | solution.py:239
  174.5 7.2 %reshape.438 = bf16[1024,2048]{1,0:T(8,128)(2,1)} reshape(bf16[8,256,1024]{2,1,0:T(8,128)(2,1)} %get-tuple-element.345) | data formatting | bytes 8388608 | tf_op jit(solution)/shard_map/reshape | solution.py:239
  181.7 3.9 fusion.102
  190.2 3.9 convolution_convert_fusion
  198.0 2.8 fusion.101
  205.6 3.3 convolution_convert_fusion.1
  209.8 4.2 all-to-all-start.4
  214.0 7.5 %reshape.441 = bf16[8,256,1024]{2,1,0:T(8,128)(2,1)} reshape(bf16[1024,2048]{1,0:T(8,128)(2,1)} %convolution_convert_fusion.1) | data formatting | bytes 8388608 | tf_op jit(solution)/shard_map/reshape | solution.py:247
  221.5 8.2 %pad_maximum_fusion = bf16[8,640,1024]{2,1,0:T(8,128)(2,1)} fusion(bf16[8,256,1024]{2,1,0:T(8,128)(2,1)} %bitcast.276, bf16[8,256,1024]{2,1,0:T(8,128)(2,1)} %reshape.441, bf16[8,128,1024]{2,1,0:T(8,128)(2,1)} %bitcast.268), kind=kLoop, calls=%fused_computation.32 | loop fusion | flops 31457280 | bytes 20971520 | tf_op jit(solution)/shard_map/concatenate | solution.py:248
  230.5 35.6 %while.28 = (s32[]{:T(128)}, f32[1024,256]{0,1:T(8,128)S(1)}, f32[1024,256]{0,1:T(8,128)S(1)}, bf16[2,512,256]{2,1,0:T(8,128)(2,1)}, s32[2]{0:T(128)S(1)}, /*ind...) while((s32[]{:T(128)}, f32[1024,256]{0,1:T(8,128)S(1)}, ...), condition=%wide.region_16.17_spmd.clone, body=%wide.region_14.16_spmd.clone.sunk | while | flops 1376253952 | bytes 78974200 | solution.py:155
  238.1 4.2 multiply_reduce_fusion.16
  255.9 4.2 multiply_reduce_fusion.16
  266.1 4.1 all-to-all-start.5
  277.3 6.6 %all-to-all-done.5 = bf16[4,256,256]{2,1,0:T(8,128)(2,1)S(1)} async-done(((bf16[4,256,256]{2,1,0:T(8,128)(2,1)}), bf16[4,256,256]{2,1,0:T(8,128)(2,1)S(1)}, u32[]{:S(2)}, u32[]{:S(2)}) %all-to-all-start.5) | async-done | bytes 524320 | tf_op jit(solution)/shard_map/all_to_all | solution.py:412
  283.9 3.5 all-to-all-start.6
  289.5 10.1 %all-to-all-done.6 = bf16[4,256,256]{1,2,0:T(8,128)(2,1)S(1)} async-done(((bf16[4,256,256]{1,2,0:T(8,128)(2,1)}), bf16[4,256,256]{1,2,0:T(8,128)(2,1)S(1)}, u32[]{:S(2)}, u32[]{:S(2)}) %all-to-all-start.6) | async-done | bytes 524320 | tf_op jit(solution)/shard_map/all_to_all | solution.py:413
  299.6 4.2 all-to-all-start.7
  310.1 3.8 all-to-all-done.7
  320.1 2.9 constant_dynamic-update-slice_fusion.3
  327.8 2.9 fusion.81
  336.9 3.2 pad_maximum_fusion.1
  340.1 5.3 fusion.51
  354.4 12.3 %collective-permute-done.8 = bf16[640,512]{1,0:T(8,128)(2,1)S(1)} collective-permute-done((bf16[640,512]{1,0:T(8,128)(2,1)S(1)}, bf16[640,512]{1,0:T(8,128)(2,1)S(1)}, u32[]{:S(2)}, u32[]{:S(2)}) %collective-permute-start.8) | collective-permute-done | bytes 655392 | tf_op jit(solution)/shard_map/ppermute | solution.py:200
  367.2 3.0 collective-permute-start.9
  371.4 9.7 %collective-permute-done.9 = bf16[640,256]{1,0:T(8,128)(2,1)S(1)} collective-permute-done((bf16[640,256]{1,0:T(8,128)(2,1)S(1)}, bf16[640,256]{1,0:T(8,128)(2,1)S(1)}, u32[]{:S(2)}, u32[]{:S(2)}) %collective-permute-start.9) | collective-permute-done | bytes 327712 | tf_op jit(solution)/shard_map/ppermute | solution.py:200
  381.5 15.9 %collective-permute-done.10 = bf16[640,256]{1,0:T(8,128)(2,1)S(1)} collective-permute-done((bf16[640,256]{1,0:T(8,128)(2,1)S(1)}, bf16[640,256]{1,0:T(8,128)(2,1)S(1)}, u32[]{:S(2)}, u32[]{:S(2)}) %collective-permute-start.10) | collective-permute-done | bytes 327712 | tf_op jit(solution)/shard_map/ppermute | solution.py:207
  399.5 22.2 %collective-permute-done.11 = bf16[640,512]{1,0:T(8,128)(2,1)S(1)} collective-permute-done((bf16[640,512]{1,0:T(8,128)(2,1)S(1)}, bf16[640,512]{1,0:T(8,128)(2,1)S(1)}, u32[]{:S(2)}, u32[]{:S(2)}) %collective-permute-start.11) | collective-permute-done | bytes 655392 | tf_op jit(solution)/shard_map/ppermute | solution.py:207
  424.7 5.0 convolution_bitcast_fusion
  441.1 4.1 multiply_reduce_fusion.10
  447.9 6.9 %multiply_reduce_fusion.8 = (f32[]{:T(128)}, f32[]{:T(128)}, f32[256,2048]{1,0:T(8,128)}, f32[256,2048]{1,0:T(8,128)}, f32[256,2048]{1,0:T(8,128)}) fusion(f32[256,2048]{1,0:T(8,128)S(1)} %copy-done.12, f32[256,2048]{1,0:T(8,128)S(1)} %copy-done.39, f32[256,2048]{1,0:T(8,128)} %param.40, bf16[256,2048]{1,0:T(8,128)(2,1)S(1)} %copy-done.34), kind=kLoop, calls=%fused_computation.82 | loop fusion | flops 9437182 | bytes 13631496 | tf_op jit(solution)/shard_map/reduce_sum | solution.py:277
  457.5 4.2 multiply_reduce_fusion.6
  464.2 10.8 %multiply_reduce_fusion.2 = (f32[]{:T(128)}, f32[]{:T(128)}, f32[256,6144]{1,0:T(8,128)S(1)}, f32[256,6144]{1,0:T(8,128)}) fusion(f32[256,6144]{1,0:T(8,128)S(1)} %bitcast.255, f32[256,6144]{1,0:T(8,128)S(1)} %bitcast.265, f32[256,6144]{1,0:T(8,128)} %param.45, f32[256,6144]{1,0:T(8,128)} %param.46), kind=kLoop, calls=%fused_computation.41 | loop fusion | flops 26738688 | bytes 37748744 | tf_op jit(solution)/shard_map/reduce_sum | solution.py:277
  499.3 7.0 %multiply_subtract_fusion = f32[256,6144]{1,0:T(8,128)} fusion(f32[256,6144]{1,0:T(8,128)S(1)} %bitcast.255, f32[]{:T(128)} %bitcast.70, f32[256,6144]{1,0:T(8,128)} %get-tuple-element.320, f32[256,6144]{1,0:T(8,128)S(1)} %get-tuple-element.319), kind=kLoop, calls=%fused_computation.37 | loop fusion | flops 12582912 | bytes 25165828 | tf_op jit(solution)/shard_map/sub | solution.py:284
  508.4 4.6 multiply_subtract_fusion.2
  513.0 3.8 collective-permute-done.19
  522.0 3.7 collective-permute-done.20
  527.2 8.6 %collective-permute-done.21 = bf16[3,128,256]{2,1,0:T(8,128)(2,1)S(1)} collective-permute-done((bf16[3,128,256]{2,1,0:T(8,128)(2,1)S(1)}, bf16[3,128,256]{2,1,0:T(8,128)(2,1)S(1)}, u32[]{:S(2)}, u32[]{:S(2)}) %collective-permute-start.21) | collective-permute-done | bytes 196640 | tf_op jit(solution)/shard_map/ppermute | solution.py:207
  539.6 7.0 %collective-permute-done.22 = bf16[3,128,512]{2,1,0:T(8,128)(2,1)S(1)} collective-permute-done((bf16[3,128,512]{2,1,0:T(8,128)(2,1)S(1)}, bf16[3,128,512]{2,1,0:T(8,128)(2,1)S(1)}, u32[]{:S(2)}, u32[]{:S(2)}) %collective-permute-start.22) | collective-permute-done | bytes 393248 | tf_op jit(solution)/shard_map/ppermute | solution.py:207
  552.3 5.6 multiply_reduce_fusion.4
  558.0 3.6 collective-permute-done.24
  561.6 3.6 collective-permute-done.25
  565.2 3.3 multiply_subtract_fusion.1
  (451 shorter events, 192.4 us)
Async XLA Ops:
  7.2 53.5 %all-gather.4.cloned.1.call-start = ((), (), s32[]{:S(2)}) async-start(), calls=%async_computation.10 | async-start | bytes 7077888 | tf_op jit(solution)/shard_map/all_gather | solution.py:188
  9.7 155.7 %all-gather.6.cloned.1.call-start = ((), (), s32[]{:S(2)}) async-start(), calls=%async_computation.13 | async-start | bytes 11796480 | tf_op jit(solution)/shard_map/all_gather | solution.py:234
  14.9 8.6 %collective-permute-start.2 = (bf16[1,1536]{1,0:T(2,128)(2,1)S(1)}, bf16[1,1536]{1,0:T(2,128)(2,1)S(1)}, u32[]{:S(2)}, u32[]{:S(2)}) collective-permute-start(bf16[1,1536]{1,0:T(2,128)(2,1)S(1)} %broadcast_in_dim.158), channel_id=1, source_target_pairs={{0,1},{1,0},{2,3},{3,2},{4,5},{5,4},{6,7},{7,6},{8,9},{9,8},{10,11... | collective-permute-start | bytes 9224 | tf_op jit(solution)/shard_map/ppermute | solution.py:175
  21.7 7.1 %collective-permute-start = (f32[3,6144]{1,0:T(4,128)S(1)}, f32[3,6144]{1,0:T(4,128)S(1)}, u32[]{:S(2)}, u32[]{:S(2)}) collective-permute-start(f32[3,6144]{1,0:T(4,128)S(1)} %fusion.38), channel_id=1, source_target_pairs={{0,1},{1,0},{2,3},{3,2},{4,5},{5,4},{6,7},{7,6},{8,9},{9,8},{10,11... | collective-permute-start | bytes 221192 | tf_op jit(solution)/shard_map/ppermute | solution.py:166
  22.3 15.0 %copy-start.56 = (f32[256]{0:T(256)}, f32[256]{0:T(256)S(1)}, u32[]{:S(2)}) copy-start(f32[256]{0:T(256)S(1)} %broadcast_multiply_fusion.2) | copy-start | bytes 3076
  22.4 14.9 %copy-start.66 = (pred[1024,3]{0,1:T(4,128)(4,1)}, pred[1024,3]{0,1:T(4,128)(4,1)S(1)}, u32[]{:S(2)}) copy-start(pred[1024,3]{0,1:T(4,128)(4,1)S(1)} %fusion.75) | copy-start | bytes 9220
  23.2 55.7 %copy-start.44 = (f32[256,32]{0,1:T(8,128)}, f32[256,32]{0,1:T(8,128)S(1)}, u32[]{:S(2)}) copy-start(f32[256,32]{0,1:T(8,128)S(1)} %get-tuple-element.413) | copy-start | bytes 98308
  23.6 3.9 collective-permute-start.3
  28.9 5.7 collective-permute-start.1
  40.4 57.2 %copy-start.17 = (bf16[256,1024]{1,0:T(8,128)(2,1)}, bf16[256,1024]{1,0:T(8,128)(2,1)S(1)}, u32[]{:S(2)}) copy-start(bf16[256,1024]{1,0:T(8,128)(2,1)S(1)} %fusion.55) | copy-start | bytes 1572868
  81.0 13.1 %all-to-all-start = ((bf16[256,4,256]{0,2,1:T(8,128)(2,1)}), bf16[256,4,256]{0,2,1:T(8,128)(2,1)S(1)}, u32[]{:S(2)}, u32[]{:S(2)}) async-start(bf16[256,4,256]{0,2,1:T(8,128)(2,1)} %convert_element_type.226), calls=%async_computation | async-start | bytes 1048576 | tf_op jit(solution)/shard_map/all_to_all | solution.py:358
  94.1 18.0 %all-to-all-start.1 = ((bf16[256,4,256]{0,2,1:T(8,128)(2,1)}), bf16[256,4,256]{0,2,1:T(8,128)(2,1)S(1)}, u32[]{:S(2)}, u32[]{:S(2)}) async-start(bf16[256,4,256]{0,2,1:T(8,128)(2,1)} %convert_element_type.227), calls=%async_computation.1 | async-start | bytes 1048576 | tf_op jit(solution)/shard_map/all_to_all | solution.py:359
  112.1 18.3 %all-to-all-start.2 = ((bf16[256,4,256]{2,0,1:T(8,128)(2,1)}), bf16[256,4,256]{2,0,1:T(8,128)(2,1)S(1)}, u32[]{:S(2)}, u32[]{:S(2)}) async-start(bf16[256,4,256]{2,0,1:T(8,128)(2,1)} %bitcast.198), calls=%async_computation.2 | async-start | bytes 1048576 | tf_op jit(solution)/shard_map/all_to_all | solution.py:360
  152.3 11.1 %all-to-all-start.3 = ((bf16[4,256,256]{2,1,0:T(8,128)(2,1)}), bf16[4,256,256]{2,1,0:T(8,128)(2,1)}, u32[]{:S(2)}, u32[]{:S(2)}) async-start(bf16[4,256,256]{2,1,0:T(8,128)(2,1)} %bitcast.26), calls=%async_computation.3 | async-start | bytes 1048576 | tf_op jit(solution)/shard_map/all_to_all | solution.py:365
  156.4 1.2 collective-permute-start.13
  185.6 12.4 %copy-start.5 = (f32[256,1024]{1,0:T(8,128)}, f32[256,1024]{1,0:T(8,128)S(1)}, u32[]{:S(2)}) copy-start(f32[256,1024]{1,0:T(8,128)S(1)} %get-tuple-element.338) | copy-start | bytes 3145732
  185.6 12.4 %copy-start.58 = (f32[256]{0:T(256)}, f32[256]{0:T(256)S(1)}, u32[]{:S(2)}) copy-start(f32[256]{0:T(256)S(1)} %broadcast_multiply_fusion.1) | copy-start | bytes 3076
  185.9 12.1 %copy-start.60 = (f32[256]{0:T(256)}, f32[256]{0:T(256)S(1)}, u32[]{:S(2)}) copy-start(f32[256]{0:T(256)S(1)} %fusion.83) | copy-start | bytes 3076
  209.8 19.9 %all-to-all-start.4 = ((bf16[256,4,256]{2,0,1:T(8,128)(2,1)}), bf16[256,4,256]{2,0,1:T(8,128)(2,1)}, u32[]{:S(2)}, u32[]{:S(2)}) async-start(bf16[256,4,256]{2,0,1:T(8,128)(2,1)} %bitcast.197), calls=%async_computation.4 | async-start | bytes 1048576 | tf_op jit(solution)/shard_map/all_to_all | solution.py:400
  213.9 137.1 %reduce-scatter.3.cloned.1.call-start = ((), (), s32[]{:S(2)}) async-start(), calls=%async_computation.11 | async-start | bytes 11796480 | tf_op jit(solution)/shard_map/reduce_scatter | solution.py:249
  230.5 39.7 %copy-start.54 = (bf16[1,3,256]{2,0,1:T(2,128)(2,1)S(1)}, bf16[1,3,256]{2,0,1:T(2,128)(2,1)}, u32[]{:S(2)}) copy-start(bf16[1,3,256]{2,0,1:T(2,128)(2,1)} %get-tuple-element.409) | copy-start | bytes 4612
  230.5 39.7 %copy-start.55 = (bf16[1,3,256]{2,0,1:T(2,128)(2,1)S(1)}, bf16[1,3,256]{2,0,1:T(2,128)(2,1)}, u32[]{:S(2)}) copy-start(bf16[1,3,256]{2,0,1:T(2,128)(2,1)} %get-tuple-element.410) | copy-start | bytes 4612
  266.1 17.8 %all-to-all-start.5 = ((bf16[4,256,256]{2,1,0:T(8,128)(2,1)}), bf16[4,256,256]{2,1,0:T(8,128)(2,1)S(1)}, u32[]{:S(2)}, u32[]{:S(2)}) async-start(bf16[4,256,256]{2,1,0:T(8,128)(2,1)} %bitcast.283), calls=%async_computation.5 | async-start | bytes 1048576 | tf_op jit(solution)/shard_map/all_to_all | solution.py:412
  270.2 3.7 collective-permute-start.14
  274.0 13.5 %collective-permute-start.15 = (bf16[4,3,256]{2,0,1:T(4,128)(2,1)S(1)}, bf16[4,3,256]{2,0,1:T(4,128)(2,1)S(1)}, u32[]{:S(2)}, u32[]{:S(2)}) collective-permute-start(bf16[4,3,256]{2,0,1:T(4,128)(2,1)S(1)} %pad_maximum_fusion.18), channel_id=1, source_target_pairs={{0,16},{4,20},{8,24},{12,28},{16,0},{20,4},{24,8},{28,12},{1,17},{... | collective-permute-start | bytes 18440 | tf_op jit(solution)/shard_map/ppermute | solution.py:175
  283.9 15.7 %all-to-all-start.6 = ((bf16[4,256,256]{1,2,0:T(8,128)(2,1)}), bf16[4,256,256]{1,2,0:T(8,128)(2,1)S(1)}, u32[]{:S(2)}, u32[]{:S(2)}) async-start(bf16[4,256,256]{1,2,0:T(8,128)(2,1)} %bitcast.196), calls=%async_computation.6 | async-start | bytes 1048576 | tf_op jit(solution)/shard_map/all_to_all | solution.py:413
  299.6 14.3 %all-to-all-start.7 = ((bf16[4,256,256]{2,1,0:T(8,128)(2,1)}), bf16[4,256,256]{2,1,0:T(8,128)(2,1)}, u32[]{:S(2)}, u32[]{:S(2)}) async-start(bf16[4,256,256]{2,1,0:T(8,128)(2,1)} %bitcast.38), calls=%async_computation.7 | async-start | bytes 1048576 | tf_op jit(solution)/shard_map/all_to_all | solution.py:414
  303.8 202.4 %reduce-scatter.5.cloned.1.call-start = ((), (), s32[]{:S(2)}) async-start(), calls=%async_computation.12 | async-start | bytes 7077888 | tf_op jit(solution)/shard_map/reduce_scatter | solution.py:485
  330.7 4.7 collective-permute-start.4
  335.4 4.8 collective-permute-start.5
  345.4 3.6 collective-permute-start.6
  346.7 7.7 %collective-permute-start.16 = (f32[1,3,6144]{2,1,0:T(4,128)S(1)}, f32[1,3,6144]{2,1,0:T(4,128)S(1)}, u32[]{:S(2)}, u32[]{:S(2)}) collective-permute-start(f32[1,3,6144]{2,1,0:T(4,128)S(1)} %add_bitcast_fusion), channel_id=1, source_target_pairs={{0,4},{4,0},{8,12},{12,8},{16,20},{20,16},{24,28},{28,24},{1,5},{5... | collective-permute-start | bytes 221192 | tf_op jit(solution)/shard_map/ppermute | solution.py:175
  349.7 84.7 %collective-permute-start.7 = (f32[2,3,256]{2,1,0:T(4,128)}, f32[2,3,256]{2,1,0:T(4,128)}, u32[]{:S(2)}, u32[]{:S(2)}) collective-permute-start(f32[2,3,256]{2,1,0:T(4,128)} %pad_maximum_fusion.16), channel_id=1, source_target_pairs={{0,2},{1,3},{2,0},{3,1},{4,6},{5,7},{6,4},{7,5},{8,10},{9,11},{10,... | collective-permute-start | bytes 18440 | tf_op jit(solution)/shard_map/ppermute | solution.py:175
  352.8 13.9 %collective-permute-start.8 = (bf16[640,512]{1,0:T(8,128)(2,1)S(1)}, bf16[640,512]{1,0:T(8,128)(2,1)S(1)}, u32[]{:S(2)}, u32[]{:S(2)}) collective-permute-start(bf16[640,512]{1,0:T(8,128)(2,1)S(1)} %select_convert_fusion), channel_id=1, source_target_pairs={{0,8},{8,0},{16,24},{24,16},{1,9},{9,1},{17,25},{25,17},{2,10},{10... | collective-permute-start | bytes 1966088 | tf_op jit(solution)/shard_map/ppermute | solution.py:200
  367.2 14.0 %collective-permute-start.9 = (bf16[640,256]{1,0:T(8,128)(2,1)S(1)}, bf16[640,256]{1,0:T(8,128)(2,1)S(1)}, u32[]{:S(2)}, u32[]{:S(2)}) collective-permute-start(bf16[640,256]{1,0:T(8,128)(2,1)S(1)} %select_convert_fusion.2), channel_id=1, source_target_pairs={{0,16},{8,24},{16,0},{24,8},{1,17},{9,25},{17,1},{25,9},{2,18},{10... | collective-permute-start | bytes 983048 | tf_op jit(solution)/shard_map/ppermute | solution.py:200
  370.3 11.1 %collective-permute-start.17 = (f32[2,3,6144]{2,1,0:T(4,128)S(1)}, f32[2,3,6144]{2,1,0:T(4,128)S(1)}, u32[]{:S(2)}, u32[]{:S(2)}) collective-permute-start(f32[2,3,6144]{2,1,0:T(4,128)S(1)} %pad_maximum_fusion.14), channel_id=1, source_target_pairs={{0,8},{4,12},{8,0},{12,4},{16,24},{20,28},{24,16},{28,20},{1,9},{5... | collective-permute-start | bytes 442376 | tf_op jit(solution)/shard_map/ppermute | solution.py:175
  381.3 16.1 %collective-permute-start.10 = (bf16[640,256]{1,0:T(8,128)(2,1)S(1)}, bf16[640,256]{1,0:T(8,128)(2,1)S(1)}, u32[]{:S(2)}, u32[]{:S(2)}) collective-permute-start(bf16[640,256]{1,0:T(8,128)(2,1)S(1)} %add_convert_fusion.1), channel_id=1, source_target_pairs={{0,16},{8,24},{16,0},{24,8},{1,17},{9,25},{17,1},{25,9},{2,18},{10... | collective-permute-start | bytes 983048 | tf_op jit(solution)/shard_map/ppermute | solution.py:207
  397.5 24.2 %collective-permute-start.11 = (bf16[640,512]{1,0:T(8,128)(2,1)S(1)}, bf16[640,512]{1,0:T(8,128)(2,1)S(1)}, u32[]{:S(2)}, u32[]{:S(2)}) collective-permute-start(bf16[640,512]{1,0:T(8,128)(2,1)S(1)} %pad_maximum_fusion.8), channel_id=1, source_target_pairs={{0,8},{8,0},{16,24},{24,16},{1,9},{9,1},{17,25},{25,17},{2,10},{10... | collective-permute-start | bytes 1966088 | tf_op jit(solution)/shard_map/ppermute | solution.py:207
  397.7 24.5 %collective-permute-start.18 = (f32[4,3,6144]{2,1,0:T(4,128)S(1)}, f32[4,3,6144]{2,1,0:T(4,128)S(1)}, u32[]{:S(2)}, u32[]{:S(2)}) collective-permute-start(f32[4,3,6144]{2,1,0:T(4,128)S(1)} %pad_maximum_fusion.12), channel_id=1, source_target_pairs={{0,16},{4,20},{8,24},{12,28},{16,0},{20,4},{24,8},{28,12},{1,17},{... | collective-permute-start | bytes 884744 | tf_op jit(solution)/shard_map/ppermute | solution.py:175
  422.1 7.5 %collective-permute-start.12 = (bf16[640,1024]{1,0:T(8,128)(2,1)S(1)}, bf16[640,1024]{1,0:T(8,128)(2,1)}, u32[]{:S(2)}, u32[]{:S(2)}) collective-permute-start(bf16[640,1024]{1,0:T(8,128)(2,1)S(1)} %pad_maximum_fusion.3), channel_id=1, source_target_pairs={{0,4},{4,0},{1,5},{5,1},{2,6},{6,2},{3,7},{7,3},{8,12},{12,8},{9,1... | collective-permute-start | bytes 3932168 | tf_op jit(solution)/shard_map/ppermute | solution.py:251
  437.2 109.7 %copy-start.52 = (f32[1536]{0:T(1024)}, f32[1536]{0:T(1024)S(1)}, u32[]{:S(2)}) copy-start(f32[1536]{0:T(1024)S(1)} %get-tuple-element.317) | copy-start | bytes 18436
  438.6 38.7 %collective-permute-start.34 = (f32[2]{0:T(128)S(1)}, f32[2]{0:T(128)S(1)}, u32[]{:S(2)}, u32[]{:S(2)}) collective-permute-start(f32[2]{0:T(128)S(1)} %pad_maximum_fusion.25), channel_id=1, source_target_pairs={{0,1},{1,0},{2,3},{3,2},{4,5},{5,4},{6,7},{7,6},{8,9},{9,8},{10,11... | collective-permute-start | bytes 32 | tf_op jit(solution)/shard_map/ppermute | solution.py:166
  441.1 23.2 %slice-start.4 = ((s8[6291456]{0:T(1024)(128)(4,1)}), s8[4194304]{0:T(1024)(128)(4,1)S(1)}, s32[]{:S(2)}) async-start(s8[6291456]{0:T(1024)(128)(4,1)} %bitcast.264), calls=%async_computation.18 | async-start | bytes 8388608
  446.6 17.6 %slice-start.5 = ((s8[6291456]{0:T(1024)(128)(4,1)}), s8[2097152]{0:T(1024)(128)(4,1)S(1)}, s32[]{:S(2)}) async-start(s8[6291456]{0:T(1024)(128)(4,1)} %bitcast.264), calls=%async_computation.19 | async-start | bytes 4194304
  446.6 33.3 %collective-permute-start.26 = (f32[1,2]{1,0:T(1,128)S(1)}, f32[1,2]{1,0:T(1,128)S(1)}, u32[]{:S(2)}, u32[]{:S(2)}) collective-permute-start(f32[1,2]{1,0:T(1,128)S(1)} %pad_maximum_fusion.21), channel_id=1, source_target_pairs={{0,1},{1,0},{2,3},{3,2},{4,5},{5,4},{6,7},{7,6},{8,9},{9,8},{10,11... | collective-permute-start | bytes 32 | tf_op jit(solution)/shard_map/ppermute | solution.py:166
  456.5 25.6 %collective-permute-start.28 = (f32[1,2]{1,0:T(1,128)S(1)}, f32[1,2]{1,0:T(1,128)S(1)}, u32[]{:S(2)}, u32[]{:S(2)}) collective-permute-start(f32[1,2]{1,0:T(1,128)S(1)} %pad_maximum_fusion.22), channel_id=1, source_target_pairs={{0,1},{1,0},{2,3},{3,2},{4,5},{5,4},{6,7},{7,6},{8,9},{9,8},{10,11... | collective-permute-start | bytes 32 | tf_op jit(solution)/shard_map/ppermute | solution.py:166
  463.0 21.7 %collective-permute-start.30 = (f32[1,2]{1,0:T(1,128)S(1)}, f32[1,2]{1,0:T(1,128)S(1)}, u32[]{:S(2)}, u32[]{:S(2)}) collective-permute-start(f32[1,2]{1,0:T(1,128)S(1)} %pad_maximum_fusion.23), channel_id=1, source_target_pairs={{0,1},{1,0},{2,3},{3,2},{4,5},{5,4},{6,7},{7,6},{8,9},{9,8},{10,11... | collective-permute-start | bytes 32 | tf_op jit(solution)/shard_map/ppermute | solution.py:166
  475.0 24.2 %copy-start.1 = (f32[256,6144]{1,0:T(8,128)}, f32[256,6144]{1,0:T(8,128)S(1)}, u32[]{:S(2)}) copy-start(f32[256,6144]{1,0:T(8,128)S(1)} %get-tuple-element.319) | copy-start | bytes 18874372
  476.4 10.5 %collective-permute-start.32 = (f32[1,2]{1,0:T(1,128)S(1)}, f32[1,2]{1,0:T(1,128)S(1)}, u32[]{:S(2)}, u32[]{:S(2)}) collective-permute-start(f32[1,2]{1,0:T(1,128)S(1)} %pad_maximum_fusion.24), channel_id=1, source_target_pairs={{0,1},{1,0},{2,3},{3,2},{4,5},{5,4},{6,7},{7,6},{8,9},{9,8},{10,11... | collective-permute-start | bytes 32 | tf_op jit(solution)/shard_map/ppermute | solution.py:166
  478.7 17.8 %collective-permute-start.35 = (f32[2]{0:T(128)S(1)}, f32[2]{0:T(128)S(1)}, u32[]{:S(2)}, u32[]{:S(2)}) collective-permute-start(f32[2]{0:T(128)S(1)} %fusion.153), channel_id=1, source_target_pairs={{0,2},{1,3},{2,0},{3,1},{4,6},{5,7},{6,4},{7,5},{8,10},{9,11},{10,... | collective-permute-start | bytes 32 | tf_op jit(solution)/shard_map/ppermute | solution.py:166
  481.3 16.6 %collective-permute-start.27 = (f32[1,2]{1,0:T(1,128)S(1)}, f32[1,2]{1,0:T(1,128)S(1)}, u32[]{:S(2)}, u32[]{:S(2)}) collective-permute-start(f32[1,2]{1,0:T(1,128)S(1)} %fusion.157), channel_id=1, source_target_pairs={{0,2},{1,3},{2,0},{3,1},{4,6},{5,7},{6,4},{7,5},{8,10},{9,11},{10,... | collective-permute-start | bytes 32 | tf_op jit(solution)/shard_map/ppermute | solution.py:166
  483.5 42.4 %collective-permute-start.29 = (f32[1,2]{1,0:T(1,128)S(1)}, f32[1,2]{1,0:T(1,128)S(1)}, u32[]{:S(2)}, u32[]{:S(2)}) collective-permute-start(f32[1,2]{1,0:T(1,128)S(1)} %fusion.156), channel_id=1, source_target_pairs={{0,2},{1,3},{2,0},{3,1},{4,6},{5,7},{6,4},{7,5},{8,10},{9,11},{10,... | collective-permute-start | bytes 32 | tf_op jit(solution)/shard_map/ppermute | solution.py:166
  486.1 3.7 collective-permute-start.31
  488.3 4.8 collective-permute-start.33
  507.8 9.0 %collective-permute-start.19 = (bf16[3,128,512]{2,1,0:T(8,128)(2,1)S(1)}, bf16[3,128,512]{2,1,0:T(8,128)(2,1)S(1)}, u32[]{:S(2)}, u32[]{:S(2)}) collective-permute-start(bf16[3,128,512]{2,1,0:T(8,128)(2,1)S(1)} %select_convert_fusion.1), channel_id=1, source_target_pairs={{0,8},{8,0},{16,24},{24,16},{1,9},{9,1},{17,25},{25,17},{2,10},{10... | collective-permute-start | bytes 1179656 | tf_op jit(solution)/shard_map/ppermute | solution.py:200
  513.0 25.0 %copy-start.20 = (f32[256,1024]{1,0:T(8,128)S(1)}, f32[256,1024]{1,0:T(8,128)}, u32[]{:S(2)}) copy-start(f32[256,1024]{1,0:T(8,128)} %param.35) | copy-start | bytes 3145732
  513.0 25.0 %copy-start.25 = (f32[256,1024]{1,0:T(8,128)S(1)}, f32[256,1024]{1,0:T(8,128)}, u32[]{:S(2)}) copy-start(f32[256,1024]{1,0:T(8,128)} %get-tuple-element.327) | copy-start | bytes 3145732
  513.0 25.0 %copy-start.26 = (f32[256,1024]{1,0:T(8,128)S(1)}, f32[256,1024]{1,0:T(8,128)}, u32[]{:S(2)}) copy-start(f32[256,1024]{1,0:T(8,128)} %get-tuple-element.328) | copy-start | bytes 3145732
  517.0 8.7 %collective-permute-start.20 = (bf16[3,128,256]{2,1,0:T(8,128)(2,1)S(1)}, bf16[3,128,256]{2,1,0:T(8,128)(2,1)S(1)}, u32[]{:S(2)}, u32[]{:S(2)}) collective-permute-start(bf16[3,128,256]{2,1,0:T(8,128)(2,1)S(1)} %select_convert_fusion.3), channel_id=1, source_target_pairs={{0,16},{8,24},{16,0},{24,8},{1,17},{9,25},{17,1},{25,9},{2,18},{10... | collective-permute-start | bytes 589832 | tf_op jit(solution)/shard_map/ppermute | solution.py:200
  525.8 10.1 %collective-permute-start.21 = (bf16[3,128,256]{2,1,0:T(8,128)(2,1)S(1)}, bf16[3,128,256]{2,1,0:T(8,128)(2,1)S(1)}, u32[]{:S(2)}, u32[]{:S(2)}) collective-permute-start(bf16[3,128,256]{2,1,0:T(8,128)(2,1)S(1)} %add_convert_fusion.4), channel_id=1, source_target_pairs={{0,16},{8,24},{16,0},{24,8},{1,17},{9,25},{17,1},{25,9},{2,18},{10... | collective-permute-start | bytes 589832 | tf_op jit(solution)/shard_map/ppermute | solution.py:207
  535.9 10.7 %collective-permute-start.22 = (bf16[3,128,512]{2,1,0:T(8,128)(2,1)S(1)}, bf16[3,128,512]{2,1,0:T(8,128)(2,1)S(1)}, u32[]{:S(2)}, u32[]{:S(2)}) collective-permute-start(bf16[3,128,512]{2,1,0:T(8,128)(2,1)S(1)} %pad_maximum_fusion.13), channel_id=1, source_target_pairs={{0,8},{8,0},{16,24},{24,16},{1,9},{9,1},{17,25},{25,17},{2,10},{10... | collective-permute-start | bytes 1179656 | tf_op jit(solution)/shard_map/ppermute | solution.py:207
  546.8 3.2 collective-permute-start.23
  557.9 3.6 collective-permute-start.24
  561.6 3.6 collective-permute-start.25
  (61 other events, 300.6 us)
Sparse Core Ops, SparseCore 0:
  10.5 50.1 all-gather.3
  63.1 77.6 all-gather.5
  229.8 96.2 reduce-scatter.2
  434.5 62.2 reduce-scatter.4

commit v9 on v8

--- a/solution.py
+++ b/solution.py
@@ -247,7 +247,7 @@
     views = [part.reshape(groups, -1, base) for part in partials]
     flat = jnp.concatenate(views, axis=1)
     piece = lax.psum_scatter(flat, ("seq", "core"), scatter_dimension=0, tiled=True)[0]
-    piece = halving_sum(piece, "z", lax.axis_size("z"))
+    piece = lax.psum(piece, "z")
     other = lax.ppermute(piece, "core", [(0, 1), (1, 0)])
     first = lax.axis_index("core") == 0
     low = jnp.where(first, piece, other)

time: 585 us -> 582 us (level)
  other arithmetic: 123 us -> 117 us
    psum x0 -> x1, waiting for transfers between devices: none -> 68.2 us  [reduce_batch(): piece = lax.psum(piece, 'z')]
    ppermute x4 -> x2, waiting for transfers between devices: 53.8 us -> 11.1 us  [halving_sum(): lax.ppermute(blocks, axis_name, [(i, i ^ step) for i in range(size)])]
    ppermute x4 -> x2, waiting for transfers between devices: 29.5 us -> 8.3 us  [halving_sum(): lax.ppermute(send, axis_name, [(i, i ^ step) for i in range(size)])]
  transfers between devices with their start and end apart: 48 -> 45, of which waited for: 26 -> 23; matrix products, arithmetic and copies ran while one was open for 41% -> 40% of each run, Pallas kernels for 0% -> 0%
where the time goes in v9:
time: 582 us; the launch traced here: 571 us
  waiting for transfers between devices  185 us (32%)
  other arithmetic  117 us (20%)
  local copies, waits for them, and re-layouts  87.8 us (15%)
  matrix products  87.5 us (15%)
  starting transfers between devices  67.7 us (12%)
  between operations  22.8 us (4%)
    psum x1, waiting for transfers between devices, reduce_batch(): piece = lax.psum(piece, 'z')  68.2 us
    reduce_sum x6, other arithmetic, lamb_update(): jnp.sum(weight * weight, axis=sum_axes, keepdims=True)  33.2 us
    all_gather x1, waiting for transfers between devices, gather_rows(): return lax.all_gather(piece, ('seq', 'core'), axis=row_axis, tiled=True)  20.3 us
    sub x6, other arithmetic, lamb_update(): return (weight - step_rate * ratio * direction, moment_new, second_new)  19.5 us
    ppermute x16, starting transfers between devices, butterfly_sum(): lax.ppermute(values, axes, [(i, i ^ step) for i in range(size)])  17.2 us
    ppermute x16, waiting for transfers between devices, butterfly_sum(): lax.ppermute(values, axes, [(i, i ^ step) for i in range(size)])  16.1 us
    ppermute x10, starting transfers between devices, doubling_gather(): other = lax.ppermute(blocks, axes, [(i, i ^ step) for i in range(size)])  15.3 us
    add x14, other arithmetic, butterfly_sum(): values + lax.ppermute(values, axes, [(i, i ^ step) for i in range(size)])  13.7 us
  transfers between devices with their start and end apart: 45, of which 23 were waited for; matrix products, arithmetic and copies ran while one was open for 40% of the time, Pallas kernels for 0%

profile of v9, /device:TPU:0, one launch (start us, length us, event | category | flops | bytes accessed | tf_op | source)
XLA Modules:
  0.0 571.5 jit_solution(787295190039095326)
XLA Ops:
  14.9 3.0 collective-permute-start.2
  18.0 3.7 fusion.38
  30.4 4.2 collective-permute-done.1
  34.6 2.7 fusion.68
  37.3 2.7 copy-done
  40.4 20.3 %all-gather.4.cloned.1.call-done = bf16[3,1024,1024]{2,1,0:T(8,128)(2,1)} async-done(((bf16[3,128,1024]{2,1,0:T(8,128)(2,1)}), bf16[3,1024,1024]{2,1,0:T(8,128)(2,1)}) %all-gather.4.cloned.1.call-update) | async-done | bytes 6291472 | tf_op jit(solution)/shard_map/all_gather | solution.py:188
  60.7 4.7 slice_bitcast_fusion.3
  65.3 2.9 copy.145
  70.4 3.0 copy.141
  75.7 2.5 fusion.28
  81.0 3.5 all-to-all-start
  86.0 8.1 %all-to-all-done = bf16[256,4,256]{0,2,1:T(8,128)(2,1)S(1)} async-done(((bf16[256,4,256]{0,2,1:T(8,128)(2,1)}), bf16[256,4,256]{0,2,1:T(8,128)(2,1)S(1)}, u32[]{:S(2)}, u32[]{:S(2)}) %all-to-all-start) | async-done | bytes 524320 | tf_op jit(solution)/shard_map/all_to_all | solution.py:358
  94.1 3.5 all-to-all-start.1
  97.6 2.9 fusion.48
  101.4 10.8 %all-to-all-done.1 = bf16[256,4,256]{0,2,1:T(8,128)(2,1)S(1)} async-done(((bf16[256,4,256]{0,2,1:T(8,128)(2,1)}), bf16[256,4,256]{0,2,1:T(8,128)(2,1)S(1)}, u32[]{:S(2)}, u32[]{:S(2)}) %all-to-all-start.1) | async-done | bytes 524320 | tf_op jit(solution)/shard_map/all_to_all | solution.py:359
  112.2 3.7 all-to-all-start.2
  118.5 11.6 %all-to-all-done.2 = bf16[256,4,256]{2,0,1:T(8,128)(2,1)S(1)} async-done(((bf16[256,4,256]{2,0,1:T(8,128)(2,1)}), bf16[256,4,256]{2,0,1:T(8,128)(2,1)S(1)}, u32[]{:S(2)}, u32[]{:S(2)}) %all-to-all-start.2) | async-done | bytes 524320 | tf_op jit(solution)/shard_map/all_to_all | solution.py:360
  132.0 20.0 %while.27 = (s32[]{:T(128)}, bf16[2,512,256]{2,1,0:T(8,128)(2,1)}, f32[2,4,512,1]{2,1,3,0:T(4,128)S(1)}, s32[2]{0:T(128)S(1)}, s32[1024]{0:T(1024)S(1)}, /*index...) while((s32[]{:T(128)}, bf16[2,512,256]{2,1,0:T(8,128)(2,1)}, ...), condition=%wide.region_9.10_spmd, body=%wide.region_6.9_spmd.sunk | while | flops 561117184 | bytes 30485712 | solution.py:110
  137.8 3.3 fusion.186
  147.8 3.3 fusion.186
  152.0 4.1 all-to-all-start.3
  158.0 5.1 all-to-all-done.3
  165.2 3.1 slice.158
  168.2 6.0 %fusion.103 = (bf16[8,256,1024]{2,1,0:T(8,128)(2,1)}, bf16[8,256,1024]{2,1,0:T(8,128)(2,1)}) fusion(bf16[8,640,1024]{2,1,0:T(8,128)(2,1)} %bitcast.265), kind=kLoop, calls=%fused_computation.287 | loop fusion | bytes 16777216 | tf_op jit(solution)/shard_map/slice | solution.py:239
  174.3 7.5 %reshape.436 = bf16[1024,2048]{1,0:T(8,128)(2,1)} reshape(bf16[8,256,1024]{2,1,0:T(8,128)(2,1)} %get-tuple-element.345) | data formatting | bytes 8388608 | tf_op jit(solution)/shard_map/reshape | solution.py:239
  181.7 3.9 fusion.102
  190.1 3.9 convolution_convert_fusion
  198.0 2.8 fusion.101
  205.6 3.3 convolution_convert_fusion.1
  209.8 4.1 all-to-all-start.4
  214.0 7.3 %reshape.439 = bf16[8,256,1024]{2,1,0:T(8,128)(2,1)} reshape(bf16[1024,2048]{1,0:T(8,128)(2,1)} %convolution_convert_fusion.1) | data formatting | bytes 8388608 | tf_op jit(solution)/shard_map/reshape | solution.py:247
  221.2 8.2 %pad_maximum_fusion = bf16[8,640,1024]{2,1,0:T(8,128)(2,1)} fusion(bf16[8,256,1024]{2,1,0:T(8,128)(2,1)} %bitcast.274, bf16[8,256,1024]{2,1,0:T(8,128)(2,1)} %reshape.439, bf16[8,128,1024]{2,1,0:T(8,128)(2,1)} %bitcast.266), kind=kLoop, calls=%fused_computation.32 | loop fusion | flops 31457280 | bytes 20971520 | tf_op jit(solution)/shard_map/concatenate | solution.py:248
  230.3 35.6 %while.28 = (s32[]{:T(128)}, f32[1024,256]{0,1:T(8,128)S(1)}, f32[1024,256]{0,1:T(8,128)S(1)}, bf16[2,512,256]{2,1,0:T(8,128)(2,1)}, s32[2]{0:T(128)S(1)}, /*ind...) while((s32[]{:T(128)}, f32[1024,256]{0,1:T(8,128)S(1)}, ...), condition=%wide.region_16.17_spmd.clone, body=%wide.region_14.16_spmd.clone.sunk | while | flops 1376253952 | bytes 78974200 | solution.py:155
  237.8 4.2 multiply_reduce_fusion.16
  255.7 4.2 multiply_reduce_fusion.16
  265.9 4.1 all-to-all-start.5
  273.7 2.5 collective-permute-start.11
  277.1 6.6 %all-to-all-done.5 = bf16[4,256,256]{2,1,0:T(8,128)(2,1)S(1)} async-done(((bf16[4,256,256]{2,1,0:T(8,128)(2,1)}), bf16[4,256,256]{2,1,0:T(8,128)(2,1)S(1)}, u32[]{:S(2)}, u32[]{:S(2)}) %all-to-all-start.5) | async-done | bytes 524320 | tf_op jit(solution)/shard_map/all_to_all | solution.py:412
  283.7 3.5 all-to-all-start.6
  289.3 10.1 %all-to-all-done.6 = bf16[4,256,256]{1,2,0:T(8,128)(2,1)S(1)} async-done(((bf16[4,256,256]{1,2,0:T(8,128)(2,1)}), bf16[4,256,256]{1,2,0:T(8,128)(2,1)S(1)}, u32[]{:S(2)}, u32[]{:S(2)}) %all-to-all-start.6) | async-done | bytes 524320 | tf_op jit(solution)/shard_map/all_to_all | solution.py:413
  299.4 4.1 all-to-all-start.7
  310.1 3.5 all-to-all-done.7
  317.3 2.4 fusion.45
  319.8 2.9 constant_dynamic-update-slice_fusion.3
  327.5 2.9 fusion.81
  339.9 3.2 pad_maximum_fusion.1
  344.5 5.3 fusion.51
  351.6 2.5 collective-permute-start.14
  355.7 68.2 %all-reduce.2.cloned.1.call-done = bf16[640,1024]{1,0:T(8,128)(2,1)} async-done(((bf16[640,1024]{1,0:T(8,128)(2,1)}), bf16[640,1024]{1,0:T(8,128)(2,1)}) %all-reduce.2.cloned.1.call-update) | async-done | bytes 1310736 | tf_op jit(solution)/shard_map/psum | solution.py:250
  424.6 4.6 convolution_bitcast_fusion
  437.8 4.7 multiply_reduce_fusion.10
  444.6 6.8 %multiply_reduce_fusion.8 = (f32[]{:T(128)}, f32[]{:T(128)}, f32[256,2048]{1,0:T(8,128)}, f32[256,2048]{1,0:T(8,128)}, f32[256,2048]{1,0:T(8,128)}) fusion(f32[256,2048]{1,0:T(8,128)S(1)} %copy-done.12, f32[256,2048]{1,0:T(8,128)S(1)} %copy-done.39, f32[256,2048]{1,0:T(8,128)} %param.40, bf16[256,2048]{1,0:T(8,128)(2,1)S(1)} %copy-done.34), kind=kLoop, calls=%fused_computation.82 | loop fusion | flops 9437182 | bytes 13631496 | tf_op jit(solution)/shard_map/reduce_sum | solution.py:277
  454.7 4.1 multiply_reduce_fusion.6
  460.8 10.8 %multiply_reduce_fusion.2 = (f32[]{:T(128)}, f32[]{:T(128)}, f32[256,6144]{1,0:T(8,128)S(1)}, f32[256,6144]{1,0:T(8,128)}) fusion(f32[256,6144]{1,0:T(8,128)S(1)} %bitcast.253, f32[256,6144]{1,0:T(8,128)S(1)} %bitcast.263, f32[256,6144]{1,0:T(8,128)} %param.45, f32[256,6144]{1,0:T(8,128)} %param.46), kind=kLoop, calls=%fused_computation.41 | loop fusion | flops 26738688 | bytes 37748744 | tf_op jit(solution)/shard_map/reduce_sum | solution.py:277
  496.8 7.0 %multiply_subtract_fusion = f32[256,6144]{1,0:T(8,128)} fusion(f32[256,6144]{1,0:T(8,128)S(1)} %bitcast.253, f32[]{:T(128)} %bitcast.69, f32[256,6144]{1,0:T(8,128)} %get-tuple-element.320, f32[256,6144]{1,0:T(8,128)S(1)} %get-tuple-element.319), kind=kLoop, calls=%fused_computation.37 | loop fusion | flops 12582912 | bytes 25165828 | tf_op jit(solution)/shard_map/sub | solution.py:284
  506.9 4.6 multiply_subtract_fusion.2
  511.5 2.7 collective-permute-done.15
  520.4 5.6 collective-permute-done.16
  527.6 7.1 %collective-permute-done.17 = bf16[3,128,256]{2,1,0:T(8,128)(2,1)S(1)} collective-permute-done((bf16[3,128,256]{2,1,0:T(8,128)(2,1)S(1)}, bf16[3,128,256]{2,1,0:T(8,128)(2,1)S(1)}, u32[]{:S(2)}, u32[]{:S(2)}) %collective-permute-start.17) | collective-permute-done | bytes 196640 | tf_op jit(solution)/shard_map/ppermute | solution.py:207
  538.6 4.0 collective-permute-done.18
  548.2 5.6 multiply_reduce_fusion.4
  554.6 2.9 collective-permute-done.20
  558.0 3.2 collective-permute-done.21
  561.2 3.3 multiply_subtract_fusion.1
  (439 shorter events, 178.9 us)
Async XLA Ops:
  7.2 53.5 %all-gather.4.cloned.1.call-start = ((), (), s32[]{:S(2)}) async-start(), calls=%async_computation.10 | async-start | bytes 7077888 | tf_op jit(solution)/shard_map/all_gather | solution.py:188
  9.7 155.5 %all-gather.6.cloned.1.call-start = ((), (), s32[]{:S(2)}) async-start(), calls=%async_computation.14 | async-start | bytes 11796480 | tf_op jit(solution)/shard_map/all_gather | solution.py:234
  14.9 8.6 %collective-permute-start.2 = (bf16[1,1536]{1,0:T(2,128)(2,1)S(1)}, bf16[1,1536]{1,0:T(2,128)(2,1)S(1)}, u32[]{:S(2)}, u32[]{:S(2)}) collective-permute-start(bf16[1,1536]{1,0:T(2,128)(2,1)S(1)} %broadcast_in_dim.158), channel_id=1, source_target_pairs={{0,1},{1,0},{2,3},{3,2},{4,5},{5,4},{6,7},{7,6},{8,9},{9,8},{10,11... | collective-permute-start | bytes 9224 | tf_op jit(solution)/shard_map/ppermute | solution.py:175
  21.7 7.1 %collective-permute-start = (f32[3,6144]{1,0:T(4,128)S(1)}, f32[3,6144]{1,0:T(4,128)S(1)}, u32[]{:S(2)}, u32[]{:S(2)}) collective-permute-start(f32[3,6144]{1,0:T(4,128)S(1)} %fusion.38), channel_id=1, source_target_pairs={{0,1},{1,0},{2,3},{3,2},{4,5},{5,4},{6,7},{7,6},{8,9},{9,8},{10,11... | collective-permute-start | bytes 221192 | tf_op jit(solution)/shard_map/ppermute | solution.py:166
  22.3 15.0 %copy-start.57 = (f32[256]{0:T(256)}, f32[256]{0:T(256)S(1)}, u32[]{:S(2)}) copy-start(f32[256]{0:T(256)S(1)} %broadcast_multiply_fusion.2) | copy-start | bytes 3076
  22.4 14.9 %copy-start.67 = (pred[1024,3]{0,1:T(4,128)(4,1)}, pred[1024,3]{0,1:T(4,128)(4,1)S(1)}, u32[]{:S(2)}) copy-start(pred[1024,3]{0,1:T(4,128)(4,1)S(1)} %fusion.75) | copy-start | bytes 9220
  23.2 55.7 %copy-start.45 = (f32[256,32]{0,1:T(8,128)}, f32[256,32]{0,1:T(8,128)S(1)}, u32[]{:S(2)}) copy-start(f32[256,32]{0,1:T(8,128)S(1)} %get-tuple-element.409) | copy-start | bytes 98308
  23.6 3.9 collective-permute-start.3
  25.3 12.0 %copy-start.65 = (f32[256]{0:T(256)}, f32[256]{0:T(256)S(1)}, u32[]{:S(2)}) copy-start(f32[256]{0:T(256)S(1)} %fusion.82) | copy-start | bytes 3076
  28.9 5.7 %collective-permute-start.1 = (f32[3,6144]{1,0:T(4,128)S(1)}, f32[3,6144]{1,0:T(4,128)S(1)}, u32[]{:S(2)}, u32[]{:S(2)}) collective-permute-start(f32[3,6144]{1,0:T(4,128)S(1)} %add.355), channel_id=1, source_target_pairs={{0,2},{1,3},{2,0},{3,1},{4,6},{5,7},{6,4},{7,5},{8,10},{9,11},{10,... | collective-permute-start | bytes 221192 | tf_op jit(solution)/shard_map/ppermute | solution.py:166
  40.4 57.2 %copy-start.17 = (bf16[256,1024]{1,0:T(8,128)(2,1)}, bf16[256,1024]{1,0:T(8,128)(2,1)S(1)}, u32[]{:S(2)}) copy-start(bf16[256,1024]{1,0:T(8,128)(2,1)S(1)} %fusion.55) | copy-start | bytes 1572868
  81.0 13.1 %all-to-all-start = ((bf16[256,4,256]{0,2,1:T(8,128)(2,1)}), bf16[256,4,256]{0,2,1:T(8,128)(2,1)S(1)}, u32[]{:S(2)}, u32[]{:S(2)}) async-start(bf16[256,4,256]{0,2,1:T(8,128)(2,1)} %convert_element_type.205), calls=%async_computation | async-start | bytes 1048576 | tf_op jit(solution)/shard_map/all_to_all | solution.py:358
  94.1 18.0 %all-to-all-start.1 = ((bf16[256,4,256]{0,2,1:T(8,128)(2,1)}), bf16[256,4,256]{0,2,1:T(8,128)(2,1)S(1)}, u32[]{:S(2)}, u32[]{:S(2)}) async-start(bf16[256,4,256]{0,2,1:T(8,128)(2,1)} %convert_element_type.206), calls=%async_computation.1 | async-start | bytes 1048576 | tf_op jit(solution)/shard_map/all_to_all | solution.py:359
  112.2 18.0 %all-to-all-start.2 = ((bf16[256,4,256]{2,0,1:T(8,128)(2,1)}), bf16[256,4,256]{2,0,1:T(8,128)(2,1)S(1)}, u32[]{:S(2)}, u32[]{:S(2)}) async-start(bf16[256,4,256]{2,0,1:T(8,128)(2,1)} %bitcast.196), calls=%async_computation.2 | async-start | bytes 1048576 | tf_op jit(solution)/shard_map/all_to_all | solution.py:360
  152.0 11.1 %all-to-all-start.3 = ((bf16[4,256,256]{2,1,0:T(8,128)(2,1)}), bf16[4,256,256]{2,1,0:T(8,128)(2,1)}, u32[]{:S(2)}, u32[]{:S(2)}) async-start(bf16[4,256,256]{2,1,0:T(8,128)(2,1)} %bitcast.26), calls=%async_computation.3 | async-start | bytes 1048576 | tf_op jit(solution)/shard_map/all_to_all | solution.py:365
  156.2 1.2 collective-permute-start.9
  185.6 12.4 %copy-start.5 = (f32[256,1024]{1,0:T(8,128)}, f32[256,1024]{1,0:T(8,128)S(1)}, u32[]{:S(2)}) copy-start(f32[256,1024]{1,0:T(8,128)S(1)} %get-tuple-element.338) | copy-start | bytes 3145732
  185.6 12.4 %copy-start.59 = (f32[256]{0:T(256)}, f32[256]{0:T(256)S(1)}, u32[]{:S(2)}) copy-start(f32[256]{0:T(256)S(1)} %broadcast_multiply_fusion.1) | copy-start | bytes 3076
  185.9 12.1 %copy-start.61 = (f32[256]{0:T(256)}, f32[256]{0:T(256)S(1)}, u32[]{:S(2)}) copy-start(f32[256]{0:T(256)S(1)} %fusion.83) | copy-start | bytes 3076
  209.8 19.7 %all-to-all-start.4 = ((bf16[256,4,256]{2,0,1:T(8,128)(2,1)}), bf16[256,4,256]{2,0,1:T(8,128)(2,1)}, u32[]{:S(2)}, u32[]{:S(2)}) async-start(bf16[256,4,256]{2,0,1:T(8,128)(2,1)} %bitcast.195), calls=%async_computation.4 | async-start | bytes 1048576 | tf_op jit(solution)/shard_map/all_to_all | solution.py:400
  213.9 137.4 %reduce-scatter.3.cloned.1.call-start = ((), (), s32[]{:S(2)}) async-start(), calls=%async_computation.11 | async-start | bytes 11796480 | tf_op jit(solution)/shard_map/reduce_scatter | solution.py:249
  230.3 39.7 %copy-start.55 = (bf16[1,3,256]{2,0,1:T(2,128)(2,1)S(1)}, bf16[1,3,256]{2,0,1:T(2,128)(2,1)}, u32[]{:S(2)}) copy-start(bf16[1,3,256]{2,0,1:T(2,128)(2,1)} %get-tuple-element.405) | copy-start | bytes 4612
  230.3 39.7 %copy-start.56 = (bf16[1,3,256]{2,0,1:T(2,128)(2,1)S(1)}, bf16[1,3,256]{2,0,1:T(2,128)(2,1)}, u32[]{:S(2)}) copy-start(bf16[1,3,256]{2,0,1:T(2,128)(2,1)} %get-tuple-element.406) | copy-start | bytes 4612
  265.9 17.8 %all-to-all-start.5 = ((bf16[4,256,256]{2,1,0:T(8,128)(2,1)}), bf16[4,256,256]{2,1,0:T(8,128)(2,1)S(1)}, u32[]{:S(2)}, u32[]{:S(2)}) async-start(bf16[4,256,256]{2,1,0:T(8,128)(2,1)} %bitcast.281), calls=%async_computation.5 | async-start | bytes 1048576 | tf_op jit(solution)/shard_map/all_to_all | solution.py:412
  270.0 3.7 collective-permute-start.10
  273.7 13.5 %collective-permute-start.11 = (bf16[4,3,256]{2,0,1:T(4,128)(2,1)S(1)}, bf16[4,3,256]{2,0,1:T(4,128)(2,1)S(1)}, u32[]{:S(2)}, u32[]{:S(2)}) collective-permute-start(bf16[4,3,256]{2,0,1:T(4,128)(2,1)S(1)} %pad_maximum_fusion.16), channel_id=1, source_target_pairs={{0,16},{4,20},{8,24},{12,28},{16,0},{20,4},{24,8},{28,12},{1,17},{... | collective-permute-start | bytes 18440 | tf_op jit(solution)/shard_map/ppermute | solution.py:175
  283.7 15.7 %all-to-all-start.6 = ((bf16[4,256,256]{1,2,0:T(8,128)(2,1)}), bf16[4,256,256]{1,2,0:T(8,128)(2,1)S(1)}, u32[]{:S(2)}, u32[]{:S(2)}) async-start(bf16[4,256,256]{1,2,0:T(8,128)(2,1)} %bitcast.194), calls=%async_computation.6 | async-start | bytes 1048576 | tf_op jit(solution)/shard_map/all_to_all | solution.py:413
  299.4 14.2 %all-to-all-start.7 = ((bf16[4,256,256]{2,1,0:T(8,128)(2,1)}), bf16[4,256,256]{2,1,0:T(8,128)(2,1)}, u32[]{:S(2)}, u32[]{:S(2)}) async-start(bf16[4,256,256]{2,1,0:T(8,128)(2,1)} %bitcast.38), calls=%async_computation.7 | async-start | bytes 1048576 | tf_op jit(solution)/shard_map/all_to_all | solution.py:414
  303.6 120.3 %all-reduce.2.cloned.1.call-start = ((), (), s32[]{:S(2)}) async-start(), calls=%async_computation.12 | async-start | bytes 2621440 | tf_op jit(solution)/shard_map/psum | solution.py:250
  330.4 4.7 collective-permute-start.4
  335.1 4.7 collective-permute-start.5
  339.8 3.2 collective-permute-start.12
  343.1 8.3 %collective-permute-start.13 = (f32[2,3,6144]{2,1,0:T(4,128)S(1)}, f32[2,3,6144]{2,1,0:T(4,128)S(1)}, u32[]{:S(2)}, u32[]{:S(2)}) collective-permute-start(f32[2,3,6144]{2,1,0:T(4,128)S(1)} %pad_maximum_fusion.12), channel_id=1, source_target_pairs={{0,8},{4,12},{8,0},{12,4},{16,24},{20,28},{24,16},{28,20},{1,9},{5... | collective-permute-start | bytes 442376 | tf_op jit(solution)/shard_map/ppermute | solution.py:175
  349.8 4.2 collective-permute-start.6
  351.4 152.4 %reduce-scatter.5.cloned.1.call-start = ((), (), s32[]{:S(2)}) async-start(), calls=%async_computation.13 | async-start | bytes 7077888 | tf_op jit(solution)/shard_map/reduce_scatter | solution.py:485
  351.6 72.2 %collective-permute-start.14 = (f32[4,3,6144]{2,1,0:T(4,128)S(1)}, f32[4,3,6144]{2,1,0:T(4,128)S(1)}, u32[]{:S(2)}, u32[]{:S(2)}) collective-permute-start(f32[4,3,6144]{2,1,0:T(4,128)S(1)} %pad_maximum_fusion.10), channel_id=1, source_target_pairs={{0,16},{4,20},{8,24},{12,28},{16,0},{20,4},{24,8},{28,12},{1,17},{... | collective-permute-start | bytes 884744 | tf_op jit(solution)/shard_map/ppermute | solution.py:175
  354.7 77.5 %collective-permute-start.7 = (f32[2,3,256]{2,1,0:T(4,128)}, f32[2,3,256]{2,1,0:T(4,128)}, u32[]{:S(2)}, u32[]{:S(2)}) collective-permute-start(f32[2,3,256]{2,1,0:T(4,128)} %pad_maximum_fusion.14), channel_id=1, source_target_pairs={{0,2},{1,3},{2,0},{3,1},{4,6},{5,7},{6,4},{7,5},{8,10},{9,11},{10,... | collective-permute-start | bytes 18440 | tf_op jit(solution)/shard_map/ppermute | solution.py:175
  423.8 5.3 collective-permute-start.8
  434.9 108.0 %copy-start.53 = (f32[1536]{0:T(1024)}, f32[1536]{0:T(1024)S(1)}, u32[]{:S(2)}) copy-start(f32[1536]{0:T(1024)S(1)} %get-tuple-element.317) | copy-start | bytes 18436
  436.3 38.2 %collective-permute-start.30 = (f32[2]{0:T(128)S(1)}, f32[2]{0:T(128)S(1)}, u32[]{:S(2)}, u32[]{:S(2)}) collective-permute-start(f32[2]{0:T(128)S(1)} %pad_maximum_fusion.23), channel_id=1, source_target_pairs={{0,1},{1,0},{2,3},{3,2},{4,5},{5,4},{6,7},{7,6},{8,9},{9,8},{10,11... | collective-permute-start | bytes 32 | tf_op jit(solution)/shard_map/ppermute | solution.py:166
  437.8 23.0 %slice-start.4 = ((s8[6291456]{0:T(1024)(128)(4,1)}), s8[4194304]{0:T(1024)(128)(4,1)S(1)}, s32[]{:S(2)}) async-start(s8[6291456]{0:T(1024)(128)(4,1)} %bitcast.262), calls=%async_computation.19 | async-start | bytes 8388608
  443.8 10.9 %copy-start.40 = (f32[512,1024]{1,0:T(8,128)S(1)}, f32[512,1024]{1,0:T(8,128)}, u32[]{:S(2)}) copy-start(f32[512,1024]{1,0:T(8,128)} %param.42) | copy-start | bytes 6291460
  443.8 10.9 %copy-start.41 = (f32[512,1024]{1,0:T(8,128)S(1)}, f32[512,1024]{1,0:T(8,128)}, u32[]{:S(2)}) copy-start(f32[512,1024]{1,0:T(8,128)} %param.43) | copy-start | bytes 6291460
  443.8 16.9 %slice-start.5 = ((s8[6291456]{0:T(1024)(128)(4,1)}), s8[2097152]{0:T(1024)(128)(4,1)S(1)}, s32[]{:S(2)}) async-start(s8[6291456]{0:T(1024)(128)(4,1)} %bitcast.262), calls=%async_computation.20 | async-start | bytes 4194304
  443.9 33.6 %collective-permute-start.22 = (f32[1,2]{1,0:T(1,128)S(1)}, f32[1,2]{1,0:T(1,128)S(1)}, u32[]{:S(2)}, u32[]{:S(2)}) collective-permute-start(f32[1,2]{1,0:T(1,128)S(1)} %pad_maximum_fusion.19), channel_id=1, source_target_pairs={{0,1},{1,0},{2,3},{3,2},{4,5},{5,4},{6,7},{7,6},{8,9},{9,8},{10,11... | collective-permute-start | bytes 32 | tf_op jit(solution)/shard_map/ppermute | solution.py:166
  453.1 26.1 %collective-permute-start.24 = (f32[1,2]{1,0:T(1,128)S(1)}, f32[1,2]{1,0:T(1,128)S(1)}, u32[]{:S(2)}, u32[]{:S(2)}) collective-permute-start(f32[1,2]{1,0:T(1,128)S(1)} %pad_maximum_fusion.20), channel_id=1, source_target_pairs={{0,1},{1,0},{2,3},{3,2},{4,5},{5,4},{6,7},{7,6},{8,9},{9,8},{10,11... | collective-permute-start | bytes 32 | tf_op jit(solution)/shard_map/ppermute | solution.py:166
  460.2 22.1 %collective-permute-start.26 = (f32[1,2]{1,0:T(1,128)S(1)}, f32[1,2]{1,0:T(1,128)S(1)}, u32[]{:S(2)}, u32[]{:S(2)}) collective-permute-start(f32[1,2]{1,0:T(1,128)S(1)} %pad_maximum_fusion.21), channel_id=1, source_target_pairs={{0,1},{1,0},{2,3},{3,2},{4,5},{5,4},{6,7},{7,6},{8,9},{9,8},{10,11... | collective-permute-start | bytes 32 | tf_op jit(solution)/shard_map/ppermute | solution.py:166
  471.6 25.2 %copy-start.1 = (f32[256,6144]{1,0:T(8,128)}, f32[256,6144]{1,0:T(8,128)S(1)}, u32[]{:S(2)}) copy-start(f32[256,6144]{1,0:T(8,128)S(1)} %get-tuple-element.319) | copy-start | bytes 18874372
  473.0 11.0 %collective-permute-start.28 = (f32[1,2]{1,0:T(1,128)S(1)}, f32[1,2]{1,0:T(1,128)S(1)}, u32[]{:S(2)}, u32[]{:S(2)}) collective-permute-start(f32[1,2]{1,0:T(1,128)S(1)} %pad_maximum_fusion.22), channel_id=1, source_target_pairs={{0,1},{1,0},{2,3},{3,2},{4,5},{5,4},{6,7},{7,6},{8,9},{9,8},{10,11... | collective-permute-start | bytes 32 | tf_op jit(solution)/shard_map/ppermute | solution.py:166
  475.8 18.2 %collective-permute-start.31 = (f32[2]{0:T(128)S(1)}, f32[2]{0:T(128)S(1)}, u32[]{:S(2)}, u32[]{:S(2)}) collective-permute-start(f32[2]{0:T(128)S(1)} %fusion.153), channel_id=1, source_target_pairs={{0,2},{1,3},{2,0},{3,1},{4,6},{5,7},{6,4},{7,5},{8,10},{9,11},{10,... | collective-permute-start | bytes 32 | tf_op jit(solution)/shard_map/ppermute | solution.py:166
  478.8 16.5 %collective-permute-start.23 = (f32[1,2]{1,0:T(1,128)S(1)}, f32[1,2]{1,0:T(1,128)S(1)}, u32[]{:S(2)}, u32[]{:S(2)}) collective-permute-start(f32[1,2]{1,0:T(1,128)S(1)} %fusion.157), channel_id=1, source_target_pairs={{0,2},{1,3},{2,0},{3,1},{4,6},{5,7},{6,4},{7,5},{8,10},{9,11},{10,... | collective-permute-start | bytes 32 | tf_op jit(solution)/shard_map/ppermute | solution.py:166
  480.6 45.6 %collective-permute-start.25 = (f32[1,2]{1,0:T(1,128)S(1)}, f32[1,2]{1,0:T(1,128)S(1)}, u32[]{:S(2)}, u32[]{:S(2)}) collective-permute-start(f32[1,2]{1,0:T(1,128)S(1)} %fusion.156), channel_id=1, source_target_pairs={{0,2},{1,3},{2,0},{3,1},{4,6},{5,7},{6,4},{7,5},{8,10},{9,11},{10,... | collective-permute-start | bytes 32 | tf_op jit(solution)/shard_map/ppermute | solution.py:166
  483.6 3.7 collective-permute-start.27
  485.4 5.3 collective-permute-start.29
  505.3 8.9 %collective-permute-start.15 = (bf16[3,128,512]{2,1,0:T(8,128)(2,1)S(1)}, bf16[3,128,512]{2,1,0:T(8,128)(2,1)S(1)}, u32[]{:S(2)}, u32[]{:S(2)}) collective-permute-start(bf16[3,128,512]{2,1,0:T(8,128)(2,1)S(1)} %select_convert_fusion), channel_id=1, source_target_pairs={{0,8},{8,0},{16,24},{24,16},{1,9},{9,1},{17,25},{25,17},{2,10},{10... | collective-permute-start | bytes 1179656 | tf_op jit(solution)/shard_map/ppermute | solution.py:200
  511.5 25.5 %copy-start.20 = (f32[256,1024]{1,0:T(8,128)S(1)}, f32[256,1024]{1,0:T(8,128)}, u32[]{:S(2)}) copy-start(f32[256,1024]{1,0:T(8,128)} %param.35) | copy-start | bytes 3145732
  511.5 25.5 %copy-start.25 = (f32[256,1024]{1,0:T(8,128)S(1)}, f32[256,1024]{1,0:T(8,128)}, u32[]{:S(2)}) copy-start(f32[256,1024]{1,0:T(8,128)} %get-tuple-element.327) | copy-start | bytes 3145732
  511.5 25.5 %copy-start.26 = (f32[256,1024]{1,0:T(8,128)S(1)}, f32[256,1024]{1,0:T(8,128)}, u32[]{:S(2)}) copy-start(f32[256,1024]{1,0:T(8,128)} %get-tuple-element.328) | copy-start | bytes 3145732
  514.4 11.6 %collective-permute-start.16 = (bf16[3,128,256]{2,1,0:T(8,128)(2,1)S(1)}, bf16[3,128,256]{2,1,0:T(8,128)(2,1)S(1)}, u32[]{:S(2)}, u32[]{:S(2)}) collective-permute-start(bf16[3,128,256]{2,1,0:T(8,128)(2,1)S(1)} %select_convert_fusion.1), channel_id=1, source_target_pairs={{0,16},{8,24},{16,0},{24,8},{1,17},{9,25},{17,1},{25,9},{2,18},{10... | collective-permute-start | bytes 589832 | tf_op jit(solution)/shard_map/ppermute | solution.py:200
  526.1 8.6 %collective-permute-start.17 = (bf16[3,128,256]{2,1,0:T(8,128)(2,1)S(1)}, bf16[3,128,256]{2,1,0:T(8,128)(2,1)S(1)}, u32[]{:S(2)}, u32[]{:S(2)}) collective-permute-start(bf16[3,128,256]{2,1,0:T(8,128)(2,1)S(1)} %add_convert_fusion.3), channel_id=1, source_target_pairs={{0,16},{8,24},{16,0},{24,8},{1,17},{9,25},{17,1},{25,9},{2,18},{10... | collective-permute-start | bytes 589832 | tf_op jit(solution)/shard_map/ppermute | solution.py:207
  534.7 7.8 %collective-permute-start.18 = (bf16[3,128,512]{2,1,0:T(8,128)(2,1)S(1)}, bf16[3,128,512]{2,1,0:T(8,128)(2,1)S(1)}, u32[]{:S(2)}, u32[]{:S(2)}) collective-permute-start(bf16[3,128,512]{2,1,0:T(8,128)(2,1)S(1)} %pad_maximum_fusion.11), channel_id=1, source_target_pairs={{0,8},{8,0},{16,24},{24,16},{1,9},{9,1},{17,25},{25,17},{2,10},{10... | collective-permute-start | bytes 1179656 | tf_op jit(solution)/shard_map/ppermute | solution.py:207
  542.8 3.2 collective-permute-start.19
  553.9 3.6 collective-permute-start.20
  557.6 3.6 collective-permute-start.21
  (59 other events, 260.0 us)
Sparse Core Ops, SparseCore 0:
  10.5 50.1 all-gather.3
  63.1 77.6 all-gather.5
  229.6 96.2 reduce-scatter.2
  351.5 72.3 all-reduce.1
  432.3 61.3 reduce-scatter.4

commit v10 on v9

--- a/solution.py
+++ b/solution.py
@@ -241,12 +241,14 @@
     return fulls
 
 
-def reduce_batch(partials):
+def reduce_batch(partials, after=None):
     groups = lax.axis_size("seq") * 2
     base = min(part.shape[1] for part in partials)
     views = [part.reshape(groups, -1, base) for part in partials]
     flat = jnp.concatenate(views, axis=1)
     piece = lax.psum_scatter(flat, ("seq", "core"), scatter_dimension=0, tiled=True)[0]
+    if after is not None:
+        piece, after = lax.optimization_barrier((piece, after))
     piece = lax.psum(piece, "z")
     other = lax.ppermute(piece, "core", [(0, 1), (1, 0)])
     first = lax.axis_index("core") == 0
@@ -471,18 +473,18 @@
         list(doubling_gather(grad_silu_part, "seq", seq_count, seq_rank)), axis=1
     )
     time_grad = jax.vjp(jax.nn.silu, time_emb)[1](grad_silu)[0]
+    qkv_piece = lax.psum_scatter(
+        grad_qkv_local.astype(jnp.bfloat16), ("seq", "core"), scatter_dimension=1, tiled=True
+    )
     batch_shares = reduce_batch(
         [
             grad_out_local.astype(jnp.bfloat16),
             grad_up_local.astype(jnp.bfloat16),
             grad_down_local.astype(jnp.bfloat16),
-        ]
-    )
-    qkv_partial, batch_shares, grad_mod_share, grad_bias_share = lax.optimization_barrier(
-        (grad_qkv_local.astype(jnp.bfloat16), batch_shares, grad_mod_share, grad_bias_share)
+        ],
+        after=qkv_piece,
     )
     grad_out, grad_up, grad_down = [share.astype(jnp.float32) for share in batch_shares]
-    qkv_piece = lax.psum_scatter(qkv_partial, ("seq", "core"), scatter_dimension=1, tiled=True)
     updated = [
         lamb_update(w_out, mom_out, var_out, grad_out, None, seq_count),
         lamb_update(w_up, mom_up, var_up, grad_up, None, seq_count),

time: 582 us -> 586 us (level)
  waiting for transfers between devices: 185 us -> 169 us
  blocking collectives: 0 us -> 9.67 us
  matrix products: 87.5 us -> 97 us
  other arithmetic: 117 us -> 108 us
  starting transfers between devices: 67.7 us -> 75.9 us
    ppermute x10, waiting for transfers between devices: 5.43 us -> 29.5 us  [doubling_gather(): other = lax.ppermute(blocks, axes, [(i, i ^ step) for i in range(size)])]
    psum x1, waiting for transfers between devices: 68.2 us -> 49.5 us  [reduce_batch(): piece = lax.psum(piece, 'z')]
    dot_general x1, matrix products: 4.59 us -> 17 us  [local(): jnp.einsum('cd,ce->de', silu_all.astype(jnp.float32), grad_mod_all, preci...]
    reduce_sum x6 -> x5, other arithmetic: 33.2 us -> 21.3 us  [lamb_update(): jnp.sum(weight * weight, axis=sum_axes, keepdims=True)]
    all_to_all x1, starting transfers between devices: 3.68 us -> 14.2 us  [local(): lax.all_to_all(value_send, 'seq', split_axis=1, concat_axis=0, tiled=True)]
    all_to_all x0 -> x1, blocking collectives: none -> 9.67 us  [local(): lax.all_to_all(attended_heads, 'seq', split_axis=0, concat_axis=1, tiled=...]
    all_to_all x1, waiting for transfers between devices: 0.01 us -> 6.63 us  [local(): lax.all_to_all(grad_attended, 'seq', split_axis=1, concat_axis=0, tiled=T...]
    all_to_all x1, waiting for transfers between devices: 11.6 us -> 5.43 us  [local(): lax.all_to_all(value_send, 'seq', split_axis=1, concat_axis=0, tiled=True)]
  transfers between devices with their start and end apart: 45 -> 44, of which waited for: 23 -> 24; matrix products, arithmetic and copies ran while one was open for 40% -> 34% of each run, Pallas kernels for 0% -> 0%
where the time goes in v10:
time: 586 us; the launch traced here: 577 us
  waiting for transfers between devices  169 us (29%)
  other arithmetic  108 us (18%)
  matrix products  97 us (17%)
  local copies, waits for them, and re-layouts  91.5 us (16%)
  starting transfers between devices  75.9 us (13%)
  between operations  22.5 us (4%)
  blocking collectives  9.67 us (2%)
    psum x1, waiting for transfers between devices, reduce_batch(): piece = lax.psum(piece, 'z')  49.5 us
    ppermute x10, waiting for transfers between devices, doubling_gather(): other = lax.ppermute(blocks, axes, [(i, i ^ step) for i in range(size)])  29.5 us
    reduce_sum x5, other arithmetic, lamb_update(): jnp.sum(weight * weight, axis=sum_axes, keepdims=True)  21.3 us
    ppermute x16, starting transfers between devices, butterfly_sum(): lax.ppermute(values, axes, [(i, i ^ step) for i in range(size)])  20.5 us
    sub x6, other arithmetic, lamb_update(): return (weight - step_rate * ratio * direction, moment_new, second_new)  20.3 us
    all_gather x1, waiting for transfers between devices, gather_rows(): return lax.all_gather(piece, ('seq', 'core'), axis=row_axis, tiled=True)  20.3 us
    dot_general x1, matrix products, local(): jnp.einsum('cd,ce->de', silu_all.astype(jnp.float32), grad_mod_all, preci...  17 us
    ppermute x10, starting transfers between devices, doubling_gather(): other = lax.ppermute(blocks, axes, [(i, i ^ step) for i in range(size)])  14.8 us
  transfers between devices with their start and end apart: 44, of which 24 were waited for; matrix products, arithmetic and copies ran while one was open for 34% of the time, Pallas kernels for 0%

profile of v10, /device:TPU:0, one launch (start us, length us, event | category | flops | bytes accessed | tf_op | source)
XLA Modules:
  0.0 577.1 jit_solution(10100440817211796575)
XLA Ops:
  14.9 3.0 collective-permute-start.2
  18.0 3.7 fusion.38
  30.4 4.2 collective-permute-done.1
  34.6 2.7 fusion.68
  37.3 2.7 copy-done
  40.4 20.3 %all-gather.4.cloned.1.call-done = bf16[3,1024,1024]{2,1,0:T(8,128)(2,1)} async-done(((bf16[3,128,1024]{2,1,0:T(8,128)(2,1)}), bf16[3,1024,1024]{2,1,0:T(8,128)(2,1)}) %all-gather.4.cloned.1.call-update) | async-done | bytes 6291472 | tf_op jit(solution)/shard_map/all_gather | solution.py:188
  60.7 4.7 slice_bitcast_fusion.3
  65.3 3.9 copy.145
  69.3 4.2 dot_general.104
  73.5 3.9 copy.141
  77.4 4.1 dot_general.101
  81.5 2.5 fusion.28
  86.7 3.5 all-to-all-start
  91.8 10.6 %all-to-all-done = bf16[256,4,256]{0,2,1:T(8,128)(2,1)S(1)} async-done(((bf16[256,4,256]{0,2,1:T(8,128)(2,1)}), bf16[256,4,256]{0,2,1:T(8,128)(2,1)S(1)}, u32[]{:S(2)}, u32[]{:S(2)}) %all-to-all-start) | async-done | bytes 524320 | tf_op jit(solution)/shard_map/all_to_all | solution.py:360
  102.4 3.5 all-to-all-start.1
  105.9 2.5 fusion.48
  109.2 10.7 %all-to-all-done.1 = bf16[256,4,256]{0,2,1:T(8,128)(2,1)S(1)} async-done(((bf16[256,4,256]{0,2,1:T(8,128)(2,1)}), bf16[256,4,256]{0,2,1:T(8,128)(2,1)S(1)}, u32[]{:S(2)}, u32[]{:S(2)}) %all-to-all-start.1) | async-done | bytes 524320 | tf_op jit(solution)/shard_map/all_to_all | solution.py:361
  119.9 14.2 %all-to-all-start.2 = ((bf16[256,4,256]{2,0,1:T(8,128)(2,1)}), bf16[256,4,256]{2,0,1:T(8,128)(2,1)S(1)}, u32[]{:S(2)}, u32[]{:S(2)}) async-start(bf16[256,4,256]{2,0,1:T(8,128)(2,1)} %bitcast.196), calls=%async_computation.2 | async-start | bytes 1048576 | tf_op jit(solution)/shard_map/all_to_all | solution.py:362
  134.9 5.4 all-to-all-done.2
  141.4 18.7 %while.27 = (s32[]{:T(128)}, bf16[2,512,256]{2,1,0:T(8,128)(2,1)S(1)}, f32[2,4,512,1]{2,1,3,0:T(4,128)S(1)}, s32[2]{0:T(128)S(1)}, s32[1024]{0:T(1024)S(1)}, /*i...) while((s32[]{:T(128)}, ...), condition=%wide.region_9.10_spmd, body=%wide.region_6.9_spmd.sunk | while | flops 561117184 | bytes 30485712 | solution.py:110
  147.2 3.3 fusion.186
  156.6 3.3 fusion.186
  160.1 9.7 %all_to_all.134 = bf16[4,256,256]{2,1,0:T(8,128)(2,1)S(1)} all-to-all(bf16[4,256,256]{2,1,0:T(8,128)(2,1)S(1)} %bitcast.283), channel_id=1, replica_groups=mesh['z'=4,'core'=2,'seq'=4] {'seq'}, dimensions={0} | all-to-all | bytes 1048576 | tf_op jit(solution)/shard_map/all_to_all | solution.py:367
  170.0 3.3 slice.158
  173.3 6.0 %fusion.103 = (bf16[8,256,1024]{2,1,0:T(8,128)(2,1)}, bf16[8,256,1024]{2,1,0:T(8,128)(2,1)}) fusion(bf16[8,640,1024]{2,1,0:T(8,128)(2,1)} %bitcast.265), kind=kLoop, calls=%fused_computation.287 | loop fusion | bytes 16777216 | tf_op jit(solution)/shard_map/slice | solution.py:239
  179.3 7.1 %reshape.436 = bf16[1024,2048]{1,0:T(8,128)(2,1)} reshape(bf16[8,256,1024]{2,1,0:T(8,128)(2,1)} %get-tuple-element.335) | data formatting | bytes 8388608 | tf_op jit(solution)/shard_map/reshape | solution.py:239
  186.4 3.7 fusion.102
  200.7 2.8 fusion.101
  207.1 4.4 all-to-all-start.4
  211.5 6.6 %all-to-all-done.4 = bf16[256,4,256]{2,0,1:T(8,128)(2,1)} async-done(((bf16[256,4,256]{2,0,1:T(8,128)(2,1)}), bf16[256,4,256]{2,0,1:T(8,128)(2,1)}, u32[]{:S(2)}, u32[]{:S(2)}) %all-to-all-start.4) | async-done | bytes 524320 | tf_op jit(solution)/shard_map/all_to_all | solution.py:402
  218.9 35.6 %while.28 = (s32[]{:T(128)}, f32[1024,256]{0,1:T(8,128)S(1)}, f32[1024,256]{0,1:T(8,128)S(1)}, bf16[2,512,256]{2,1,0:T(8,128)(2,1)}, s32[2]{0:T(128)S(1)}, /*ind...) while((s32[]{:T(128)}, f32[1024,256]{0,1:T(8,128)S(1)}, ...), condition=%wide.region_16.17_spmd.clone, body=%wide.region_14.16_spmd.clone.sunk | while | flops 1376253952 | bytes 78974200 | solution.py:155
  224.1 2.4 fusion.198
  226.5 4.2 multiply_reduce_fusion.16
  241.9 2.4 fusion.198
  244.3 4.2 multiply_reduce_fusion.16
  254.5 3.5 all-to-all-start.5
  259.9 5.1 all-to-all-done.5
  265.0 3.9 all-to-all-start.6
  272.0 5.4 all-to-all-done.6
  277.4 3.5 all-to-all-start.7
  290.0 3.1 pad_maximum_fusion.1
  298.7 2.4 collective-permute-start.24
  304.0 6.4 %convolution_convert_fusion = bf16[2048,1024]{1,0:T(8,128)(2,1)} fusion(bf16[256,1024]{1,0:T(8,128)(2,1)S(1)} %copy-done.20, f32[256,6144]{1,0:T(8,128)} %copy-done, f32[256,2048]{1,0:T(8,128)} %copy-done.74), kind=kOutput, calls=%fused_computation.43 | convolution fusion | flops 1081344000 | bytes 7864320 | tf_op jit(solution)/shard_map/nf,nd->fd/dot_general | solution.py:380
  319.7 2.9 fusion.81
  324.2 3.3 convolution_convert_fusion.1
  331.7 7.3 %reshape.439 = bf16[8,256,1024]{2,1,0:T(8,128)(2,1)} reshape(bf16[1024,2048]{1,0:T(8,128)(2,1)} %convolution_convert_fusion.1) | data formatting | bytes 8388608 | tf_op jit(solution)/shard_map/reshape | solution.py:247
  339.1 5.6 fusion.51
  346.1 10.6 %pad_maximum_fusion = bf16[8,640,1024]{2,1,0:T(8,128)(2,1)} fusion(bf16[8,256,1024]{2,1,0:T(8,128)(2,1)} %bitcast.274, bf16[8,256,1024]{2,1,0:T(8,128)(2,1)S(1)} %copy-done.4, bf16[8,128,1024]{2,1,0:T(8,128)(2,1)S(1)} %bitcast.266), kind=kLoop, calls=%fused_computation.32 | loop fusion | flops 31457280 | bytes 20971520 | tf_op jit(solution)/shard_map/concatenate | solution.py:248
  357.5 3.0 collective-permute-done.7
  362.1 4.2 collective-permute-done.26
  366.5 2.4 collective-permute-start.27
  369.6 14.6 %collective-permute-done.27 = f32[4,3,6144]{2,1,0:T(4,128)S(1)} collective-permute-done((f32[4,3,6144]{2,1,0:T(4,128)S(1)}, f32[4,3,6144]{2,1,0:T(4,128)S(1)}, u32[]{:S(2)}, u32[]{:S(2)}) %collective-permute-start.27) | collective-permute-done | bytes 294944 | tf_op jit(solution)/shard_map/ppermute | solution.py:175
  390.2 6.0 %collective-permute-done.8 = bf16[3,128,512]{2,1,0:T(8,128)(2,1)} collective-permute-done((bf16[3,128,512]{2,1,0:T(8,128)(2,1)S(1)}, bf16[3,128,512]{2,1,0:T(8,128)(2,1)}, u32[]{:S(2)}, u32[]{:S(2)}) %collective-permute-start.8) | collective-permute-done | bytes 393248 | tf_op jit(solution)/shard_map/ppermute | solution.py:200
  397.4 2.9 collective-permute-start.9
  400.4 17.0 %multiply_reduce_fusion.2 = (f32[]{:T(128)}, f32[]{:T(128)}, f32[256,6144]{1,0:T(8,128)S(1)}, f32[256,6144]{1,0:T(8,128)}, f32[256,6144]{1,0:T(8,128)}) fusion(f32[256,6144]{1,0:T(8,128)} %param.44, f32[256,6144]{1,0:T(8,128)} %param.45, f32[256,6144]{1,0:T(8,128)} %param.46, f32[8,3,6144]{2,1,0:T(4,128)S(1)} %pad_maximum_fusion.4, ...), kind=kOutput, calls=%fused_computation.41 | convolution fusion | flops 479748096 | bytes 38350856 | tf_op jit(solution)/shard_map/cd,ce->de/dot_general | solution.py:466
  423.6 6.7 %collective-permute-done.10 = bf16[3,128,256]{2,1,0:T(8,128)(2,1)S(1)} collective-permute-done((bf16[3,128,256]{2,1,0:T(8,128)(2,1)S(1)}, bf16[3,128,256]{2,1,0:T(8,128)(2,1)S(1)}, u32[]{:S(2)}, u32[]{:S(2)}) %collective-permute-start.10) | collective-permute-done | bytes 196640 | tf_op jit(solution)/shard_map/ppermute | solution.py:207
  431.9 2.6 collective-permute-start.29
  441.8 7.1 %multiply_subtract_fusion = f32[256,6144]{1,0:T(8,128)} fusion(f32[256,6144]{1,0:T(8,128)S(1)} %bitcast.255, f32[]{:T(128)} %bitcast.69, f32[256,6144]{1,0:T(8,128)} %get-tuple-element.310, f32[256,6144]{1,0:T(8,128)S(1)} %get-tuple-element.309), kind=kLoop, calls=%fused_computation.37 | loop fusion | flops 12582912 | bytes 25165828 | tf_op jit(solution)/shard_map/sub | solution.py:286
  454.8 8.3 %multiply_reduce_fusion.4 = (f32[3]{0:T(128)S(1)}, f32[3]{0:T(128)S(1)}, f32[3,256,1024]{2,1,0:T(8,128)}, f32[3,256,1024]{2,1,0:T(8,128)}, f32[3,256,1024]{2,1,0:T(8,128)}) fusion(f32[3,256,1024]{2,1,0:T(8,128)S(1)} %copy-done.7, f32[3,256,1024]{2,1,0:T(8,128)} %param.33, f32[3,256,1024]{2,1,0:T(8,128)} %param.34, ...), kind=kLoop, calls=%fused_computation.52 | loop fusion | flops 16515066 | bytes 20447256 | tf_op jit(solution)/shard_map/reduce_sum | solution.py:279
  464.6 49.5 %all-reduce.2.cloned.1.call-done = bf16[640,1024]{1,0:T(8,128)(2,1)} async-done(((bf16[640,1024]{1,0:T(8,128)(2,1)}), bf16[640,1024]{1,0:T(8,128)(2,1)}) %all-reduce.2.cloned.1.call-update) | async-done | bytes 1310736 | tf_op jit(solution)/shard_map/psum | solution.py:252
  517.8 6.2 %multiply_subtract_fusion.1 = f32[3,256,1024]{2,1,0:T(8,128)} fusion(f32[3,256,1024]{2,1,0:T(8,128)S(1)} %copy-done.7, f32[3]{0:T(128)S(1)} %multiply_bitcast_fusion, f32[3,256,1024]{2,1,0:T(8,128)} %get-tuple-element.321, f32[3,256,1024]{2,1,0:T(8,128)} %get-tuple-element.320), kind=kLoop, calls=%fused_computation.48 | loop fusion | flops 6291456 | bytes 12582924 | tf_op jit(solution)/shard_map/sub | solution.py:286
  527.4 4.2 multiply_reduce_fusion.10
  534.5 3.7 multiply_reduce_fusion.8
  540.1 3.7 multiply_reduce_fusion.6
  (440 shorter events, 172.9 us)
Async XLA Ops:
  7.2 53.4 %all-gather.4.cloned.1.call-start = ((), (), s32[]{:S(2)}) async-start(), calls=%async_computation.10 | async-start | bytes 7077888 | tf_op jit(solution)/shard_map/all_gather | solution.py:188
  9.7 160.3 %all-gather.6.cloned.1.call-start = ((), (), s32[]{:S(2)}) async-start(), calls=%async_computation.14 | async-start | bytes 11796480 | tf_op jit(solution)/shard_map/all_gather | solution.py:234
  14.9 8.7 %collective-permute-start.2 = (bf16[1,1536]{1,0:T(2,128)(2,1)S(1)}, bf16[1,1536]{1,0:T(2,128)(2,1)S(1)}, u32[]{:S(2)}, u32[]{:S(2)}) collective-permute-start(bf16[1,1536]{1,0:T(2,128)(2,1)S(1)} %broadcast_in_dim.158), channel_id=1, source_target_pairs={{0,1},{1,0},{2,3},{3,2},{4,5},{5,4},{6,7},{7,6},{8,9},{9,8},{10,11... | collective-permute-start | bytes 9224 | tf_op jit(solution)/shard_map/ppermute | solution.py:175
  21.7 7.1 %collective-permute-start = (f32[3,6144]{1,0:T(4,128)S(1)}, f32[3,6144]{1,0:T(4,128)S(1)}, u32[]{:S(2)}, u32[]{:S(2)}) collective-permute-start(f32[3,6144]{1,0:T(4,128)S(1)} %fusion.38), channel_id=1, source_target_pairs={{0,1},{1,0},{2,3},{3,2},{4,5},{5,4},{6,7},{7,6},{8,9},{9,8},{10,11... | collective-permute-start | bytes 221192 | tf_op jit(solution)/shard_map/ppermute | solution.py:166
  22.3 15.0 %copy-start.63 = (f32[256]{0:T(256)}, f32[256]{0:T(256)S(1)}, u32[]{:S(2)}) copy-start(f32[256]{0:T(256)S(1)} %broadcast_multiply_fusion.2) | copy-start | bytes 3076
  22.4 14.9 %copy-start.69 = (pred[1024,3]{0,1:T(4,128)(4,1)}, pred[1024,3]{0,1:T(4,128)(4,1)S(1)}, u32[]{:S(2)}) copy-start(pred[1024,3]{0,1:T(4,128)(4,1)S(1)} %fusion.75) | copy-start | bytes 9220
  23.2 61.5 %copy-start.51 = (f32[256,32]{0,1:T(8,128)}, f32[256,32]{0,1:T(8,128)S(1)}, u32[]{:S(2)}) copy-start(f32[256,32]{0,1:T(8,128)S(1)} %get-tuple-element.399) | copy-start | bytes 98308
  23.6 4.0 collective-permute-start.3
  28.9 5.7 collective-permute-start.1
  40.4 65.5 %copy-start.15 = (bf16[256,1024]{1,0:T(8,128)(2,1)}, bf16[256,1024]{1,0:T(8,128)(2,1)S(1)}, u32[]{:S(2)}) copy-start(bf16[256,1024]{1,0:T(8,128)(2,1)S(1)} %fusion.55) | copy-start | bytes 1572868
  86.7 15.7 %all-to-all-start = ((bf16[256,4,256]{0,2,1:T(8,128)(2,1)}), bf16[256,4,256]{0,2,1:T(8,128)(2,1)S(1)}, u32[]{:S(2)}, u32[]{:S(2)}) async-start(bf16[256,4,256]{0,2,1:T(8,128)(2,1)} %convert_element_type.205), calls=%async_computation | async-start | bytes 1048576 | tf_op jit(solution)/shard_map/all_to_all | solution.py:360
  102.4 17.5 %all-to-all-start.1 = ((bf16[256,4,256]{0,2,1:T(8,128)(2,1)}), bf16[256,4,256]{0,2,1:T(8,128)(2,1)S(1)}, u32[]{:S(2)}, u32[]{:S(2)}) async-start(bf16[256,4,256]{0,2,1:T(8,128)(2,1)} %convert_element_type.206), calls=%async_computation.1 | async-start | bytes 1048576 | tf_op jit(solution)/shard_map/all_to_all | solution.py:361
  119.9 20.5 %all-to-all-start.2 = ((bf16[256,4,256]{2,0,1:T(8,128)(2,1)}), bf16[256,4,256]{2,0,1:T(8,128)(2,1)S(1)}, u32[]{:S(2)}, u32[]{:S(2)}) async-start(bf16[256,4,256]{2,0,1:T(8,128)(2,1)} %bitcast.196), calls=%async_computation.2 | async-start | bytes 1048576 | tf_op jit(solution)/shard_map/all_to_all | solution.py:362
  170.0 16.4 %copy-start.21 = (bf16[256,4,256]{0,2,1:T(8,128)(2,1)}, bf16[256,4,256]{0,2,1:T(8,128)(2,1)S(1)}, u32[]{:S(2)}) copy-start(bf16[256,4,256]{0,2,1:T(8,128)(2,1)S(1)} %copy.154) | copy-start | bytes 1572868
  207.1 11.0 %all-to-all-start.4 = ((bf16[256,4,256]{2,0,1:T(8,128)(2,1)}), bf16[256,4,256]{2,0,1:T(8,128)(2,1)}, u32[]{:S(2)}, u32[]{:S(2)}) async-start(bf16[256,4,256]{2,0,1:T(8,128)(2,1)} %bitcast.195), calls=%async_computation.4 | async-start | bytes 1048576 | tf_op jit(solution)/shard_map/all_to_all | solution.py:402
  254.5 10.5 %all-to-all-start.5 = ((bf16[4,256,256]{2,1,0:T(8,128)(2,1)}), bf16[4,256,256]{2,1,0:T(8,128)(2,1)S(1)}, u32[]{:S(2)}, u32[]{:S(2)}) async-start(bf16[4,256,256]{2,1,0:T(8,128)(2,1)} %bitcast.282), calls=%async_computation.5 | async-start | bytes 1048576 | tf_op jit(solution)/shard_map/all_to_all | solution.py:414
  265.0 12.4 %all-to-all-start.6 = ((bf16[4,256,256]{1,2,0:T(8,128)(2,1)}), bf16[4,256,256]{1,2,0:T(8,128)(2,1)S(1)}, u32[]{:S(2)}, u32[]{:S(2)}) async-start(bf16[4,256,256]{1,2,0:T(8,128)(2,1)} %bitcast.194), calls=%async_computation.6 | async-start | bytes 1048576 | tf_op jit(solution)/shard_map/all_to_all | solution.py:415
  277.4 10.0 %all-to-all-start.7 = ((bf16[4,256,256]{2,1,0:T(8,128)(2,1)}), bf16[4,256,256]{2,1,0:T(8,128)(2,1)S(1)}, u32[]{:S(2)}, u32[]{:S(2)}) async-start(bf16[4,256,256]{2,1,0:T(8,128)(2,1)} %bitcast.38), calls=%async_computation.7 | async-start | bytes 1048576 | tf_op jit(solution)/shard_map/all_to_all | solution.py:416
  280.9 103.5 %reduce-scatter.3.cloned.1.call-start = ((), (), s32[]{:S(2)}) async-start(), calls=%async_computation.11 | async-start | bytes 7077888 | tf_op jit(solution)/shard_map/reduce_scatter | solution.py:476
  293.2 17.2 %slice-start.4 = ((s8[6291456]{0:T(1024)(128)(4,1)}), s8[2097152]{0:T(1024)(128)(4,1)S(1)}, s32[]{:S(2)}) async-start(s8[6291456]{0:T(1024)(128)(4,1)} %bitcast.262), calls=%async_computation.19 | async-start | bytes 4194304
  293.2 160.0 %reduce-scatter.5.cloned.1.call-start = ((), (), s32[]{:S(2)}) async-start(), calls=%async_computation.12 | async-start | bytes 11796480 | tf_op jit(solution)/shard_map/reduce_scatter | solution.py:249
  293.8 1.2 collective-permute-start.22
  295.0 3.7 collective-permute-start.23
  298.7 4.6 collective-permute-start.24
  322.7 6.9 %collective-permute-start.4 = (f32[3,6144]{1,0:T(4,128)S(1)}, f32[3,6144]{1,0:T(4,128)S(1)}, u32[]{:S(2)}, u32[]{:S(2)}) collective-permute-start(f32[3,6144]{1,0:T(4,128)S(1)} %fusion.81), channel_id=1, source_target_pairs={{0,1},{1,0},{2,3},{3,2},{4,5},{5,4},{6,7},{7,6},{8,9},{9,8},{10,11... | collective-permute-start | bytes 221192 | tf_op jit(solution)/shard_map/ppermute | solution.py:166
  329.6 9.5 %collective-permute-start.5 = (f32[3,6144]{1,0:T(4,128)S(1)}, f32[3,6144]{1,0:T(4,128)S(1)}, u32[]{:S(2)}, u32[]{:S(2)}) collective-permute-start(f32[3,6144]{1,0:T(4,128)S(1)} %add.381), channel_id=1, source_target_pairs={{0,2},{1,3},{2,0},{3,1},{4,6},{5,7},{6,4},{7,5},{8,10},{9,11},{10,... | collective-permute-start | bytes 221192 | tf_op jit(solution)/shard_map/ppermute | solution.py:166
  344.7 12.1 %collective-permute-start.6 = (f32[1,3,256]{2,1,0:T(4,128)S(1)}, f32[1,3,256]{2,1,0:T(4,128)S(1)}, u32[]{:S(2)}, u32[]{:S(2)}) collective-permute-start(f32[1,3,256]{2,1,0:T(4,128)S(1)} %fusion.51), channel_id=1, source_target_pairs={{0,1},{1,0},{2,3},{3,2},{4,5},{5,4},{6,7},{7,6},{8,9},{9,8},{10,11... | collective-permute-start | bytes 9224 | tf_op jit(solution)/shard_map/ppermute | solution.py:175
  356.7 157.4 %all-reduce.2.cloned.1.call-start = ((), (), s32[]{:S(2)}) async-start(), calls=%async_computation.13 | async-start | bytes 2621440 | tf_op jit(solution)/shard_map/psum | solution.py:252
  356.8 3.7 collective-permute-start.7
  357.4 3.1 collective-permute-start.25
  360.6 5.7 collective-permute-start.26
  366.5 17.7 %collective-permute-start.27 = (f32[4,3,6144]{2,1,0:T(4,128)S(1)}, f32[4,3,6144]{2,1,0:T(4,128)S(1)}, u32[]{:S(2)}, u32[]{:S(2)}) collective-permute-start(f32[4,3,6144]{2,1,0:T(4,128)S(1)} %pad_maximum_fusion.8), channel_id=1, source_target_pairs={{0,16},{4,20},{8,24},{12,28},{16,0},{20,4},{24,8},{28,12},{1,17},{... | collective-permute-start | bytes 884744 | tf_op jit(solution)/shard_map/ppermute | solution.py:175
  385.8 10.4 %collective-permute-start.8 = (bf16[3,128,512]{2,1,0:T(8,128)(2,1)S(1)}, bf16[3,128,512]{2,1,0:T(8,128)(2,1)}, u32[]{:S(2)}, u32[]{:S(2)}) collective-permute-start(bf16[3,128,512]{2,1,0:T(8,128)(2,1)S(1)} %select_convert_fusion), channel_id=1, source_target_pairs={{0,8},{8,0},{16,24},{24,16},{1,9},{9,1},{17,25},{25,17},{2,10},{10... | collective-permute-start | bytes 1179656 | tf_op jit(solution)/shard_map/ppermute | solution.py:200
  386.5 13.9 %copy-start.70 = (bf16[4,3,256]{2,0,1:T(4,128)(2,1)S(1)}, bf16[4,3,256]{2,0,1:T(4,128)(2,1)}, u32[]{:S(2)}) copy-start(bf16[4,3,256]{2,0,1:T(4,128)(2,1)} %get-tuple-element.381) | copy-start | bytes 18436
  386.5 13.9 %copy-start.71 = (bf16[4,3,256]{2,0,1:T(4,128)(2,1)S(1)}, bf16[4,3,256]{2,0,1:T(4,128)(2,1)}, u32[]{:S(2)}) copy-start(bf16[4,3,256]{2,0,1:T(4,128)(2,1)} %get-tuple-element.382) | copy-start | bytes 18436
  386.9 30.5 %copy-start.60 = (f32[1536]{0:T(1024)}, f32[1536]{0:T(1024)S(1)}, u32[]{:S(2)}) copy-start(f32[1536]{0:T(1024)S(1)} %dynamic-slice_reduce_fusion) | copy-start | bytes 18436
  388.2 64.3 %copy-start.61 = (f32[1536]{0:T(1024)}, f32[1536]{0:T(1024)S(1)}, u32[]{:S(2)}) copy-start(f32[1536]{0:T(1024)S(1)} %get-tuple-element.307) | copy-start | bytes 18436
  388.2 64.3 %copy-start.62 = (f32[1536]{0:T(1024)}, f32[1536]{0:T(1024)S(1)}, u32[]{:S(2)}) copy-start(f32[1536]{0:T(1024)S(1)} %get-tuple-element.308) | copy-start | bytes 18436
  389.6 30.3 %collective-permute-start.30 = (f32[2]{0:T(128)S(1)}, f32[2]{0:T(128)S(1)}, u32[]{:S(2)}, u32[]{:S(2)}) collective-permute-start(f32[2]{0:T(128)S(1)} %pad_maximum_fusion.20), channel_id=1, source_target_pairs={{0,1},{1,0},{2,3},{3,2},{4,5},{5,4},{6,7},{7,6},{8,9},{9,8},{10,11... | collective-permute-start | bytes 32 | tf_op jit(solution)/shard_map/ppermute | solution.py:166
  397.4 21.9 %collective-permute-start.9 = (bf16[3,128,256]{2,1,0:T(8,128)(2,1)S(1)}, bf16[3,128,256]{2,1,0:T(8,128)(2,1)S(1)}, u32[]{:S(2)}, u32[]{:S(2)}) collective-permute-start(bf16[3,128,256]{2,1,0:T(8,128)(2,1)S(1)} %select_convert_fusion.1), channel_id=1, source_target_pairs={{0,16},{8,24},{16,0},{24,8},{1,17},{9,25},{17,1},{25,9},{2,18},{10... | collective-permute-start | bytes 589832 | tf_op jit(solution)/shard_map/ppermute | solution.py:200
  400.4 41.4 %slice-start = ((s8[6291456]{0:T(1024)(128)(4,1)}), s8[4194304]{0:T(1024)(128)(4,1)S(1)}, s32[]{:S(2)}) async-start(s8[6291456]{0:T(1024)(128)(4,1)} %bitcast.254), calls=%async_computation.15 | async-start | bytes 8388608
  400.4 41.4 %slice-start.1 = ((s8[6291456]{0:T(1024)(128)(4,1)}), s8[2097152]{0:T(1024)(128)(4,1)S(1)}, s32[]{:S(2)}) async-start(s8[6291456]{0:T(1024)(128)(4,1)} %bitcast.254), calls=%async_computation.16 | async-start | bytes 4194304
  417.4 31.5 %copy-start.17 = (f32[256,6144]{1,0:T(8,128)}, f32[256,6144]{1,0:T(8,128)S(1)}, u32[]{:S(2)}) copy-start(f32[256,6144]{1,0:T(8,128)S(1)} %get-tuple-element.309) | copy-start | bytes 18874372
  418.8 11.7 %collective-permute-start.28 = (f32[1,2]{1,0:T(1,128)S(1)}, f32[1,2]{1,0:T(1,128)S(1)}, u32[]{:S(2)}, u32[]{:S(2)}) collective-permute-start(f32[1,2]{1,0:T(1,128)S(1)} %pad_maximum_fusion.19), channel_id=1, source_target_pairs={{0,1},{1,0},{2,3},{3,2},{4,5},{5,4},{6,7},{7,6},{8,9},{9,8},{10,11... | collective-permute-start | bytes 32 | tf_op jit(solution)/shard_map/ppermute | solution.py:166
  419.5 10.9 %collective-permute-start.10 = (bf16[3,128,256]{2,1,0:T(8,128)(2,1)S(1)}, bf16[3,128,256]{2,1,0:T(8,128)(2,1)S(1)}, u32[]{:S(2)}, u32[]{:S(2)}) collective-permute-start(bf16[3,128,256]{2,1,0:T(8,128)(2,1)S(1)} %add_convert_fusion.3), channel_id=1, source_target_pairs={{0,16},{8,24},{16,0},{24,8},{1,17},{9,25},{17,1},{25,9},{2,18},{10... | collective-permute-start | bytes 589832 | tf_op jit(solution)/shard_map/ppermute | solution.py:207
  421.3 27.6 %collective-permute-start.31 = (f32[2]{0:T(128)S(1)}, f32[2]{0:T(128)S(1)}, u32[]{:S(2)}, u32[]{:S(2)}) collective-permute-start(f32[2]{0:T(128)S(1)} %fusion.153), channel_id=1, source_target_pairs={{0,2},{1,3},{2,0},{3,1},{4,6},{5,7},{6,4},{7,5},{8,10},{9,11},{10,... | collective-permute-start | bytes 32 | tf_op jit(solution)/shard_map/ppermute | solution.py:166
  430.4 10.2 %collective-permute-start.11 = (bf16[3,128,512]{2,1,0:T(8,128)(2,1)S(1)}, bf16[3,128,512]{2,1,0:T(8,128)(2,1)S(1)}, u32[]{:S(2)}, u32[]{:S(2)}) collective-permute-start(bf16[3,128,512]{2,1,0:T(8,128)(2,1)S(1)} %pad_maximum_fusion.7), channel_id=1, source_target_pairs={{0,8},{8,0},{16,24},{24,16},{1,9},{9,1},{17,25},{25,17},{2,10},{10... | collective-permute-start | bytes 1179656 | tf_op jit(solution)/shard_map/ppermute | solution.py:207
  431.9 4.3 collective-permute-start.29
  441.8 11.4 %collective-permute-start.12 = (bf16[3,128,1024]{2,1,0:T(8,128)(2,1)}, bf16[3,128,1024]{2,1,0:T(8,128)(2,1)}, u32[]{:S(2)}, u32[]{:S(2)}) collective-permute-start(bf16[3,128,1024]{2,1,0:T(8,128)(2,1)} %pad_maximum_fusion.3), channel_id=1, source_target_pairs={{0,4},{4,0},{1,5},{5,1},{2,6},{6,2},{3,7},{7,3},{8,12},{12,8},{9,1... | collective-permute-start | bytes 2359304 | tf_op jit(solution)/shard_map/ppermute | solution.py:496
  463.2 51.0 %collective-permute-start.13 = (f32[3,1,2]{0,2,1:T(2,128)S(1)}, f32[3,1,2]{0,2,1:T(2,128)S(1)}, u32[]{:S(2)}, u32[]{:S(2)}) collective-permute-start(f32[3,1,2]{0,2,1:T(2,128)S(1)} %pad_maximum_fusion.15), channel_id=1, source_target_pairs={{0,1},{1,0},{2,3},{3,2},{4,5},{5,4},{6,7},{7,6},{8,9},{9,8},{10,11... | collective-permute-start | bytes 80 | tf_op jit(solution)/shard_map/ppermute | solution.py:166
  514.1 9.9 %collective-permute-start.15 = (bf16[640,1024]{1,0:T(8,128)(2,1)}, bf16[640,1024]{1,0:T(8,128)(2,1)S(1)}, u32[]{:S(2)}, u32[]{:S(2)}) collective-permute-start(bf16[640,1024]{1,0:T(8,128)(2,1)} %all-reduce.2.cloned.1.call-done), channel_id=1, source_target_pairs={{0,4},{4,0},{1,5},{5,1},{2,6},{6,2},{3,7},{7,3},{8,12},{12,8},{9,1... | collective-permute-start | bytes 3932168 | tf_op jit(solution)/shard_map/ppermute | solution.py:253
  514.1 3.6 collective-permute-start.14
  531.6 32.4 %copy-start.26 = (f32[256,1024]{1,0:T(8,128)}, f32[256,1024]{1,0:T(8,128)S(1)}, u32[]{:S(2)}) copy-start(f32[256,1024]{1,0:T(8,128)S(1)} %get-tuple-element.317) | copy-start | bytes 3145732
  531.6 32.4 %copy-start.27 = (f32[256,1024]{1,0:T(8,128)}, f32[256,1024]{1,0:T(8,128)S(1)}, u32[]{:S(2)}) copy-start(f32[256,1024]{1,0:T(8,128)S(1)} %get-tuple-element.318) | copy-start | bytes 3145732
  533.0 13.6 %collective-permute-start.16 = (f32[1,2]{1,0:T(1,128)S(1)}, f32[1,2]{1,0:T(1,128)S(1)}, u32[]{:S(2)}, u32[]{:S(2)}) collective-permute-start(f32[1,2]{1,0:T(1,128)S(1)} %pad_maximum_fusion.16), channel_id=1, source_target_pairs={{0,1},{1,0},{2,3},{3,2},{4,5},{5,4},{6,7},{7,6},{8,9},{9,8},{10,11... | collective-permute-start | bytes 32 | tf_op jit(solution)/shard_map/ppermute | solution.py:166
  538.2 27.3 %copy-start.11 = (f32[256,2048]{1,0:T(8,128)}, f32[256,2048]{1,0:T(8,128)S(1)}, u32[]{:S(2)}) copy-start(f32[256,2048]{1,0:T(8,128)S(1)} %get-tuple-element.314) | copy-start | bytes 6291460
  538.2 27.3 %copy-start.12 = (f32[256,2048]{1,0:T(8,128)}, f32[256,2048]{1,0:T(8,128)S(1)}, u32[]{:S(2)}) copy-start(f32[256,2048]{1,0:T(8,128)S(1)} %get-tuple-element.315) | copy-start | bytes 6291460
  539.5 10.0 %collective-permute-start.18 = (f32[1,2]{1,0:T(1,128)S(1)}, f32[1,2]{1,0:T(1,128)S(1)}, u32[]{:S(2)}, u32[]{:S(2)}) collective-permute-start(f32[1,2]{1,0:T(1,128)S(1)} %pad_maximum_fusion.17), channel_id=1, source_target_pairs={{0,1},{1,0},{2,3},{3,2},{4,5},{5,4},{6,7},{7,6},{8,9},{9,8},{10,11... | collective-permute-start | bytes 32 | tf_op jit(solution)/shard_map/ppermute | solution.py:166
  543.8 24.1 %copy-start.13 = (f32[512,1024]{1,0:T(8,128)}, f32[512,1024]{1,0:T(8,128)S(1)}, u32[]{:S(2)}) copy-start(f32[512,1024]{1,0:T(8,128)S(1)} %get-tuple-element.311) | copy-start | bytes 6291460
  543.8 24.1 %copy-start.14 = (f32[512,1024]{1,0:T(8,128)}, f32[512,1024]{1,0:T(8,128)S(1)}, u32[]{:S(2)}) copy-start(f32[512,1024]{1,0:T(8,128)S(1)} %get-tuple-element.312) | copy-start | bytes 6291460
  545.1 6.2 %collective-permute-start.20 = (f32[1,2]{1,0:T(1,128)S(1)}, f32[1,2]{1,0:T(1,128)S(1)}, u32[]{:S(2)}, u32[]{:S(2)}) collective-permute-start(f32[1,2]{1,0:T(1,128)S(1)} %pad_maximum_fusion.18), channel_id=1, source_target_pairs={{0,1},{1,0},{2,3},{3,2},{4,5},{5,4},{6,7},{7,6},{8,9},{9,8},{10,11... | collective-permute-start | bytes 32 | tf_op jit(solution)/shard_map/ppermute | solution.py:166
  548.0 6.1 %collective-permute-start.17 = (f32[1,2]{1,0:T(1,128)S(1)}, f32[1,2]{1,0:T(1,128)S(1)}, u32[]{:S(2)}, u32[]{:S(2)}) collective-permute-start(f32[1,2]{1,0:T(1,128)S(1)} %fusion.157), channel_id=1, source_target_pairs={{0,2},{1,3},{2,0},{3,1},{4,6},{5,7},{6,4},{7,5},{8,10},{9,11},{10,... | collective-permute-start | bytes 32 | tf_op jit(solution)/shard_map/ppermute | solution.py:166
  550.7 6.7 %collective-permute-start.19 = (f32[1,2]{1,0:T(1,128)S(1)}, f32[1,2]{1,0:T(1,128)S(1)}, u32[]{:S(2)}, u32[]{:S(2)}) collective-permute-start(f32[1,2]{1,0:T(1,128)S(1)} %fusion.156), channel_id=1, source_target_pairs={{0,2},{1,3},{2,0},{3,1},{4,6},{5,7},{6,4},{7,5},{8,10},{9,11},{10,... | collective-permute-start | bytes 32 | tf_op jit(solution)/shard_map/ppermute | solution.py:166
  552.6 8.1 %collective-permute-start.21 = (f32[1,2]{1,0:T(1,128)S(1)}, f32[1,2]{1,0:T(1,128)S(1)}, u32[]{:S(2)}, u32[]{:S(2)}) collective-permute-start(f32[1,2]{1,0:T(1,128)S(1)} %fusion.155), channel_id=1, source_target_pairs={{0,2},{1,3},{2,0},{3,1},{4,6},{5,7},{6,4},{7,5},{8,10},{9,11},{10,... | collective-permute-start | bytes 32 | tf_op jit(solution)/shard_map/ppermute | solution.py:166
  (61 other events, 272.9 us)
Sparse Core Ops, SparseCore 0:
  10.5 50.1 all-gather.3
  63.1 71.5 all-gather.5
  293.3 64.5 reduce-scatter.2
  361.3 81.9 reduce-scatter.4
  453.3 60.7 all-reduce.1

commit v11 on v10

--- a/solution.py
+++ b/solution.py
@@ -2,6 +2,7 @@
 import jax.numpy as jnp
 from jax import lax
 from jax.sharding import Mesh, PartitionSpec as P
+
 
 HEAD_DIM = 64
 
@@ -95,7 +96,7 @@
     block_rows = min(512, frame_count)
 
     def one_block(block_index):
-        row_start, window, query_rows, keys_win, values_win, masked = block_inputs(
+        _, _, _, _, values_win, masked = block_inputs(
             queries, keys_all, values, owners, usable, block_index, block_rows, span
         )
         row_max = jnp.max(masked, axis=-1, keepdims=True)
@@ -120,7 +121,7 @@
     def one_block(sums, block_data):
         key_sum, value_sum = sums
         block_index, log_total = block_data
-        row_start, window, query_rows, keys_win, values_win, masked = block_inputs(
+        row_start, _, query_rows, keys_win, values_win, masked = block_inputs(
             queries, keys_all, values, owners, usable, block_index, block_rows, span
         )
         grad_rows = lax.dynamic_slice_in_dim(grad_attended, row_start, block_rows, 0).reshape(
@@ -211,16 +212,6 @@
         )
         step //= 2
     return blocks
-
-
-def reduce_rows(partial, row_axis):
-    piece = lax.psum_scatter(partial, ("seq", "core"), scatter_dimension=row_axis, tiled=True)
-    piece = halving_sum(piece, "z", lax.axis_size("z"))
-    other = lax.ppermute(piece, "core", [(0, 1), (1, 0)])
-    first = lax.axis_index("core") == 0
-    return jnp.concatenate(
-        [jnp.where(first, piece, other), jnp.where(first, other, piece)], axis=row_axis
-    )
 
 
 def gather_batch(shards):
@@ -400,6 +391,9 @@
         "ne,de->nd", grad_proj, out_full, preferred_element_type=jnp.float32
     ).astype(jnp.bfloat16)
     grad_heads = lax.all_to_all(grad_attended, "seq", split_axis=1, concat_axis=0, tiled=True)
+    grad_heads, grad_out_local, grad_up_local, grad_down_local = lax.optimization_barrier(
+        (grad_heads, grad_out_local, grad_up_local, grad_down_local)
+    )
     grad_query_heads, grad_key_heads, grad_value_heads = attend_backward(
         query_heads,
         key_heads,
@@ -489,6 +483,8 @@
         lamb_update(w_out, mom_out, var_out, grad_out, None, seq_count),
         lamb_update(w_up, mom_up, var_up, grad_up, None, seq_count),
         lamb_update(w_down, mom_down, var_down, grad_down, None, seq_count),
+    ]
+    updated += [
         lamb_update(w_mod, mom_mod, var_mod, grad_mod_share, None, seq_count),
         lamb_update(b_mod, mom_bias, var_bias, grad_bias_share, None, seq_count),
     ]

time: 586 us -> 574 us (0.980)
  blocking collectives: 9.67 us -> 0 us
  starting transfers between devices: 75.9 us -> 68.8 us
    all_to_all x1, starting transfers between devices: 14.2 us -> 3.65 us  [local(): lax.all_to_all(value_send, 'seq', split_axis=1, concat_axis=0, tiled=True)]
    all_to_all x1 -> x0, blocking collectives: 9.67 us -> none  [local(): lax.all_to_all(attended_heads, 'seq', split_axis=0, concat_axis=1, tiled=...]
    all_to_all x0 -> x1, waiting for transfers between devices: none -> 6.9 us  [local(): lax.all_to_all(attended_heads, 'seq', split_axis=0, concat_axis=1, tiled=...]
    all_to_all x1, waiting for transfers between devices: 6.63 us -> 0.11 us  [local(): lax.all_to_all(grad_attended, 'seq', split_axis=1, concat_axis=0, tiled=T...]
  transfers between devices with their start and end apart: 44 -> 45, of which waited for: 24 -> 24; matrix products, arithmetic and copies ran while one was open for 34% -> 35% of each run, Pallas kernels for 0% -> 0%
where the time goes in v11:
time: 574 us; the launch traced here: 563 us
  waiting for transfers between devices  169 us (29%)
  other arithmetic  108 us (19%)
  matrix products  102 us (18%)
  local copies, waits for them, and re-layouts  90.4 us (16%)
  starting transfers between devices  68.8 us (12%)
  between operations  22.5 us (4%)
    psum x1, waiting for transfers between devices, reduce_batch(): piece = lax.psum(piece, 'z')  47.6 us
    ppermute x10, waiting for transfers between devices, doubling_gather(): other = lax.ppermute(blocks, axes, [(i, i ^ step) for i in range(size)])  27.5 us
    reduce_sum x5, other arithmetic, lamb_update(): jnp.sum(weight * weight, axis=sum_axes, keepdims=True)  21.3 us
    all_gather x1, waiting for transfers between devices, gather_rows(): return lax.all_gather(piece, ('seq', 'core'), axis=row_axis, tiled=True)  20.3 us
    sub x6, other arithmetic, lamb_update(): return (weight - step_rate * ratio * direction, moment_new, second_new)  20.2 us
    ppermute x16, starting transfers between devices, butterfly_sum(): lax.ppermute(values, axes, [(i, i ^ step) for i in range(size)])  17.5 us
    dot_general x1, matrix products, local(): jnp.einsum('cd,ce->de', silu_all.astype(jnp.float32), grad_mod_all, preci...  16.5 us
    ppermute x10, starting transfers between devices, doubling_gather(): other = lax.ppermute(blocks, axes, [(i, i ^ step) for i in range(size)])  15.8 us
  transfers between devices with their start and end apart: 45, of which 24 were waited for; matrix products, arithmetic and copies ran while one was open for 35% of the time, Pallas kernels for 0%

profile of v11, /device:TPU:0, one launch (start us, length us, event | category | flops | bytes accessed | tf_op | source)
XLA Modules:
  0.0 563.2 jit_solution(17374788272497952467)
XLA Ops:
  14.9 3.0 collective-permute-start.2
  18.0 3.7 fusion.38
  30.4 4.2 collective-permute-done.1
  34.6 2.7 fusion.68
  37.3 2.7 copy-done
  40.4 20.3 %all-gather.4.cloned.1.call-done = bf16[3,1024,1024]{2,1,0:T(8,128)(2,1)} async-done(((bf16[3,128,1024]{2,1,0:T(8,128)(2,1)}), bf16[3,1024,1024]{2,1,0:T(8,128)(2,1)}) %all-gather.4.cloned.1.call-update) | async-done | bytes 6291472 | tf_op jit(solution)/shard_map/all_gather | solution.py:189
  60.6 4.7 slice_bitcast_fusion.3
  65.3 2.9 copy.145
  70.4 3.0 copy.141
  75.7 2.5 fusion.28
  81.0 3.5 all-to-all-start
  86.0 8.1 %all-to-all-done = bf16[256,4,256]{0,2,1:T(8,128)(2,1)S(1)} async-done(((bf16[256,4,256]{0,2,1:T(8,128)(2,1)}), bf16[256,4,256]{0,2,1:T(8,128)(2,1)S(1)}, u32[]{:S(2)}, u32[]{:S(2)}) %all-to-all-start) | async-done | bytes 524320 | tf_op jit(solution)/shard_map/all_to_all | solution.py:351
  94.1 3.5 all-to-all-start.1
  97.6 2.9 fusion.48
  101.4 10.8 %all-to-all-done.1 = bf16[256,4,256]{0,2,1:T(8,128)(2,1)S(1)} async-done(((bf16[256,4,256]{0,2,1:T(8,128)(2,1)}), bf16[256,4,256]{0,2,1:T(8,128)(2,1)S(1)}, u32[]{:S(2)}, u32[]{:S(2)}) %all-to-all-start.1) | async-done | bytes 524320 | tf_op jit(solution)/shard_map/all_to_all | solution.py:352
  112.1 3.6 all-to-all-start.2
  120.3 9.8 %all-to-all-done.2 = bf16[256,4,256]{2,0,1:T(8,128)(2,1)S(1)} async-done(((bf16[256,4,256]{2,0,1:T(8,128)(2,1)}), bf16[256,4,256]{2,0,1:T(8,128)(2,1)S(1)}, u32[]{:S(2)}, u32[]{:S(2)}) %all-to-all-start.2) | async-done | bytes 524320 | tf_op jit(solution)/shard_map/all_to_all | solution.py:353
  132.0 20.0 %while.27 = (s32[]{:T(128)}, bf16[2,512,256]{2,1,0:T(8,128)(2,1)}, f32[2,4,512,1]{2,1,3,0:T(4,128)S(1)}, s32[2]{0:T(128)S(1)}, s32[1024]{0:T(1024)S(1)}, /*index...) while((s32[]{:T(128)}, bf16[2,512,256]{2,1,0:T(8,128)(2,1)}, ...), condition=%wide.region_9.10_spmd, body=%wide.region_6.9_spmd.sunk | while | flops 561117184 | bytes 30485712 | solution.py:111
  137.8 3.3 fusion.189
  147.8 3.3 fusion.189
  152.0 4.1 all-to-all-start.3
  156.2 6.9 %all-to-all-done.3 = bf16[4,256,256]{2,1,0:T(8,128)(2,1)} async-done(((bf16[4,256,256]{2,1,0:T(8,128)(2,1)}), bf16[4,256,256]{2,1,0:T(8,128)(2,1)}, u32[]{:S(2)}, u32[]{:S(2)}) %all-to-all-start.3) | async-done | bytes 524320 | tf_op jit(solution)/shard_map/all_to_all | solution.py:358
  165.1 3.1 slice.158
  168.2 6.0 %fusion.104 = (bf16[8,256,1024]{2,1,0:T(8,128)(2,1)}, bf16[8,256,1024]{2,1,0:T(8,128)(2,1)}) fusion(bf16[8,640,1024]{2,1,0:T(8,128)(2,1)} %bitcast.263), kind=kLoop, calls=%fused_computation.285 | loop fusion | bytes 16777216 | tf_op jit(solution)/shard_map/slice | solution.py:230
  174.2 7.1 %reshape.436 = bf16[1024,2048]{1,0:T(8,128)(2,1)} reshape(bf16[8,256,1024]{2,1,0:T(8,128)(2,1)} %get-tuple-element.343) | data formatting | bytes 8388608 | tf_op jit(solution)/shard_map/reshape | solution.py:230
  181.3 3.9 fusion.103
  189.9 3.9 fusion.88
  197.8 2.8 fusion.102
  204.2 4.5 all-to-all-start.4
  208.8 3.2 fusion.116
  212.0 3.3 fusion.117
  216.2 35.7 %while.28 = (s32[]{:T(128)}, f32[1024,256]{0,1:T(8,128)S(1)}, f32[1024,256]{0,1:T(8,128)S(1)}, bf16[2,512,256]{2,1,0:T(8,128)(2,1)}, s32[2]{0:T(128)S(1)}, /*ind...) while((s32[]{:T(128)}, f32[1024,256]{0,1:T(8,128)S(1)}, ...), condition=%wide.region_16.17_spmd.clone, body=%wide.region_14.16_spmd.clone.sunk | while | flops 1376253952 | bytes 78974200 | solution.py:156
  221.4 2.4 fusion.201
  223.8 4.2 multiply_reduce_fusion.16
  241.6 4.2 multiply_reduce_fusion.16
  252.0 4.1 all-to-all-start.5
  258.0 4.7 all-to-all-done.5
  262.7 3.5 all-to-all-start.6
  269.3 3.4 all-to-all-done.6
  272.7 3.5 all-to-all-start.7
  285.2 3.1 pad_maximum_fusion.1
  296.3 2.7 fusion.45
  299.1 3.3 constant_dynamic-update-slice_fusion.3
  307.3 2.8 fusion.81
  311.9 2.5 collective-permute-start.24
  318.3 7.1 %reshape.439 = bf16[8,256,1024]{2,1,0:T(8,128)(2,1)} reshape(bf16[1024,2048]{1,0:T(8,128)(2,1)} %fusion.117) | data formatting | bytes 8388608 | tf_op jit(solution)/shard_map/reshape | solution.py:238
  325.4 5.6 fusion.51
  332.4 10.6 %pad_maximum_fusion = bf16[8,640,1024]{2,1,0:T(8,128)(2,1)} fusion(bf16[8,256,1024]{2,1,0:T(8,128)(2,1)} %bitcast.272, bf16[8,256,1024]{2,1,0:T(8,128)(2,1)S(1)} %copy-done.4, bf16[8,128,1024]{2,1,0:T(8,128)(2,1)S(1)} %bitcast.264), kind=kLoop, calls=%fused_computation.32 | loop fusion | flops 31457280 | bytes 20971520 | tf_op jit(solution)/shard_map/concatenate | solution.py:239
  345.1 2.5 collective-permute-done.7
  349.2 4.2 collective-permute-done.26
  353.7 2.6 collective-permute-start.27
  356.9 15.3 %collective-permute-done.27 = f32[4,3,6144]{2,1,0:T(4,128)S(1)} collective-permute-done((f32[4,3,6144]{2,1,0:T(4,128)S(1)}, f32[4,3,6144]{2,1,0:T(4,128)S(1)}, u32[]{:S(2)}, u32[]{:S(2)}) %collective-permute-start.27) | collective-permute-done | bytes 294944 | tf_op jit(solution)/shard_map/ppermute | solution.py:176
  377.9 6.0 %collective-permute-done.8 = bf16[3,128,512]{2,1,0:T(8,128)(2,1)} collective-permute-done((bf16[3,128,512]{2,1,0:T(8,128)(2,1)S(1)}, bf16[3,128,512]{2,1,0:T(8,128)(2,1)}, u32[]{:S(2)}, u32[]{:S(2)}) %collective-permute-start.8) | collective-permute-done | bytes 393248 | tf_op jit(solution)/shard_map/ppermute | solution.py:201
  385.2 3.4 collective-permute-start.9
  388.7 16.5 %multiply_reduce_fusion.2 = (f32[]{:T(128)}, f32[]{:T(128)}, f32[256,6144]{1,0:T(8,128)S(1)}, f32[256,6144]{1,0:T(8,128)}, f32[256,6144]{1,0:T(8,128)}) fusion(f32[256,6144]{1,0:T(8,128)} %param.44, f32[256,6144]{1,0:T(8,128)} %param.45, f32[256,6144]{1,0:T(8,128)} %param.46, f32[8,3,6144]{2,1,0:T(4,128)S(1)} %pad_maximum_fusion.4, ...), kind=kOutput, calls=%fused_computation.41 | convolution fusion | flops 479748096 | bytes 38350856 | tf_op jit(solution)/shard_map/cd,ce->de/dot_general | solution.py:460
  409.4 8.5 %collective-permute-done.10 = bf16[3,128,256]{2,1,0:T(8,128)(2,1)S(1)} collective-permute-done((bf16[3,128,256]{2,1,0:T(8,128)(2,1)S(1)}, bf16[3,128,256]{2,1,0:T(8,128)(2,1)S(1)}, u32[]{:S(2)}, u32[]{:S(2)}) %collective-permute-start.10) | collective-permute-done | bytes 196640 | tf_op jit(solution)/shard_map/ppermute | solution.py:208
  420.3 2.7 collective-permute-done.29
  429.3 7.0 %multiply_subtract_fusion = f32[256,6144]{1,0:T(8,128)} fusion(f32[256,6144]{1,0:T(8,128)S(1)} %bitcast.255, f32[]{:T(128)} %bitcast.69, f32[256,6144]{1,0:T(8,128)} %get-tuple-element.318, f32[256,6144]{1,0:T(8,128)S(1)} %get-tuple-element.317), kind=kLoop, calls=%fused_computation.37 | loop fusion | flops 12582912 | bytes 25165828 | tf_op jit(solution)/shard_map/sub | solution.py:277
  442.3 8.3 %multiply_reduce_fusion.4 = (f32[3]{0:T(128)S(1)}, f32[3]{0:T(128)S(1)}, f32[3,256,1024]{2,1,0:T(8,128)}, f32[3,256,1024]{2,1,0:T(8,128)}, f32[3,256,1024]{2,1,0:T(8,128)}) fusion(f32[3,256,1024]{2,1,0:T(8,128)S(1)} %copy-done.7, f32[3,256,1024]{2,1,0:T(8,128)} %param.33, f32[3,256,1024]{2,1,0:T(8,128)} %param.34, ...), kind=kLoop, calls=%fused_computation.50 | loop fusion | flops 16515066 | bytes 20447256 | tf_op jit(solution)/shard_map/reduce_sum | solution.py:270
  452.6 47.6 %all-reduce.2.cloned.1.call-done = bf16[640,1024]{1,0:T(8,128)(2,1)} async-done(((bf16[640,1024]{1,0:T(8,128)(2,1)}), bf16[640,1024]{1,0:T(8,128)(2,1)}) %all-reduce.2.cloned.1.call-update) | async-done | bytes 1310736 | tf_op jit(solution)/shard_map/psum | solution.py:243
  503.9 6.2 %multiply_subtract_fusion.1 = f32[3,256,1024]{2,1,0:T(8,128)} fusion(f32[3,256,1024]{2,1,0:T(8,128)S(1)} %copy-done.7, f32[3]{0:T(128)S(1)} %multiply_bitcast_fusion, f32[3,256,1024]{2,1,0:T(8,128)} %get-tuple-element.329, f32[3,256,1024]{2,1,0:T(8,128)} %get-tuple-element.328), kind=kLoop, calls=%fused_computation.46 | loop fusion | flops 6291456 | bytes 12582924 | tf_op jit(solution)/shard_map/sub | solution.py:277
  513.5 4.2 multiply_reduce_fusion.10
  520.6 3.7 multiply_reduce_fusion.8
  526.2 3.8 multiply_reduce_fusion.6
  (422 shorter events, 180.2 us)
Async XLA Ops:
  7.2 53.4 %all-gather.4.cloned.1.call-start = ((), (), s32[]{:S(2)}) async-start(), calls=%async_computation.10 | async-start | bytes 7077888 | tf_op jit(solution)/shard_map/all_gather | solution.py:189
  9.7 155.4 %all-gather.6.cloned.1.call-start = ((), (), s32[]{:S(2)}) async-start(), calls=%async_computation.14 | async-start | bytes 11796480 | tf_op jit(solution)/shard_map/all_gather | solution.py:225
  14.9 8.7 %collective-permute-start.2 = (bf16[1,1536]{1,0:T(2,128)(2,1)S(1)}, bf16[1,1536]{1,0:T(2,128)(2,1)S(1)}, u32[]{:S(2)}, u32[]{:S(2)}) collective-permute-start(bf16[1,1536]{1,0:T(2,128)(2,1)S(1)} %broadcast_in_dim.158), channel_id=1, source_target_pairs={{0,1},{1,0},{2,3},{3,2},{4,5},{5,4},{6,7},{7,6},{8,9},{9,8},{10,11... | collective-permute-start | bytes 9224 | tf_op jit(solution)/shard_map/ppermute | solution.py:176
  21.7 7.1 %collective-permute-start = (f32[3,6144]{1,0:T(4,128)S(1)}, f32[3,6144]{1,0:T(4,128)S(1)}, u32[]{:S(2)}, u32[]{:S(2)}) collective-permute-start(f32[3,6144]{1,0:T(4,128)S(1)} %fusion.38), channel_id=1, source_target_pairs={{0,1},{1,0},{2,3},{3,2},{4,5},{5,4},{6,7},{7,6},{8,9},{9,8},{10,11... | collective-permute-start | bytes 221192 | tf_op jit(solution)/shard_map/ppermute | solution.py:167
  22.3 15.0 %copy-start.57 = (f32[256]{0:T(256)}, f32[256]{0:T(256)S(1)}, u32[]{:S(2)}) copy-start(f32[256]{0:T(256)S(1)} %broadcast_multiply_fusion.2) | copy-start | bytes 3076
  22.4 14.9 %copy-start.63 = (pred[1024,3]{0,1:T(4,128)(4,1)}, pred[1024,3]{0,1:T(4,128)(4,1)S(1)}, u32[]{:S(2)}) copy-start(pred[1024,3]{0,1:T(4,128)(4,1)S(1)} %fusion.75) | copy-start | bytes 9220
  23.2 55.7 %copy-start.45 = (f32[256,32]{0,1:T(8,128)}, f32[256,32]{0,1:T(8,128)S(1)}, u32[]{:S(2)}) copy-start(f32[256,32]{0,1:T(8,128)S(1)} %get-tuple-element.407) | copy-start | bytes 98308
  23.6 4.0 collective-permute-start.3
  28.9 5.7 %collective-permute-start.1 = (f32[3,6144]{1,0:T(4,128)S(1)}, f32[3,6144]{1,0:T(4,128)S(1)}, u32[]{:S(2)}, u32[]{:S(2)}) collective-permute-start(f32[3,6144]{1,0:T(4,128)S(1)} %add.355), channel_id=1, source_target_pairs={{0,2},{1,3},{2,0},{3,1},{4,6},{5,7},{6,4},{7,5},{8,10},{9,11},{10,... | collective-permute-start | bytes 221192 | tf_op jit(solution)/shard_map/ppermute | solution.py:167
  40.4 57.2 %copy-start.16 = (bf16[256,1024]{1,0:T(8,128)(2,1)}, bf16[256,1024]{1,0:T(8,128)(2,1)S(1)}, u32[]{:S(2)}) copy-start(bf16[256,1024]{1,0:T(8,128)(2,1)S(1)} %fusion.55) | copy-start | bytes 1572868
  81.0 13.1 %all-to-all-start = ((bf16[256,4,256]{0,2,1:T(8,128)(2,1)}), bf16[256,4,256]{0,2,1:T(8,128)(2,1)S(1)}, u32[]{:S(2)}, u32[]{:S(2)}) async-start(bf16[256,4,256]{0,2,1:T(8,128)(2,1)} %convert_element_type.205), calls=%async_computation | async-start | bytes 1048576 | tf_op jit(solution)/shard_map/all_to_all | solution.py:351
  94.1 18.0 %all-to-all-start.1 = ((bf16[256,4,256]{0,2,1:T(8,128)(2,1)}), bf16[256,4,256]{0,2,1:T(8,128)(2,1)S(1)}, u32[]{:S(2)}, u32[]{:S(2)}) async-start(bf16[256,4,256]{0,2,1:T(8,128)(2,1)} %convert_element_type.206), calls=%async_computation.1 | async-start | bytes 1048576 | tf_op jit(solution)/shard_map/all_to_all | solution.py:352
  112.1 18.0 %all-to-all-start.2 = ((bf16[256,4,256]{2,0,1:T(8,128)(2,1)}), bf16[256,4,256]{2,0,1:T(8,128)(2,1)S(1)}, u32[]{:S(2)}, u32[]{:S(2)}) async-start(bf16[256,4,256]{2,0,1:T(8,128)(2,1)} %bitcast.196), calls=%async_computation.2 | async-start | bytes 1048576 | tf_op jit(solution)/shard_map/all_to_all | solution.py:353
  152.0 11.1 %all-to-all-start.3 = ((bf16[4,256,256]{2,1,0:T(8,128)(2,1)}), bf16[4,256,256]{2,1,0:T(8,128)(2,1)}, u32[]{:S(2)}, u32[]{:S(2)}) async-start(bf16[4,256,256]{2,1,0:T(8,128)(2,1)} %bitcast.26), calls=%async_computation.3 | async-start | bytes 1048576 | tf_op jit(solution)/shard_map/all_to_all | solution.py:358
  204.2 11.2 %all-to-all-start.4 = ((bf16[256,4,256]{2,0,1:T(8,128)(2,1)}), bf16[256,4,256]{2,0,1:T(8,128)(2,1)}, u32[]{:S(2)}, u32[]{:S(2)}) async-start(bf16[256,4,256]{2,0,1:T(8,128)(2,1)} %bitcast.280), calls=%async_computation.4 | async-start | bytes 1048576 | tf_op jit(solution)/shard_map/all_to_all | solution.py:393
  252.0 10.7 %all-to-all-start.5 = ((bf16[4,256,256]{2,1,0:T(8,128)(2,1)}), bf16[4,256,256]{2,1,0:T(8,128)(2,1)S(1)}, u32[]{:S(2)}, u32[]{:S(2)}) async-start(bf16[4,256,256]{2,1,0:T(8,128)(2,1)} %bitcast.281), calls=%async_computation.5 | async-start | bytes 1048576 | tf_op jit(solution)/shard_map/all_to_all | solution.py:408
  262.7 10.0 %all-to-all-start.6 = ((bf16[4,256,256]{1,2,0:T(8,128)(2,1)}), bf16[4,256,256]{1,2,0:T(8,128)(2,1)S(1)}, u32[]{:S(2)}, u32[]{:S(2)}) async-start(bf16[4,256,256]{1,2,0:T(8,128)(2,1)} %bitcast.194), calls=%async_computation.6 | async-start | bytes 1048576 | tf_op jit(solution)/shard_map/all_to_all | solution.py:409
  272.7 10.0 %all-to-all-start.7 = ((bf16[4,256,256]{2,1,0:T(8,128)(2,1)}), bf16[4,256,256]{2,1,0:T(8,128)(2,1)S(1)}, u32[]{:S(2)}, u32[]{:S(2)}) async-start(bf16[4,256,256]{2,1,0:T(8,128)(2,1)} %bitcast.38), calls=%async_computation.7 | async-start | bytes 1048576 | tf_op jit(solution)/shard_map/all_to_all | solution.py:410
  276.2 96.2 %reduce-scatter.3.cloned.1.call-start = ((), (), s32[]{:S(2)}) async-start(), calls=%async_computation.11 | async-start | bytes 7077888 | tf_op jit(solution)/shard_map/reduce_scatter | solution.py:470
  288.4 152.3 %reduce-scatter.5.cloned.1.call-start = ((), (), s32[]{:S(2)}) async-start(), calls=%async_computation.12 | async-start | bytes 11796480 | tf_op jit(solution)/shard_map/reduce_scatter | solution.py:240
  289.0 1.2 collective-permute-start.22
  290.2 3.7 collective-permute-start.23
  310.2 5.7 %collective-permute-start.4 = (f32[3,6144]{1,0:T(4,128)S(1)}, f32[3,6144]{1,0:T(4,128)S(1)}, u32[]{:S(2)}, u32[]{:S(2)}) collective-permute-start(f32[3,6144]{1,0:T(4,128)S(1)} %fusion.81), channel_id=1, source_target_pairs={{0,1},{1,0},{2,3},{3,2},{4,5},{5,4},{6,7},{7,6},{8,9},{9,8},{10,11... | collective-permute-start | bytes 221192 | tf_op jit(solution)/shard_map/ppermute | solution.py:167
  311.9 5.8 %collective-permute-start.24 = (bf16[4,3,256]{2,0,1:T(4,128)(2,1)S(1)}, bf16[4,3,256]{2,0,1:T(4,128)(2,1)S(1)}, u32[]{:S(2)}, u32[]{:S(2)}) collective-permute-start(bf16[4,3,256]{2,0,1:T(4,128)(2,1)S(1)} %pad_maximum_fusion.13), channel_id=1, source_target_pairs={{0,16},{4,20},{8,24},{12,28},{16,0},{20,4},{24,8},{28,12},{1,17},{... | collective-permute-start | bytes 18440 | tf_op jit(solution)/shard_map/ppermute | solution.py:176
  315.9 9.5 %collective-permute-start.5 = (f32[3,6144]{1,0:T(4,128)S(1)}, f32[3,6144]{1,0:T(4,128)S(1)}, u32[]{:S(2)}, u32[]{:S(2)}) collective-permute-start(f32[3,6144]{1,0:T(4,128)S(1)} %add.381), channel_id=1, source_target_pairs={{0,2},{1,3},{2,0},{3,1},{4,6},{5,7},{6,4},{7,5},{8,10},{9,11},{10,... | collective-permute-start | bytes 221192 | tf_op jit(solution)/shard_map/ppermute | solution.py:167
  331.0 12.5 %collective-permute-start.6 = (f32[1,3,256]{2,1,0:T(4,128)S(1)}, f32[1,3,256]{2,1,0:T(4,128)S(1)}, u32[]{:S(2)}, u32[]{:S(2)}) collective-permute-start(f32[1,3,256]{2,1,0:T(4,128)S(1)} %fusion.51), channel_id=1, source_target_pairs={{0,1},{1,0},{2,3},{3,2},{4,5},{5,4},{6,7},{7,6},{8,9},{9,8},{10,11... | collective-permute-start | bytes 9224 | tf_op jit(solution)/shard_map/ppermute | solution.py:176
  343.0 13.2 %copy-start.49 = (f32[3,1024]{1,0:T(4,128)S(1)}, f32[3,1024]{1,0:T(4,128)}, u32[]{:S(2)}) copy-start(f32[3,1024]{1,0:T(4,128)} %param.29) | copy-start | bytes 36868
  343.0 157.1 %all-reduce.2.cloned.1.call-start = ((), (), s32[]{:S(2)}) async-start(), calls=%async_computation.13 | async-start | bytes 2621440 | tf_op jit(solution)/shard_map/psum | solution.py:243
  343.5 4.0 collective-permute-start.7
  345.0 2.6 collective-permute-start.25
  347.7 5.8 %collective-permute-start.26 = (f32[2,3,6144]{2,1,0:T(4,128)S(1)}, f32[2,3,6144]{2,1,0:T(4,128)S(1)}, u32[]{:S(2)}, u32[]{:S(2)}) collective-permute-start(f32[2,3,6144]{2,1,0:T(4,128)S(1)} %pad_maximum_fusion.9), channel_id=1, source_target_pairs={{0,8},{4,12},{8,0},{12,4},{16,24},{20,28},{24,16},{28,20},{1,9},{5... | collective-permute-start | bytes 442376 | tf_op jit(solution)/shard_map/ppermute | solution.py:176
  353.7 18.5 %collective-permute-start.27 = (f32[4,3,6144]{2,1,0:T(4,128)S(1)}, f32[4,3,6144]{2,1,0:T(4,128)S(1)}, u32[]{:S(2)}, u32[]{:S(2)}) collective-permute-start(f32[4,3,6144]{2,1,0:T(4,128)S(1)} %pad_maximum_fusion.8), channel_id=1, source_target_pairs={{0,16},{4,20},{8,24},{12,28},{16,0},{20,4},{24,8},{28,12},{1,17},{... | collective-permute-start | bytes 884744 | tf_op jit(solution)/shard_map/ppermute | solution.py:176
  373.8 10.2 %collective-permute-start.8 = (bf16[3,128,512]{2,1,0:T(8,128)(2,1)S(1)}, bf16[3,128,512]{2,1,0:T(8,128)(2,1)}, u32[]{:S(2)}, u32[]{:S(2)}) collective-permute-start(bf16[3,128,512]{2,1,0:T(8,128)(2,1)S(1)} %select_convert_fusion), channel_id=1, source_target_pairs={{0,8},{8,0},{16,24},{24,16},{1,9},{9,1},{17,25},{25,17},{2,10},{10... | collective-permute-start | bytes 1179656 | tf_op jit(solution)/shard_map/ppermute | solution.py:201
  374.8 13.9 %copy-start.64 = (bf16[4,3,256]{2,0,1:T(4,128)(2,1)S(1)}, bf16[4,3,256]{2,0,1:T(4,128)(2,1)}, u32[]{:S(2)}) copy-start(bf16[4,3,256]{2,0,1:T(4,128)(2,1)} %get-tuple-element.389) | copy-start | bytes 18436
  374.8 13.9 %copy-start.65 = (bf16[4,3,256]{2,0,1:T(4,128)(2,1)S(1)}, bf16[4,3,256]{2,0,1:T(4,128)(2,1)}, u32[]{:S(2)}) copy-start(bf16[4,3,256]{2,0,1:T(4,128)(2,1)} %get-tuple-element.390) | copy-start | bytes 18436
  375.2 30.0 %copy-start.54 = (f32[1536]{0:T(1024)}, f32[1536]{0:T(1024)S(1)}, u32[]{:S(2)}) copy-start(f32[1536]{0:T(1024)S(1)} %dynamic-slice_reduce_fusion) | copy-start | bytes 18436
  376.5 63.5 %copy-start.55 = (f32[1536]{0:T(1024)}, f32[1536]{0:T(1024)S(1)}, u32[]{:S(2)}) copy-start(f32[1536]{0:T(1024)S(1)} %get-tuple-element.315) | copy-start | bytes 18436
  376.5 63.5 %copy-start.56 = (f32[1536]{0:T(1024)}, f32[1536]{0:T(1024)S(1)}, u32[]{:S(2)}) copy-start(f32[1536]{0:T(1024)S(1)} %get-tuple-element.316) | copy-start | bytes 18436
  377.9 28.9 %collective-permute-start.30 = (f32[2]{0:T(128)S(1)}, f32[2]{0:T(128)S(1)}, u32[]{:S(2)}, u32[]{:S(2)}) collective-permute-start(f32[2]{0:T(128)S(1)} %pad_maximum_fusion.20), channel_id=1, source_target_pairs={{0,1},{1,0},{2,3},{3,2},{4,5},{5,4},{6,7},{7,6},{8,9},{9,8},{10,11... | collective-permute-start | bytes 32 | tf_op jit(solution)/shard_map/ppermute | solution.py:167
  385.2 21.5 %collective-permute-start.9 = (bf16[3,128,256]{2,1,0:T(8,128)(2,1)S(1)}, bf16[3,128,256]{2,1,0:T(8,128)(2,1)S(1)}, u32[]{:S(2)}, u32[]{:S(2)}) collective-permute-start(bf16[3,128,256]{2,1,0:T(8,128)(2,1)S(1)} %select_convert_fusion.1), channel_id=1, source_target_pairs={{0,16},{8,24},{16,0},{24,8},{1,17},{9,25},{17,1},{25,9},{2,18},{10... | collective-permute-start | bytes 589832 | tf_op jit(solution)/shard_map/ppermute | solution.py:201
  388.7 40.6 %slice-start = ((s8[6291456]{0:T(1024)(128)(4,1)}), s8[4194304]{0:T(1024)(128)(4,1)S(1)}, s32[]{:S(2)}) async-start(s8[6291456]{0:T(1024)(128)(4,1)} %bitcast.254), calls=%async_computation.15 | async-start | bytes 8388608
  388.7 40.6 %slice-start.1 = ((s8[6291456]{0:T(1024)(128)(4,1)}), s8[2097152]{0:T(1024)(128)(4,1)S(1)}, s32[]{:S(2)}) async-start(s8[6291456]{0:T(1024)(128)(4,1)} %bitcast.254), calls=%async_computation.16 | async-start | bytes 4194304
  405.2 31.1 %copy-start.18 = (f32[256,6144]{1,0:T(8,128)}, f32[256,6144]{1,0:T(8,128)S(1)}, u32[]{:S(2)}) copy-start(f32[256,6144]{1,0:T(8,128)S(1)} %get-tuple-element.317) | copy-start | bytes 18874372
  406.6 11.4 %collective-permute-start.28 = (f32[1,2]{1,0:T(1,128)S(1)}, f32[1,2]{1,0:T(1,128)S(1)}, u32[]{:S(2)}, u32[]{:S(2)}) collective-permute-start(f32[1,2]{1,0:T(1,128)S(1)} %pad_maximum_fusion.19), channel_id=1, source_target_pairs={{0,1},{1,0},{2,3},{3,2},{4,5},{5,4},{6,7},{7,6},{8,9},{9,8},{10,11... | collective-permute-start | bytes 32 | tf_op jit(solution)/shard_map/ppermute | solution.py:167
  406.8 11.1 %collective-permute-start.10 = (bf16[3,128,256]{2,1,0:T(8,128)(2,1)S(1)}, bf16[3,128,256]{2,1,0:T(8,128)(2,1)S(1)}, u32[]{:S(2)}, u32[]{:S(2)}) collective-permute-start(bf16[3,128,256]{2,1,0:T(8,128)(2,1)S(1)} %add_convert_fusion.3), channel_id=1, source_target_pairs={{0,16},{8,24},{16,0},{24,8},{1,17},{9,25},{17,1},{25,9},{2,18},{10... | collective-permute-start | bytes 589832 | tf_op jit(solution)/shard_map/ppermute | solution.py:208
  408.3 28.1 %collective-permute-start.31 = (f32[2]{0:T(128)S(1)}, f32[2]{0:T(128)S(1)}, u32[]{:S(2)}, u32[]{:S(2)}) collective-permute-start(f32[2]{0:T(128)S(1)} %fusion.156), channel_id=1, source_target_pairs={{0,2},{1,3},{2,0},{3,1},{4,6},{5,7},{6,4},{7,5},{8,10},{9,11},{10,... | collective-permute-start | bytes 32 | tf_op jit(solution)/shard_map/ppermute | solution.py:167
  417.9 10.2 %collective-permute-start.11 = (bf16[3,128,512]{2,1,0:T(8,128)(2,1)S(1)}, bf16[3,128,512]{2,1,0:T(8,128)(2,1)S(1)}, u32[]{:S(2)}, u32[]{:S(2)}) collective-permute-start(bf16[3,128,512]{2,1,0:T(8,128)(2,1)S(1)} %pad_maximum_fusion.7), channel_id=1, source_target_pairs={{0,8},{8,0},{16,24},{24,16},{1,9},{9,1},{17,25},{25,17},{2,10},{10... | collective-permute-start | bytes 1179656 | tf_op jit(solution)/shard_map/ppermute | solution.py:208
  419.4 3.6 collective-permute-start.29
  429.3 11.4 %collective-permute-start.12 = (bf16[3,128,1024]{2,1,0:T(8,128)(2,1)}, bf16[3,128,1024]{2,1,0:T(8,128)(2,1)}, u32[]{:S(2)}, u32[]{:S(2)}) collective-permute-start(bf16[3,128,1024]{2,1,0:T(8,128)(2,1)} %pad_maximum_fusion.3), channel_id=1, source_target_pairs={{0,4},{4,0},{1,5},{5,1},{2,6},{6,2},{3,7},{7,3},{8,12},{12,8},{9,1... | collective-permute-start | bytes 2359304 | tf_op jit(solution)/shard_map/ppermute | solution.py:492
  450.7 49.5 %collective-permute-start.13 = (f32[3,1,2]{0,2,1:T(2,128)S(1)}, f32[3,1,2]{0,2,1:T(2,128)S(1)}, u32[]{:S(2)}, u32[]{:S(2)}) collective-permute-start(f32[3,1,2]{0,2,1:T(2,128)S(1)} %pad_maximum_fusion.15), channel_id=1, source_target_pairs={{0,1},{1,0},{2,3},{3,2},{4,5},{5,4},{6,7},{7,6},{8,9},{9,8},{10,11... | collective-permute-start | bytes 80 | tf_op jit(solution)/shard_map/ppermute | solution.py:167
  500.2 9.9 %collective-permute-start.15 = (bf16[640,1024]{1,0:T(8,128)(2,1)}, bf16[640,1024]{1,0:T(8,128)(2,1)S(1)}, u32[]{:S(2)}, u32[]{:S(2)}) collective-permute-start(bf16[640,1024]{1,0:T(8,128)(2,1)} %all-reduce.2.cloned.1.call-done), channel_id=1, source_target_pairs={{0,4},{4,0},{1,5},{5,1},{2,6},{6,2},{3,7},{7,3},{8,12},{12,8},{9,1... | collective-permute-start | bytes 3932168 | tf_op jit(solution)/shard_map/ppermute | solution.py:244
  500.2 3.6 collective-permute-start.14
  517.6 32.5 %copy-start.24 = (f32[256,1024]{1,0:T(8,128)}, f32[256,1024]{1,0:T(8,128)S(1)}, u32[]{:S(2)}) copy-start(f32[256,1024]{1,0:T(8,128)S(1)} %get-tuple-element.325) | copy-start | bytes 3145732
  517.6 32.5 %copy-start.25 = (f32[256,1024]{1,0:T(8,128)}, f32[256,1024]{1,0:T(8,128)S(1)}, u32[]{:S(2)}) copy-start(f32[256,1024]{1,0:T(8,128)S(1)} %get-tuple-element.326) | copy-start | bytes 3145732
  519.0 13.7 %collective-permute-start.16 = (f32[1,2]{1,0:T(1,128)S(1)}, f32[1,2]{1,0:T(1,128)S(1)}, u32[]{:S(2)}, u32[]{:S(2)}) collective-permute-start(f32[1,2]{1,0:T(1,128)S(1)} %pad_maximum_fusion.16), channel_id=1, source_target_pairs={{0,1},{1,0},{2,3},{3,2},{4,5},{5,4},{6,7},{7,6},{8,9},{9,8},{10,11... | collective-permute-start | bytes 32 | tf_op jit(solution)/shard_map/ppermute | solution.py:167
  524.3 27.4 %copy-start.12 = (f32[256,2048]{1,0:T(8,128)}, f32[256,2048]{1,0:T(8,128)S(1)}, u32[]{:S(2)}) copy-start(f32[256,2048]{1,0:T(8,128)S(1)} %get-tuple-element.322) | copy-start | bytes 6291460
  524.3 27.4 %copy-start.13 = (f32[256,2048]{1,0:T(8,128)}, f32[256,2048]{1,0:T(8,128)S(1)}, u32[]{:S(2)}) copy-start(f32[256,2048]{1,0:T(8,128)S(1)} %get-tuple-element.323) | copy-start | bytes 6291460
  525.7 9.9 %collective-permute-start.18 = (f32[1,2]{1,0:T(1,128)S(1)}, f32[1,2]{1,0:T(1,128)S(1)}, u32[]{:S(2)}, u32[]{:S(2)}) collective-permute-start(f32[1,2]{1,0:T(1,128)S(1)} %pad_maximum_fusion.17), channel_id=1, source_target_pairs={{0,1},{1,0},{2,3},{3,2},{4,5},{5,4},{6,7},{7,6},{8,9},{9,8},{10,11... | collective-permute-start | bytes 32 | tf_op jit(solution)/shard_map/ppermute | solution.py:167
  530.0 24.1 %copy-start.14 = (f32[512,1024]{1,0:T(8,128)}, f32[512,1024]{1,0:T(8,128)S(1)}, u32[]{:S(2)}) copy-start(f32[512,1024]{1,0:T(8,128)S(1)} %get-tuple-element.319) | copy-start | bytes 6291460
  530.0 24.1 %copy-start.15 = (f32[512,1024]{1,0:T(8,128)}, f32[512,1024]{1,0:T(8,128)S(1)}, u32[]{:S(2)}) copy-start(f32[512,1024]{1,0:T(8,128)S(1)} %get-tuple-element.320) | copy-start | bytes 6291460
  531.3 6.2 %collective-permute-start.20 = (f32[1,2]{1,0:T(1,128)S(1)}, f32[1,2]{1,0:T(1,128)S(1)}, u32[]{:S(2)}, u32[]{:S(2)}) collective-permute-start(f32[1,2]{1,0:T(1,128)S(1)} %pad_maximum_fusion.18), channel_id=1, source_target_pairs={{0,1},{1,0},{2,3},{3,2},{4,5},{5,4},{6,7},{7,6},{8,9},{9,8},{10,11... | collective-permute-start | bytes 32 | tf_op jit(solution)/shard_map/ppermute | solution.py:167
  534.1 6.1 %collective-permute-start.17 = (f32[1,2]{1,0:T(1,128)S(1)}, f32[1,2]{1,0:T(1,128)S(1)}, u32[]{:S(2)}, u32[]{:S(2)}) collective-permute-start(f32[1,2]{1,0:T(1,128)S(1)} %fusion.160), channel_id=1, source_target_pairs={{0,2},{1,3},{2,0},{3,1},{4,6},{5,7},{6,4},{7,5},{8,10},{9,11},{10,... | collective-permute-start | bytes 32 | tf_op jit(solution)/shard_map/ppermute | solution.py:167
  536.9 6.6 %collective-permute-start.19 = (f32[1,2]{1,0:T(1,128)S(1)}, f32[1,2]{1,0:T(1,128)S(1)}, u32[]{:S(2)}, u32[]{:S(2)}) collective-permute-start(f32[1,2]{1,0:T(1,128)S(1)} %fusion.159), channel_id=1, source_target_pairs={{0,2},{1,3},{2,0},{3,1},{4,6},{5,7},{6,4},{7,5},{8,10},{9,11},{10,... | collective-permute-start | bytes 32 | tf_op jit(solution)/shard_map/ppermute | solution.py:167
  538.7 8.2 %collective-permute-start.21 = (f32[1,2]{1,0:T(1,128)S(1)}, f32[1,2]{1,0:T(1,128)S(1)}, u32[]{:S(2)}, u32[]{:S(2)}) collective-permute-start(f32[1,2]{1,0:T(1,128)S(1)} %fusion.158), channel_id=1, source_target_pairs={{0,2},{1,3},{2,0},{3,1},{4,6},{5,7},{6,4},{7,5},{8,10},{9,11},{10,... | collective-permute-start | bytes 32 | tf_op jit(solution)/shard_map/ppermute | solution.py:167
  (53 other events, 223.6 us)
Sparse Core Ops, SparseCore 0:
  10.5 50.1 all-gather.3
  63.1 77.6 all-gather.5
  288.5 63.8 reduce-scatter.2
  355.7 81.9 reduce-scatter.4
  440.8 59.2 all-reduce.1

commit v12 on v11

--- a/solution.py
+++ b/solution.py
@@ -263,18 +263,26 @@
     return shares
 
 
-def lamb_update(weight, moment, second, grad, sum_axes, seq_count):
-    moment_new, second_new, direction = adam_direction(weight, moment, second, grad)
-    sums = jnp.concatenate(
-        [
-            jnp.sum(weight * weight, axis=sum_axes, keepdims=True),
-            jnp.sum(direction * direction, axis=sum_axes, keepdims=True),
-        ],
-        axis=-1,
-    )
-    sums = butterfly_sum(sums, "seq", seq_count)
-    ratio = jnp.sqrt(sums[..., :1]) * lax.rsqrt(sums[..., 1:] + 1e-06)
-    return (weight - step_rate * ratio * direction, moment_new, second_new)
+def lamb_group(entries, seq_count):
+    steps = []
+    flat = []
+    for weight, moment, second, grad, sum_axes in entries:
+        moment_new, second_new, direction = adam_direction(weight, moment, second, grad)
+        weight_sq = jnp.sum(weight * weight, axis=sum_axes, keepdims=True)
+        update_sq = jnp.sum(direction * direction, axis=sum_axes, keepdims=True)
+        steps.append((weight, moment_new, second_new, direction, weight_sq.shape))
+        flat += [weight_sq.reshape(-1), update_sq.reshape(-1)]
+    sums = butterfly_sum(jnp.concatenate(flat), "seq", seq_count)
+    results = []
+    offset = 0
+    for weight, moment_new, second_new, direction, shape in steps:
+        count = flat[len(results) * 2].size
+        weight_sq = sums[offset : offset + count].reshape(shape)
+        update_sq = sums[offset + count : offset + 2 * count].reshape(shape)
+        offset += 2 * count
+        ratio = jnp.sqrt(weight_sq) * lax.rsqrt(update_sq + 1e-06)
+        results.append((weight - step_rate * ratio * direction, moment_new, second_new))
+    return results
 
 
 def adam_direction(weight, moment, second, grad):
@@ -479,15 +487,21 @@
         after=qkv_piece,
     )
     grad_out, grad_up, grad_down = [share.astype(jnp.float32) for share in batch_shares]
-    updated = [
-        lamb_update(w_out, mom_out, var_out, grad_out, None, seq_count),
-        lamb_update(w_up, mom_up, var_up, grad_up, None, seq_count),
-        lamb_update(w_down, mom_down, var_down, grad_down, None, seq_count),
-    ]
-    updated += [
-        lamb_update(w_mod, mom_mod, var_mod, grad_mod_share, None, seq_count),
-        lamb_update(b_mod, mom_bias, var_bias, grad_bias_share, None, seq_count),
-    ]
+    updated = lamb_group(
+        [
+            (w_out, mom_out, var_out, grad_out, None),
+            (w_up, mom_up, var_up, grad_up, None),
+            (w_down, mom_down, var_down, grad_down, None),
+        ],
+        seq_count,
+    )
+    updated += lamb_group(
+        [
+            (w_mod, mom_mod, var_mod, grad_mod_share, None),
+            (b_mod, mom_bias, var_bias, grad_bias_share, None),
+        ],
+        seq_count,
+    )
     qkv_piece = halving_sum(qkv_piece, "z", lax.axis_size("z"))
     qkv_other = lax.ppermute(qkv_piece, "core", [(0, 1), (1, 0)])
     qkv_first = lax.axis_index("core") == 0
@@ -495,7 +509,7 @@
         [jnp.where(qkv_first, qkv_piece, qkv_other), jnp.where(qkv_first, qkv_other, qkv_piece)],
         axis=1,
     ).astype(jnp.float32)
-    updated = [lamb_update(w_qkv, mom_qkv, var_qkv, grad_qkv, (1, 2), seq_count)] + updated
+    updated = lamb_group([(w_qkv, mom_qkv, var_qkv, grad_qkv, (1, 2))], seq_count) + updated
     totals = (grad_qkv, grad_out, grad_up, grad_down, grad_mod_share, grad_bias_share)
     new_masters = [entry[0] for entry in updated]
     new_moments = [entry[1] for entry in updated]

time: 574 us -> 574 us (level)
  waiting for transfers between devices: 169 us -> 180 us
  starting transfers between devices: 68.8 us -> 58.6 us
  other arithmetic: 108 us -> 102 us
    add x14 -> x8, other arithmetic: 13.9 us -> 5.47 us  [butterfly_sum(): values + lax.ppermute(values, axes, [(i, i ^ step) for i in range(size)])]
    ppermute x16 -> x10, starting transfers between devices: 17.5 us -> 10.7 us  [butterfly_sum(): lax.ppermute(values, axes, [(i, i ^ step) for i in range(size)])]
    ppermute x16 -> x10, waiting for transfers between devices: 11.8 us -> 17.4 us  [butterfly_sum(): lax.ppermute(values, axes, [(i, i ^ step) for i in range(size)])]
  transfers between devices with their start and end apart: 45 -> 39, of which waited for: 24 -> 26; matrix products, arithmetic and copies ran while one was open for 35% -> 32% of each run, Pallas kernels for 0% -> 0%
where the time goes in v12:
time: 574 us; the launch traced here: 564 us
  waiting for transfers between devices  180 us (31%)
  other arithmetic  102 us (18%)
  matrix products  102 us (18%)
  local copies, waits for them, and re-layouts  95 us (17%)
  starting transfers between devices  58.6 us (10%)
  between operations  22.6 us (4%)
    psum x1, waiting for transfers between devices, reduce_batch(): piece = lax.psum(piece, 'z')  49.5 us
    ppermute x10, waiting for transfers between devices, doubling_gather(): other = lax.ppermute(blocks, axes, [(i, i ^ step) for i in range(size)])  31.4 us
    sub x6, other arithmetic, lamb_group(): weight - step_rate * ratio * direction  25.6 us
    all_gather x1, waiting for transfers between devices, gather_rows(): return lax.all_gather(piece, ('seq', 'core'), axis=row_axis, tiled=True)  20.3 us
    ppermute x10, waiting for transfers between devices, butterfly_sum(): lax.ppermute(values, axes, [(i, i ^ step) for i in range(size)])  17.4 us
    dot_general x1, matrix products, local(): jnp.einsum('cd,ce->de', silu_all.astype(jnp.float32), grad_mod_all, preci...  17.4 us
    reduce_sum x3, other arithmetic, lamb_group(): update_sq = jnp.sum(direction * direction, axis=sum_axes, keepdims=True)  14.3 us
    ppermute x10, starting transfers between devices, doubling_gather(): other = lax.ppermute(blocks, axes, [(i, i ^ step) for i in range(size)])  14 us
  transfers between devices with their start and end apart: 39, of which 26 were waited for; matrix products, arithmetic and copies ran while one was open for 32% of the time, Pallas kernels for 0%

profile of v12, /device:TPU:0, one launch (start us, length us, event | category | flops | bytes accessed | tf_op | source)
XLA Modules:
  0.0 563.6 jit_solution(2376211698717935357)
XLA Ops:
  14.9 3.0 collective-permute-start.2
  18.0 3.7 fusion.38
  30.4 4.2 collective-permute-done.1
  34.6 2.7 fusion.68
  37.3 2.7 copy-done
  40.4 20.3 %all-gather.4.cloned.1.call-done = bf16[3,1024,1024]{2,1,0:T(8,128)(2,1)} async-done(((bf16[3,128,1024]{2,1,0:T(8,128)(2,1)}), bf16[3,1024,1024]{2,1,0:T(8,128)(2,1)}) %all-gather.4.cloned.1.call-update) | async-done | bytes 6291472 | tf_op jit(solution)/shard_map/all_gather | solution.py:189
  60.6 4.7 slice_bitcast_fusion.3
  65.3 2.9 copy.145
  70.4 3.0 copy.141
  81.0 3.5 all-to-all-start
  86.0 8.1 %all-to-all-done = bf16[256,4,256]{0,2,1:T(8,128)(2,1)S(1)} async-done(((bf16[256,4,256]{0,2,1:T(8,128)(2,1)}), bf16[256,4,256]{0,2,1:T(8,128)(2,1)S(1)}, u32[]{:S(2)}, u32[]{:S(2)}) %all-to-all-start) | async-done | bytes 524320 | tf_op jit(solution)/shard_map/all_to_all | solution.py:359
  94.1 3.5 all-to-all-start.1
  97.6 2.9 fusion.48
  101.4 10.8 %all-to-all-done.1 = bf16[256,4,256]{0,2,1:T(8,128)(2,1)S(1)} async-done(((bf16[256,4,256]{0,2,1:T(8,128)(2,1)}), bf16[256,4,256]{0,2,1:T(8,128)(2,1)S(1)}, u32[]{:S(2)}, u32[]{:S(2)}) %all-to-all-start.1) | async-done | bytes 524320 | tf_op jit(solution)/shard_map/all_to_all | solution.py:360
  112.1 3.6 all-to-all-start.2
  120.3 9.8 %all-to-all-done.2 = bf16[256,4,256]{2,0,1:T(8,128)(2,1)S(1)} async-done(((bf16[256,4,256]{2,0,1:T(8,128)(2,1)}), bf16[256,4,256]{2,0,1:T(8,128)(2,1)S(1)}, u32[]{:S(2)}, u32[]{:S(2)}) %all-to-all-start.2) | async-done | bytes 524320 | tf_op jit(solution)/shard_map/all_to_all | solution.py:361
  132.0 20.0 %while.27 = (s32[]{:T(128)}, bf16[2,512,256]{2,1,0:T(8,128)(2,1)}, f32[2,4,512,1]{2,1,3,0:T(4,128)S(1)}, s32[2]{0:T(128)S(1)}, s32[1024]{0:T(1024)S(1)}, /*index...) while((s32[]{:T(128)}, bf16[2,512,256]{2,1,0:T(8,128)(2,1)}, ...), condition=%wide.region_9.10_spmd, body=%wide.region_6.9_spmd.sunk | while | flops 561117184 | bytes 30485712 | solution.py:111
  137.8 3.3 fusion.177
  147.8 3.3 fusion.177
  152.0 4.2 all-to-all-start.3
  156.2 6.9 %all-to-all-done.3 = bf16[4,256,256]{2,1,0:T(8,128)(2,1)} async-done(((bf16[4,256,256]{2,1,0:T(8,128)(2,1)}), bf16[4,256,256]{2,1,0:T(8,128)(2,1)}, u32[]{:S(2)}, u32[]{:S(2)}) %all-to-all-start.3) | async-done | bytes 524320 | tf_op jit(solution)/shard_map/all_to_all | solution.py:366
  165.1 3.1 slice.158
  168.2 6.0 %fusion.103 = (bf16[8,256,1024]{2,1,0:T(8,128)(2,1)}, bf16[8,256,1024]{2,1,0:T(8,128)(2,1)}) fusion(bf16[8,640,1024]{2,1,0:T(8,128)(2,1)} %bitcast.257), kind=kLoop, calls=%fused_computation.280 | loop fusion | bytes 16777216 | tf_op jit(solution)/shard_map/slice | solution.py:230
  174.2 7.1 %reshape.475 = bf16[1024,2048]{1,0:T(8,128)(2,1)} reshape(bf16[8,256,1024]{2,1,0:T(8,128)(2,1)} %get-tuple-element.343) | data formatting | bytes 8388608 | tf_op jit(solution)/shard_map/reshape | solution.py:230
  181.3 3.9 fusion.102
  190.0 3.9 fusion.87
  197.8 2.8 fusion.101
  204.2 4.5 all-to-all-start.4
  208.8 3.2 fusion.112
  212.0 3.3 fusion.113
  216.3 35.8 %while.28 = (s32[]{:T(128)}, f32[1024,256]{0,1:T(8,128)S(1)}, f32[1024,256]{0,1:T(8,128)S(1)}, bf16[2,512,256]{2,1,0:T(8,128)(2,1)}, s32[2]{0:T(128)S(1)}, /*ind...) while((s32[]{:T(128)}, f32[1024,256]{0,1:T(8,128)S(1)}, ...), condition=%wide.region_16.17_spmd.clone, body=%wide.region_14.16_spmd.clone.sunk | while | flops 1376253952 | bytes 78974200 | solution.py:156
  223.8 4.2 multiply_reduce_fusion.16
  241.6 4.2 multiply_reduce_fusion.16
  252.0 4.1 all-to-all-start.5
  258.0 4.7 all-to-all-done.5
  262.7 3.5 all-to-all-start.6
  269.3 3.4 all-to-all-done.6
  272.7 3.5 all-to-all-start.7
  285.3 3.1 pad_maximum_fusion.1
  296.4 2.7 fusion.45
  299.1 3.3 constant_dynamic-update-slice_fusion.3
  307.4 2.8 fusion.81
  314.4 7.1 %reshape.478 = bf16[8,256,1024]{2,1,0:T(8,128)(2,1)} reshape(bf16[1024,2048]{1,0:T(8,128)(2,1)} %fusion.113) | data formatting | bytes 8388608 | tf_op jit(solution)/shard_map/reshape | solution.py:238
  322.4 11.0 %pad_maximum_fusion = bf16[8,640,1024]{2,1,0:T(8,128)(2,1)} fusion(bf16[8,256,1024]{2,1,0:T(8,128)(2,1)} %bitcast.266, bf16[8,256,1024]{2,1,0:T(8,128)(2,1)} %reshape.478, bf16[8,128,1024]{2,1,0:T(8,128)(2,1)S(1)} %bitcast.258), kind=kLoop, calls=%fused_computation.32 | loop fusion | flops 31457280 | bytes 20971520 | tf_op jit(solution)/shard_map/concatenate | solution.py:239
  333.5 5.4 fusion.51
  344.0 2.7 collective-permute-done.7
  348.3 4.2 collective-permute-done.22
  354.4 16.7 %collective-permute-done.23 = f32[4,3,6144]{2,1,0:T(4,128)S(1)} collective-permute-done((f32[4,3,6144]{2,1,0:T(4,128)S(1)}, f32[4,3,6144]{2,1,0:T(4,128)S(1)}, u32[]{:S(2)}, u32[]{:S(2)}) %collective-permute-start.23) | collective-permute-done | bytes 294944 | tf_op jit(solution)/shard_map/ppermute | solution.py:176
  373.1 10.0 %collective-permute-done.8 = bf16[3,128,512]{2,1,0:T(8,128)(2,1)S(1)} collective-permute-done((bf16[3,128,512]{2,1,0:T(8,128)(2,1)S(1)}, bf16[3,128,512]{2,1,0:T(8,128)(2,1)S(1)}, u32[]{:S(2)}, u32[]{:S(2)}) %collective-permute-start.8) | collective-permute-done | bytes 393248 | tf_op jit(solution)/shard_map/ppermute | solution.py:201
  385.6 17.4 %multiply_reduce_fusion.2 = (f32[]{:T(128)}, f32[]{:T(128)}, f32[256,6144]{1,0:T(8,128)}, f32[256,6144]{1,0:T(8,128)}, f32[256,6144]{1,0:T(8,128)}) fusion(f32[256,6144]{1,0:T(8,128)} %param.44, f32[256,6144]{1,0:T(8,128)} %param.45, f32[256,6144]{1,0:T(8,128)} %param.46, f32[8,3,6144]{2,1,0:T(4,128)S(1)} %pad_maximum_fusion.4, ...), kind=kOutput, calls=%fused_computation.41 | convolution fusion | flops 479748096 | bytes 38350856 | tf_op jit(solution)/shard_map/cd,ce->de/dot_general | solution.py:468
  405.4 2.7 pad_maximum_fusion.16
  408.7 5.8 %collective-permute-done.10 = bf16[3,128,256]{2,1,0:T(8,128)(2,1)S(1)} collective-permute-done((bf16[3,128,256]{2,1,0:T(8,128)(2,1)S(1)}, bf16[3,128,256]{2,1,0:T(8,128)(2,1)S(1)}, u32[]{:S(2)}, u32[]{:S(2)}) %collective-permute-start.10) | collective-permute-done | bytes 196640 | tf_op jit(solution)/shard_map/ppermute | solution.py:208
  414.7 2.7 fusion.152
  417.4 3.6 collective-permute-done.25
  420.9 2.7 fusion.154
  427.5 10.1 %multiply_subtract_fusion = f32[256,6144]{1,0:T(8,128)} fusion(f32[256,6144]{1,0:T(8,128)} %param.44, f32[]{:T(128)} %bitcast.68, f32[256,6144]{1,0:T(8,128)} %get-tuple-element.316, f32[256,6144]{1,0:T(8,128)} %get-tuple-element.315), kind=kLoop, calls=%fused_computation.37 | loop fusion | flops 12582912 | bytes 25165828 | tf_op jit(solution)/shard_map/sub | solution.py:284
  442.3 8.3 %multiply_reduce_fusion.4 = (f32[3]{0:T(128)S(1)}, f32[3]{0:T(128)S(1)}, f32[3,256,1024]{2,1,0:T(8,128)}, f32[3,256,1024]{2,1,0:T(8,128)}, f32[3,256,1024]{2,1,0:T(8,128)}) fusion(f32[3,256,1024]{2,1,0:T(8,128)S(1)} %copy-done.6, f32[3,256,1024]{2,1,0:T(8,128)} %param.33, f32[3,256,1024]{2,1,0:T(8,128)} %param.34, ...), kind=kLoop, calls=%fused_computation.50 | loop fusion | flops 16515066 | bytes 20447256 | tf_op jit(solution)/shard_map/reduce_sum | solution.py:271
  450.6 49.5 %all-reduce.2.cloned.1.call-done = bf16[640,1024]{1,0:T(8,128)(2,1)} async-done(((bf16[640,1024]{1,0:T(8,128)(2,1)}), bf16[640,1024]{1,0:T(8,128)(2,1)}) %all-reduce.2.cloned.1.call-update) | async-done | bytes 1310736 | tf_op jit(solution)/shard_map/psum | solution.py:243
  507.5 6.3 %multiply_subtract_fusion.1 = f32[3,256,1024]{2,1,0:T(8,128)} fusion(f32[3,256,1024]{2,1,0:T(8,128)S(1)} %copy-done.6, f32[3]{0:T(128)S(1)} %rsqrt_multiply_fusion, f32[3,256,1024]{2,1,0:T(8,128)} %get-tuple-element.329, f32[3,256,1024]{2,1,0:T(8,128)} %get-tuple-element.328), kind=kLoop, calls=%fused_computation.46 | loop fusion | flops 6291456 | bytes 12582924 | tf_op jit(solution)/shard_map/sub | solution.py:284
  517.7 4.4 multiply_reduce_fusion.9
  522.1 5.8 %multiply_reduce_fusion.7 = (f32[]{:T(128)}, f32[]{:T(128)}, f32[256,2048]{1,0:T(8,128)}, f32[256,2048]{1,0:T(8,128)}, f32[256,2048]{1,0:T(8,128)}) fusion(f32[256,2048]{1,0:T(8,128)S(1)} %copy-done.8, f32[256,2048]{1,0:T(8,128)S(1)} %copy-done.37, f32[256,2048]{1,0:T(8,128)} %param.40, bf16[128,2048]{1,0:T(8,128)(2,1)S(1)} %copy-done.32, ...), kind=kLoop, calls=%fused_computation.77 | loop fusion | flops 11010046 | bytes 13631496 | tf_op jit(solution)/shard_map/reduce_sum | solution.py:272
  528.0 4.1 multiply_reduce_fusion.5
  532.1 3.9 concatenate.80
  547.8 3.1 multiply_subtract_fusion.4
  (389 shorter events, 166.5 us)
Async XLA Ops:
  7.2 53.4 %all-gather.4.cloned.1.call-start = ((), (), s32[]{:S(2)}) async-start(), calls=%async_computation.10 | async-start | bytes 7077888 | tf_op jit(solution)/shard_map/all_gather | solution.py:189
  9.7 155.4 %all-gather.6.cloned.1.call-start = ((), (), s32[]{:S(2)}) async-start(), calls=%async_computation.14 | async-start | bytes 11796480 | tf_op jit(solution)/shard_map/all_gather | solution.py:225
  11.1 6.8 %copy-start.48 = (f32[3,1024]{1,0:T(4,128)S(1)}, f32[3,1024]{1,0:T(4,128)}, u32[]{:S(2)}) copy-start(f32[3,1024]{1,0:T(4,128)} %param.29) | copy-start | bytes 36868
  14.9 8.7 %collective-permute-start.2 = (bf16[1,1536]{1,0:T(2,128)(2,1)S(1)}, bf16[1,1536]{1,0:T(2,128)(2,1)S(1)}, u32[]{:S(2)}, u32[]{:S(2)}) collective-permute-start(bf16[1,1536]{1,0:T(2,128)(2,1)S(1)} %broadcast_in_dim.128), channel_id=1, source_target_pairs={{0,1},{1,0},{2,3},{3,2},{4,5},{5,4},{6,7},{7,6},{8,9},{9,8},{10,11... | collective-permute-start | bytes 9224 | tf_op jit(solution)/shard_map/ppermute | solution.py:176
  21.7 7.1 %collective-permute-start = (f32[3,6144]{1,0:T(4,128)S(1)}, f32[3,6144]{1,0:T(4,128)S(1)}, u32[]{:S(2)}, u32[]{:S(2)}) collective-permute-start(f32[3,6144]{1,0:T(4,128)S(1)} %fusion.38), channel_id=1, source_target_pairs={{0,1},{1,0},{2,3},{3,2},{4,5},{5,4},{6,7},{7,6},{8,9},{9,8},{10,11... | collective-permute-start | bytes 221192 | tf_op jit(solution)/shard_map/ppermute | solution.py:167
  22.3 15.0 %copy-start.55 = (f32[256]{0:T(256)}, f32[256]{0:T(256)S(1)}, u32[]{:S(2)}) copy-start(f32[256]{0:T(256)S(1)} %broadcast_multiply_fusion.2) | copy-start | bytes 3076
  22.4 14.9 %copy-start.61 = (pred[1024,3]{0,1:T(4,128)(4,1)}, pred[1024,3]{0,1:T(4,128)(4,1)S(1)}, u32[]{:S(2)}) copy-start(pred[1024,3]{0,1:T(4,128)(4,1)S(1)} %fusion.75) | copy-start | bytes 9220
  23.2 55.7 %copy-start.45 = (f32[256,32]{0,1:T(8,128)}, f32[256,32]{0,1:T(8,128)S(1)}, u32[]{:S(2)}) copy-start(f32[256,32]{0,1:T(8,128)S(1)} %get-tuple-element.407) | copy-start | bytes 98308
  23.6 4.0 collective-permute-start.3
  25.3 12.0 %copy-start.59 = (f32[256]{0:T(256)}, f32[256]{0:T(256)S(1)}, u32[]{:S(2)}) copy-start(f32[256]{0:T(256)S(1)} %fusion.82) | copy-start | bytes 3076
  28.9 5.7 %collective-permute-start.1 = (f32[3,6144]{1,0:T(4,128)S(1)}, f32[3,6144]{1,0:T(4,128)S(1)}, u32[]{:S(2)}, u32[]{:S(2)}) collective-permute-start(f32[3,6144]{1,0:T(4,128)S(1)} %add.342), channel_id=1, source_target_pairs={{0,2},{1,3},{2,0},{3,1},{4,6},{5,7},{6,4},{7,5},{8,10},{9,11},{10,... | collective-permute-start | bytes 221192 | tf_op jit(solution)/shard_map/ppermute | solution.py:167
  40.4 57.2 %copy-start.16 = (bf16[256,1024]{1,0:T(8,128)(2,1)}, bf16[256,1024]{1,0:T(8,128)(2,1)S(1)}, u32[]{:S(2)}) copy-start(bf16[256,1024]{1,0:T(8,128)(2,1)S(1)} %fusion.55) | copy-start | bytes 1572868
  81.0 13.1 %all-to-all-start = ((bf16[256,4,256]{0,2,1:T(8,128)(2,1)}), bf16[256,4,256]{0,2,1:T(8,128)(2,1)S(1)}, u32[]{:S(2)}, u32[]{:S(2)}) async-start(bf16[256,4,256]{0,2,1:T(8,128)(2,1)} %convert_element_type.205), calls=%async_computation | async-start | bytes 1048576 | tf_op jit(solution)/shard_map/all_to_all | solution.py:359
  94.1 18.0 %all-to-all-start.1 = ((bf16[256,4,256]{0,2,1:T(8,128)(2,1)}), bf16[256,4,256]{0,2,1:T(8,128)(2,1)S(1)}, u32[]{:S(2)}, u32[]{:S(2)}) async-start(bf16[256,4,256]{0,2,1:T(8,128)(2,1)} %convert_element_type.206), calls=%async_computation.1 | async-start | bytes 1048576 | tf_op jit(solution)/shard_map/all_to_all | solution.py:360
  112.1 18.0 %all-to-all-start.2 = ((bf16[256,4,256]{2,0,1:T(8,128)(2,1)}), bf16[256,4,256]{2,0,1:T(8,128)(2,1)S(1)}, u32[]{:S(2)}, u32[]{:S(2)}) async-start(bf16[256,4,256]{2,0,1:T(8,128)(2,1)} %bitcast.192), calls=%async_computation.2 | async-start | bytes 1048576 | tf_op jit(solution)/shard_map/all_to_all | solution.py:361
  152.0 11.1 %all-to-all-start.3 = ((bf16[4,256,256]{2,1,0:T(8,128)(2,1)}), bf16[4,256,256]{2,1,0:T(8,128)(2,1)}, u32[]{:S(2)}, u32[]{:S(2)}) async-start(bf16[4,256,256]{2,1,0:T(8,128)(2,1)} %bitcast.26), calls=%async_computation.3 | async-start | bytes 1048576 | tf_op jit(solution)/shard_map/all_to_all | solution.py:366
  181.3 8.6 %slice-start = ((s8[6291456]{0:T(1024)(128)(4,1)}), s8[4194304]{0:T(1024)(128)(4,1)S(1)}, s32[]{:S(2)}) async-start(s8[6291456]{0:T(1024)(128)(4,1)} %bitcast.250), calls=%async_computation.15 | async-start | bytes 8388608
  185.2 12.7 %copy-start.4 = (f32[256,1024]{1,0:T(8,128)}, f32[256,1024]{1,0:T(8,128)S(1)}, u32[]{:S(2)}) copy-start(f32[256,1024]{1,0:T(8,128)S(1)} %get-tuple-element.336) | copy-start | bytes 3145732
  185.5 4.5 slice-start.1
  202.6 6.2 %copy-start.21 = (bf16[256,4,256]{0,2,1:T(8,128)(2,1)S(1)}, bf16[256,4,256]{0,2,1:T(8,128)(2,1)}, u32[]{:S(2)}) copy-start(bf16[256,4,256]{0,2,1:T(8,128)(2,1)} %copy.154) | copy-start | bytes 1572868
  204.2 11.2 %all-to-all-start.4 = ((bf16[256,4,256]{2,0,1:T(8,128)(2,1)}), bf16[256,4,256]{2,0,1:T(8,128)(2,1)}, u32[]{:S(2)}, u32[]{:S(2)}) async-start(bf16[256,4,256]{2,0,1:T(8,128)(2,1)} %bitcast.274), calls=%async_computation.4 | async-start | bytes 1048576 | tf_op jit(solution)/shard_map/all_to_all | solution.py:401
  252.0 10.7 %all-to-all-start.5 = ((bf16[4,256,256]{2,1,0:T(8,128)(2,1)}), bf16[4,256,256]{2,1,0:T(8,128)(2,1)S(1)}, u32[]{:S(2)}, u32[]{:S(2)}) async-start(bf16[4,256,256]{2,1,0:T(8,128)(2,1)} %bitcast.275), calls=%async_computation.5 | async-start | bytes 1048576 | tf_op jit(solution)/shard_map/all_to_all | solution.py:416
  262.7 10.0 %all-to-all-start.6 = ((bf16[4,256,256]{1,2,0:T(8,128)(2,1)}), bf16[4,256,256]{1,2,0:T(8,128)(2,1)S(1)}, u32[]{:S(2)}, u32[]{:S(2)}) async-start(bf16[4,256,256]{1,2,0:T(8,128)(2,1)} %bitcast.190), calls=%async_computation.6 | async-start | bytes 1048576 | tf_op jit(solution)/shard_map/all_to_all | solution.py:417
  272.7 10.0 %all-to-all-start.7 = ((bf16[4,256,256]{2,1,0:T(8,128)(2,1)}), bf16[4,256,256]{2,1,0:T(8,128)(2,1)S(1)}, u32[]{:S(2)}, u32[]{:S(2)}) async-start(bf16[4,256,256]{2,1,0:T(8,128)(2,1)} %bitcast.38), calls=%async_computation.7 | async-start | bytes 1048576 | tf_op jit(solution)/shard_map/all_to_all | solution.py:418
  276.2 95.0 %reduce-scatter.3.cloned.1.call-start = ((), (), s32[]{:S(2)}) async-start(), calls=%async_computation.11 | async-start | bytes 7077888 | tf_op jit(solution)/shard_map/reduce_scatter | solution.py:478
  288.4 150.9 %reduce-scatter.5.cloned.1.call-start = ((), (), s32[]{:S(2)}) async-start(), calls=%async_computation.12 | async-start | bytes 11796480 | tf_op jit(solution)/shard_map/reduce_scatter | solution.py:240
  289.1 1.2 collective-permute-start.18
  290.3 3.7 collective-permute-start.19
  310.2 11.2 %collective-permute-start.4 = (f32[3,6144]{1,0:T(4,128)S(1)}, f32[3,6144]{1,0:T(4,128)S(1)}, u32[]{:S(2)}, u32[]{:S(2)}) collective-permute-start(f32[3,6144]{1,0:T(4,128)S(1)} %fusion.81), channel_id=1, source_target_pairs={{0,1},{1,0},{2,3},{3,2},{4,5},{5,4},{6,7},{7,6},{8,9},{9,8},{10,11... | collective-permute-start | bytes 221192 | tf_op jit(solution)/shard_map/ppermute | solution.py:167
  311.9 10.6 %copy-start.10 = (bf16[1024,1024]{1,0:T(8,128)(2,1)S(1)}, bf16[1024,1024]{1,0:T(8,128)(2,1)}, u32[]{:S(2)}) copy-start(bf16[1024,1024]{1,0:T(8,128)(2,1)} %fusion.112) | copy-start | bytes 6291460
  311.9 28.3 %collective-permute-start.20 = (bf16[4,3,256]{2,0,1:T(4,128)(2,1)S(1)}, bf16[4,3,256]{2,0,1:T(4,128)(2,1)S(1)}, u32[]{:S(2)}, u32[]{:S(2)}) collective-permute-start(bf16[4,3,256]{2,0,1:T(4,128)(2,1)S(1)} %pad_maximum_fusion.13), channel_id=1, source_target_pairs={{0,16},{4,20},{8,24},{12,28},{16,0},{20,4},{24,8},{28,12},{1,17},{... | collective-permute-start | bytes 18440 | tf_op jit(solution)/shard_map/ppermute | solution.py:176
  321.5 12.0 %collective-permute-start.5 = (f32[3,6144]{1,0:T(4,128)S(1)}, f32[3,6144]{1,0:T(4,128)S(1)}, u32[]{:S(2)}, u32[]{:S(2)}) collective-permute-start(f32[3,6144]{1,0:T(4,128)S(1)} %add.368), channel_id=1, source_target_pairs={{0,2},{1,3},{2,0},{3,1},{4,6},{5,7},{6,4},{7,5},{8,10},{9,11},{10,... | collective-permute-start | bytes 221192 | tf_op jit(solution)/shard_map/ppermute | solution.py:167
  333.5 20.3 %copy-start.49 = (f32[3,1024]{1,0:T(4,128)S(1)}, f32[3,1024]{1,0:T(4,128)}, u32[]{:S(2)}) copy-start(f32[3,1024]{1,0:T(4,128)} %param.29) | copy-start | bytes 36868
  333.5 166.6 %all-reduce.2.cloned.1.call-start = ((), (), s32[]{:S(2)}) async-start(), calls=%async_computation.13 | async-start | bytes 2621440 | tf_op jit(solution)/shard_map/psum | solution.py:243
  339.0 3.6 collective-permute-start.6
  342.6 4.0 collective-permute-start.7
  343.9 2.8 collective-permute-start.21
  346.8 5.7 %collective-permute-start.22 = (f32[2,3,6144]{2,1,0:T(4,128)S(1)}, f32[2,3,6144]{2,1,0:T(4,128)S(1)}, u32[]{:S(2)}, u32[]{:S(2)}) collective-permute-start(f32[2,3,6144]{2,1,0:T(4,128)S(1)} %pad_maximum_fusion.9), channel_id=1, source_target_pairs={{0,8},{4,12},{8,0},{12,4},{16,24},{20,28},{24,16},{28,20},{1,9},{5... | collective-permute-start | bytes 442376 | tf_op jit(solution)/shard_map/ppermute | solution.py:176
  352.7 18.4 %collective-permute-start.23 = (f32[4,3,6144]{2,1,0:T(4,128)S(1)}, f32[4,3,6144]{2,1,0:T(4,128)S(1)}, u32[]{:S(2)}, u32[]{:S(2)}) collective-permute-start(f32[4,3,6144]{2,1,0:T(4,128)S(1)} %pad_maximum_fusion.8), channel_id=1, source_target_pairs={{0,16},{4,20},{8,24},{12,28},{16,0},{20,4},{24,8},{28,12},{1,17},{... | collective-permute-start | bytes 884744 | tf_op jit(solution)/shard_map/ppermute | solution.py:176
  372.8 10.3 %collective-permute-start.8 = (bf16[3,128,512]{2,1,0:T(8,128)(2,1)S(1)}, bf16[3,128,512]{2,1,0:T(8,128)(2,1)S(1)}, u32[]{:S(2)}, u32[]{:S(2)}) collective-permute-start(bf16[3,128,512]{2,1,0:T(8,128)(2,1)S(1)} %select_convert_fusion), channel_id=1, source_target_pairs={{0,8},{8,0},{16,24},{24,16},{1,9},{9,1},{17,25},{25,17},{2,10},{10... | collective-permute-start | bytes 1179656 | tf_op jit(solution)/shard_map/ppermute | solution.py:201
  383.3 20.0 %collective-permute-start.9 = (bf16[3,128,256]{2,1,0:T(8,128)(2,1)S(1)}, bf16[3,128,256]{2,1,0:T(8,128)(2,1)S(1)}, u32[]{:S(2)}, u32[]{:S(2)}) collective-permute-start(bf16[3,128,256]{2,1,0:T(8,128)(2,1)S(1)} %select_convert_fusion.1), channel_id=1, source_target_pairs={{0,16},{8,24},{16,0},{24,8},{1,17},{9,25},{17,1},{25,9},{2,18},{10... | collective-permute-start | bytes 589832 | tf_op jit(solution)/shard_map/ppermute | solution.py:201
  385.6 18.6 %copy-start.51 = (f32[1536]{0:T(1024)S(1)}, f32[1536]{0:T(1024)}, u32[]{:S(2)}) copy-start(f32[1536]{0:T(1024)} %param.47) | copy-start | bytes 18436
  385.6 18.6 %copy-start.62 = (f32[1536]{0:T(1024)S(1)}, f32[1536]{0:T(1024)}, u32[]{:S(2)}) copy-start(f32[1536]{0:T(1024)} %param.48) | copy-start | bytes 18436
  385.6 18.6 %copy-start.63 = (f32[1536]{0:T(1024)S(1)}, f32[1536]{0:T(1024)}, u32[]{:S(2)}) copy-start(f32[1536]{0:T(1024)} %param.49) | copy-start | bytes 18436
  403.3 34.3 %copy-start.54 = (f32[1536]{0:T(1024)}, f32[1536]{0:T(1024)S(1)}, u32[]{:S(2)}) copy-start(f32[1536]{0:T(1024)S(1)} %dynamic-slice_reduce_fusion) | copy-start | bytes 18436
  403.4 11.1 %collective-permute-start.10 = (bf16[3,128,256]{2,1,0:T(8,128)(2,1)S(1)}, bf16[3,128,256]{2,1,0:T(8,128)(2,1)S(1)}, u32[]{:S(2)}, u32[]{:S(2)}) collective-permute-start(bf16[3,128,256]{2,1,0:T(8,128)(2,1)S(1)} %add_convert_fusion.3), channel_id=1, source_target_pairs={{0,16},{8,24},{16,0},{24,8},{1,17},{9,25},{17,1},{25,9},{2,18},{10... | collective-permute-start | bytes 589832 | tf_op jit(solution)/shard_map/ppermute | solution.py:208
  408.1 6.6 %collective-permute-start.24 = (f32[4]{0:T(128)S(1)}, f32[4]{0:T(128)S(1)}, u32[]{:S(2)}, u32[]{:S(2)}) collective-permute-start(f32[4]{0:T(128)S(1)} %pad_maximum_fusion.16), channel_id=1, source_target_pairs={{0,1},{1,0},{2,3},{3,2},{4,5},{5,4},{6,7},{7,6},{8,9},{9,8},{10,11... | collective-permute-start | bytes 56 | tf_op jit(solution)/shard_map/ppermute | solution.py:167
  414.6 11.0 %collective-permute-start.11 = (bf16[3,128,512]{2,1,0:T(8,128)(2,1)S(1)}, bf16[3,128,512]{2,1,0:T(8,128)(2,1)S(1)}, u32[]{:S(2)}, u32[]{:S(2)}) collective-permute-start(bf16[3,128,512]{2,1,0:T(8,128)(2,1)S(1)} %pad_maximum_fusion.7), channel_id=1, source_target_pairs={{0,8},{8,0},{16,24},{24,16},{1,9},{9,1},{17,25},{25,17},{2,10},{10... | collective-permute-start | bytes 1179656 | tf_op jit(solution)/shard_map/ppermute | solution.py:208
  417.3 3.6 collective-permute-start.25
  427.5 13.2 %collective-permute-start.12 = (bf16[3,128,1024]{2,1,0:T(8,128)(2,1)}, bf16[3,128,1024]{2,1,0:T(8,128)(2,1)}, u32[]{:S(2)}, u32[]{:S(2)}) collective-permute-start(bf16[3,128,1024]{2,1,0:T(8,128)(2,1)} %pad_maximum_fusion.3), channel_id=1, source_target_pairs={{0,4},{4,0},{1,5},{5,1},{2,6},{6,2},{3,7},{7,3},{8,12},{12,8},{9,1... | collective-permute-start | bytes 2359304 | tf_op jit(solution)/shard_map/ppermute | solution.py:506
  437.6 4.7 copy-start.6
  500.1 13.6 %collective-permute-start.15 = (bf16[640,1024]{1,0:T(8,128)(2,1)}, bf16[640,1024]{1,0:T(8,128)(2,1)S(1)}, u32[]{:S(2)}, u32[]{:S(2)}) collective-permute-start(bf16[640,1024]{1,0:T(8,128)(2,1)} %all-reduce.2.cloned.1.call-done), channel_id=1, source_target_pairs={{0,4},{4,0},{1,5},{5,1},{2,6},{6,2},{3,7},{7,3},{8,12},{12,8},{9,1... | collective-permute-start | bytes 3932168 | tf_op jit(solution)/shard_map/ppermute | solution.py:244
  500.2 3.6 collective-permute-start.13
  503.9 3.6 collective-permute-start.14
  507.5 6.3 %copy-start.41 = (bf16[640,1024]{1,0:T(8,128)(2,1)S(1)}, bf16[640,1024]{1,0:T(8,128)(2,1)}, u32[]{:S(2)}) copy-start(bf16[640,1024]{1,0:T(8,128)(2,1)} %all-reduce.2.cloned.1.call-done) | copy-start | bytes 3932164
  522.1 5.9 %copy-start.7 = (f32[512,1024]{1,0:T(8,128)S(1)}, f32[512,1024]{1,0:T(8,128)}, u32[]{:S(2)}) copy-start(f32[512,1024]{1,0:T(8,128)} %param.41) | copy-start | bytes 6291460
  522.1 5.9 %copy-start.35 = (bf16[256,1024]{1,0:T(8,128)(2,1)S(1)}, bf16[256,1024]{1,0:T(8,128)(2,1)}, u32[]{:S(2)}) copy-start(bf16[256,1024]{1,0:T(8,128)(2,1)} %get-tuple-element.355) | copy-start | bytes 1572868
  522.1 5.9 %copy-start.36 = (bf16[256,1024]{1,0:T(8,128)(2,1)S(1)}, bf16[256,1024]{1,0:T(8,128)(2,1)}, u32[]{:S(2)}) copy-start(bf16[256,1024]{1,0:T(8,128)(2,1)} %get-tuple-element.357) | copy-start | bytes 1572868
  522.1 5.9 %copy-start.38 = (f32[512,1024]{1,0:T(8,128)S(1)}, f32[512,1024]{1,0:T(8,128)}, u32[]{:S(2)}) copy-start(f32[512,1024]{1,0:T(8,128)} %param.42) | copy-start | bytes 6291460
  522.1 5.9 %copy-start.39 = (f32[512,1024]{1,0:T(8,128)S(1)}, f32[512,1024]{1,0:T(8,128)}, u32[]{:S(2)}) copy-start(f32[512,1024]{1,0:T(8,128)} %param.43) | copy-start | bytes 6291460
  535.9 14.9 %copy-start.14 = (f32[512,1024]{1,0:T(8,128)S(1)}, f32[512,1024]{1,0:T(8,128)}, u32[]{:S(2)}) copy-start(f32[512,1024]{1,0:T(8,128)} %get-tuple-element.319) | copy-start | bytes 6291460
  535.9 14.9 %copy-start.15 = (f32[512,1024]{1,0:T(8,128)S(1)}, f32[512,1024]{1,0:T(8,128)}, u32[]{:S(2)}) copy-start(f32[512,1024]{1,0:T(8,128)} %get-tuple-element.320) | copy-start | bytes 6291460
  535.9 3.6 collective-permute-start.16
  539.6 3.6 collective-permute-start.17
  (43 other events, 120.2 us)
Sparse Core Ops, SparseCore 0:
  10.5 50.1 all-gather.3
  63.1 77.6 all-gather.5
  288.5 63.8 reduce-scatter.2
  355.8 81.9 reduce-scatter.4
  440.0 60.0 all-reduce.1

commit v13 on v12

--- a/solution.py
+++ b/solution.py
@@ -487,15 +487,7 @@
         after=qkv_piece,
     )
     grad_out, grad_up, grad_down = [share.astype(jnp.float32) for share in batch_shares]
-    updated = lamb_group(
-        [
-            (w_out, mom_out, var_out, grad_out, None),
-            (w_up, mom_up, var_up, grad_up, None),
-            (w_down, mom_down, var_down, grad_down, None),
-        ],
-        seq_count,
-    )
-    updated += lamb_group(
+    mod_updated = lamb_group(
         [
             (w_mod, mom_mod, var_mod, grad_mod_share, None),
             (b_mod, mom_bias, var_bias, grad_bias_share, None),
@@ -509,7 +501,18 @@
         [jnp.where(qkv_first, qkv_piece, qkv_other), jnp.where(qkv_first, qkv_other, qkv_piece)],
         axis=1,
     ).astype(jnp.float32)
-    updated = lamb_group([(w_qkv, mom_qkv, var_qkv, grad_qkv, (1, 2))], seq_count) + updated
+    updated = (
+        lamb_group(
+            [
+                (w_qkv, mom_qkv, var_qkv, grad_qkv, (1, 2)),
+                (w_out, mom_out, var_out, grad_out, None),
+                (w_up, mom_up, var_up, grad_up, None),
+                (w_down, mom_down, var_down, grad_down, None),
+            ],
+            seq_count,
+        )
+        + mod_updated
+    )
     totals = (grad_qkv, grad_out, grad_up, grad_down, grad_mod_share, grad_bias_share)
     new_masters = [entry[0] for entry in updated]
     new_moments = [entry[1] for entry in updated]

time: 574 us -> 584 us (1.017)
  waiting for transfers between devices: 180 us -> 187 us
  local copies, waits for them, and re-layouts: 95 us -> 101 us
    reduce_sum x3 -> x4, other arithmetic: 14.3 us -> 23.2 us  [lamb_group(): update_sq = jnp.sum(direction * direction, axis=sum_axes, keepdims=True)]
    reduce_sum x2 -> x1, other arithmetic: 9.54 us -> 1.21 us  [lamb_group(): weight_sq = jnp.sum(weight * weight, axis=sum_axes, keepdims=True)]
    reduce_scatter x1, waiting for transfers between devices: 0.02 us -> 7.09 us  [reduce_batch(): lax.psum_scatter(flat, ('seq', 'core'), scatter_dimension=0, tiled=True)[0]]
    ppermute x10 -> x8, waiting for transfers between devices: 17.4 us -> 18.9 us  [butterfly_sum(): lax.ppermute(values, axes, [(i, i ^ step) for i in range(size)])]
  transfers between devices with their start and end apart: 39 -> 37, of which waited for: 26 -> 26; matrix products, arithmetic and copies ran while one was open for 32% -> 30% of each run, Pallas kernels for 0% -> 0%
where the time goes in v13:
time: 584 us; the launch traced here: 573 us
  waiting for transfers between devices  187 us (32%)
  other arithmetic  103 us (18%)
  local copies, waits for them, and re-layouts  101 us (17%)
  matrix products  99.2 us (17%)
  starting transfers between devices  57.5 us (10%)
  between operations  22.9 us (4%)
    psum x1, waiting for transfers between devices, reduce_batch(): piece = lax.psum(piece, 'z')  50.8 us
    ppermute x10, waiting for transfers between devices, doubling_gather(): other = lax.ppermute(blocks, axes, [(i, i ^ step) for i in range(size)])  29.1 us
    sub x6, other arithmetic, lamb_group(): weight - step_rate * ratio * direction  24.5 us
    reduce_sum x4, other arithmetic, lamb_group(): update_sq = jnp.sum(direction * direction, axis=sum_axes, keepdims=True)  23.2 us
    all_gather x1, waiting for transfers between devices, gather_rows(): return lax.all_gather(piece, ('seq', 'core'), axis=row_axis, tiled=True)  20.3 us
    ppermute x8, waiting for transfers between devices, butterfly_sum(): lax.ppermute(values, axes, [(i, i ^ step) for i in range(size)])  18.9 us
    dot_general x1, matrix products, local(): jnp.einsum('cd,ce->de', silu_all.astype(jnp.float32), grad_mod_all, preci...  17.7 us
    ppermute x10, starting transfers between devices, doubling_gather(): other = lax.ppermute(blocks, axes, [(i, i ^ step) for i in range(size)])  14.8 us
  transfers between devices with their start and end apart: 37, of which 26 were waited for; matrix products, arithmetic and copies ran while one was open for 30% of the time, Pallas kernels for 0%

profile of v13, /device:TPU:0, one launch (start us, length us, event | category | flops | bytes accessed | tf_op | source)
XLA Modules:
  0.0 573.3 jit_solution(12726504084665292571)
XLA Ops:
  14.9 3.0 collective-permute-start.2
  18.0 3.7 fusion.38
  30.4 4.2 collective-permute-done.1
  34.6 2.7 fusion.68
  37.3 2.7 copy-done
  40.4 20.3 %all-gather.4.cloned.1.call-done = bf16[3,1024,1024]{2,1,0:T(8,128)(2,1)} async-done(((bf16[3,128,1024]{2,1,0:T(8,128)(2,1)}), bf16[3,1024,1024]{2,1,0:T(8,128)(2,1)}) %all-gather.4.cloned.1.call-update) | async-done | bytes 6291472 | tf_op jit(solution)/shard_map/all_gather | solution.py:189
  60.6 4.7 slice_bitcast_fusion.3
  65.3 2.9 copy.145
  70.4 3.0 copy.141
  81.0 3.5 all-to-all-start
  86.0 8.1 %all-to-all-done = bf16[256,4,256]{0,2,1:T(8,128)(2,1)S(1)} async-done(((bf16[256,4,256]{0,2,1:T(8,128)(2,1)}), bf16[256,4,256]{0,2,1:T(8,128)(2,1)S(1)}, u32[]{:S(2)}, u32[]{:S(2)}) %all-to-all-start) | async-done | bytes 524320 | tf_op jit(solution)/shard_map/all_to_all | solution.py:359
  94.1 3.5 all-to-all-start.1
  97.6 2.9 fusion.48
  101.4 10.8 %all-to-all-done.1 = bf16[256,4,256]{0,2,1:T(8,128)(2,1)S(1)} async-done(((bf16[256,4,256]{0,2,1:T(8,128)(2,1)}), bf16[256,4,256]{0,2,1:T(8,128)(2,1)S(1)}, u32[]{:S(2)}, u32[]{:S(2)}) %all-to-all-start.1) | async-done | bytes 524320 | tf_op jit(solution)/shard_map/all_to_all | solution.py:360
  112.1 3.6 all-to-all-start.2
  120.3 9.8 %all-to-all-done.2 = bf16[256,4,256]{2,0,1:T(8,128)(2,1)S(1)} async-done(((bf16[256,4,256]{2,0,1:T(8,128)(2,1)}), bf16[256,4,256]{2,0,1:T(8,128)(2,1)S(1)}, u32[]{:S(2)}, u32[]{:S(2)}) %all-to-all-start.2) | async-done | bytes 524320 | tf_op jit(solution)/shard_map/all_to_all | solution.py:361
  132.0 20.0 %while.27 = (s32[]{:T(128)}, bf16[2,512,256]{2,1,0:T(8,128)(2,1)}, f32[2,4,512,1]{2,1,3,0:T(4,128)S(1)}, s32[2]{0:T(128)S(1)}, s32[1024]{0:T(1024)S(1)}, /*index...) while((s32[]{:T(128)}, bf16[2,512,256]{2,1,0:T(8,128)(2,1)}, ...), condition=%wide.region_9.10_spmd, body=%wide.region_6.9_spmd.sunk | while | flops 561117184 | bytes 30485712 | solution.py:111
  137.8 3.3 fusion.176
  147.8 3.3 fusion.176
  152.0 4.1 all-to-all-start.3
  156.2 6.9 %all-to-all-done.3 = bf16[4,256,256]{2,1,0:T(8,128)(2,1)} async-done(((bf16[4,256,256]{2,1,0:T(8,128)(2,1)}), bf16[4,256,256]{2,1,0:T(8,128)(2,1)}, u32[]{:S(2)}, u32[]{:S(2)}) %all-to-all-start.3) | async-done | bytes 524320 | tf_op jit(solution)/shard_map/all_to_all | solution.py:366
  165.1 3.1 slice.158
  168.2 6.0 %fusion.103 = (bf16[8,256,1024]{2,1,0:T(8,128)(2,1)}, bf16[8,256,1024]{2,1,0:T(8,128)(2,1)}) fusion(bf16[8,640,1024]{2,1,0:T(8,128)(2,1)} %bitcast.259), kind=kLoop, calls=%fused_computation.279 | loop fusion | bytes 16777216 | tf_op jit(solution)/shard_map/slice | solution.py:230
  174.2 7.1 %reshape.475 = bf16[1024,2048]{1,0:T(8,128)(2,1)} reshape(bf16[8,256,1024]{2,1,0:T(8,128)(2,1)} %get-tuple-element.343) | data formatting | bytes 8388608 | tf_op jit(solution)/shard_map/reshape | solution.py:230
  181.3 3.9 fusion.102
  190.0 3.9 fusion.87
  197.9 2.8 fusion.101
  204.3 4.5 all-to-all-start.4
  208.9 3.2 fusion.112
  212.1 3.3 fusion.113
  216.3 35.8 %while.28 = (s32[]{:T(128)}, f32[1024,256]{0,1:T(8,128)S(1)}, f32[1024,256]{0,1:T(8,128)S(1)}, bf16[2,512,256]{2,1,0:T(8,128)(2,1)}, s32[2]{0:T(128)S(1)}, /*ind...) while((s32[]{:T(128)}, f32[1024,256]{0,1:T(8,128)S(1)}, ...), condition=%wide.region_16.17_spmd.clone, body=%wide.region_14.16_spmd.clone.sunk | while | flops 1376253952 | bytes 78974200 | solution.py:156
  223.9 4.2 multiply_reduce_fusion.16
  241.7 4.2 multiply_reduce_fusion.16
  252.1 4.1 all-to-all-start.5
  258.0 4.7 all-to-all-done.5
  262.7 3.5 all-to-all-start.6
  269.3 3.4 all-to-all-done.6
  272.7 3.5 all-to-all-start.7
  287.1 3.1 pad_maximum_fusion.1
  293.7 7.3 %reshape.478 = bf16[8,256,1024]{2,1,0:T(8,128)(2,1)} reshape(bf16[1024,2048]{1,0:T(8,128)(2,1)} %fusion.113) | data formatting | bytes 8388608 | tf_op jit(solution)/shard_map/reshape | solution.py:238
  301.0 11.4 %pad_maximum_fusion = bf16[8,640,1024]{2,1,0:T(8,128)(2,1)} fusion(bf16[8,256,1024]{2,1,0:T(8,128)(2,1)} %bitcast.268, bf16[8,256,1024]{2,1,0:T(8,128)(2,1)} %reshape.478, bf16[8,128,1024]{2,1,0:T(8,128)(2,1)S(1)} %bitcast.260), kind=kLoop, calls=%fused_computation.32 | loop fusion | flops 31457280 | bytes 20971520 | tf_op jit(solution)/shard_map/concatenate | solution.py:239
  318.4 2.9 constant_dynamic-update-slice_fusion.3
  326.1 3.1 fusion.81
  330.8 5.2 collective-permute-done.4
  343.6 3.4 collective-permute-done.6
  352.7 4.5 collective-permute-done.20
  360.5 15.6 %collective-permute-done.21 = f32[4,3,6144]{2,1,0:T(4,128)S(1)} collective-permute-done((f32[4,3,6144]{2,1,0:T(4,128)S(1)}, f32[4,3,6144]{2,1,0:T(4,128)S(1)}, u32[]{:S(2)}, u32[]{:S(2)}) %collective-permute-start.21) | collective-permute-done | bytes 294944 | tf_op jit(solution)/shard_map/ppermute | solution.py:176
  378.3 9.7 %collective-permute-done.8 = bf16[3,128,512]{2,1,0:T(8,128)(2,1)S(1)} collective-permute-done((bf16[3,128,512]{2,1,0:T(8,128)(2,1)S(1)}, bf16[3,128,512]{2,1,0:T(8,128)(2,1)S(1)}, u32[]{:S(2)}, u32[]{:S(2)}) %collective-permute-start.8) | collective-permute-done | bytes 393248 | tf_op jit(solution)/shard_map/ppermute | solution.py:201
  388.2 2.7 collective-permute-start.9
  391.0 17.7 %multiply_reduce_fusion.2 = (f32[]{:T(128)}, f32[]{:T(128)}, f32[256,6144]{1,0:T(8,128)}, f32[256,6144]{1,0:T(8,128)}, f32[256,6144]{1,0:T(8,128)}) fusion(f32[256,6144]{1,0:T(8,128)} %param.44, f32[256,6144]{1,0:T(8,128)} %param.45, f32[256,6144]{1,0:T(8,128)} %param.46, f32[8,3,6144]{2,1,0:T(4,128)S(1)} %pad_maximum_fusion.4, ...), kind=kOutput, calls=%fused_computation.41 | convolution fusion | flops 479748096 | bytes 38350856 | tf_op jit(solution)/shard_map/cd,ce->de/dot_general | solution.py:468
  413.8 6.4 %collective-permute-done.10 = bf16[3,128,256]{2,1,0:T(8,128)(2,1)S(1)} collective-permute-done((bf16[3,128,256]{2,1,0:T(8,128)(2,1)S(1)}, bf16[3,128,256]{2,1,0:T(8,128)(2,1)S(1)}, u32[]{:S(2)}, u32[]{:S(2)}) %collective-permute-start.10) | collective-permute-done | bytes 196640 | tf_op jit(solution)/shard_map/ppermute | solution.py:208
  420.4 2.7 fusion.152
  423.4 3.3 collective-permute-done.23
  433.3 7.1 %reduce-scatter.5.cloned.1.call-done = bf16[1,640,1024]{2,1,0:T(8,128)(2,1)} async-done(((bf16[8,640,1024]{2,1,0:T(8,128)(2,1)}), bf16[1,640,1024]{2,1,0:T(8,128)(2,1)}) %reduce-scatter.5.cloned.1.call-update) | async-done | bytes 1310736 | tf_op jit(solution)/shard_map/reduce_scatter | solution.py:240
  440.4 9.9 %multiply_subtract_fusion = f32[256,6144]{1,0:T(8,128)} fusion(f32[256,6144]{1,0:T(8,128)} %param.44, f32[]{:T(128)} %bitcast.68, f32[256,6144]{1,0:T(8,128)} %get-tuple-element.316, f32[256,6144]{1,0:T(8,128)} %get-tuple-element.315), kind=kLoop, calls=%fused_computation.37 | loop fusion | flops 12582912 | bytes 25165828 | tf_op jit(solution)/shard_map/sub | solution.py:284
  452.0 50.8 %all-reduce.2.cloned.1.call-done = bf16[640,1024]{1,0:T(8,128)(2,1)} async-done(((bf16[640,1024]{1,0:T(8,128)(2,1)}), bf16[640,1024]{1,0:T(8,128)(2,1)}) %all-reduce.2.cloned.1.call-update) | async-done | bytes 1310736 | tf_op jit(solution)/shard_map/psum | solution.py:243
  505.7 8.5 %multiply_reduce_fusion.3 = (f32[3]{0:T(128)S(1)}, f32[3]{0:T(128)S(1)}, f32[3,256,1024]{2,1,0:T(8,128)}, f32[3,256,1024]{2,1,0:T(8,128)}, f32[3,256,1024]{2,1,0:T(8,128)}) fusion(f32[3,256,1024]{2,1,0:T(8,128)S(1)} %copy-done.6, f32[3,256,1024]{2,1,0:T(8,128)} %param.33, f32[3,256,1024]{2,1,0:T(8,128)} %param.34, ...), kind=kLoop, calls=%fused_computation.47 | loop fusion | flops 16515066 | bytes 20447256 | tf_op jit(solution)/shard_map/reduce_sum | solution.py:272
  521.3 4.8 multiply_reduce_fusion.9
  526.1 5.8 %multiply_reduce_fusion.7 = (f32[]{:T(128)}, f32[]{:T(128)}, f32[256,2048]{1,0:T(8,128)}, f32[256,2048]{1,0:T(8,128)}, f32[256,2048]{1,0:T(8,128)}) fusion(f32[256,2048]{1,0:T(8,128)S(1)} %copy-done.11, f32[256,2048]{1,0:T(8,128)S(1)} %copy-done.41, f32[256,2048]{1,0:T(8,128)} %param.40, bf16[128,2048]{1,0:T(8,128)(2,1)S(1)} %copy-done.33, ...), kind=kLoop, calls=%fused_computation.77 | loop fusion | flops 11010046 | bytes 13631496 | tf_op jit(solution)/shard_map/reduce_sum | solution.py:272
  531.9 4.1 multiply_reduce_fusion.5
  536.0 3.9 concatenate.76
  552.0 3.4 multiply_subtract_fusion.4
  555.5 4.2 multiply_subtract_fusion.2
  563.2 3.3 multiply_subtract_fusion.1
  (411 shorter events, 170.3 us)
Async XLA Ops:
  7.2 53.4 %all-gather.4.cloned.1.call-start = ((), (), s32[]{:S(2)}) async-start(), calls=%async_computation.10 | async-start | bytes 7077888 | tf_op jit(solution)/shard_map/all_gather | solution.py:189
  9.7 155.4 %all-gather.6.cloned.1.call-start = ((), (), s32[]{:S(2)}) async-start(), calls=%async_computation.14 | async-start | bytes 11796480 | tf_op jit(solution)/shard_map/all_gather | solution.py:225
  11.1 6.8 %copy-start.53 = (f32[3,1024]{1,0:T(4,128)S(1)}, f32[3,1024]{1,0:T(4,128)}, u32[]{:S(2)}) copy-start(f32[3,1024]{1,0:T(4,128)} %param.29) | copy-start | bytes 36868
  14.9 8.7 %collective-permute-start.2 = (bf16[1,1536]{1,0:T(2,128)(2,1)S(1)}, bf16[1,1536]{1,0:T(2,128)(2,1)S(1)}, u32[]{:S(2)}, u32[]{:S(2)}) collective-permute-start(bf16[1,1536]{1,0:T(2,128)(2,1)S(1)} %broadcast_in_dim.128), channel_id=1, source_target_pairs={{0,1},{1,0},{2,3},{3,2},{4,5},{5,4},{6,7},{7,6},{8,9},{9,8},{10,11... | collective-permute-start | bytes 9224 | tf_op jit(solution)/shard_map/ppermute | solution.py:176
  21.7 7.1 %collective-permute-start = (f32[3,6144]{1,0:T(4,128)S(1)}, f32[3,6144]{1,0:T(4,128)S(1)}, u32[]{:S(2)}, u32[]{:S(2)}) collective-permute-start(f32[3,6144]{1,0:T(4,128)S(1)} %fusion.38), channel_id=1, source_target_pairs={{0,1},{1,0},{2,3},{3,2},{4,5},{5,4},{6,7},{7,6},{8,9},{9,8},{10,11... | collective-permute-start | bytes 221192 | tf_op jit(solution)/shard_map/ppermute | solution.py:167
  22.3 15.0 %copy-start.61 = (f32[256]{0:T(256)}, f32[256]{0:T(256)S(1)}, u32[]{:S(2)}) copy-start(f32[256]{0:T(256)S(1)} %broadcast_multiply_fusion.2) | copy-start | bytes 3076
  22.4 14.9 %copy-start.73 = (pred[1024,3]{0,1:T(4,128)(4,1)}, pred[1024,3]{0,1:T(4,128)(4,1)S(1)}, u32[]{:S(2)}) copy-start(pred[1024,3]{0,1:T(4,128)(4,1)S(1)} %fusion.75) | copy-start | bytes 9220
  23.2 55.7 %copy-start.50 = (f32[256,32]{0,1:T(8,128)}, f32[256,32]{0,1:T(8,128)S(1)}, u32[]{:S(2)}) copy-start(f32[256,32]{0,1:T(8,128)S(1)} %get-tuple-element.407) | copy-start | bytes 98308
  23.6 4.0 collective-permute-start.3
  25.3 12.0 %copy-start.69 = (f32[256]{0:T(256)}, f32[256]{0:T(256)S(1)}, u32[]{:S(2)}) copy-start(f32[256]{0:T(256)S(1)} %fusion.82) | copy-start | bytes 3076
  28.9 5.7 collective-permute-start.1
  40.4 57.2 %copy-start.18 = (bf16[256,1024]{1,0:T(8,128)(2,1)}, bf16[256,1024]{1,0:T(8,128)(2,1)S(1)}, u32[]{:S(2)}) copy-start(bf16[256,1024]{1,0:T(8,128)(2,1)S(1)} %fusion.55) | copy-start | bytes 1572868
  81.0 13.1 %all-to-all-start = ((bf16[256,4,256]{0,2,1:T(8,128)(2,1)}), bf16[256,4,256]{0,2,1:T(8,128)(2,1)S(1)}, u32[]{:S(2)}, u32[]{:S(2)}) async-start(bf16[256,4,256]{0,2,1:T(8,128)(2,1)} %convert_element_type.205), calls=%async_computation | async-start | bytes 1048576 | tf_op jit(solution)/shard_map/all_to_all | solution.py:359
  94.1 18.0 %all-to-all-start.1 = ((bf16[256,4,256]{0,2,1:T(8,128)(2,1)}), bf16[256,4,256]{0,2,1:T(8,128)(2,1)S(1)}, u32[]{:S(2)}, u32[]{:S(2)}) async-start(bf16[256,4,256]{0,2,1:T(8,128)(2,1)} %convert_element_type.206), calls=%async_computation.1 | async-start | bytes 1048576 | tf_op jit(solution)/shard_map/all_to_all | solution.py:360
  112.1 18.0 %all-to-all-start.2 = ((bf16[256,4,256]{2,0,1:T(8,128)(2,1)}), bf16[256,4,256]{2,0,1:T(8,128)(2,1)S(1)}, u32[]{:S(2)}, u32[]{:S(2)}) async-start(bf16[256,4,256]{2,0,1:T(8,128)(2,1)} %bitcast.192), calls=%async_computation.2 | async-start | bytes 1048576 | tf_op jit(solution)/shard_map/all_to_all | solution.py:361
  152.0 11.1 %all-to-all-start.3 = ((bf16[4,256,256]{2,1,0:T(8,128)(2,1)}), bf16[4,256,256]{2,1,0:T(8,128)(2,1)}, u32[]{:S(2)}, u32[]{:S(2)}) async-start(bf16[4,256,256]{2,1,0:T(8,128)(2,1)} %bitcast.26), calls=%async_computation.3 | async-start | bytes 1048576 | tf_op jit(solution)/shard_map/all_to_all | solution.py:366
  181.3 8.6 %slice-start.2 = ((s8[6291456]{0:T(1024)(128)(4,1)}), s8[4194304]{0:T(1024)(128)(4,1)S(1)}, s32[]{:S(2)}) async-start(s8[6291456]{0:T(1024)(128)(4,1)} %bitcast.252), calls=%async_computation.17 | async-start | bytes 8388608
  185.2 12.7 %copy-start.4 = (f32[256,1024]{1,0:T(8,128)}, f32[256,1024]{1,0:T(8,128)S(1)}, u32[]{:S(2)}) copy-start(f32[256,1024]{1,0:T(8,128)S(1)} %get-tuple-element.336) | copy-start | bytes 3145732
  185.2 12.7 %copy-start.63 = (f32[256]{0:T(256)}, f32[256]{0:T(256)S(1)}, u32[]{:S(2)}) copy-start(f32[256]{0:T(256)S(1)} %broadcast_multiply_fusion.1) | copy-start | bytes 3076
  185.4 12.4 %copy-start.65 = (f32[256]{0:T(256)}, f32[256]{0:T(256)S(1)}, u32[]{:S(2)}) copy-start(f32[256]{0:T(256)S(1)} %fusion.83) | copy-start | bytes 3076
  202.7 6.2 %copy-start.22 = (bf16[256,4,256]{0,2,1:T(8,128)(2,1)S(1)}, bf16[256,4,256]{0,2,1:T(8,128)(2,1)}, u32[]{:S(2)}) copy-start(bf16[256,4,256]{0,2,1:T(8,128)(2,1)} %copy.154) | copy-start | bytes 1572868
  204.3 11.2 %all-to-all-start.4 = ((bf16[256,4,256]{2,0,1:T(8,128)(2,1)}), bf16[256,4,256]{2,0,1:T(8,128)(2,1)}, u32[]{:S(2)}, u32[]{:S(2)}) async-start(bf16[256,4,256]{2,0,1:T(8,128)(2,1)} %bitcast.276), calls=%async_computation.4 | async-start | bytes 1048576 | tf_op jit(solution)/shard_map/all_to_all | solution.py:401
  252.1 10.7 %all-to-all-start.5 = ((bf16[4,256,256]{2,1,0:T(8,128)(2,1)}), bf16[4,256,256]{2,1,0:T(8,128)(2,1)S(1)}, u32[]{:S(2)}, u32[]{:S(2)}) async-start(bf16[4,256,256]{2,1,0:T(8,128)(2,1)} %bitcast.277), calls=%async_computation.5 | async-start | bytes 1048576 | tf_op jit(solution)/shard_map/all_to_all | solution.py:416
  262.7 10.0 %all-to-all-start.6 = ((bf16[4,256,256]{1,2,0:T(8,128)(2,1)}), bf16[4,256,256]{1,2,0:T(8,128)(2,1)S(1)}, u32[]{:S(2)}, u32[]{:S(2)}) async-start(bf16[4,256,256]{1,2,0:T(8,128)(2,1)} %bitcast.190), calls=%async_computation.6 | async-start | bytes 1048576 | tf_op jit(solution)/shard_map/all_to_all | solution.py:417
  272.7 10.0 %all-to-all-start.7 = ((bf16[4,256,256]{2,1,0:T(8,128)(2,1)}), bf16[4,256,256]{2,1,0:T(8,128)(2,1)S(1)}, u32[]{:S(2)}, u32[]{:S(2)}) async-start(bf16[4,256,256]{2,1,0:T(8,128)(2,1)} %bitcast.38), calls=%async_computation.7 | async-start | bytes 1048576 | tf_op jit(solution)/shard_map/all_to_all | solution.py:418
  276.3 100.0 %reduce-scatter.3.cloned.1.call-start = ((), (), s32[]{:S(2)}) async-start(), calls=%async_computation.11 | async-start | bytes 7077888 | tf_op jit(solution)/shard_map/reduce_scatter | solution.py:478
  282.1 8.1 %copy-start.39 = (bf16[256,1024]{0,1:T(8,128)(2,1)}, bf16[256,1024]{0,1:T(8,128)(2,1)S(1)}, u32[]{:S(2)}) copy-start(bf16[256,1024]{0,1:T(8,128)(2,1)S(1)} %convert_element_type.229) | copy-start | bytes 1572868
  290.3 150.1 %reduce-scatter.5.cloned.1.call-start = ((), (), s32[]{:S(2)}) async-start(), calls=%async_computation.12 | async-start | bytes 11796480 | tf_op jit(solution)/shard_map/reduce_scatter | solution.py:240
  290.9 1.2 collective-permute-start.16
  292.2 8.9 %copy-start.13 = (bf16[1024,1024]{1,0:T(8,128)(2,1)S(1)}, bf16[1024,1024]{1,0:T(8,128)(2,1)}, u32[]{:S(2)}) copy-start(bf16[1024,1024]{1,0:T(8,128)(2,1)} %fusion.112) | copy-start | bytes 6291460
  292.2 38.6 %collective-permute-start.17 = (bf16[2,3,256]{2,0,1:T(2,128)(2,1)S(1)}, bf16[2,3,256]{2,0,1:T(2,128)(2,1)S(1)}, u32[]{:S(2)}, u32[]{:S(2)}) collective-permute-start(bf16[2,3,256]{2,0,1:T(2,128)(2,1)S(1)} %pad_maximum_fusion.14), channel_id=1, source_target_pairs={{0,8},{4,12},{8,0},{12,4},{16,24},{20,28},{24,16},{28,20},{1,9},{5... | collective-permute-start | bytes 9224 | tf_op jit(solution)/shard_map/ppermute | solution.py:176
  312.5 190.3 %all-reduce.2.cloned.1.call-start = ((), (), s32[]{:S(2)}) async-start(), calls=%async_computation.13 | async-start | bytes 2621440 | tf_op jit(solution)/shard_map/psum | solution.py:243
  324.7 16.1 %slice-start = ((s8[6291456]{0:T(1024)(128)(4,1)}), s8[4194304]{0:T(1024)(128)(4,1)S(1)}, s32[]{:S(2)}) async-start(s8[6291456]{0:T(1024)(128)(4,1)} %bitcast.250), calls=%async_computation.15 | async-start | bytes 8388608
  326.0 14.8 %slice-start.1 = ((s8[6291456]{0:T(1024)(128)(4,1)}), s8[2097152]{0:T(1024)(128)(4,1)S(1)}, s32[]{:S(2)}) async-start(s8[6291456]{0:T(1024)(128)(4,1)} %bitcast.250), calls=%async_computation.16 | async-start | bytes 4194304
  329.2 6.8 %collective-permute-start.4 = (f32[3,6144]{1,0:T(4,128)S(1)}, f32[3,6144]{1,0:T(4,128)S(1)}, u32[]{:S(2)}, u32[]{:S(2)}) collective-permute-start(f32[3,6144]{1,0:T(4,128)S(1)} %fusion.81), channel_id=1, source_target_pairs={{0,1},{1,0},{2,3},{3,2},{4,5},{5,4},{6,7},{7,6},{8,9},{9,8},{10,11... | collective-permute-start | bytes 221192 | tf_op jit(solution)/shard_map/ppermute | solution.py:167
  336.1 4.7 collective-permute-start.5
  337.6 22.2 %copy-start.54 = (f32[3,1024]{1,0:T(4,128)S(1)}, f32[3,1024]{1,0:T(4,128)}, u32[]{:S(2)}) copy-start(f32[3,1024]{1,0:T(4,128)} %param.29) | copy-start | bytes 36868
  337.6 6.0 %collective-permute-start.18 = (bf16[4,3,256]{2,0,1:T(4,128)(2,1)S(1)}, bf16[4,3,256]{2,0,1:T(4,128)(2,1)S(1)}, u32[]{:S(2)}, u32[]{:S(2)}) collective-permute-start(bf16[4,3,256]{2,0,1:T(4,128)(2,1)S(1)} %pad_maximum_fusion.13), channel_id=1, source_target_pairs={{0,16},{4,20},{8,24},{12,28},{16,0},{20,4},{24,8},{28,12},{1,17},{... | collective-permute-start | bytes 18440 | tf_op jit(solution)/shard_map/ppermute | solution.py:176
  343.3 3.8 collective-permute-start.6
  347.1 4.0 collective-permute-start.7
  348.7 2.4 collective-permute-start.19
  351.2 6.0 %collective-permute-start.20 = (f32[2,3,6144]{2,1,0:T(4,128)S(1)}, f32[2,3,6144]{2,1,0:T(4,128)S(1)}, u32[]{:S(2)}, u32[]{:S(2)}) collective-permute-start(f32[2,3,6144]{2,1,0:T(4,128)S(1)} %pad_maximum_fusion.9), channel_id=1, source_target_pairs={{0,8},{4,12},{8,0},{12,4},{16,24},{20,28},{24,16},{28,20},{1,9},{5... | collective-permute-start | bytes 442376 | tf_op jit(solution)/shard_map/ppermute | solution.py:176
  357.4 18.7 %collective-permute-start.21 = (f32[4,3,6144]{2,1,0:T(4,128)S(1)}, f32[4,3,6144]{2,1,0:T(4,128)S(1)}, u32[]{:S(2)}, u32[]{:S(2)}) collective-permute-start(f32[4,3,6144]{2,1,0:T(4,128)S(1)} %pad_maximum_fusion.8), channel_id=1, source_target_pairs={{0,16},{4,20},{8,24},{12,28},{16,0},{20,4},{24,8},{28,12},{1,17},{... | collective-permute-start | bytes 884744 | tf_op jit(solution)/shard_map/ppermute | solution.py:176
  377.7 10.3 %collective-permute-start.8 = (bf16[3,128,512]{2,1,0:T(8,128)(2,1)S(1)}, bf16[3,128,512]{2,1,0:T(8,128)(2,1)S(1)}, u32[]{:S(2)}, u32[]{:S(2)}) collective-permute-start(bf16[3,128,512]{2,1,0:T(8,128)(2,1)S(1)} %select_convert_fusion), channel_id=1, source_target_pairs={{0,8},{8,0},{16,24},{24,16},{1,9},{9,1},{17,25},{25,17},{2,10},{10... | collective-permute-start | bytes 1179656 | tf_op jit(solution)/shard_map/ppermute | solution.py:201
  388.2 20.8 %collective-permute-start.9 = (bf16[3,128,256]{2,1,0:T(8,128)(2,1)S(1)}, bf16[3,128,256]{2,1,0:T(8,128)(2,1)S(1)}, u32[]{:S(2)}, u32[]{:S(2)}) collective-permute-start(bf16[3,128,256]{2,1,0:T(8,128)(2,1)S(1)} %select_convert_fusion.1), channel_id=1, source_target_pairs={{0,16},{8,24},{16,0},{24,8},{1,17},{9,25},{17,1},{25,9},{2,18},{10... | collective-permute-start | bytes 589832 | tf_op jit(solution)/shard_map/ppermute | solution.py:201
  391.0 18.2 %copy-start.56 = (f32[1536]{0:T(1024)S(1)}, f32[1536]{0:T(1024)}, u32[]{:S(2)}) copy-start(f32[1536]{0:T(1024)} %param.47) | copy-start | bytes 18436
  391.0 18.2 %copy-start.74 = (f32[1536]{0:T(1024)S(1)}, f32[1536]{0:T(1024)}, u32[]{:S(2)}) copy-start(f32[1536]{0:T(1024)} %param.48) | copy-start | bytes 18436
  391.0 18.2 %copy-start.75 = (f32[1536]{0:T(1024)S(1)}, f32[1536]{0:T(1024)}, u32[]{:S(2)}) copy-start(f32[1536]{0:T(1024)} %param.49) | copy-start | bytes 18436
  409.0 31.4 %copy-start.59 = (f32[1536]{0:T(1024)}, f32[1536]{0:T(1024)S(1)}, u32[]{:S(2)}) copy-start(f32[1536]{0:T(1024)S(1)} %dynamic-slice_reduce_fusion) | copy-start | bytes 18436
  409.1 11.1 %collective-permute-start.10 = (bf16[3,128,256]{2,1,0:T(8,128)(2,1)S(1)}, bf16[3,128,256]{2,1,0:T(8,128)(2,1)S(1)}, u32[]{:S(2)}, u32[]{:S(2)}) collective-permute-start(bf16[3,128,256]{2,1,0:T(8,128)(2,1)S(1)} %add_convert_fusion.3), channel_id=1, source_target_pairs={{0,16},{8,24},{16,0},{24,8},{1,17},{9,25},{17,1},{25,9},{2,18},{10... | collective-permute-start | bytes 589832 | tf_op jit(solution)/shard_map/ppermute | solution.py:208
  413.1 7.2 %collective-permute-start.22 = (f32[4]{0:T(128)S(1)}, f32[4]{0:T(128)S(1)}, u32[]{:S(2)}, u32[]{:S(2)}) collective-permute-start(f32[4]{0:T(128)S(1)} %pad_maximum_fusion.15), channel_id=1, source_target_pairs={{0,1},{1,0},{2,3},{3,2},{4,5},{5,4},{6,7},{7,6},{8,9},{9,8},{10,11... | collective-permute-start | bytes 56 | tf_op jit(solution)/shard_map/ppermute | solution.py:167
  420.3 11.1 %collective-permute-start.11 = (bf16[3,128,512]{2,1,0:T(8,128)(2,1)S(1)}, bf16[3,128,512]{2,1,0:T(8,128)(2,1)S(1)}, u32[]{:S(2)}, u32[]{:S(2)}) collective-permute-start(bf16[3,128,512]{2,1,0:T(8,128)(2,1)S(1)} %pad_maximum_fusion.7), channel_id=1, source_target_pairs={{0,8},{8,0},{16,24},{24,16},{1,9},{9,1},{17,25},{25,17},{2,10},{10... | collective-permute-start | bytes 1179656 | tf_op jit(solution)/shard_map/ppermute | solution.py:208
  423.0 3.7 collective-permute-start.23
  433.3 70.8 %collective-permute-start.12 = (bf16[3,128,1024]{2,1,0:T(8,128)(2,1)}, bf16[3,128,1024]{2,1,0:T(8,128)(2,1)}, u32[]{:S(2)}, u32[]{:S(2)}) collective-permute-start(bf16[3,128,1024]{2,1,0:T(8,128)(2,1)} %pad_maximum_fusion.3), channel_id=1, source_target_pairs={{0,4},{4,0},{1,5},{5,1},{2,6},{6,2},{3,7},{7,3},{8,12},{12,8},{9,1... | collective-permute-start | bytes 2359304 | tf_op jit(solution)/shard_map/ppermute | solution.py:498
  440.4 62.3 %copy-start.60 = (f32[1536]{0:T(1024)S(1)}, f32[1536]{0:T(1024)}, u32[]{:S(2)}) copy-start(f32[1536]{0:T(1024)} %get-tuple-element.317) | copy-start | bytes 18436
  450.4 55.4 %copy-start.6 = (f32[3,256,1024]{2,1,0:T(8,128)S(1)}, f32[3,256,1024]{2,1,0:T(8,128)}, u32[]{:S(2)}) copy-start(f32[3,256,1024]{2,1,0:T(8,128)} %param.32) | copy-start | bytes 9437188
  502.8 11.5 %collective-permute-start.13 = (bf16[640,1024]{1,0:T(8,128)(2,1)}, bf16[640,1024]{1,0:T(8,128)(2,1)S(1)}, u32[]{:S(2)}, u32[]{:S(2)}) collective-permute-start(bf16[640,1024]{1,0:T(8,128)(2,1)} %all-reduce.2.cloned.1.call-done), channel_id=1, source_target_pairs={{0,4},{4,0},{1,5},{5,1},{2,6},{6,2},{3,7},{7,3},{8,12},{12,8},{9,1... | collective-permute-start | bytes 3932168 | tf_op jit(solution)/shard_map/ppermute | solution.py:244
  505.7 8.5 %copy-start.45 = (bf16[640,1024]{1,0:T(8,128)(2,1)S(1)}, bf16[640,1024]{1,0:T(8,128)(2,1)}, u32[]{:S(2)}) copy-start(bf16[640,1024]{1,0:T(8,128)(2,1)} %all-reduce.2.cloned.1.call-done) | copy-start | bytes 3932164
  526.1 5.9 %copy-start.9 = (f32[512,1024]{1,0:T(8,128)S(1)}, f32[512,1024]{1,0:T(8,128)}, u32[]{:S(2)}) copy-start(f32[512,1024]{1,0:T(8,128)} %param.41) | copy-start | bytes 6291460
  526.1 5.8 %copy-start.37 = (bf16[256,1024]{1,0:T(8,128)(2,1)S(1)}, bf16[256,1024]{1,0:T(8,128)(2,1)}, u32[]{:S(2)}) copy-start(bf16[256,1024]{1,0:T(8,128)(2,1)} %get-tuple-element.355) | copy-start | bytes 1572868
  540.0 15.5 %copy-start.10 = (f32[512,1024]{1,0:T(8,128)S(1)}, f32[512,1024]{1,0:T(8,128)}, u32[]{:S(2)}) copy-start(f32[512,1024]{1,0:T(8,128)} %param.41) | copy-start | bytes 6291460
  540.0 15.5 %copy-start.17 = (f32[512,1024]{1,0:T(8,128)S(1)}, f32[512,1024]{1,0:T(8,128)}, u32[]{:S(2)}) copy-start(f32[512,1024]{1,0:T(8,128)} %get-tuple-element.319) | copy-start | bytes 6291460
  540.0 3.6 collective-permute-start.14
  543.6 3.6 collective-permute-start.15
  (55 other events, 160.9 us)
Sparse Core Ops, SparseCore 0:
  10.5 50.1 all-gather.3
  63.1 77.6 all-gather.5
  290.4 64.6 reduce-scatter.2
  358.5 81.8 reduce-scatter.4
  442.6 60.1 all-reduce.1

commit v14 on v12

--- a/solution.py
+++ b/solution.py
@@ -243,20 +243,18 @@
     piece = lax.psum(piece, "z")
     other = lax.ppermute(piece, "core", [(0, 1), (1, 0)])
     first = lax.axis_index("core") == 0
-    low = jnp.where(first, piece, other)
-    high = jnp.where(first, other, piece)
     shares = []
     offset = 0
     for part, view in zip(partials, views):
         rows = view.shape[1]
         shape = (-1, part.shape[1])
+        mine = piece[offset : offset + rows].reshape(shape)
+        theirs = other[offset : offset + rows].reshape(shape)
         shares.append(
-            jnp.concatenate(
-                [
-                    low[offset : offset + rows].reshape(shape),
-                    high[offset : offset + rows].reshape(shape),
-                ],
-                axis=0,
+            jnp.where(
+                first,
+                jnp.concatenate([mine, theirs], axis=0),
+                jnp.concatenate([theirs, mine], axis=0),
             )
         )
         offset += rows

time: 574 us -> 573 us (level)
  transfers between devices with their start and end apart: 39 -> 39, of which waited for: 26 -> 25; matrix products, arithmetic and copies ran while one was open for 32% -> 32% of each run, Pallas kernels for 0% -> 0%
where the time goes in v14:
time: 573 us; the launch traced here: 562 us
  waiting for transfers between devices  179 us (31%)
  matrix products  102 us (18%)
  local copies, waits for them, and re-layouts  99.3 us (17%)
  other arithmetic  99.3 us (17%)
  starting transfers between devices  57.1 us (10%)
  between operations  22.6 us (4%)
    psum x1, waiting for transfers between devices, reduce_batch(): piece = lax.psum(piece, 'z')  50.1 us
    ppermute x10, waiting for transfers between devices, doubling_gather(): other = lax.ppermute(blocks, axes, [(i, i ^ step) for i in range(size)])  31.3 us
    sub x6, other arithmetic, lamb_group(): weight - step_rate * ratio * direction  24.9 us
    all_gather x1, waiting for transfers between devices, gather_rows(): return lax.all_gather(piece, ('seq', 'core'), axis=row_axis, tiled=True)  20.3 us
    dot_general x1, matrix products, local(): jnp.einsum('cd,ce->de', silu_all.astype(jnp.float32), grad_mod_all, preci...  17.4 us
    ppermute x10, waiting for transfers between devices, butterfly_sum(): lax.ppermute(values, axes, [(i, i ^ step) for i in range(size)])  15.3 us
    ppermute x10, starting transfers between devices, doubling_gather(): other = lax.ppermute(blocks, axes, [(i, i ^ step) for i in range(size)])  14 us
    reduce_sum x3, other arithmetic, lamb_group(): update_sq = jnp.sum(direction * direction, axis=sum_axes, keepdims=True)  12.7 us
  transfers between devices with their start and end apart: 39, of which 25 were waited for; matrix products, arithmetic and copies ran while one was open for 32% of the time, Pallas kernels for 0%

profile of v14, /device:TPU:0, one launch (start us, length us, event | category | flops | bytes accessed | tf_op | source)
XLA Modules:
  0.0 562.5 jit_solution(12694545608671261944)
XLA Ops:
  14.9 3.0 collective-permute-start.2
  18.0 3.7 fusion.38
  30.4 4.2 collective-permute-done.1
  34.6 2.7 fusion.71
  37.3 2.7 copy-done
  40.4 20.3 %all-gather.4.cloned.1.call-done = bf16[3,1024,1024]{2,1,0:T(8,128)(2,1)} async-done(((bf16[3,128,1024]{2,1,0:T(8,128)(2,1)}), bf16[3,1024,1024]{2,1,0:T(8,128)(2,1)}) %all-gather.4.cloned.1.call-update) | async-done | bytes 6291472 | tf_op jit(solution)/shard_map/all_gather | solution.py:189
  60.6 4.7 slice_bitcast_fusion.3
  65.3 2.9 copy.145
  70.4 3.0 copy.141
  81.0 3.5 all-to-all-start
  86.0 8.1 %all-to-all-done = bf16[256,4,256]{0,2,1:T(8,128)(2,1)S(1)} async-done(((bf16[256,4,256]{0,2,1:T(8,128)(2,1)}), bf16[256,4,256]{0,2,1:T(8,128)(2,1)S(1)}, u32[]{:S(2)}, u32[]{:S(2)}) %all-to-all-start) | async-done | bytes 524320 | tf_op jit(solution)/shard_map/all_to_all | solution.py:357
  94.1 3.5 all-to-all-start.1
  97.6 2.9 fusion.48
  101.4 10.8 %all-to-all-done.1 = bf16[256,4,256]{0,2,1:T(8,128)(2,1)S(1)} async-done(((bf16[256,4,256]{0,2,1:T(8,128)(2,1)}), bf16[256,4,256]{0,2,1:T(8,128)(2,1)S(1)}, u32[]{:S(2)}, u32[]{:S(2)}) %all-to-all-start.1) | async-done | bytes 524320 | tf_op jit(solution)/shard_map/all_to_all | solution.py:358
  112.1 3.6 all-to-all-start.2
  120.3 9.8 %all-to-all-done.2 = bf16[256,4,256]{2,0,1:T(8,128)(2,1)S(1)} async-done(((bf16[256,4,256]{2,0,1:T(8,128)(2,1)}), bf16[256,4,256]{2,0,1:T(8,128)(2,1)S(1)}, u32[]{:S(2)}, u32[]{:S(2)}) %all-to-all-start.2) | async-done | bytes 524320 | tf_op jit(solution)/shard_map/all_to_all | solution.py:359
  132.0 20.0 %while.27 = (s32[]{:T(128)}, bf16[2,512,256]{2,1,0:T(8,128)(2,1)}, f32[2,4,512,1]{2,1,3,0:T(4,128)S(1)}, s32[2]{0:T(128)S(1)}, s32[1024]{0:T(1024)S(1)}, /*index...) while((s32[]{:T(128)}, bf16[2,512,256]{2,1,0:T(8,128)(2,1)}, ...), condition=%wide.region_9.10_spmd, body=%wide.region_6.9_spmd.sunk | while | flops 561117184 | bytes 30485712 | solution.py:111
  137.8 3.3 fusion.183
  147.8 3.3 fusion.183
  152.0 4.1 all-to-all-start.3
  156.2 6.9 %all-to-all-done.3 = bf16[4,256,256]{2,1,0:T(8,128)(2,1)} async-done(((bf16[4,256,256]{2,1,0:T(8,128)(2,1)}), bf16[4,256,256]{2,1,0:T(8,128)(2,1)}, u32[]{:S(2)}, u32[]{:S(2)}) %all-to-all-start.3) | async-done | bytes 524320 | tf_op jit(solution)/shard_map/all_to_all | solution.py:364
  165.1 3.1 slice.158
  168.2 6.0 %fusion.109 = (bf16[8,256,1024]{2,1,0:T(8,128)(2,1)}, bf16[8,256,1024]{2,1,0:T(8,128)(2,1)}) fusion(bf16[8,640,1024]{2,1,0:T(8,128)(2,1)} %bitcast.257), kind=kLoop, calls=%fused_computation.281 | loop fusion | bytes 16777216 | tf_op jit(solution)/shard_map/slice | solution.py:230
  174.2 7.1 %reshape.475 = bf16[1024,2048]{1,0:T(8,128)(2,1)} reshape(bf16[8,256,1024]{2,1,0:T(8,128)(2,1)} %get-tuple-element.343) | data formatting | bytes 8388608 | tf_op jit(solution)/shard_map/reshape | solution.py:230
  181.3 3.9 fusion.108
  189.9 3.9 fusion.90
  197.8 2.8 fusion.107
  204.2 4.5 all-to-all-start.4
  208.8 3.2 fusion.118
  212.0 3.3 fusion.119
  216.2 35.8 %while.28 = (s32[]{:T(128)}, f32[1024,256]{0,1:T(8,128)S(1)}, f32[1024,256]{0,1:T(8,128)S(1)}, bf16[2,512,256]{2,1,0:T(8,128)(2,1)}, s32[2]{0:T(128)S(1)}, /*ind...) while((s32[]{:T(128)}, f32[1024,256]{0,1:T(8,128)S(1)}, ...), condition=%wide.region_16.17_spmd.clone, body=%wide.region_14.16_spmd.clone.sunk | while | flops 1376253952 | bytes 78974200 | solution.py:156
  223.8 4.2 multiply_reduce_fusion.16
  241.6 4.2 multiply_reduce_fusion.16
  252.0 4.1 all-to-all-start.5
  258.0 4.7 all-to-all-done.5
  262.7 3.5 all-to-all-start.6
  269.3 3.4 all-to-all-done.6
  272.7 3.5 all-to-all-start.7
  285.2 3.1 pad_maximum_fusion.1
  296.3 2.7 fusion.45
  299.1 3.3 constant_dynamic-update-slice_fusion.3
  307.3 2.8 fusion.84
  314.3 7.1 %reshape.478 = bf16[8,256,1024]{2,1,0:T(8,128)(2,1)} reshape(bf16[1024,2048]{1,0:T(8,128)(2,1)} %fusion.119) | data formatting | bytes 8388608 | tf_op jit(solution)/shard_map/reshape | solution.py:238
  322.4 11.0 %pad_maximum_fusion = bf16[8,640,1024]{2,1,0:T(8,128)(2,1)} fusion(bf16[8,256,1024]{2,1,0:T(8,128)(2,1)} %bitcast.266, bf16[8,256,1024]{2,1,0:T(8,128)(2,1)} %reshape.478, bf16[8,128,1024]{2,1,0:T(8,128)(2,1)S(1)} %bitcast.258), kind=kLoop, calls=%fused_computation.32 | loop fusion | flops 31457280 | bytes 20971520 | tf_op jit(solution)/shard_map/concatenate | solution.py:239
  333.5 5.4 fusion.51
  343.9 2.7 collective-permute-done.7
  348.3 4.2 collective-permute-done.22
  354.4 16.7 %collective-permute-done.23 = f32[4,3,6144]{2,1,0:T(4,128)S(1)} collective-permute-done((f32[4,3,6144]{2,1,0:T(4,128)S(1)}, f32[4,3,6144]{2,1,0:T(4,128)S(1)}, u32[]{:S(2)}, u32[]{:S(2)}) %collective-permute-start.23) | collective-permute-done | bytes 294944 | tf_op jit(solution)/shard_map/ppermute | solution.py:176
  373.1 10.0 %collective-permute-done.8 = bf16[3,128,512]{2,1,0:T(8,128)(2,1)S(1)} collective-permute-done((bf16[3,128,512]{2,1,0:T(8,128)(2,1)S(1)}, bf16[3,128,512]{2,1,0:T(8,128)(2,1)S(1)}, u32[]{:S(2)}, u32[]{:S(2)}) %collective-permute-start.8) | collective-permute-done | bytes 393248 | tf_op jit(solution)/shard_map/ppermute | solution.py:201
  385.6 17.4 %multiply_reduce_fusion.2 = (f32[]{:T(128)}, f32[]{:T(128)}, f32[256,6144]{1,0:T(8,128)}, f32[256,6144]{1,0:T(8,128)}, f32[256,6144]{1,0:T(8,128)}) fusion(f32[256,6144]{1,0:T(8,128)} %param.44, f32[256,6144]{1,0:T(8,128)} %param.45, f32[256,6144]{1,0:T(8,128)} %param.46, f32[8,3,6144]{2,1,0:T(4,128)S(1)} %pad_maximum_fusion.4, ...), kind=kOutput, calls=%fused_computation.41 | convolution fusion | flops 479748096 | bytes 38350856 | tf_op jit(solution)/shard_map/cd,ce->de/dot_general | solution.py:466
  404.8 2.7 pad_maximum_fusion.16
  408.1 6.4 %collective-permute-done.10 = bf16[3,128,256]{2,1,0:T(8,128)(2,1)S(1)} collective-permute-done((bf16[3,128,256]{2,1,0:T(8,128)(2,1)S(1)}, bf16[3,128,256]{2,1,0:T(8,128)(2,1)S(1)}, u32[]{:S(2)}, u32[]{:S(2)}) %collective-permute-start.10) | collective-permute-done | bytes 196640 | tf_op jit(solution)/shard_map/ppermute | solution.py:208
  414.7 2.7 fusion.158
  417.4 3.6 collective-permute-done.25
  420.9 2.7 fusion.160
  427.5 10.1 %multiply_subtract_fusion = f32[256,6144]{1,0:T(8,128)} fusion(f32[256,6144]{1,0:T(8,128)} %param.44, f32[]{:T(128)} %bitcast.68, f32[256,6144]{1,0:T(8,128)} %get-tuple-element.316, f32[256,6144]{1,0:T(8,128)} %get-tuple-element.315), kind=kLoop, calls=%fused_computation.37 | loop fusion | flops 12582912 | bytes 25165828 | tf_op jit(solution)/shard_map/sub | solution.py:282
  441.6 8.3 %multiply_reduce_fusion.4 = (f32[3]{0:T(128)S(1)}, f32[3]{0:T(128)S(1)}, f32[3,256,1024]{2,1,0:T(8,128)}, f32[3,256,1024]{2,1,0:T(8,128)}, f32[3,256,1024]{2,1,0:T(8,128)}) fusion(f32[3,256,1024]{2,1,0:T(8,128)S(1)} %copy-done.6, f32[3,256,1024]{2,1,0:T(8,128)} %param.33, f32[3,256,1024]{2,1,0:T(8,128)} %param.34, ...), kind=kLoop, calls=%fused_computation.50 | loop fusion | flops 16515066 | bytes 20447256 | tf_op jit(solution)/shard_map/reduce_sum | solution.py:269
  450.0 50.1 %all-reduce.2.cloned.1.call-done = bf16[640,1024]{1,0:T(8,128)(2,1)} async-done(((bf16[640,1024]{1,0:T(8,128)(2,1)}), bf16[640,1024]{1,0:T(8,128)(2,1)}) %all-reduce.2.cloned.1.call-update) | async-done | bytes 1310736 | tf_op jit(solution)/shard_map/psum | solution.py:243
  503.8 6.3 %multiply_subtract_fusion.1 = f32[3,256,1024]{2,1,0:T(8,128)} fusion(f32[3,256,1024]{2,1,0:T(8,128)S(1)} %copy-done.6, f32[3]{0:T(128)S(1)} %rsqrt_multiply_fusion, f32[3,256,1024]{2,1,0:T(8,128)} %get-tuple-element.329, f32[3,256,1024]{2,1,0:T(8,128)} %get-tuple-element.328), kind=kLoop, calls=%fused_computation.46 | loop fusion | flops 6291456 | bytes 12582924 | tf_op jit(solution)/shard_map/sub | solution.py:282
  517.1 4.1 multiply_reduce_fusion.9
  521.3 4.3 multiply_reduce_fusion.7
  526.6 4.2 multiply_reduce_fusion.5
  530.9 3.9 concatenate.92
  546.7 3.1 multiply_subtract_fusion.4
  (396 shorter events, 165.7 us)
Async XLA Ops:
  7.2 53.4 %all-gather.4.cloned.1.call-start = ((), (), s32[]{:S(2)}) async-start(), calls=%async_computation.10 | async-start | bytes 7077888 | tf_op jit(solution)/shard_map/all_gather | solution.py:189
  9.7 155.4 %all-gather.6.cloned.1.call-start = ((), (), s32[]{:S(2)}) async-start(), calls=%async_computation.14 | async-start | bytes 11796480 | tf_op jit(solution)/shard_map/all_gather | solution.py:225
  11.1 6.8 %copy-start.50 = (f32[3,1024]{1,0:T(4,128)S(1)}, f32[3,1024]{1,0:T(4,128)}, u32[]{:S(2)}) copy-start(f32[3,1024]{1,0:T(4,128)} %param.29) | copy-start | bytes 36868
  14.9 8.7 %collective-permute-start.2 = (bf16[1,1536]{1,0:T(2,128)(2,1)S(1)}, bf16[1,1536]{1,0:T(2,128)(2,1)S(1)}, u32[]{:S(2)}, u32[]{:S(2)}) collective-permute-start(bf16[1,1536]{1,0:T(2,128)(2,1)S(1)} %broadcast_in_dim.128), channel_id=1, source_target_pairs={{0,1},{1,0},{2,3},{3,2},{4,5},{5,4},{6,7},{7,6},{8,9},{9,8},{10,11... | collective-permute-start | bytes 9224 | tf_op jit(solution)/shard_map/ppermute | solution.py:176
  21.7 7.1 %collective-permute-start = (f32[3,6144]{1,0:T(4,128)S(1)}, f32[3,6144]{1,0:T(4,128)S(1)}, u32[]{:S(2)}, u32[]{:S(2)}) collective-permute-start(f32[3,6144]{1,0:T(4,128)S(1)} %fusion.38), channel_id=1, source_target_pairs={{0,1},{1,0},{2,3},{3,2},{4,5},{5,4},{6,7},{7,6},{8,9},{9,8},{10,11... | collective-permute-start | bytes 221192 | tf_op jit(solution)/shard_map/ppermute | solution.py:167
  22.3 15.0 %copy-start.59 = (f32[256]{0:T(256)}, f32[256]{0:T(256)S(1)}, u32[]{:S(2)}) copy-start(f32[256]{0:T(256)S(1)} %broadcast_multiply_fusion.2) | copy-start | bytes 3076
  22.4 14.9 %copy-start.65 = (pred[1024,3]{0,1:T(4,128)(4,1)}, pred[1024,3]{0,1:T(4,128)(4,1)S(1)}, u32[]{:S(2)}) copy-start(pred[1024,3]{0,1:T(4,128)(4,1)S(1)} %fusion.78) | copy-start | bytes 9220
  23.2 55.7 %copy-start.47 = (f32[256,32]{0,1:T(8,128)}, f32[256,32]{0,1:T(8,128)S(1)}, u32[]{:S(2)}) copy-start(f32[256,32]{0,1:T(8,128)S(1)} %get-tuple-element.405) | copy-start | bytes 98308
  23.6 4.0 collective-permute-start.3
  25.3 12.0 %copy-start.63 = (f32[256]{0:T(256)}, f32[256]{0:T(256)S(1)}, u32[]{:S(2)}) copy-start(f32[256]{0:T(256)S(1)} %fusion.85) | copy-start | bytes 3076
  28.9 5.7 %collective-permute-start.1 = (f32[3,6144]{1,0:T(4,128)S(1)}, f32[3,6144]{1,0:T(4,128)S(1)}, u32[]{:S(2)}, u32[]{:S(2)}) collective-permute-start(f32[3,6144]{1,0:T(4,128)S(1)} %add.342), channel_id=1, source_target_pairs={{0,2},{1,3},{2,0},{3,1},{4,6},{5,7},{6,4},{7,5},{8,10},{9,11},{10,... | collective-permute-start | bytes 221192 | tf_op jit(solution)/shard_map/ppermute | solution.py:167
  40.4 57.2 %copy-start.16 = (bf16[256,1024]{1,0:T(8,128)(2,1)}, bf16[256,1024]{1,0:T(8,128)(2,1)S(1)}, u32[]{:S(2)}) copy-start(bf16[256,1024]{1,0:T(8,128)(2,1)S(1)} %fusion.55) | copy-start | bytes 1572868
  81.0 13.1 %all-to-all-start = ((bf16[256,4,256]{0,2,1:T(8,128)(2,1)}), bf16[256,4,256]{0,2,1:T(8,128)(2,1)S(1)}, u32[]{:S(2)}, u32[]{:S(2)}) async-start(bf16[256,4,256]{0,2,1:T(8,128)(2,1)} %convert_element_type.205), calls=%async_computation | async-start | bytes 1048576 | tf_op jit(solution)/shard_map/all_to_all | solution.py:357
  94.1 18.0 %all-to-all-start.1 = ((bf16[256,4,256]{0,2,1:T(8,128)(2,1)}), bf16[256,4,256]{0,2,1:T(8,128)(2,1)S(1)}, u32[]{:S(2)}, u32[]{:S(2)}) async-start(bf16[256,4,256]{0,2,1:T(8,128)(2,1)} %convert_element_type.206), calls=%async_computation.1 | async-start | bytes 1048576 | tf_op jit(solution)/shard_map/all_to_all | solution.py:358
  112.1 18.0 %all-to-all-start.2 = ((bf16[256,4,256]{2,0,1:T(8,128)(2,1)}), bf16[256,4,256]{2,0,1:T(8,128)(2,1)S(1)}, u32[]{:S(2)}, u32[]{:S(2)}) async-start(bf16[256,4,256]{2,0,1:T(8,128)(2,1)} %bitcast.192), calls=%async_computation.2 | async-start | bytes 1048576 | tf_op jit(solution)/shard_map/all_to_all | solution.py:359
  152.0 11.1 %all-to-all-start.3 = ((bf16[4,256,256]{2,1,0:T(8,128)(2,1)}), bf16[4,256,256]{2,1,0:T(8,128)(2,1)}, u32[]{:S(2)}, u32[]{:S(2)}) async-start(bf16[4,256,256]{2,1,0:T(8,128)(2,1)} %bitcast.26), calls=%async_computation.3 | async-start | bytes 1048576 | tf_op jit(solution)/shard_map/all_to_all | solution.py:364
  181.3 8.6 %slice-start = ((s8[6291456]{0:T(1024)(128)(4,1)}), s8[4194304]{0:T(1024)(128)(4,1)S(1)}, s32[]{:S(2)}) async-start(s8[6291456]{0:T(1024)(128)(4,1)} %bitcast.250), calls=%async_computation.15 | async-start | bytes 8388608
  185.2 12.7 %copy-start.4 = (f32[256,1024]{1,0:T(8,128)}, f32[256,1024]{1,0:T(8,128)S(1)}, u32[]{:S(2)}) copy-start(f32[256,1024]{1,0:T(8,128)S(1)} %get-tuple-element.336) | copy-start | bytes 3145732
  202.6 6.2 %copy-start.21 = (bf16[256,4,256]{0,2,1:T(8,128)(2,1)S(1)}, bf16[256,4,256]{0,2,1:T(8,128)(2,1)}, u32[]{:S(2)}) copy-start(bf16[256,4,256]{0,2,1:T(8,128)(2,1)} %copy.154) | copy-start | bytes 1572868
  204.2 11.2 %all-to-all-start.4 = ((bf16[256,4,256]{2,0,1:T(8,128)(2,1)}), bf16[256,4,256]{2,0,1:T(8,128)(2,1)}, u32[]{:S(2)}, u32[]{:S(2)}) async-start(bf16[256,4,256]{2,0,1:T(8,128)(2,1)} %bitcast.274), calls=%async_computation.4 | async-start | bytes 1048576 | tf_op jit(solution)/shard_map/all_to_all | solution.py:399
  252.0 10.7 %all-to-all-start.5 = ((bf16[4,256,256]{2,1,0:T(8,128)(2,1)}), bf16[4,256,256]{2,1,0:T(8,128)(2,1)S(1)}, u32[]{:S(2)}, u32[]{:S(2)}) async-start(bf16[4,256,256]{2,1,0:T(8,128)(2,1)} %bitcast.275), calls=%async_computation.5 | async-start | bytes 1048576 | tf_op jit(solution)/shard_map/all_to_all | solution.py:414
  262.7 10.0 %all-to-all-start.6 = ((bf16[4,256,256]{1,2,0:T(8,128)(2,1)}), bf16[4,256,256]{1,2,0:T(8,128)(2,1)S(1)}, u32[]{:S(2)}, u32[]{:S(2)}) async-start(bf16[4,256,256]{1,2,0:T(8,128)(2,1)} %bitcast.190), calls=%async_computation.6 | async-start | bytes 1048576 | tf_op jit(solution)/shard_map/all_to_all | solution.py:415
  272.7 10.0 %all-to-all-start.7 = ((bf16[4,256,256]{2,1,0:T(8,128)(2,1)}), bf16[4,256,256]{2,1,0:T(8,128)(2,1)S(1)}, u32[]{:S(2)}, u32[]{:S(2)}) async-start(bf16[4,256,256]{2,1,0:T(8,128)(2,1)} %bitcast.38), calls=%async_computation.7 | async-start | bytes 1048576 | tf_op jit(solution)/shard_map/all_to_all | solution.py:416
  276.2 95.1 %reduce-scatter.3.cloned.1.call-start = ((), (), s32[]{:S(2)}) async-start(), calls=%async_computation.11 | async-start | bytes 7077888 | tf_op jit(solution)/shard_map/reduce_scatter | solution.py:476
  288.4 151.5 %reduce-scatter.5.cloned.1.call-start = ((), (), s32[]{:S(2)}) async-start(), calls=%async_computation.12 | async-start | bytes 11796480 | tf_op jit(solution)/shard_map/reduce_scatter | solution.py:240
  289.0 1.2 collective-permute-start.18
  290.2 3.7 collective-permute-start.19
  310.2 11.2 %collective-permute-start.4 = (f32[3,6144]{1,0:T(4,128)S(1)}, f32[3,6144]{1,0:T(4,128)S(1)}, u32[]{:S(2)}, u32[]{:S(2)}) collective-permute-start(f32[3,6144]{1,0:T(4,128)S(1)} %fusion.84), channel_id=1, source_target_pairs={{0,1},{1,0},{2,3},{3,2},{4,5},{5,4},{6,7},{7,6},{8,9},{9,8},{10,11... | collective-permute-start | bytes 221192 | tf_op jit(solution)/shard_map/ppermute | solution.py:167
  311.9 10.6 %copy-start.10 = (bf16[1024,1024]{1,0:T(8,128)(2,1)S(1)}, bf16[1024,1024]{1,0:T(8,128)(2,1)}, u32[]{:S(2)}) copy-start(bf16[1024,1024]{1,0:T(8,128)(2,1)} %fusion.118) | copy-start | bytes 6291460
  311.9 28.3 %collective-permute-start.20 = (bf16[4,3,256]{2,0,1:T(4,128)(2,1)S(1)}, bf16[4,3,256]{2,0,1:T(4,128)(2,1)S(1)}, u32[]{:S(2)}, u32[]{:S(2)}) collective-permute-start(bf16[4,3,256]{2,0,1:T(4,128)(2,1)S(1)} %pad_maximum_fusion.13), channel_id=1, source_target_pairs={{0,16},{4,20},{8,24},{12,28},{16,0},{20,4},{24,8},{28,12},{1,17},{... | collective-permute-start | bytes 18440 | tf_op jit(solution)/shard_map/ppermute | solution.py:176
  321.5 12.1 %collective-permute-start.5 = (f32[3,6144]{1,0:T(4,128)S(1)}, f32[3,6144]{1,0:T(4,128)S(1)}, u32[]{:S(2)}, u32[]{:S(2)}) collective-permute-start(f32[3,6144]{1,0:T(4,128)S(1)} %add.368), channel_id=1, source_target_pairs={{0,2},{1,3},{2,0},{3,1},{4,6},{5,7},{6,4},{7,5},{8,10},{9,11},{10,... | collective-permute-start | bytes 221192 | tf_op jit(solution)/shard_map/ppermute | solution.py:167
  333.4 20.3 %copy-start.51 = (f32[3,1024]{1,0:T(4,128)S(1)}, f32[3,1024]{1,0:T(4,128)}, u32[]{:S(2)}) copy-start(f32[3,1024]{1,0:T(4,128)} %param.29) | copy-start | bytes 36868
  333.5 166.6 %all-reduce.2.cloned.1.call-start = ((), (), s32[]{:S(2)}) async-start(), calls=%async_computation.13 | async-start | bytes 2621440 | tf_op jit(solution)/shard_map/psum | solution.py:243
  339.0 3.6 collective-permute-start.6
  342.6 4.0 collective-permute-start.7
  343.9 2.8 collective-permute-start.21
  346.7 5.7 %collective-permute-start.22 = (f32[2,3,6144]{2,1,0:T(4,128)S(1)}, f32[2,3,6144]{2,1,0:T(4,128)S(1)}, u32[]{:S(2)}, u32[]{:S(2)}) collective-permute-start(f32[2,3,6144]{2,1,0:T(4,128)S(1)} %pad_maximum_fusion.9), channel_id=1, source_target_pairs={{0,8},{4,12},{8,0},{12,4},{16,24},{20,28},{24,16},{28,20},{1,9},{5... | collective-permute-start | bytes 442376 | tf_op jit(solution)/shard_map/ppermute | solution.py:176
  352.6 18.4 %collective-permute-start.23 = (f32[4,3,6144]{2,1,0:T(4,128)S(1)}, f32[4,3,6144]{2,1,0:T(4,128)S(1)}, u32[]{:S(2)}, u32[]{:S(2)}) collective-permute-start(f32[4,3,6144]{2,1,0:T(4,128)S(1)} %pad_maximum_fusion.8), channel_id=1, source_target_pairs={{0,16},{4,20},{8,24},{12,28},{16,0},{20,4},{24,8},{28,12},{1,17},{... | collective-permute-start | bytes 884744 | tf_op jit(solution)/shard_map/ppermute | solution.py:176
  372.8 10.3 %collective-permute-start.8 = (bf16[3,128,512]{2,1,0:T(8,128)(2,1)S(1)}, bf16[3,128,512]{2,1,0:T(8,128)(2,1)S(1)}, u32[]{:S(2)}, u32[]{:S(2)}) collective-permute-start(bf16[3,128,512]{2,1,0:T(8,128)(2,1)S(1)} %select_convert_fusion), channel_id=1, source_target_pairs={{0,8},{8,0},{16,24},{24,16},{1,9},{9,1},{17,25},{25,17},{2,10},{10... | collective-permute-start | bytes 1179656 | tf_op jit(solution)/shard_map/ppermute | solution.py:201
  383.3 20.0 %collective-permute-start.9 = (bf16[3,128,256]{2,1,0:T(8,128)(2,1)S(1)}, bf16[3,128,256]{2,1,0:T(8,128)(2,1)S(1)}, u32[]{:S(2)}, u32[]{:S(2)}) collective-permute-start(bf16[3,128,256]{2,1,0:T(8,128)(2,1)S(1)} %select_convert_fusion.1), channel_id=1, source_target_pairs={{0,16},{8,24},{16,0},{24,8},{1,17},{9,25},{17,1},{25,9},{2,18},{10... | collective-permute-start | bytes 589832 | tf_op jit(solution)/shard_map/ppermute | solution.py:201
  385.6 18.6 %copy-start.53 = (f32[1536]{0:T(1024)S(1)}, f32[1536]{0:T(1024)}, u32[]{:S(2)}) copy-start(f32[1536]{0:T(1024)} %param.47) | copy-start | bytes 18436
  385.6 18.6 %copy-start.66 = (f32[1536]{0:T(1024)S(1)}, f32[1536]{0:T(1024)}, u32[]{:S(2)}) copy-start(f32[1536]{0:T(1024)} %param.48) | copy-start | bytes 18436
  385.6 18.6 %copy-start.67 = (f32[1536]{0:T(1024)S(1)}, f32[1536]{0:T(1024)}, u32[]{:S(2)}) copy-start(f32[1536]{0:T(1024)} %param.49) | copy-start | bytes 18436
  403.3 34.3 %copy-start.56 = (f32[1536]{0:T(1024)}, f32[1536]{0:T(1024)S(1)}, u32[]{:S(2)}) copy-start(f32[1536]{0:T(1024)S(1)} %dynamic-slice_reduce_fusion) | copy-start | bytes 18436
  403.4 11.1 %collective-permute-start.10 = (bf16[3,128,256]{2,1,0:T(8,128)(2,1)S(1)}, bf16[3,128,256]{2,1,0:T(8,128)(2,1)S(1)}, u32[]{:S(2)}, u32[]{:S(2)}) collective-permute-start(bf16[3,128,256]{2,1,0:T(8,128)(2,1)S(1)} %add_convert_fusion.3), channel_id=1, source_target_pairs={{0,16},{8,24},{16,0},{24,8},{1,17},{9,25},{17,1},{25,9},{2,18},{10... | collective-permute-start | bytes 589832 | tf_op jit(solution)/shard_map/ppermute | solution.py:208
  404.8 34.5 %copy-start.57 = (f32[1536]{0:T(1024)}, f32[1536]{0:T(1024)S(1)}, u32[]{:S(2)}) copy-start(f32[1536]{0:T(1024)S(1)} %get-tuple-element.317) | copy-start | bytes 18436
  404.8 34.5 %copy-start.58 = (f32[1536]{0:T(1024)}, f32[1536]{0:T(1024)S(1)}, u32[]{:S(2)}) copy-start(f32[1536]{0:T(1024)S(1)} %get-tuple-element.318) | copy-start | bytes 18436
  407.5 7.2 %collective-permute-start.24 = (f32[4]{0:T(128)S(1)}, f32[4]{0:T(128)S(1)}, u32[]{:S(2)}, u32[]{:S(2)}) collective-permute-start(f32[4]{0:T(128)S(1)} %pad_maximum_fusion.16), channel_id=1, source_target_pairs={{0,1},{1,0},{2,3},{3,2},{4,5},{5,4},{6,7},{7,6},{8,9},{9,8},{10,11... | collective-permute-start | bytes 56 | tf_op jit(solution)/shard_map/ppermute | solution.py:167
  414.6 11.0 %collective-permute-start.11 = (bf16[3,128,512]{2,1,0:T(8,128)(2,1)S(1)}, bf16[3,128,512]{2,1,0:T(8,128)(2,1)S(1)}, u32[]{:S(2)}, u32[]{:S(2)}) collective-permute-start(bf16[3,128,512]{2,1,0:T(8,128)(2,1)S(1)} %pad_maximum_fusion.7), channel_id=1, source_target_pairs={{0,8},{8,0},{16,24},{24,16},{1,9},{9,1},{17,25},{25,17},{2,10},{10... | collective-permute-start | bytes 1179656 | tf_op jit(solution)/shard_map/ppermute | solution.py:208
  417.4 3.6 collective-permute-start.25
  427.5 12.5 %collective-permute-start.12 = (bf16[3,128,1024]{2,1,0:T(8,128)(2,1)}, bf16[3,128,1024]{2,1,0:T(8,128)(2,1)}, u32[]{:S(2)}, u32[]{:S(2)}) collective-permute-start(bf16[3,128,1024]{2,1,0:T(8,128)(2,1)} %pad_maximum_fusion.3), channel_id=1, source_target_pairs={{0,4},{4,0},{1,5},{5,1},{2,6},{6,2},{3,7},{7,3},{8,12},{12,8},{9,1... | collective-permute-start | bytes 2359304 | tf_op jit(solution)/shard_map/ppermute | solution.py:504
  450.0 50.1 %collective-permute-start.13 = (f32[6]{0:T(128)S(1)}, f32[6]{0:T(128)S(1)}, u32[]{:S(2)}, u32[]{:S(2)}) collective-permute-start(f32[6]{0:T(128)S(1)} %pad_maximum_fusion.15), channel_id=1, source_target_pairs={{0,1},{1,0},{2,3},{3,2},{4,5},{5,4},{6,7},{7,6},{8,9},{9,8},{10,11... | collective-permute-start | bytes 80 | tf_op jit(solution)/shard_map/ppermute | solution.py:167
  500.1 12.8 %collective-permute-start.15 = (bf16[640,1024]{1,0:T(8,128)(2,1)}, bf16[640,1024]{1,0:T(8,128)(2,1)}, u32[]{:S(2)}, u32[]{:S(2)}) collective-permute-start(bf16[640,1024]{1,0:T(8,128)(2,1)} %all-reduce.2.cloned.1.call-done), channel_id=1, source_target_pairs={{0,4},{4,0},{1,5},{5,1},{2,6},{6,2},{3,7},{7,3},{8,12},{12,8},{9,1... | collective-permute-start | bytes 3932168 | tf_op jit(solution)/shard_map/ppermute | solution.py:244
  500.2 3.6 collective-permute-start.14
  503.8 6.3 %copy-start.42 = (bf16[640,1024]{1,0:T(8,128)(2,1)S(1)}, bf16[640,1024]{1,0:T(8,128)(2,1)}, u32[]{:S(2)}) copy-start(bf16[640,1024]{1,0:T(8,128)(2,1)} %all-reduce.2.cloned.1.call-done) | copy-start | bytes 3932164
  511.0 6.1 %copy-start.18 = (f32[256,1024]{1,0:T(8,128)S(1)}, f32[256,1024]{1,0:T(8,128)}, u32[]{:S(2)}) copy-start(f32[256,1024]{1,0:T(8,128)} %param.35) | copy-start | bytes 3145732
  511.0 6.1 %copy-start.44 = (f32[256,1024]{1,0:T(8,128)S(1)}, f32[256,1024]{1,0:T(8,128)}, u32[]{:S(2)}) copy-start(f32[256,1024]{1,0:T(8,128)} %param.36) | copy-start | bytes 3145732
  515.9 5.3 copy-start.38
  521.3 4.7 copy-start.39
  521.3 5.3 copy-start.40
  534.7 15.0 %copy-start.14 = (f32[512,1024]{1,0:T(8,128)S(1)}, f32[512,1024]{1,0:T(8,128)}, u32[]{:S(2)}) copy-start(f32[512,1024]{1,0:T(8,128)} %get-tuple-element.319) | copy-start | bytes 6291460
  534.7 15.0 %copy-start.15 = (f32[512,1024]{1,0:T(8,128)S(1)}, f32[512,1024]{1,0:T(8,128)}, u32[]{:S(2)}) copy-start(f32[512,1024]{1,0:T(8,128)} %get-tuple-element.320) | copy-start | bytes 6291460
  534.7 3.6 collective-permute-start.16
  538.4 3.6 collective-permute-start.17
  (47 other events, 137.0 us)
Sparse Core Ops, SparseCore 0:
  10.5 50.1 all-gather.3
  63.1 77.6 all-gather.5
  288.5 63.8 reduce-scatter.2
  355.7 81.9 reduce-scatter.4
  440.1 59.9 all-reduce.1
